TPU v7x, 256 devices: a whole 4x4x8 slice. The times are simulated.
256 devices in a mesh: dp: 32 (over y, x, core), seq: 8 (over z).
Axes of the slice: x: 4, y: 4, z: 8, core: 2. Of those that a mesh axis runs over, the one named last changes fastest.
Arguments:
- tokens: bfloat16 [32, 1024, 1024], P('dp', 'seq'), may hold values from -6 to 6
- cotangent: bfloat16 [32, 1024, 1024], P('dp', 'seq'), may hold values from -6 to 6
- stamps: int32 [32, 1024], P('dp'), may hold values from 0 to 1113088, as said below
- lengths: int32 [32], P('dp'), may hold values from 128 to 1024, as said below
- w_qkvu: bfloat16 [1024, 4096], P('dp'), may hold values from -0.1875 to 0.1875
- w_out: bfloat16 [1024, 1024], P('dp'), may hold values from -0.1875 to 0.1875
- gain_in: float32 [1024], replicated, may hold values from 0.25 to 1.75
- gain_out: float32 [1024], replicated, may hold values from 0.25 to 1.75
- bias_table: float32 [8, 16], replicated, may hold values from -4 to 4
Outputs:
- mixed: bfloat16 [32, 1024, 1024], P('dp', 'seq')
- input_grad: bfloat16 [32, 1024, 1024], P('dp', 'seq')
- out_weight_grad: float32 [1024, 1024], P('dp')
Inputs may be any that keep to these rules, and one draw needn't show every extreme that they name: `lengths`: each stream has 128 valid actions or more; some stream is full. `stamps`: timestamps never fall along a stream, and consecutive ones differ by less than 64.
All inputs are finite; a program needn't handle non-finite values.
Results may differ from a plain program's by a relative error of at most 0.019.
Values may be sent and summed in bfloat16 or wider, within the bound.
No kernel may reach another device: no remote copies, remote signals or barrier semaphores. Data moves between devices by JAX's collectives and lax.ppermute only.
A program may use at most 128 MiB of HBM per device.

v0:
```python
import jax
import jax.numpy as jnp
from jax import lax
from jax.experimental import pallas as pl
from jax.experimental.pallas import tpu as pltpu
from jax.sharding import Mesh
from jax.sharding import PartitionSpec as P


H = 8
DH = 128
D = 1024
T = 128
S = 1024
NB = 16
TI = 256
CH = 32
DP = ("dp_0", "dp_1", "dp_2")
EPS = 1e-05
MSG = 144
LIMIT = 48000
F32 = jnp.float32
BF16 = jnp.bfloat16

VMEM = pl.BlockSpec(memory_space=pltpu.VMEM)
SMEM = pl.BlockSpec(memory_space=pltpu.SMEM)


def sigmoid(v):
    return 0.5 * jnp.tanh(0.5 * v) + 0.5


def nt(a, b):
    return lax.dot_general(a, b, (((1,), (1,)), ((), ())), preferred_element_type=F32)


def tn(a, b):
    return lax.dot_general(a, b, (((0,), (0,)), ((), ())), preferred_element_type=F32)


def mm(a, b):
    return jnp.dot(a, b, preferred_element_type=F32)


def norm_kernel(x_ref, gain_ref, a_ref, b_ref):
    x = x_ref[...].astype(F32)
    c = x - jnp.mean(x, axis=-1, keepdims=True)
    var = jnp.mean(c * c, axis=-1, keepdims=True)
    n = (c * lax.rsqrt(var + EPS) * gain_ref[...]).astype(BF16)
    a_ref[...] = n[:64]
    b_ref[...] = n[64:]


ARRIVALS = (
    [(0, 0), (0, 1)]
    + [(-k, 0) for k in (1, 2, 3, 4)]
    + [(-k, 1) for k in (1, 2, 3)]
    + [(k, 0) for k in (1, 2, 3)]
    + [(k, 1) for k in (1, 2, 3, 4)]
)


def forward_kernel(*refs):
    meta, bias_ref = refs[0], refs[1]
    blocks = refs[2:18]
    ws_ref, row_ref = refs[18:20]
    msg_ref, proj_ref, w_ref, g_ref = refs[20:24]
    x_all, col_sc, q_sc, k_sc, vt_sc, s_sc = refs[24:]
    me, length = meta[0], meta[1]
    for (far, half), blk in zip(ARRIVALS, blocks):
        at = lax.rem(me + far + H, H) * T + half * 64
        x_all[pl.ds(pl.multiple_of(at, 64), 64), :] = blk[...]
    proj_ref[...] = mm(x_all[...], ws_ref[...])
    for c in range(8):
        cols = slice(c * T, (c + 1) * T)
        col_sc[cols, :] = jnp.broadcast_to(row_ref[:, cols], (T, T)).T
    for c in range(8):
        rows = slice(c * T, (c + 1) * T)
        p = proj_ref[rows, :]
        a = p * sigmoid(p)
        vt_sc[:, rows] = a[:, :DH].T.astype(BF16)
        q_sc[rows, :] = a[:, DH : 2 * DH].astype(BF16)
        k_sc[rows, :] = a[:, 2 * DH :].astype(BF16)
    scale = DH ** (-0.5)
    levels = [bias_ref[me, b] for b in range(NB)]

    def tile(i0, j0, diagonal):
        s_sc[...] = nt(k_sc[pl.ds(j0, TI), :], q_sc[i0 : i0 + TI, :])
        for c in range(TI // CH):
            rows = pl.ds(j0 + c * CH, CH)
            col = col_sc[rows, :]
            e = row_ref[:, i0 : i0 + TI] - jnp.concatenate([col, col], axis=1)
            bias = jnp.full((CH, TI), levels[0], F32)
            for b in range(1, NB):
                bias = jnp.where(e >= float(2**b - 1), levels[b], bias)
            s = s_sc[c * CH : (c + 1) * CH, :] * scale + bias
            sg = sigmoid(s)
            w = s * sg
            g = sg + w * (1.0 - sg)
            if diagonal:
                jj = lax.broadcasted_iota(jnp.int32, (CH, TI), 0) + c * CH
                ii = lax.broadcasted_iota(jnp.int32, (CH, TI), 1)
                keep = jj <= ii
                w = jnp.where(keep, w, 0.0)
                g = jnp.where(keep, g, 0.0)
            w_ref[rows, i0 : i0 + TI] = w.astype(BF16)
            g_ref[rows, i0 : i0 + TI] = g.astype(BF16)

    for bi in range(S // TI):
        i0 = bi * TI
        if bi:

            def below(bj, carry, i0=i0):
                tile(i0, pl.multiple_of(bj * TI, TI), False)
                return carry

            lax.fori_loop(0, bi, below, 0)
        tile(i0, i0, True)
        att = mm(vt_sc[:, : i0 + TI], w_ref[: i0 + TI, i0 : i0 + TI])
        pos = lax.broadcasted_iota(jnp.int32, (DH, TI), 1) + i0
        att = jnp.where(pos < length, att, 0.0)
        mean = jnp.mean(att, axis=0, keepdims=True)
        high = mean.astype(BF16)
        left = mean - high.astype(F32)
        mid = left.astype(BF16)
        low = (left - mid.astype(F32)).astype(BF16)
        kept = high.astype(F32) + mid.astype(F32) + low.astype(F32)
        centred = (att - kept).astype(BF16)
        which = lax.broadcasted_iota(jnp.int32, (16, TI), 0)
        tail = jnp.where(
            which == 0,
            high.astype(F32),
            jnp.where(which == 1, mid.astype(F32), jnp.where(which == 2, low.astype(F32), 0.0)),
        ).astype(BF16)
        for t in range(TI // T):
            dest = bi * (TI // T) + t
            msg_ref[dest, :DH, :] = centred[:, t * T : (t + 1) * T]
            msg_ref[dest, DH:, :] = tail[:, t * T : (t + 1) * T]


def tail_kernel(
    meta,
    msg_ref,
    na_ref,
    nb_ref,
    x_ref,
    cot_ref,
    wg_ref,
    wo_ref,
    gain_ref,
    mixed_ref,
    datt_ref,
    dpg_ref,
    own_ref,
    send_ref,
    att_sc,
):
    me, length, core = meta[0], meta[1], meta[2]
    for h in range(H):
        blk = msg_ref[h].astype(F32)
        att_t = blk[:DH] + (blk[DH : DH + 1] + blk[DH + 1 : DH + 2] + blk[DH + 2 : DH + 3])
        att_sc[:, h * DH : (h + 1) * DH] = att_t.T
    pg = jnp.concatenate([mm(na_ref[...], wg_ref[...]), mm(nb_ref[...], wg_ref[...])], axis=0)
    cot = cot_ref[...]
    d_mix = nt(cot, wo_ref[...])
    att = att_sc[...]
    gain = gain_ref[...]
    c = att - jnp.mean(att, axis=-1, keepdims=True)
    var = jnp.mean(c * c, axis=-1, keepdims=True)
    r = lax.rsqrt(var + EPS)
    xhat = c * r
    normed_att = xhat * gain
    sg = sigmoid(pg)
    gate = pg * sg
    mixed_rows = (normed_att * gate).astype(BF16)
    mixed_ref[...] = (x_ref[...].astype(F32) + mm(mixed_rows, wo_ref[...])).astype(BF16)
    dpg_ref[...] = (d_mix * normed_att * (sg + gate * (1.0 - sg))).astype(BF16)
    u = d_mix * gate * gain
    d_att = r * (
        u
        - jnp.mean(u, axis=-1, keepdims=True)
        - xhat * jnp.mean(u * xhat, axis=-1, keepdims=True)
    )
    pos = lax.broadcasted_iota(jnp.int32, (T, D), 0) + me * T
    d_att = jnp.where(pos < length, d_att, 0.0).astype(BF16)
    for h in range(H):
        cols = slice(h * DH, (h + 1) * DH)
        datt_ref[h] = d_att[:, cols]
        part = tn(mixed_rows[:, cols], cot).astype(BF16)
        for t in range(2):
            at = slice((2 * h + t) * 32, (2 * h + t + 1) * 32)
            even, odd = part[t * 64 : t * 64 + 32], part[t * 64 + 32 : t * 64 + 64]
            own_ref[at, :] = jnp.where(core == 0, even, odd)
            send_ref[at, :] = jnp.where(core == 0, odd, even)


def gate_kernel(dpg_ref, wg_ref, out_ref):
    out_ref[...] = nt(dpg_ref[...], wg_ref[...])


def backward_kernel(*refs):
    meta, d_ref, proj_ref, w_ref, g_ref = refs[:5]
    outs = refs[5:13]
    q_sc, k_sc, kt_sc, v_sc, ds_sc, dqt_sc, out_ref = refs[13:]
    for c in range(8):
        rows = slice(c * T, (c + 1) * T)
        p = proj_ref[rows, :]
        a = p * sigmoid(p)
        v_sc[rows, :] = a[:, :DH].astype(BF16)
        q_sc[rows, :] = a[:, DH : 2 * DH].astype(BF16)
        k_sc[rows, :] = a[:, 2 * DH :].astype(BF16)
        kt_sc[:, rows] = a[:, 2 * DH :].T.astype(BF16)
    scale = DH ** (-0.5)
    d = d_ref[...].reshape(S, DH)
    for bj in range(S // TI):
        j0 = bj * TI
        rows = slice(j0, j0 + TI)
        dw = nt(v_sc[rows, :], d[j0:, :])
        ds_sc[rows, j0:] = (dw * g_ref[rows, j0:].astype(F32)).astype(BF16)
        dk = mm(ds_sc[rows, j0:], q_sc[j0:, :]) * scale
        dv = mm(w_ref[rows, j0:], d[j0:, :])
        for t in range(TI // T):
            at = slice(j0 + t * T, j0 + (t + 1) * T)
            dest = bj * (TI // T) + t
            for n, grad in ((0, dv), (2, dk)):
                p = proj_ref[at, n * DH : (n + 1) * DH]
                sg = sigmoid(p)
                slope = sg * (1.0 + p * (1.0 - sg))
                out_ref[dest, :, n * DH : (n + 1) * DH] = (
                    grad[t * T : (t + 1) * T] * slope
                ).astype(BF16)
    for bi in range(S // TI):
        i0 = bi * TI
        dqt_sc[:, i0 : i0 + TI] = (
            mm(kt_sc[:, : i0 + TI], ds_sc[: i0 + TI, i0 : i0 + TI]) * scale
        )
    for t in range(8):
        at = slice(t * T, (t + 1) * T)
        p = proj_ref[at, DH : 2 * DH]
        sg = sigmoid(p)
        slope = sg * (1.0 + p * (1.0 - sg))
        out_ref[t, :, DH : 2 * DH] = (dqt_sc[:, at].T * slope).astype(BF16)
    for k in range(H):
        outs[k][...] = out_ref[lax.rem(meta[0] + k, H)]


def final_kernel(*refs):
    meta = refs[0]
    blocks = refs[1:9]
    back_ref, w_ref, x_ref, cot_ref, gain_ref, out_ref, msg_ref, lhs, acc = refs[9:]
    b = pl.program_id(0)

    @pl.when(b == 0)
    def _():
        for k in range(H):
            msg_ref[lax.rem(meta[0] - k + H, H)] = blocks[k][...]
        for n in range(3):
            for h in range(H):
                lhs[n, :, h * DH : (h + 1) * DH] = msg_ref[h, :, n * DH : (n + 1) * DH]
        acc[...] = back_ref[...]

    acc[...] += nt(lhs[b], w_ref[...])

    @pl.when(b == 2)
    def _():
        x = x_ref[...].astype(F32)
        c = x - jnp.mean(x, axis=-1, keepdims=True)
        var = jnp.mean(c * c, axis=-1, keepdims=True)
        r = lax.rsqrt(var + EPS)
        xhat = c * r
        u = acc[...] * gain_ref[...]
        dx = r * (
            u
            - jnp.mean(u, axis=-1, keepdims=True)
            - xhat * jnp.mean(u * xhat, axis=-1, keepdims=True)
        )
        out_ref[...] = (cot_ref[...].astype(F32) + dx).astype(BF16)


def params(**more):
    return pltpu.CompilerParams(vmem_limit_bytes=LIMIT * 1024, **more)


def cost(us):
    flops = int(us * 3.0e8)
    return pl.CostEstimate(flops=flops, bytes_accessed=1 << 20, transcendentals=0)


def paired(value, axis, mask):
    count = lax.axis_size(axis)
    return lax.ppermute(value, axis, [(i, i ^ mask) for i in range(count)])


def shifted(value, by):
    return lax.ppermute(value, "seq", [(i, (i + by) % H) for i in range(H)])


def layer(tokens, cotangent, stamps, lengths, w_qkvu, w_out, gain_in, gain_out, bias_table):
    x = tokens[0]
    cot = cotangent[0]
    me = lax.axis_index("seq")
    core = lax.axis_index("dp_2")
    meta = jnp.stack([me, lengths[0], core]).astype(jnp.int32)
    gain_in = gain_in.reshape(1, D)
    gain_out = gain_out.reshape(1, D)
    stamp_row = stamps.astype(F32)

    na, nb = pl.pallas_call(
        norm_kernel,
        out_shape=[jax.ShapeDtypeStruct((64, D), BF16)] * 2,
        in_specs=[VMEM, VMEM],
        out_specs=[VMEM, VMEM],
        compiler_params=params(),
        cost_estimate=cost(1),
        name="norm",
    )(x, gain_in)

    w_full = lax.all_gather(jnp.concatenate([w_qkvu, w_out], axis=1), DP, axis=0, tiled=True)

    head_w = jnp.concatenate(
        [
            lax.dynamic_slice_in_dim(w_qkvu, part * D + me * DH, DH, axis=1)
            for part in (1, 2, 3)
        ],
        axis=1,
    )
    copies = jnp.broadcast_to(head_w[None], (32, *head_w.shape))
    ws = lax.all_to_all(copies, DP, 0, 0, tiled=True)
    ws = ws.reshape(D, 3 * DH)

    arrived = {(0, 0): na, (0, 1): nb}
    for k in range(1, 5):
        arrived[(-k, 0)] = shifted(arrived[(1 - k, 0)], 1)
        arrived[(k, 1)] = shifted(arrived[(k - 1, 1)], -1)
        if k < 4:
            arrived[(-k, 1)] = shifted(arrived[(1 - k, 1)], 1)
            arrived[(k, 0)] = shifted(arrived[(k - 1, 0)], -1)

    msg, proj, weight, slope = pl.pallas_call(
        forward_kernel,
        out_shape=[
            jax.ShapeDtypeStruct((H, MSG, T), BF16),
            jax.ShapeDtypeStruct((S, 3 * DH), F32),
            jax.ShapeDtypeStruct((S, S), BF16),
            jax.ShapeDtypeStruct((S, S), BF16),
        ],
        in_specs=[SMEM, SMEM] + [VMEM] * 18,
        out_specs=[VMEM] * 4,
        scratch_shapes=[
            pltpu.VMEM((S, D), BF16),
            pltpu.VMEM((S, T), F32),
            pltpu.VMEM((S, DH), BF16),
            pltpu.VMEM((S, DH), BF16),
            pltpu.VMEM((DH, S), BF16),
            pltpu.VMEM((TI, TI), F32),
        ],
        compiler_params=params(),
        cost_estimate=cost(10),
        name="attend",
    )(meta, bias_table, *[arrived[a] for a in ARRIVALS], ws, stamp_row)

    att_msg = lax.all_to_all(msg, "seq", 0, 0, tiled=True)

    mixed, d_att, d_pg, w_own, w_send = pl.pallas_call(
        tail_kernel,
        grid=(1,),
        out_shape=[
            jax.ShapeDtypeStruct((T, D), BF16),
            jax.ShapeDtypeStruct((H, T, DH), BF16),
            jax.ShapeDtypeStruct((T, D), BF16),
            jax.ShapeDtypeStruct((D // 2, D), BF16),
            jax.ShapeDtypeStruct((D // 2, D), BF16),
        ],
        in_specs=[SMEM]
        + [VMEM] * 5
        + [
            pl.BlockSpec((D, D), lambda i: (0, 0)),
            pl.BlockSpec((D, D), lambda i: (0, 4)),
            VMEM,
        ],
        out_specs=[VMEM] * 5,
        scratch_shapes=[pltpu.VMEM((T, D), F32)],
        compiler_params=params(),
        cost_estimate=cost(5),
        name="tail",
    )(meta, att_msg, na, nb, x, cot, w_full, w_full, gain_out)

    d_all = lax.all_to_all(d_att, "seq", 0, 0, tiled=True)

    gate_call = pl.pallas_call(
        gate_kernel,
        grid=(1,),
        out_shape=jax.ShapeDtypeStruct((T, D), F32),
        in_specs=[VMEM, pl.BlockSpec((D, D), lambda i: (0, 0))],
        out_specs=VMEM,
        compiler_params=params(),
        cost_estimate=cost(2),
        name="gate",
    )
    gate_back = gate_call(d_pg, w_full)

    other = paired(w_send, "dp_2", 1)
    pair = (w_own.astype(F32) + other.astype(F32)).astype(BF16)
    pair, d_all = lax.optimization_barrier((pair, d_all))
    planes = lax.all_to_all(pair.reshape(16, 32, D), ("dp_0", "dp_1"), 0, 0, tiled=True)

    attend_back = pl.pallas_call(
        backward_kernel,
        out_shape=[jax.ShapeDtypeStruct((T, 3 * DH), BF16)] * H,
        in_specs=[SMEM] + [VMEM] * 4,
        out_specs=[VMEM] * H,
        scratch_shapes=[
            pltpu.VMEM((S, DH), BF16),
            pltpu.VMEM((S, DH), BF16),
            pltpu.VMEM((DH, S), BF16),
            pltpu.VMEM((S, DH), BF16),
            pltpu.VMEM((S, S), BF16),
            pltpu.VMEM((DH, S), F32),
            pltpu.VMEM((H, T, 3 * DH), BF16),
        ],
        compiler_params=params(),
        cost_estimate=cost(6),
        name="attend_back",
    )
    d_proj = attend_back(meta, d_all, proj, weight, slope)

    total = jnp.sum(planes.astype(F32), axis=0)
    for mask in (1, 3, 7):
        own = total.astype(BF16)
        far = paired(own, "seq", mask)
        total = own.astype(F32) + far.astype(F32)
    w_grad = total

    d_rows = {0: d_proj[0]}
    for k in (4, 5, 3, 6, 2, 7, 1):
        d_rows[k] = shifted(d_proj[k], k)

    final = pl.pallas_call(
        final_kernel,
        grid=(3,),
        out_shape=jax.ShapeDtypeStruct((T, D), BF16),
        in_specs=[SMEM]
        + [VMEM] * (H + 1)
        + [pl.BlockSpec((D, D), lambda b: (0, b + 1)), VMEM, VMEM, VMEM],
        out_specs=VMEM,
        scratch_shapes=[
            pltpu.VMEM((H, T, 3 * DH), BF16),
            pltpu.VMEM((3, T, D), BF16),
            pltpu.VMEM((T, D), F32),
        ],
        compiler_params=params(dimension_semantics=("arbitrary",)),
        cost_estimate=cost(5),
        name="final",
    )
    input_grad = final(
        meta, *[d_rows[k] for k in range(H)], gate_back, w_full, x, cot, gain_in
    )

    return (mixed[None], input_grad[None], w_grad)


def solution(mesh):
    finer = Mesh(mesh.devices.reshape(4, 4, 2, mesh.shape["seq"]), (*DP, "seq"))
    placed = (
        P(DP, "seq", None),
        P(DP, "seq", None),
        P(DP, None),
        P(DP),
        P(DP, None),
        P(DP, None),
        P(),
        P(),
        P(),
    )
    return jax.shard_map(
        layer,
        mesh=finer,
        in_specs=placed,
        out_specs=(P(DP, "seq", None), P(DP, "seq", None), P(DP, None)),
        check_vma=False,
    )
```

profile of v0, /device:TPU:1, one launch (start us, length us, event | category | flops | bytes accessed | tf_op | source)
XLA Modules:
  0.0 175.6 jit_solution(17248405966352799369)
XLA Ops:
  7.2 1.8 pad_maximum_fusion
  10.7 8.6 %all-to-all-start = ((bf16[32,32,384]{2,1,0:T(8,128)(2,1)}), bf16[32,32,384]{2,1,0:T(8,128)(2,1)S(1)}, u32[]{:S(2)}, u32[]{:S(2)}) async-start(bf16[32,32,384]{2,1,0:T(8,128)(2,1)} %broadcast_in_dim.12), calls=%async_computation | async-start | bytes 1572864 | tf_op jit(solution)/shard_map/all_to_all | solution.py:328
  19.6 5.7 %collective-permute-start.10 = (bf16[64,1024]{1,0:T(8,128)(2,1)S(1)}, bf16[64,1024]{1,0:T(8,128)(2,1)S(1)}, u32[]{:S(2)}, u32[]{:S(2)}) collective-permute-start(bf16[64,1024]{1,0:T(8,128)(2,1)S(1)} %get-tuple-element.25.refs_3_.nb_ref), channel_id=1, source_target_pairs={{0,7},{1,0},{2,1},{3,2},{4,3},{5,4},{6,5},{7,6},{8,15},{9,8},{10,9... | collective-permute-start | bytes 393224 | tf_op jit(solution)/shard_map/ppermute | solution.py:295
  25.2 2.7 %collective-permute-start.7 = (bf16[64,1024]{1,0:T(8,128)(2,1)S(1)}, bf16[64,1024]{1,0:T(8,128)(2,1)S(1)}, u32[]{:S(2)}, u32[]{:S(2)}) collective-permute-start(bf16[64,1024]{1,0:T(8,128)(2,1)S(1)} %get-tuple-element.24.refs_2_.na_ref), channel_id=1, source_target_pairs={{0,7},{1,0},{2,1},{3,2},{4,3},{5,4},{6,5},{7,6},{8,15},{9,8},{10,9... | collective-permute-start | bytes 393224 | tf_op jit(solution)/shard_map/ppermute | solution.py:295
  27.9 3.3 %collective-permute-start.11 = (bf16[64,1024]{1,0:T(8,128)(2,1)S(1)}, bf16[64,1024]{1,0:T(8,128)(2,1)S(1)}, u32[]{:S(2)}, u32[]{:S(2)}) collective-permute-start(bf16[64,1024]{1,0:T(8,128)(2,1)S(1)} %collective-permute-done.10.refs_14_), channel_id=1, source_target_pairs={{0,7},{1,0},{2,1},{3,2},{4,3},{5,4},{6,5},{7,6},{8,15},{9,8},{10,9... | collective-permute-start | bytes 393224 | tf_op jit(solution)/shard_map/ppermute | solution.py:295
  31.3 2.6 %collective-permute-done.4.refs_8_ = bf16[64,1024]{1,0:T(8,128)(2,1)S(1)} collective-permute-done((bf16[64,1024]{1,0:T(8,128)(2,1)S(1)}, bf16[64,1024]{1,0:T(8,128)(2,1)S(1)}, u32[]{:S(2)}, u32[]{:S(2)}) %collective-permute-start.4) | collective-permute-done | bytes 131104 | tf_op jit(solution)/shard_map/ppermute | solution.py:295
  33.9 2.7 %collective-permute-start.8 = (bf16[64,1024]{1,0:T(8,128)(2,1)S(1)}, bf16[64,1024]{1,0:T(8,128)(2,1)S(1)}, u32[]{:S(2)}, u32[]{:S(2)}) collective-permute-start(bf16[64,1024]{1,0:T(8,128)(2,1)S(1)} %collective-permute-done.7.refs_11_), channel_id=1, source_target_pairs={{0,7},{1,0},{2,1},{3,2},{4,3},{5,4},{6,5},{7,6},{8,15},{9,8},{10,9... | collective-permute-start | bytes 393224 | tf_op jit(solution)/shard_map/ppermute | solution.py:295
  38.0 2.7 %collective-permute-done.5.refs_9_ = bf16[64,1024]{1,0:T(8,128)(2,1)S(1)} collective-permute-done((bf16[64,1024]{1,0:T(8,128)(2,1)S(1)}, bf16[64,1024]{1,0:T(8,128)(2,1)S(1)}, u32[]{:S(2)}, u32[]{:S(2)}) %collective-permute-start.5) | collective-permute-done | bytes 131104 | tf_op jit(solution)/shard_map/ppermute | solution.py:295
  40.7 2.7 %collective-permute-start.9 = (bf16[64,1024]{1,0:T(8,128)(2,1)S(1)}, bf16[64,1024]{1,0:T(8,128)(2,1)S(1)}, u32[]{:S(2)}, u32[]{:S(2)}) collective-permute-start(bf16[64,1024]{1,0:T(8,128)(2,1)S(1)} %collective-permute-done.8.refs_12_), channel_id=1, source_target_pairs={{0,7},{1,0},{2,1},{3,2},{4,3},{5,4},{6,5},{7,6},{8,15},{9,8},{10,9... | collective-permute-start | bytes 393224 | tf_op jit(solution)/shard_map/ppermute | solution.py:295
  48.3 2.5 %collective-permute-done.3.refs_7_ = bf16[64,1024]{1,0:T(8,128)(2,1)S(1)} collective-permute-done((bf16[64,1024]{1,0:T(8,128)(2,1)S(1)}, bf16[64,1024]{1,0:T(8,128)(2,1)S(1)}, u32[]{:S(2)}, u32[]{:S(2)}) %collective-permute-start.3) | collective-permute-done | bytes 131104 | tf_op jit(solution)/shard_map/ppermute | solution.py:295
  50.7 7.9 %attend.1 = (bf16[8,144,128]{2,1,0:T(8,128)(2,1)S(1)}, f32[1024,384]{1,0:T(8,128)S(1)}, bf16[1024,1024]{1,0:T(8,128)(2,1)S(1)}, bf16[1024,1024]{1,0:T(8,128)(2,1)}) custom-call(s32[3]{0:T(128)S(1)} %pad_add_fusion.refs_0_.meta, f32[8,16]{1,0:T(8,128)S(1)} %copy-done.4, bf16[64,1024]{1,0:T(8,128)(2,1)S(1)} %get-tuple-element.24.refs_2_.na_ref, ...), custom_call_target="tpu_custom_call" | custom-call | flops 3000000000 | bytes 1048576 | tf_op jit(solution)/shard_map/attend/pallas_call | solution.py:339
  61.1 12.0 %all_to_all.20.msg_ref = bf16[8,144,128]{2,1,0:T(8,128)(2,1)S(1)} all-to-all(bf16[8,144,128]{2,1,0:T(8,128)(2,1)S(1)} %get-tuple-element.26), channel_id=1, replica_groups=mesh['dp_0'=4,'dp_1'=4,'dp_2'=2,'seq'=8] {'seq'}, dimensions={0} | all-to-all | bytes 589824 | tf_op jit(solution)/shard_map/all_to_all | solution.py:362
  73.1 6.4 %all-gather.2.cloned.1.call-done.wg_ref.wo_ref.refs_10_ = bf16[1024,5120]{1,0:T(8,128)(2,1)} async-done(((bf16[32,5120]{1,0:T(8,128)(2,1)}), bf16[1024,5120]{1,0:T(8,128)(2,1)}) %all-gather.2.cloned.1.call-update) | async-done | bytes 10485776 | tf_op jit(solution)/shard_map/all_gather | solution.py:318
  79.5 5.0 %tail.1 = (bf16[128,1024]{1,0:T(8,128)(2,1)}, bf16[8,128,128]{2,1,0:T(8,128)(2,1)}, bf16[128,1024]{1,0:T(8,128)(2,1)S(1)}, bf16[512,1024]{1,0:T(8,128)(2,1)S(1)}, bf16[512,1024]{1,0:T(8,128)(2,1)S(1)}) custom-call(s32[3]{0:T(128)S(1)} %pad_add_fusion.refs_0_.meta, bf16[8,144,128]{2,1,0:T(8,128)(2,1)S(1)} %all_to_all.20.msg_ref, ...), custom_call_target="tpu_custom_call" | custom-call | flops 1500000000 | bytes 1048576 | tf_op jit(solution)/shard_map/tail/pallas_call | solution.py:364
  84.8 6.7 %all-to-all-start.2 = ((bf16[8,128,128]{2,1,0:T(8,128)(2,1)}), bf16[8,128,128]{2,1,0:T(8,128)(2,1)S(1)}, u32[]{:S(2)}, u32[]{:S(2)}) async-start(bf16[8,128,128]{2,1,0:T(8,128)(2,1)} %get-tuple-element.30), calls=%async_computation.2 | async-start | bytes 524288 | tf_op jit(solution)/shard_map/all_to_all | solution.py:388
  91.6 1.6 add_convert_fusion
  93.2 10.2 %all-to-all-done.2.refs_1_ = bf16[8,128,128]{2,1,0:T(8,128)(2,1)S(1)} async-done(((bf16[8,128,128]{2,1,0:T(8,128)(2,1)}), bf16[8,128,128]{2,1,0:T(8,128)(2,1)S(1)}, u32[]{:S(2)}, u32[]{:S(2)}) %all-to-all-start.2) | async-done | bytes 262176 | tf_op jit(solution)/shard_map/all_to_all | solution.py:388
  103.4 20.6 %all_to_all.21 = bf16[16,32,1024]{2,1,0:T(8,128)(2,1)S(1)} all-to-all(bf16[16,32,1024]{2,1,0:T(8,128)(2,1)S(1)} %bitcast.19), channel_id=1, replica_groups=mesh['dp_0'=4,'dp_1'=4,'dp_2'=2,'seq'=8] {'dp_0','dp_1'}, dimensions={0} | all-to-all | bytes 2097152 | tf_op jit(solution)/shard_map/all_to_all | solution.py:405
  124.3 1.6 copy-done.6
  125.9 1.6 copy-done.7
  127.5 1.4 copy-done.9
  128.9 2.4 %attend_back.1 = (bf16[128,384]{1,0:T(8,128)(2,1)S(1)}, bf16[128,384]{1,0:T(8,128)(2,1)S(1)}, bf16[128,384]{1,0:T(8,128)(2,1)S(1)}, bf16[128,384]{1,0:T(8,128)(2...) custom-call(s32[3]{0:T(128)S(1)} %pad_add_fusion.refs_0_.meta, ...), custom_call_target="tpu_custom_call" | custom-call | flops 1800000000 | bytes 1048576 | tf_op jit(solution)/shard_map/attend_back/pallas_call | solution.py:425
  131.3 1.5 collective-permute-start.15
  134.0 2.4 %gate.1.refs_9_ = f32[128,1024]{1,0:T(8,128)S(1)} custom-call(bf16[128,1024]{1,0:T(8,128)(2,1)S(1)} %get-tuple-element.43.dpg_ref, bf16[1024,5120]{1,0:T(8,128)(2,1)} %all-gather.2.cloned.1.call-done.wg_ref.wo_ref.refs_10_), custom_call_target="tpu_custom_call" | custom-call | flops 600000000 | bytes 1048576 | tf_op jit(solution)/shard_map/gate/pallas_call | solution.py:400
  136.5 2.4 %collective-permute-start.17 = (bf16[128,384]{1,0:T(8,128)(2,1)S(1)}, bf16[128,384]{1,0:T(8,128)(2,1)S(1)}, u32[]{:S(2)}, u32[]{:S(2)}) collective-permute-start(bf16[128,384]{1,0:T(8,128)(2,1)S(1)} %get-tuple-element.38), channel_id=1, source_target_pairs={{0,3},{1,4},{2,5},{3,6},{4,7},{5,0},{6,1},{7,2},{8,11},{9,12},{10,... | collective-permute-start | bytes 294920 | tf_op jit(solution)/shard_map/ppermute | solution.py:295
  138.9 2.3 %collective-permute-start.18 = (bf16[128,384]{1,0:T(8,128)(2,1)S(1)}, bf16[128,384]{1,0:T(8,128)(2,1)S(1)}, u32[]{:S(2)}, u32[]{:S(2)}) collective-permute-start(bf16[128,384]{1,0:T(8,128)(2,1)S(1)} %get-tuple-element.39), channel_id=1, source_target_pairs={{0,4},{1,5},{2,6},{3,7},{4,0},{5,1},{6,2},{7,3},{8,12},{9,13},{10,... | collective-permute-start | bytes 294920 | tf_op jit(solution)/shard_map/ppermute | solution.py:295
  141.2 4.4 %collective-permute-start.19 = (bf16[128,384]{1,0:T(8,128)(2,1)S(1)}, bf16[128,384]{1,0:T(8,128)(2,1)S(1)}, u32[]{:S(2)}, u32[]{:S(2)}) collective-permute-start(bf16[128,384]{1,0:T(8,128)(2,1)S(1)} %get-tuple-element.40), channel_id=1, source_target_pairs={{0,5},{1,6},{2,7},{3,0},{4,1},{5,2},{6,3},{7,4},{8,13},{9,14},{10,... | collective-permute-start | bytes 294920 | tf_op jit(solution)/shard_map/ppermute | solution.py:295
  146.0 6.7 %collective-permute-done.17.refs_4_ = bf16[128,384]{1,0:T(8,128)(2,1)S(1)} collective-permute-done((bf16[128,384]{1,0:T(8,128)(2,1)S(1)}, bf16[128,384]{1,0:T(8,128)(2,1)S(1)}, u32[]{:S(2)}, u32[]{:S(2)}) %collective-permute-start.17) | collective-permute-done | bytes 98336 | tf_op jit(solution)/shard_map/ppermute | solution.py:295
  152.6 2.2 %collective-permute-done.19.refs_6_ = bf16[128,384]{1,0:T(8,128)(2,1)S(1)} collective-permute-done((bf16[128,384]{1,0:T(8,128)(2,1)S(1)}, bf16[128,384]{1,0:T(8,128)(2,1)S(1)}, u32[]{:S(2)}, u32[]{:S(2)}) %collective-permute-start.19) | collective-permute-done | bytes 98336 | tf_op jit(solution)/shard_map/ppermute | solution.py:295
  154.9 3.5 %collective-permute-done.20.refs_7_ = bf16[128,384]{1,0:T(8,128)(2,1)S(1)} collective-permute-done((bf16[128,384]{1,0:T(8,128)(2,1)S(1)}, bf16[128,384]{1,0:T(8,128)(2,1)S(1)}, u32[]{:S(2)}, u32[]{:S(2)}) %collective-permute-start.20) | collective-permute-done | bytes 98336 | tf_op jit(solution)/shard_map/ppermute | solution.py:295
  158.4 3.5 %collective-permute-done.21.refs_8_ = bf16[128,384]{1,0:T(8,128)(2,1)S(1)} collective-permute-done((bf16[128,384]{1,0:T(8,128)(2,1)S(1)}, bf16[128,384]{1,0:T(8,128)(2,1)S(1)}, u32[]{:S(2)}, u32[]{:S(2)}) %collective-permute-start.21) | collective-permute-done | bytes 98336 | tf_op jit(solution)/shard_map/ppermute | solution.py:295
  161.9 6.3 %final.1 = bf16[128,1024]{1,0:T(8,128)(2,1)} custom-call(s32[3]{0:T(128)S(1)} %pad_add_fusion.refs_0_.meta, bf16[128,384]{1,0:T(8,128)(2,1)S(1)} %get-tuple-element.35.refs_1_, bf16[128,384]{1,0:T(8,128)(2,1)S(1)} %collective-permute-done.15.refs_2_, bf16[128,384]{1,0:T(8,128)(2,1)S(1)} %collective-permute-done.16.refs_3_, ...), custom_call_target="tpu_custom_call" | custom-call | flops 1500000000 | bytes 1048576 | tf_op jit(solution)/shard_map/final/pallas_call | solution.py:455
  (66 shorter events, 13.0 us)
Async XLA Ops:
  7.2 72.4 %all-gather.2.cloned.1.call-start = ((), (), s32[]{:S(2)}) async-start(), calls=%async_computation.4 | async-start | bytes 10813440 | tf_op jit(solution)/shard_map/all_gather | solution.py:318
  9.0 36.5 %copy-start.10 = (s32[1,1024]{1,0:T(1,128)S(1)}, s32[1,1024]{1,0:T(1,128)}, u32[]{:S(2)}) copy-start(s32[1,1024]{1,0:T(1,128)} %param.11) | copy-start | bytes 12292
  9.0 41.7 %copy-start.4 = (f32[8,16]{1,0:T(8,128)S(1)}, f32[8,16]{1,0:T(8,128)}, u32[]{:S(2)}) copy-start(f32[8,16]{1,0:T(8,128)} %refs_1_.1) | copy-start | bytes 1540
  10.7 40.0 %all-to-all-start = ((bf16[32,32,384]{2,1,0:T(8,128)(2,1)}), bf16[32,32,384]{2,1,0:T(8,128)(2,1)S(1)}, u32[]{:S(2)}, u32[]{:S(2)}) async-start(bf16[32,32,384]{2,1,0:T(8,128)(2,1)} %broadcast_in_dim.12), calls=%async_computation | async-start | bytes 1572864 | tf_op jit(solution)/shard_map/all_to_all | solution.py:328
  19.6 8.4 %collective-permute-start.10 = (bf16[64,1024]{1,0:T(8,128)(2,1)S(1)}, bf16[64,1024]{1,0:T(8,128)(2,1)S(1)}, u32[]{:S(2)}, u32[]{:S(2)}) collective-permute-start(bf16[64,1024]{1,0:T(8,128)(2,1)S(1)} %get-tuple-element.25.refs_3_.nb_ref), channel_id=1, source_target_pairs={{0,7},{1,0},{2,1},{3,2},{4,3},{5,4},{6,5},{7,6},{8,15},{9,8},{10,9... | collective-permute-start | bytes 393224 | tf_op jit(solution)/shard_map/ppermute | solution.py:295
  25.2 6.0 %collective-permute-start = (bf16[64,1024]{1,0:T(8,128)(2,1)S(1)}, bf16[64,1024]{1,0:T(8,128)(2,1)S(1)}, u32[]{:S(2)}, u32[]{:S(2)}) collective-permute-start(bf16[64,1024]{1,0:T(8,128)(2,1)S(1)} %get-tuple-element.24.refs_2_.na_ref), channel_id=1, source_target_pairs={{0,1},{1,2},{2,3},{3,4},{4,5},{5,6},{6,7},{7,0},{8,9},{9,10},{10,1... | collective-permute-start | bytes 393224 | tf_op jit(solution)/shard_map/ppermute | solution.py:295
  25.2 8.7 %collective-permute-start.4 = (bf16[64,1024]{1,0:T(8,128)(2,1)S(1)}, bf16[64,1024]{1,0:T(8,128)(2,1)S(1)}, u32[]{:S(2)}, u32[]{:S(2)}) collective-permute-start(bf16[64,1024]{1,0:T(8,128)(2,1)S(1)} %get-tuple-element.25.refs_3_.nb_ref), channel_id=1, source_target_pairs={{0,1},{1,2},{2,3},{3,4},{4,5},{5,6},{6,7},{7,0},{8,9},{9,10},{10,1... | collective-permute-start | bytes 393224 | tf_op jit(solution)/shard_map/ppermute | solution.py:295
  25.2 8.7 %collective-permute-start.7 = (bf16[64,1024]{1,0:T(8,128)(2,1)S(1)}, bf16[64,1024]{1,0:T(8,128)(2,1)S(1)}, u32[]{:S(2)}, u32[]{:S(2)}) collective-permute-start(bf16[64,1024]{1,0:T(8,128)(2,1)S(1)} %get-tuple-element.24.refs_2_.na_ref), channel_id=1, source_target_pairs={{0,7},{1,0},{2,1},{3,2},{4,3},{5,4},{6,5},{7,6},{8,15},{9,8},{10,9... | collective-permute-start | bytes 393224 | tf_op jit(solution)/shard_map/ppermute | solution.py:295
  27.9 8.6 %collective-permute-start.11 = (bf16[64,1024]{1,0:T(8,128)(2,1)S(1)}, bf16[64,1024]{1,0:T(8,128)(2,1)S(1)}, u32[]{:S(2)}, u32[]{:S(2)}) collective-permute-start(bf16[64,1024]{1,0:T(8,128)(2,1)S(1)} %collective-permute-done.10.refs_14_), channel_id=1, source_target_pairs={{0,7},{1,0},{2,1},{3,2},{4,3},{5,4},{6,5},{7,6},{8,15},{9,8},{10,9... | collective-permute-start | bytes 393224 | tf_op jit(solution)/shard_map/ppermute | solution.py:295
  31.3 5.4 %collective-permute-start.1 = (bf16[64,1024]{1,0:T(8,128)(2,1)S(1)}, bf16[64,1024]{1,0:T(8,128)(2,1)S(1)}, u32[]{:S(2)}, u32[]{:S(2)}) collective-permute-start(bf16[64,1024]{1,0:T(8,128)(2,1)S(1)} %collective-permute-done.refs_4_), channel_id=1, source_target_pairs={{0,1},{1,2},{2,3},{3,4},{4,5},{5,6},{6,7},{7,0},{8,9},{9,10},{10,1... | collective-permute-start | bytes 393224 | tf_op jit(solution)/shard_map/ppermute | solution.py:295
  33.9 6.8 %collective-permute-start.5 = (bf16[64,1024]{1,0:T(8,128)(2,1)S(1)}, bf16[64,1024]{1,0:T(8,128)(2,1)S(1)}, u32[]{:S(2)}, u32[]{:S(2)}) collective-permute-start(bf16[64,1024]{1,0:T(8,128)(2,1)S(1)} %collective-permute-done.4.refs_8_), channel_id=1, source_target_pairs={{0,1},{1,2},{2,3},{3,4},{4,5},{5,6},{6,7},{7,0},{8,9},{9,10},{10,1... | collective-permute-start | bytes 393224 | tf_op jit(solution)/shard_map/ppermute | solution.py:295
  33.9 6.8 %collective-permute-start.8 = (bf16[64,1024]{1,0:T(8,128)(2,1)S(1)}, bf16[64,1024]{1,0:T(8,128)(2,1)S(1)}, u32[]{:S(2)}, u32[]{:S(2)}) collective-permute-start(bf16[64,1024]{1,0:T(8,128)(2,1)S(1)} %collective-permute-done.7.refs_11_), channel_id=1, source_target_pairs={{0,7},{1,0},{2,1},{3,2},{4,3},{5,4},{6,5},{7,6},{8,15},{9,8},{10,9... | collective-permute-start | bytes 393224 | tf_op jit(solution)/shard_map/ppermute | solution.py:295
  36.6 6.8 %collective-permute-start.12 = (bf16[64,1024]{1,0:T(8,128)(2,1)S(1)}, bf16[64,1024]{1,0:T(8,128)(2,1)S(1)}, u32[]{:S(2)}, u32[]{:S(2)}) collective-permute-start(bf16[64,1024]{1,0:T(8,128)(2,1)S(1)} %collective-permute-done.11.refs_15_), channel_id=1, source_target_pairs={{0,7},{1,0},{2,1},{3,2},{4,3},{5,4},{6,5},{7,6},{8,15},{9,8},{10,9... | collective-permute-start | bytes 393224 | tf_op jit(solution)/shard_map/ppermute | solution.py:295
  36.7 7.4 %collective-permute-start.2 = (bf16[64,1024]{1,0:T(8,128)(2,1)S(1)}, bf16[64,1024]{1,0:T(8,128)(2,1)S(1)}, u32[]{:S(2)}, u32[]{:S(2)}) collective-permute-start(bf16[64,1024]{1,0:T(8,128)(2,1)S(1)} %collective-permute-done.1.refs_5_), channel_id=1, source_target_pairs={{0,1},{1,2},{2,3},{3,4},{4,5},{5,6},{6,7},{7,0},{8,9},{9,10},{10,1... | collective-permute-start | bytes 393224 | tf_op jit(solution)/shard_map/ppermute | solution.py:295
  40.7 6.2 %collective-permute-start.6 = (bf16[64,1024]{1,0:T(8,128)(2,1)S(1)}, bf16[64,1024]{1,0:T(8,128)(2,1)S(1)}, u32[]{:S(2)}, u32[]{:S(2)}) collective-permute-start(bf16[64,1024]{1,0:T(8,128)(2,1)S(1)} %collective-permute-done.5.refs_9_), channel_id=1, source_target_pairs={{0,1},{1,2},{2,3},{3,4},{4,5},{5,6},{6,7},{7,0},{8,9},{9,10},{10,1... | collective-permute-start | bytes 393224 | tf_op jit(solution)/shard_map/ppermute | solution.py:295
  40.7 6.2 %collective-permute-start.9 = (bf16[64,1024]{1,0:T(8,128)(2,1)S(1)}, bf16[64,1024]{1,0:T(8,128)(2,1)S(1)}, u32[]{:S(2)}, u32[]{:S(2)}) collective-permute-start(bf16[64,1024]{1,0:T(8,128)(2,1)S(1)} %collective-permute-done.8.refs_12_), channel_id=1, source_target_pairs={{0,7},{1,0},{2,1},{3,2},{4,3},{5,4},{6,5},{7,6},{8,15},{9,8},{10,9... | collective-permute-start | bytes 393224 | tf_op jit(solution)/shard_map/ppermute | solution.py:295
  43.4 4.9 %collective-permute-start.13 = (bf16[64,1024]{1,0:T(8,128)(2,1)S(1)}, bf16[64,1024]{1,0:T(8,128)(2,1)S(1)}, u32[]{:S(2)}, u32[]{:S(2)}) collective-permute-start(bf16[64,1024]{1,0:T(8,128)(2,1)S(1)} %collective-permute-done.12.refs_16_), channel_id=1, source_target_pairs={{0,7},{1,0},{2,1},{3,2},{4,3},{5,4},{6,5},{7,6},{8,15},{9,8},{10,9... | collective-permute-start | bytes 393224 | tf_op jit(solution)/shard_map/ppermute | solution.py:295
  44.1 6.6 %collective-permute-start.3 = (bf16[64,1024]{1,0:T(8,128)(2,1)S(1)}, bf16[64,1024]{1,0:T(8,128)(2,1)S(1)}, u32[]{:S(2)}, u32[]{:S(2)}) collective-permute-start(bf16[64,1024]{1,0:T(8,128)(2,1)S(1)} %collective-permute-done.2.refs_6_), channel_id=1, source_target_pairs={{0,1},{1,2},{2,3},{3,4},{4,5},{5,6},{6,7},{7,0},{8,9},{9,10},{10,1... | collective-permute-start | bytes 393224 | tf_op jit(solution)/shard_map/ppermute | solution.py:295
  50.7 28.8 %copy-start.1 = (bf16[1,128,1024]{2,1,0:T(8,128)(2,1)S(1)}, bf16[1,128,1024]{2,1,0:T(8,128)(2,1)}, u32[]{:S(2)}) copy-start(bf16[1,128,1024]{2,1,0:T(8,128)(2,1)} %param.10) | copy-start | bytes 786436
  50.7 28.8 %copy-start.3 = (f32[1024]{0:T(1024)S(1)}, f32[1024]{0:T(1024)}, u32[]{:S(2)}) copy-start(f32[1024]{0:T(1024)} %param.16) | copy-start | bytes 12292
  84.6 7.0 %collective-permute-start.14 = (bf16[512,1024]{1,0:T(8,128)(2,1)S(1)}, bf16[512,1024]{1,0:T(8,128)(2,1)}, u32[]{:S(2)}, u32[]{:S(2)}) collective-permute-start(bf16[512,1024]{1,0:T(8,128)(2,1)S(1)} %get-tuple-element.29), channel_id=1, source_target_pairs={{0,8},{8,0},{1,9},{9,1},{2,10},{10,2},{3,11},{11,3},{4,12},{12,4},... | collective-permute-start | bytes 3145736 | tf_op jit(solution)/shard_map/ppermute | solution.py:291
  84.8 18.5 %all-to-all-start.2 = ((bf16[8,128,128]{2,1,0:T(8,128)(2,1)}), bf16[8,128,128]{2,1,0:T(8,128)(2,1)S(1)}, u32[]{:S(2)}, u32[]{:S(2)}) async-start(bf16[8,128,128]{2,1,0:T(8,128)(2,1)} %get-tuple-element.30), calls=%async_computation.2 | async-start | bytes 524288 | tf_op jit(solution)/shard_map/all_to_all | solution.py:388
  124.2 8.6 %collective-permute-start.22 = (bf16[32,1024]{1,0:T(8,128)(2,1)S(1)}, bf16[32,1024]{1,0:T(8,128)(2,1)S(1)}, u32[]{:S(2)}, u32[]{:S(2)}) collective-permute-start(bf16[32,1024]{1,0:T(8,128)(2,1)S(1)} %reduce_sum.12), channel_id=1, source_target_pairs={{0,1},{1,0},{2,3},{3,2},{4,5},{5,4},{6,7},{7,6},{8,9},{9,8},{10,11... | collective-permute-start | bytes 196616 | tf_op jit(solution)/shard_map/ppermute | solution.py:291
  131.3 9.9 %collective-permute-start.15 = (bf16[128,384]{1,0:T(8,128)(2,1)S(1)}, bf16[128,384]{1,0:T(8,128)(2,1)S(1)}, u32[]{:S(2)}, u32[]{:S(2)}) collective-permute-start(bf16[128,384]{1,0:T(8,128)(2,1)S(1)} %get-tuple-element.36), channel_id=1, source_target_pairs={{0,1},{1,2},{2,3},{3,4},{4,5},{5,6},{6,7},{7,0},{8,9},{9,10},{10,1... | collective-permute-start | bytes 294920 | tf_op jit(solution)/shard_map/ppermute | solution.py:295
  132.8 12.8 %collective-permute-start.16 = (bf16[128,384]{1,0:T(8,128)(2,1)S(1)}, bf16[128,384]{1,0:T(8,128)(2,1)S(1)}, u32[]{:S(2)}, u32[]{:S(2)}) collective-permute-start(bf16[128,384]{1,0:T(8,128)(2,1)S(1)} %get-tuple-element.37), channel_id=1, source_target_pairs={{0,2},{1,3},{2,4},{3,5},{4,6},{5,7},{6,0},{7,1},{8,10},{9,11},{10,... | collective-permute-start | bytes 294920 | tf_op jit(solution)/shard_map/ppermute | solution.py:295
  132.8 12.8 %collective-permute-start.23 = (bf16[32,1024]{1,0:T(8,128)(2,1)S(1)}, bf16[32,1024]{1,0:T(8,128)(2,1)S(1)}, u32[]{:S(2)}, u32[]{:S(2)}) collective-permute-start(bf16[32,1024]{1,0:T(8,128)(2,1)S(1)} %add_convert_fusion.2), channel_id=1, source_target_pairs={{0,3},{1,2},{2,1},{3,0},{4,7},{5,6},{6,5},{7,4},{8,11},{9,10},{10,... | collective-permute-start | bytes 196616 | tf_op jit(solution)/shard_map/ppermute | solution.py:291
  136.5 16.1 %collective-permute-start.17 = (bf16[128,384]{1,0:T(8,128)(2,1)S(1)}, bf16[128,384]{1,0:T(8,128)(2,1)S(1)}, u32[]{:S(2)}, u32[]{:S(2)}) collective-permute-start(bf16[128,384]{1,0:T(8,128)(2,1)S(1)} %get-tuple-element.38), channel_id=1, source_target_pairs={{0,3},{1,4},{2,5},{3,6},{4,7},{5,0},{6,1},{7,2},{8,11},{9,12},{10,... | collective-permute-start | bytes 294920 | tf_op jit(solution)/shard_map/ppermute | solution.py:295
  138.9 13.7 %collective-permute-start.18 = (bf16[128,384]{1,0:T(8,128)(2,1)S(1)}, bf16[128,384]{1,0:T(8,128)(2,1)S(1)}, u32[]{:S(2)}, u32[]{:S(2)}) collective-permute-start(bf16[128,384]{1,0:T(8,128)(2,1)S(1)} %get-tuple-element.39), channel_id=1, source_target_pairs={{0,4},{1,5},{2,6},{3,7},{4,0},{5,1},{6,2},{7,3},{8,12},{9,13},{10,... | collective-permute-start | bytes 294920 | tf_op jit(solution)/shard_map/ppermute | solution.py:295
  141.2 13.7 %collective-permute-start.19 = (bf16[128,384]{1,0:T(8,128)(2,1)S(1)}, bf16[128,384]{1,0:T(8,128)(2,1)S(1)}, u32[]{:S(2)}, u32[]{:S(2)}) collective-permute-start(bf16[128,384]{1,0:T(8,128)(2,1)S(1)} %get-tuple-element.40), channel_id=1, source_target_pairs={{0,5},{1,6},{2,7},{3,0},{4,1},{5,2},{6,3},{7,4},{8,13},{9,14},{10,... | collective-permute-start | bytes 294920 | tf_op jit(solution)/shard_map/ppermute | solution.py:295
  145.6 12.8 %collective-permute-start.20 = (bf16[128,384]{1,0:T(8,128)(2,1)S(1)}, bf16[128,384]{1,0:T(8,128)(2,1)S(1)}, u32[]{:S(2)}, u32[]{:S(2)}) collective-permute-start(bf16[128,384]{1,0:T(8,128)(2,1)S(1)} %get-tuple-element.41), channel_id=1, source_target_pairs={{0,6},{1,7},{2,0},{3,1},{4,2},{5,3},{6,4},{7,5},{8,14},{9,15},{10,... | collective-permute-start | bytes 294920 | tf_op jit(solution)/shard_map/ppermute | solution.py:295
  145.6 16.3 %collective-permute-start.21 = (bf16[128,384]{1,0:T(8,128)(2,1)S(1)}, bf16[128,384]{1,0:T(8,128)(2,1)S(1)}, u32[]{:S(2)}, u32[]{:S(2)}) collective-permute-start(bf16[128,384]{1,0:T(8,128)(2,1)S(1)} %get-tuple-element.42), channel_id=1, source_target_pairs={{0,7},{1,0},{2,1},{3,2},{4,3},{5,4},{6,5},{7,6},{8,15},{9,8},{10,9... | collective-permute-start | bytes 294920 | tf_op jit(solution)/shard_map/ppermute | solution.py:295
  152.6 15.5 %collective-permute-start.24 = (bf16[32,1024]{1,0:T(8,128)(2,1)S(1)}, bf16[32,1024]{1,0:T(8,128)(2,1)S(1)}, u32[]{:S(2)}, u32[]{:S(2)}) collective-permute-start(bf16[32,1024]{1,0:T(8,128)(2,1)S(1)} %add_convert_fusion.1), channel_id=1, source_target_pairs={{0,7},{1,6},{2,5},{3,4},{4,3},{5,2},{6,1},{7,0},{8,15},{9,14},{10,... | collective-permute-start | bytes 196616 | tf_op jit(solution)/shard_map/ppermute | solution.py:291
  (7 other events, 31.3 us)
Sparse Core Ops, SparseCore 0:
  10.5 68.9 all-gather.1
where the time goes:
time: 176 us
  starting transfers between devices  47.9 us (27%)
  waiting for transfers between devices  42.9 us (24%)
  blocking collectives  32.7 us (19%)
  Pallas kernels  24.2 us (14%)
  between operations  14.9 us (8%)
  local copies, waits for them, and re-layouts  8.72 us (5%)
  other arithmetic  4.37 us (2%)
    ppermute x21, starting transfers between devices, shifted(): return lax.ppermute(value, 'seq', [(i, (i + by) % H) for i in range(H)])  30.9 us
    ppermute x21, waiting for transfers between devices, shifted(): return lax.ppermute(value, 'seq', [(i, (i + by) % H) for i in range(H)])  26.3 us
    all_to_all x1, blocking collectives, layer(): lax.all_to_all(pair.reshape(16, 32, D), ('dp_0', 'dp_1'), 0, 0, tiled=True)  20.6 us
    all_to_all x1, blocking collectives, layer(): att_msg = lax.all_to_all(msg, 'seq', 0, 0, tiled=True)  12 us
    all_to_all x1, waiting for transfers between devices, layer(): d_all = lax.all_to_all(d_att, 'seq', 0, 0, tiled=True)  10.2 us
    all_to_all x1, starting transfers between devices, layer(): ws = lax.all_to_all(copies, DP, 0, 0, tiled=True)  8.58 us
    pallas_call x1, Pallas kernels, layer(): pl.pallas_call(forward_kernel, out_shape=[jax.ShapeDtypeStruct((H, MSG, T...  7.9 us
    unnamed x22, local copies, waits for them, and re-layouts  7.04 us
  transfers between devices with their start and end apart: 28, of which 11 were waited for; matrix products, arithmetic and copies ran while one was open for 2% of the time, Pallas kernels for 11%

commit v1 on v0

--- a/solution.py
+++ b/solution.py
@@ -18,9 +18,11 @@
 DP = ("dp_0", "dp_1", "dp_2")
 EPS = 1e-05
 MSG = 144
-LIMIT = 48000
+LIMIT = 52000
 F32 = jnp.float32
 BF16 = jnp.bfloat16
+
+ORDER = (4, 5, 3, 6, 2, 7, 1)
 
 VMEM = pl.BlockSpec(memory_space=pltpu.VMEM)
 SMEM = pl.BlockSpec(memory_space=pltpu.SMEM)
@@ -70,7 +72,13 @@
     for (far, half), blk in zip(ARRIVALS, blocks):
         at = lax.rem(me + far + H, H) * T + half * 64
         x_all[pl.ds(pl.multiple_of(at, 64), 64), :] = blk[...]
-    proj_ref[...] = mm(x_all[...], ws_ref[...])
+
+    def project(c, carry):
+        rows = pl.ds(pl.multiple_of(c * TI, TI), TI)
+        proj_ref[rows, :] = mm(x_all[rows, :], ws_ref[...])
+        return carry
+
+    lax.fori_loop(0, S // TI, project, 0)
     for c in range(8):
         cols = slice(c * T, (c + 1) * T)
         col_sc[cols, :] = jnp.broadcast_to(row_ref[:, cols], (T, T)).T
@@ -86,25 +94,30 @@
 
     def tile(i0, j0, diagonal):
         s_sc[...] = nt(k_sc[pl.ds(j0, TI), :], q_sc[i0 : i0 + TI, :])
-        for c in range(TI // CH):
-            rows = pl.ds(j0 + c * CH, CH)
+
+        def chunk(c, carry):
+            at = pl.multiple_of(c * CH, CH)
+            rows = pl.ds(pl.multiple_of(j0 + at, CH), CH)
             col = col_sc[rows, :]
             e = row_ref[:, i0 : i0 + TI] - jnp.concatenate([col, col], axis=1)
             bias = jnp.full((CH, TI), levels[0], F32)
             for b in range(1, NB):
                 bias = jnp.where(e >= float(2**b - 1), levels[b], bias)
-            s = s_sc[c * CH : (c + 1) * CH, :] * scale + bias
+            s = s_sc[pl.ds(at, CH), :] * scale + bias
             sg = sigmoid(s)
             w = s * sg
             g = sg + w * (1.0 - sg)
             if diagonal:
-                jj = lax.broadcasted_iota(jnp.int32, (CH, TI), 0) + c * CH
+                jj = lax.broadcasted_iota(jnp.int32, (CH, TI), 0) + at
                 ii = lax.broadcasted_iota(jnp.int32, (CH, TI), 1)
                 keep = jj <= ii
                 w = jnp.where(keep, w, 0.0)
                 g = jnp.where(keep, g, 0.0)
             w_ref[rows, i0 : i0 + TI] = w.astype(BF16)
             g_ref[rows, i0 : i0 + TI] = g.astype(BF16)
+            return carry
+
+        lax.fori_loop(0, TI // CH, chunk, 0, unroll=2)
 
     for bi in range(S // TI):
         i0 = bi * TI
@@ -149,20 +162,30 @@
     wo_ref,
     gain_ref,
     mixed_ref,
-    datt_ref,
     dpg_ref,
     own_ref,
     send_ref,
-    att_sc,
+    *more,
 ):
+    datt_out, (att_sc, datt_ref, rows_sc, pg_sc, dmix_sc) = more[:H], more[H:]
     me, length, core = meta[0], meta[1], meta[2]
     for h in range(H):
         blk = msg_ref[h].astype(F32)
         att_t = blk[:DH] + (blk[DH : DH + 1] + blk[DH + 1 : DH + 2] + blk[DH + 2 : DH + 3])
         att_sc[:, h * DH : (h + 1) * DH] = att_t.T
-    pg = jnp.concatenate([mm(na_ref[...], wg_ref[...]), mm(nb_ref[...], wg_ref[...])], axis=0)
+    rows_sc[:64, :] = na_ref[...]
+    rows_sc[64:, :] = nb_ref[...]
     cot = cot_ref[...]
-    d_mix = nt(cot, wo_ref[...])
+
+    def columns(n, carry):
+        at = pl.ds(pl.multiple_of(n * 256, 256), 256)
+        pg_sc[:, at] = mm(rows_sc[...], wg_ref[:, at])
+        dmix_sc[:, at] = nt(cot, wo_ref[at, :])
+        return carry
+
+    lax.fori_loop(0, D // 256, columns, 0)
+    pg = pg_sc[...]
+    d_mix = dmix_sc[...]
     att = att_sc[...]
     gain = gain_ref[...]
     c = att - jnp.mean(att, axis=-1, keepdims=True)
@@ -173,7 +196,7 @@
     sg = sigmoid(pg)
     gate = pg * sg
     mixed_rows = (normed_att * gate).astype(BF16)
-    mixed_ref[...] = (x_ref[...].astype(F32) + mm(mixed_rows, wo_ref[...])).astype(BF16)
+    rows_sc[...] = mixed_rows
     dpg_ref[...] = (d_mix * normed_att * (sg + gate * (1.0 - sg))).astype(BF16)
     u = d_mix * gate * gain
     d_att = r * (
@@ -184,24 +207,47 @@
     pos = lax.broadcasted_iota(jnp.int32, (T, D), 0) + me * T
     d_att = jnp.where(pos < length, d_att, 0.0).astype(BF16)
     for h in range(H):
-        cols = slice(h * DH, (h + 1) * DH)
-        datt_ref[h] = d_att[:, cols]
-        part = tn(mixed_rows[:, cols], cot).astype(BF16)
+        datt_ref[h] = d_att[:, h * DH : (h + 1) * DH]
+
+    def head(h, carry):
+        part = tn(rows_sc[:, pl.ds(pl.multiple_of(h * DH, DH), DH)], cot).astype(BF16)
         for t in range(2):
-            at = slice((2 * h + t) * 32, (2 * h + t + 1) * 32)
+            at = pl.ds(pl.multiple_of((2 * h + t) * 32, 32), 32)
             even, odd = part[t * 64 : t * 64 + 32], part[t * 64 + 32 : t * 64 + 64]
             own_ref[at, :] = jnp.where(core == 0, even, odd)
             send_ref[at, :] = jnp.where(core == 0, odd, even)
+        return carry
+
+    lax.fori_loop(0, H, head, 0)
+
+    def mix(n, carry):
+        at = pl.ds(pl.multiple_of(n * 256, 256), 256)
+        mixed_ref[:, at] = (
+            x_ref[:, at].astype(F32) + mm(rows_sc[...], wo_ref[:, at])
+        ).astype(BF16)
+        return carry
+
+    lax.fori_loop(0, D // 256, mix, 0)
+    for k in range(H):
+        datt_out[k][...] = datt_ref[lax.rem(me + k, H)]
 
 
 def gate_kernel(dpg_ref, wg_ref, out_ref):
-    out_ref[...] = nt(dpg_ref[...], wg_ref[...])
+    def columns(n, carry):
+        at = pl.ds(pl.multiple_of(n * 256, 256), 256)
+        out_ref[:, at] = nt(dpg_ref[...], wg_ref[at, :])
+        return carry
+
+    lax.fori_loop(0, D // 256, columns, 0)
 
 
 def backward_kernel(*refs):
-    meta, d_ref, proj_ref, w_ref, g_ref = refs[:5]
-    outs = refs[5:13]
-    q_sc, k_sc, kt_sc, v_sc, ds_sc, dqt_sc, out_ref = refs[13:]
+    meta, blocks = refs[0], refs[1:9]
+    proj_ref, w_ref, g_ref = refs[9:12]
+    outs = refs[12:20]
+    q_sc, k_sc, kt_sc, v_sc, ds_sc, dqt_sc, out_ref, d_ref = refs[20:]
+    for k in range(H):
+        d_ref[lax.rem(meta[0] - k + H, H)] = blocks[k][...]
     for c in range(8):
         rows = slice(c * T, (c + 1) * T)
         p = proj_ref[rows, :]
@@ -259,7 +305,12 @@
                 lhs[n, :, h * DH : (h + 1) * DH] = msg_ref[h, :, n * DH : (n + 1) * DH]
         acc[...] = back_ref[...]
 
-    acc[...] += nt(lhs[b], w_ref[...])
+    def columns(n, carry):
+        at = pl.ds(pl.multiple_of(n * 256, 256), 256)
+        acc[:, at] += nt(lhs[b], w_ref[at, :])
+        return carry
+
+    lax.fori_loop(0, D // 256, columns, 0)
 
     @pl.when(b == 2)
     def _():
@@ -277,8 +328,8 @@
         out_ref[...] = (cot_ref[...].astype(F32) + dx).astype(BF16)
 
 
-def params(**more):
-    return pltpu.CompilerParams(vmem_limit_bytes=LIMIT * 1024, **more)
+def params(kib=LIMIT, **more):
+    return pltpu.CompilerParams(vmem_limit_bytes=kib * 1024, **more)
 
 
 def cost(us):
@@ -315,7 +366,10 @@
         name="norm",
     )(x, gain_in)
 
-    w_full = lax.all_gather(jnp.concatenate([w_qkvu, w_out], axis=1), DP, axis=0, tiled=True)
+    w_early = lax.all_gather(
+        jnp.concatenate([w_qkvu[:, :D], w_out], axis=1), DP, axis=0, tiled=True
+    )
+    w_late = lax.all_gather(w_qkvu[:, D:], DP, axis=0, tiled=True)
 
     head_w = jnp.concatenate(
         [
@@ -361,31 +415,39 @@
 
     att_msg = lax.all_to_all(msg, "seq", 0, 0, tiled=True)
 
-    mixed, d_att, d_pg, w_own, w_send = pl.pallas_call(
+    mixed, d_pg, w_own, w_send, *d_att = pl.pallas_call(
         tail_kernel,
         grid=(1,),
         out_shape=[
             jax.ShapeDtypeStruct((T, D), BF16),
-            jax.ShapeDtypeStruct((H, T, DH), BF16),
             jax.ShapeDtypeStruct((T, D), BF16),
             jax.ShapeDtypeStruct((D // 2, D), BF16),
             jax.ShapeDtypeStruct((D // 2, D), BF16),
-        ],
+        ]
+        + [jax.ShapeDtypeStruct((T, DH), BF16)] * H,
         in_specs=[SMEM]
         + [VMEM] * 5
         + [
             pl.BlockSpec((D, D), lambda i: (0, 0)),
-            pl.BlockSpec((D, D), lambda i: (0, 4)),
+            pl.BlockSpec((D, D), lambda i: (0, 1)),
             VMEM,
         ],
-        out_specs=[VMEM] * 5,
-        scratch_shapes=[pltpu.VMEM((T, D), F32)],
+        out_specs=[VMEM] * (4 + H),
+        scratch_shapes=[
+            pltpu.VMEM((T, D), F32),
+            pltpu.VMEM((H, T, DH), BF16),
+            pltpu.VMEM((T, D), BF16),
+            pltpu.VMEM((T, D), F32),
+            pltpu.VMEM((T, D), F32),
+        ],
         compiler_params=params(),
         cost_estimate=cost(5),
         name="tail",
-    )(meta, att_msg, na, nb, x, cot, w_full, w_full, gain_out)
-
-    d_all = lax.all_to_all(d_att, "seq", 0, 0, tiled=True)
+    )(meta, att_msg, na, nb, x, cot, w_early, w_early, gain_out)
+
+    d_all = {0: d_att[0]}
+    for k in ORDER:
+        d_all[k] = shifted(d_att[k], k)
 
     gate_call = pl.pallas_call(
         gate_kernel,
@@ -397,17 +459,15 @@
         cost_estimate=cost(2),
         name="gate",
     )
-    gate_back = gate_call(d_pg, w_full)
+    gate_back = gate_call(d_pg, w_early)
 
     other = paired(w_send, "dp_2", 1)
     pair = (w_own.astype(F32) + other.astype(F32)).astype(BF16)
-    pair, d_all = lax.optimization_barrier((pair, d_all))
-    planes = lax.all_to_all(pair.reshape(16, 32, D), ("dp_0", "dp_1"), 0, 0, tiled=True)
 
     attend_back = pl.pallas_call(
         backward_kernel,
         out_shape=[jax.ShapeDtypeStruct((T, 3 * DH), BF16)] * H,
-        in_specs=[SMEM] + [VMEM] * 4,
+        in_specs=[SMEM] + [VMEM] * (3 + H),
         out_specs=[VMEM] * H,
         scratch_shapes=[
             pltpu.VMEM((S, DH), BF16),
@@ -417,12 +477,17 @@
             pltpu.VMEM((S, S), BF16),
             pltpu.VMEM((DH, S), F32),
             pltpu.VMEM((H, T, 3 * DH), BF16),
-        ],
-        compiler_params=params(),
+            pltpu.VMEM((H, T, DH), BF16),
+        ],
+        compiler_params=params(24000),
         cost_estimate=cost(6),
         name="attend_back",
     )
-    d_proj = attend_back(meta, d_all, proj, weight, slope)
+    d_proj = attend_back(meta, *[d_all[k] for k in range(H)], proj, weight, slope)
+
+    pair, first = lax.optimization_barrier((pair, d_proj[0]))
+    d_proj = [first, *d_proj[1:]]
+    planes = lax.all_to_all(pair.reshape(16, 32, D), ("dp_0", "dp_1"), 0, 0, tiled=True)
 
     total = jnp.sum(planes.astype(F32), axis=0)
     for mask in (1, 3, 7):
@@ -432,7 +497,7 @@
     w_grad = total
 
     d_rows = {0: d_proj[0]}
-    for k in (4, 5, 3, 6, 2, 7, 1):
+    for k in ORDER:
         d_rows[k] = shifted(d_proj[k], k)
 
     final = pl.pallas_call(
@@ -441,7 +506,7 @@
         out_shape=jax.ShapeDtypeStruct((T, D), BF16),
         in_specs=[SMEM]
         + [VMEM] * (H + 1)
-        + [pl.BlockSpec((D, D), lambda b: (0, b + 1)), VMEM, VMEM, VMEM],
+        + [pl.BlockSpec((D, D), lambda b: (0, b)), VMEM, VMEM, VMEM],
         out_specs=VMEM,
         scratch_shapes=[
             pltpu.VMEM((H, T, 3 * DH), BF16),
@@ -453,7 +518,7 @@
         name="final",
     )
     input_grad = final(
-        meta, *[d_rows[k] for k in range(H)], gate_back, w_full, x, cot, gain_in
+        meta, *[d_rows[k] for k in range(H)], gate_back, w_late, x, cot, gain_in
     )
 
     return (mixed[None], input_grad[None], w_grad)

time: 176 us -> 187 us (1.062)
  the two profiles are of different devices: /device:TPU:1 before, /device:TPU:32 now
where the time goes in v1:
time: 187 us; the launch traced here: 186 us
  starting transfers between devices  63.9 us (34%)
  blocking collectives  42.2 us (23%)
  Pallas kernels  33.5 us (18%)
  waiting for transfers between devices  24.7 us (13%)
  between operations  14.9 us (8%)
  local copies, waits for them, and re-layouts  4.22 us (2%)
  other arithmetic  2.91 us (2%)
    ppermute x28, starting transfers between devices, shifted(): return lax.ppermute(value, 'seq', [(i, (i + by) % H) for i in range(H)])  49.8 us
    all_to_all x1, blocking collectives, layer(): lax.all_to_all(pair.reshape(16, 32, D), ('dp_0', 'dp_1'), 0, 0, tiled=True)  28.5 us
    ppermute x28, waiting for transfers between devices, shifted(): return lax.ppermute(value, 'seq', [(i, (i + by) % H) for i in range(H)])  20.9 us
    all_to_all x1, blocking collectives, layer(): att_msg = lax.all_to_all(msg, 'seq', 0, 0, tiled=True)  13.7 us
    pallas_call x1, Pallas kernels, layer(): pl.pallas_call(forward_kernel, out_shape=[jax.ShapeDtypeStruct((H, MSG, T...  11.9 us
    pallas_call x1, Pallas kernels, layer(): pl.pallas_call(tail_kernel, grid=(1,), out_shape=[jax.ShapeDtypeStruct((T...  8.96 us
    all_to_all x1, starting transfers between devices, layer(): ws = lax.all_to_all(copies, DP, 0, 0, tiled=True)  7.32 us
    pallas_call x1, Pallas kernels, layer(): final(meta, *[d_rows[k] for k in range(H)], gate_back, w_late, x, cot, ga...  7.13 us
  transfers between devices with their start and end apart: 35, of which 12 were waited for; matrix products, arithmetic and copies ran while one was open for 3% of the time, Pallas kernels for 14%

profile of v1, /device:TPU:32, one launch (start us, length us, event | category | flops | bytes accessed | tf_op | source)
XLA Modules:
  0.0 186.3 jit_solution(15237928548288063933)
XLA Ops:
  13.0 7.3 %all-to-all-start = ((bf16[32,32,384]{2,1,0:T(8,128)(2,1)}), bf16[32,32,384]{2,1,0:T(8,128)(2,1)S(1)}, u32[]{:S(2)}, u32[]{:S(2)}) async-start(bf16[32,32,384]{2,1,0:T(8,128)(2,1)} %broadcast_in_dim.12), calls=%async_computation | async-start | bytes 1572864 | tf_op jit(solution)/shard_map/all_to_all | solution.py:382
  20.8 1.9 %collective-permute-start = (bf16[64,1024]{1,0:T(8,128)(2,1)S(1)}, bf16[64,1024]{1,0:T(8,128)(2,1)S(1)}, u32[]{:S(2)}, u32[]{:S(2)}) collective-permute-start(bf16[64,1024]{1,0:T(8,128)(2,1)S(1)} %get-tuple-element.31.refs_2_.na_ref), channel_id=1, source_target_pairs={{0,1},{1,2},{2,3},{3,4},{4,5},{5,6},{6,7},{7,0},{8,9},{9,10},{10,1... | collective-permute-start | bytes 393224 | tf_op jit(solution)/shard_map/ppermute | solution.py:346
  22.8 1.9 %collective-permute-start.4 = (bf16[64,1024]{1,0:T(8,128)(2,1)S(1)}, bf16[64,1024]{1,0:T(8,128)(2,1)S(1)}, u32[]{:S(2)}, u32[]{:S(2)}) collective-permute-start(bf16[64,1024]{1,0:T(8,128)(2,1)S(1)} %get-tuple-element.32.refs_3_.nb_ref), channel_id=1, source_target_pairs={{0,1},{1,2},{2,3},{3,4},{4,5},{5,6},{6,7},{7,0},{8,9},{9,10},{10,1... | collective-permute-start | bytes 393224 | tf_op jit(solution)/shard_map/ppermute | solution.py:346
  24.7 2.0 %collective-permute-start.7 = (bf16[64,1024]{1,0:T(8,128)(2,1)S(1)}, bf16[64,1024]{1,0:T(8,128)(2,1)S(1)}, u32[]{:S(2)}, u32[]{:S(2)}) collective-permute-start(bf16[64,1024]{1,0:T(8,128)(2,1)S(1)} %get-tuple-element.31.refs_2_.na_ref), channel_id=1, source_target_pairs={{0,7},{1,0},{2,1},{3,2},{4,3},{5,4},{6,5},{7,6},{8,15},{9,8},{10,9... | collective-permute-start | bytes 393224 | tf_op jit(solution)/shard_map/ppermute | solution.py:346
  26.7 3.3 %collective-permute-start.11 = (bf16[64,1024]{1,0:T(8,128)(2,1)S(1)}, bf16[64,1024]{1,0:T(8,128)(2,1)S(1)}, u32[]{:S(2)}, u32[]{:S(2)}) collective-permute-start(bf16[64,1024]{1,0:T(8,128)(2,1)S(1)} %collective-permute-done.10.refs_14_), channel_id=1, source_target_pairs={{0,7},{1,0},{2,1},{3,2},{4,3},{5,4},{6,5},{7,6},{8,15},{9,8},{10,9... | collective-permute-start | bytes 393224 | tf_op jit(solution)/shard_map/ppermute | solution.py:346
  31.0 2.1 %collective-permute-done.4.refs_8_ = bf16[64,1024]{1,0:T(8,128)(2,1)S(1)} collective-permute-done((bf16[64,1024]{1,0:T(8,128)(2,1)S(1)}, bf16[64,1024]{1,0:T(8,128)(2,1)S(1)}, u32[]{:S(2)}, u32[]{:S(2)}) %collective-permute-start.4) | collective-permute-done | bytes 131104 | tf_op jit(solution)/shard_map/ppermute | solution.py:346
  33.2 3.0 %collective-permute-start.8 = (bf16[64,1024]{1,0:T(8,128)(2,1)S(1)}, bf16[64,1024]{1,0:T(8,128)(2,1)S(1)}, u32[]{:S(2)}, u32[]{:S(2)}) collective-permute-start(bf16[64,1024]{1,0:T(8,128)(2,1)S(1)} %collective-permute-done.7.refs_11_), channel_id=1, source_target_pairs={{0,7},{1,0},{2,1},{3,2},{4,3},{5,4},{6,5},{7,6},{8,15},{9,8},{10,9... | collective-permute-start | bytes 393224 | tf_op jit(solution)/shard_map/ppermute | solution.py:346
  36.1 3.2 %collective-permute-start.12 = (bf16[64,1024]{1,0:T(8,128)(2,1)S(1)}, bf16[64,1024]{1,0:T(8,128)(2,1)S(1)}, u32[]{:S(2)}, u32[]{:S(2)}) collective-permute-start(bf16[64,1024]{1,0:T(8,128)(2,1)S(1)} %collective-permute-done.11.refs_15_), channel_id=1, source_target_pairs={{0,7},{1,0},{2,1},{3,2},{4,3},{5,4},{6,5},{7,6},{8,15},{9,8},{10,9... | collective-permute-start | bytes 393224 | tf_op jit(solution)/shard_map/ppermute | solution.py:346
  40.0 4.5 %collective-permute-start.9 = (bf16[64,1024]{1,0:T(8,128)(2,1)S(1)}, bf16[64,1024]{1,0:T(8,128)(2,1)S(1)}, u32[]{:S(2)}, u32[]{:S(2)}) collective-permute-start(bf16[64,1024]{1,0:T(8,128)(2,1)S(1)} %collective-permute-done.8.refs_12_), channel_id=1, source_target_pairs={{0,7},{1,0},{2,1},{3,2},{4,3},{5,4},{6,5},{7,6},{8,15},{9,8},{10,9... | collective-permute-start | bytes 393224 | tf_op jit(solution)/shard_map/ppermute | solution.py:346
  44.6 3.2 %collective-permute-start.13 = (bf16[64,1024]{1,0:T(8,128)(2,1)S(1)}, bf16[64,1024]{1,0:T(8,128)(2,1)S(1)}, u32[]{:S(2)}, u32[]{:S(2)}) collective-permute-start(bf16[64,1024]{1,0:T(8,128)(2,1)S(1)} %collective-permute-done.12.refs_16_), channel_id=1, source_target_pairs={{0,7},{1,0},{2,1},{3,2},{4,3},{5,4},{6,5},{7,6},{8,15},{9,8},{10,9... | collective-permute-start | bytes 393224 | tf_op jit(solution)/shard_map/ppermute | solution.py:346
  48.6 1.8 collective-permute-done.13.refs_17_
  50.3 2.5 %collective-permute-done.3.refs_7_ = bf16[64,1024]{1,0:T(8,128)(2,1)S(1)} collective-permute-done((bf16[64,1024]{1,0:T(8,128)(2,1)S(1)}, bf16[64,1024]{1,0:T(8,128)(2,1)S(1)}, u32[]{:S(2)}, u32[]{:S(2)}) %collective-permute-start.3) | collective-permute-done | bytes 131104 | tf_op jit(solution)/shard_map/ppermute | solution.py:346
  52.8 11.9 %attend.1 = (bf16[8,144,128]{2,1,0:T(8,128)(2,1)S(1)}, f32[1024,384]{1,0:T(8,128)}, bf16[1024,1024]{1,0:T(8,128)(2,1)}, bf16[1024,1024]{1,0:T(8,128)(2,1)}) custom-call(s32[3]{0:T(128)S(1)} %pad_add_fusion.refs_0_.meta, f32[8,16]{1,0:T(8,128)S(1)} %copy-done.4, bf16[64,1024]{1,0:T(8,128)(2,1)S(1)} %get-tuple-element.31.refs_2_.na_ref, ...), custom_call_target="tpu_custom_call" | custom-call | flops 3000000000 | bytes 1048576 | tf_op jit(solution)/shard_map/attend/pallas_call | solution.py:393
  64.7 13.7 %all_to_all.15.msg_ref = bf16[8,144,128]{2,1,0:T(8,128)(2,1)S(1)} all-to-all(bf16[8,144,128]{2,1,0:T(8,128)(2,1)S(1)} %get-tuple-element.33), channel_id=1, replica_groups=mesh['dp_0'=4,'dp_1'=4,'dp_2'=2,'seq'=8] {'seq'}, dimensions={0} | all-to-all | bytes 589824 | tf_op jit(solution)/shard_map/all_to_all | solution.py:416
  78.4 9.0 %tail.1 = (bf16[128,1024]{1,0:T(8,128)(2,1)}, bf16[128,1024]{1,0:T(8,128)(2,1)S(1)}, bf16[512,1024]{1,0:T(8,128)(2,1)S(1)}, bf16[512,1024]{1,0:T(8,128)(2,1)}, b...) custom-call(s32[3]{0:T(128)S(1)} %pad_add_fusion.refs_0_.meta, ...), custom_call_target="tpu_custom_call" | custom-call | flops 1500000000 | bytes 1048576 | tf_op jit(solution)/shard_map/tail/pallas_call | solution.py:418
  88.5 3.0 %collective-permute-start.17 = (bf16[128,128]{1,0:T(8,128)(2,1)S(1)}, bf16[128,128]{1,0:T(8,128)(2,1)S(1)}, u32[]{:S(2)}, u32[]{:S(2)}) collective-permute-start(bf16[128,128]{1,0:T(8,128)(2,1)S(1)} %get-tuple-element.40), channel_id=1, source_target_pairs={{0,3},{1,4},{2,5},{3,6},{4,7},{5,0},{6,1},{7,2},{8,11},{9,12},{10,... | collective-permute-start | bytes 98312 | tf_op jit(solution)/shard_map/ppermute | solution.py:346
  91.5 2.9 %collective-permute-start.18 = (bf16[128,128]{1,0:T(8,128)(2,1)S(1)}, bf16[128,128]{1,0:T(8,128)(2,1)S(1)}, u32[]{:S(2)}, u32[]{:S(2)}) collective-permute-start(bf16[128,128]{1,0:T(8,128)(2,1)S(1)} %get-tuple-element.41), channel_id=1, source_target_pairs={{0,4},{1,5},{2,6},{3,7},{4,0},{5,1},{6,2},{7,3},{8,12},{9,13},{10,... | collective-permute-start | bytes 98312 | tf_op jit(solution)/shard_map/ppermute | solution.py:346
  94.5 4.5 %collective-permute-start.19 = (bf16[128,128]{1,0:T(8,128)(2,1)S(1)}, bf16[128,128]{1,0:T(8,128)(2,1)S(1)}, u32[]{:S(2)}, u32[]{:S(2)}) collective-permute-start(bf16[128,128]{1,0:T(8,128)(2,1)S(1)} %get-tuple-element.42), channel_id=1, source_target_pairs={{0,5},{1,6},{2,7},{3,0},{4,1},{5,2},{6,3},{7,4},{8,13},{9,14},{10,... | collective-permute-start | bytes 98312 | tf_op jit(solution)/shard_map/ppermute | solution.py:346
  100.0 2.6 %collective-permute-done.19.refs_6_ = bf16[128,128]{1,0:T(8,128)(2,1)S(1)} collective-permute-done((bf16[128,128]{1,0:T(8,128)(2,1)S(1)}, bf16[128,128]{1,0:T(8,128)(2,1)S(1)}, u32[]{:S(2)}, u32[]{:S(2)}) %collective-permute-start.19) | collective-permute-done | bytes 32800 | tf_op jit(solution)/shard_map/ppermute | solution.py:346
  103.8 2.4 %attend_back.1 = (bf16[128,384]{1,0:T(8,128)(2,1)S(1)}, bf16[128,384]{1,0:T(8,128)(2,1)S(1)}, bf16[128,384]{1,0:T(8,128)(2,1)S(1)}, bf16[128,384]{1,0:T(8,128)(2...) custom-call(s32[3]{0:T(128)S(1)} %pad_add_fusion.refs_0_.meta, ...), custom_call_target="tpu_custom_call" | custom-call | flops 1800000000 | bytes 1048576 | tf_op jit(solution)/shard_map/attend_back/pallas_call | solution.py:486
  106.6 28.5 %all_to_all.16 = bf16[16,32,1024]{2,1,0:T(8,128)(2,1)S(1)} all-to-all(bf16[16,32,1024]{2,1,0:T(8,128)(2,1)S(1)} %bitcast.19), channel_id=1, replica_groups=mesh['dp_0'=4,'dp_1'=4,'dp_2'=2,'seq'=8] {'dp_0','dp_1'}, dimensions={0} | all-to-all | bytes 2097152 | tf_op jit(solution)/shard_map/all_to_all | solution.py:490
  135.9 3.7 %collective-permute-done.29 = bf16[32,1024]{1,0:T(8,128)(2,1)S(1)} collective-permute-done((bf16[32,1024]{1,0:T(8,128)(2,1)S(1)}, bf16[32,1024]{1,0:T(8,128)(2,1)S(1)}, u32[]{:S(2)}, u32[]{:S(2)}) %collective-permute-start.29) | collective-permute-done | bytes 65568 | tf_op jit(solution)/shard_map/ppermute | solution.py:342
  141.8 4.1 %collective-permute-start.23 = (bf16[128,384]{1,0:T(8,128)(2,1)S(1)}, bf16[128,384]{1,0:T(8,128)(2,1)S(1)}, u32[]{:S(2)}, u32[]{:S(2)}) collective-permute-start(bf16[128,384]{1,0:T(8,128)(2,1)S(1)} %get-tuple-element.51), channel_id=1, source_target_pairs={{0,2},{1,3},{2,4},{3,5},{4,6},{5,7},{6,0},{7,1},{8,10},{9,11},{10,... | collective-permute-start | bytes 294920 | tf_op jit(solution)/shard_map/ppermute | solution.py:346
  146.0 4.5 %collective-permute-start.31 = (bf16[32,1024]{1,0:T(8,128)(2,1)S(1)}, bf16[32,1024]{1,0:T(8,128)(2,1)S(1)}, u32[]{:S(2)}, u32[]{:S(2)}) collective-permute-start(bf16[32,1024]{1,0:T(8,128)(2,1)S(1)} %add_convert_fusion.1), channel_id=1, source_target_pairs={{0,7},{1,6},{2,5},{3,4},{4,3},{5,2},{6,1},{7,0},{8,15},{9,14},{10,... | collective-permute-start | bytes 196616 | tf_op jit(solution)/shard_map/ppermute | solution.py:342
  150.5 2.8 %gate.1.refs_9_ = f32[128,1024]{1,0:T(8,128)S(1)} custom-call(bf16[128,1024]{1,0:T(8,128)(2,1)S(1)} %get-tuple-element.57.dpg_ref, bf16[1024,2048]{1,0:T(8,128)(2,1)} %all-gather.3.cloned.1.call-done.wg_ref.wo_ref), custom_call_target="tpu_custom_call" | custom-call | flops 600000000 | bytes 1048576 | tf_op jit(solution)/shard_map/gate/pallas_call | solution.py:462
  153.3 1.9 %collective-permute-start.24 = (bf16[128,384]{1,0:T(8,128)(2,1)S(1)}, bf16[128,384]{1,0:T(8,128)(2,1)S(1)}, u32[]{:S(2)}, u32[]{:S(2)}) collective-permute-start(bf16[128,384]{1,0:T(8,128)(2,1)S(1)} %get-tuple-element.52), channel_id=1, source_target_pairs={{0,3},{1,4},{2,5},{3,6},{4,7},{5,0},{6,1},{7,2},{8,11},{9,12},{10,... | collective-permute-start | bytes 294920 | tf_op jit(solution)/shard_map/ppermute | solution.py:346
  155.2 3.3 %collective-permute-start.25 = (bf16[128,384]{1,0:T(8,128)(2,1)S(1)}, bf16[128,384]{1,0:T(8,128)(2,1)S(1)}, u32[]{:S(2)}, u32[]{:S(2)}) collective-permute-start(bf16[128,384]{1,0:T(8,128)(2,1)S(1)} %get-tuple-element.53), channel_id=1, source_target_pairs={{0,4},{1,5},{2,6},{3,7},{4,0},{5,1},{6,2},{7,3},{8,12},{9,13},{10,... | collective-permute-start | bytes 294920 | tf_op jit(solution)/shard_map/ppermute | solution.py:346
  159.7 1.9 %collective-permute-start.27 = (bf16[128,384]{1,0:T(8,128)(2,1)S(1)}, bf16[128,384]{1,0:T(8,128)(2,1)S(1)}, u32[]{:S(2)}, u32[]{:S(2)}) collective-permute-start(bf16[128,384]{1,0:T(8,128)(2,1)S(1)} %get-tuple-element.55), channel_id=1, source_target_pairs={{0,6},{1,7},{2,0},{3,1},{4,2},{5,3},{6,4},{7,5},{8,14},{9,15},{10,... | collective-permute-start | bytes 294920 | tf_op jit(solution)/shard_map/ppermute | solution.py:346
  163.2 2.6 %collective-permute-done.25.refs_5_ = bf16[128,384]{1,0:T(8,128)(2,1)S(1)} collective-permute-done((bf16[128,384]{1,0:T(8,128)(2,1)S(1)}, bf16[128,384]{1,0:T(8,128)(2,1)S(1)}, u32[]{:S(2)}, u32[]{:S(2)}) %collective-permute-start.25) | collective-permute-done | bytes 98336 | tf_op jit(solution)/shard_map/ppermute | solution.py:346
  165.8 3.1 %collective-permute-done.26.refs_6_ = bf16[128,384]{1,0:T(8,128)(2,1)S(1)} collective-permute-done((bf16[128,384]{1,0:T(8,128)(2,1)S(1)}, bf16[128,384]{1,0:T(8,128)(2,1)S(1)}, u32[]{:S(2)}, u32[]{:S(2)}) %collective-permute-start.26) | collective-permute-done | bytes 98336 | tf_op jit(solution)/shard_map/ppermute | solution.py:346
  170.6 1.7 collective-permute-done.28.refs_8_
  172.4 7.1 %final.1 = bf16[128,1024]{1,0:T(8,128)(2,1)} custom-call(s32[3]{0:T(128)S(1)} %pad_add_fusion.refs_0_.meta, bf16[128,384]{1,0:T(8,128)(2,1)S(1)} %get-tuple-element.49.refs_1_, bf16[128,384]{1,0:T(8,128)(2,1)S(1)} %collective-permute-done.22.refs_2_, bf16[128,384]{1,0:T(8,128)(2,1)S(1)} %collective-permute-done.23.refs_3_, ...), custom_call_target="tpu_custom_call" | custom-call | flops 1500000000 | bytes 1048576 | tf_op jit(solution)/shard_map/final/pallas_call | solution.py:520
  (79 shorter events, 19.3 us)
Async XLA Ops:
  7.2 71.2 %all-gather.3.cloned.1.call-start = ((), (), s32[]{:S(2)}) async-start(), calls=%async_computation.3 | async-start | bytes 4325376 | tf_op jit(solution)/shard_map/all_gather | solution.py:369
  9.7 162.7 %all-gather.5.cloned.1.call-start = ((), (), s32[]{:S(2)}) async-start(), calls=%async_computation.4 | async-start | bytes 6488064 | tf_op jit(solution)/shard_map/all_gather | solution.py:372
  13.0 39.7 %all-to-all-start = ((bf16[32,32,384]{2,1,0:T(8,128)(2,1)}), bf16[32,32,384]{2,1,0:T(8,128)(2,1)S(1)}, u32[]{:S(2)}, u32[]{:S(2)}) async-start(bf16[32,32,384]{2,1,0:T(8,128)(2,1)} %broadcast_in_dim.12), calls=%async_computation | async-start | bytes 1572864 | tf_op jit(solution)/shard_map/all_to_all | solution.py:382
  20.7 6.1 %collective-permute-start.10 = (bf16[64,1024]{1,0:T(8,128)(2,1)S(1)}, bf16[64,1024]{1,0:T(8,128)(2,1)S(1)}, u32[]{:S(2)}, u32[]{:S(2)}) collective-permute-start(bf16[64,1024]{1,0:T(8,128)(2,1)S(1)} %get-tuple-element.32.refs_3_.nb_ref), channel_id=1, source_target_pairs={{0,7},{1,0},{2,1},{3,2},{4,3},{5,4},{6,5},{7,6},{8,15},{9,8},{10,9... | collective-permute-start | bytes 393224 | tf_op jit(solution)/shard_map/ppermute | solution.py:346
  20.8 10.2 %collective-permute-start = (bf16[64,1024]{1,0:T(8,128)(2,1)S(1)}, bf16[64,1024]{1,0:T(8,128)(2,1)S(1)}, u32[]{:S(2)}, u32[]{:S(2)}) collective-permute-start(bf16[64,1024]{1,0:T(8,128)(2,1)S(1)} %get-tuple-element.31.refs_2_.na_ref), channel_id=1, source_target_pairs={{0,1},{1,2},{2,3},{3,4},{4,5},{5,6},{6,7},{7,0},{8,9},{9,10},{10,1... | collective-permute-start | bytes 393224 | tf_op jit(solution)/shard_map/ppermute | solution.py:346
  22.8 10.4 %collective-permute-start.4 = (bf16[64,1024]{1,0:T(8,128)(2,1)S(1)}, bf16[64,1024]{1,0:T(8,128)(2,1)S(1)}, u32[]{:S(2)}, u32[]{:S(2)}) collective-permute-start(bf16[64,1024]{1,0:T(8,128)(2,1)S(1)} %get-tuple-element.32.refs_3_.nb_ref), channel_id=1, source_target_pairs={{0,1},{1,2},{2,3},{3,4},{4,5},{5,6},{6,7},{7,0},{8,9},{9,10},{10,1... | collective-permute-start | bytes 393224 | tf_op jit(solution)/shard_map/ppermute | solution.py:346
  24.7 8.5 %collective-permute-start.7 = (bf16[64,1024]{1,0:T(8,128)(2,1)S(1)}, bf16[64,1024]{1,0:T(8,128)(2,1)S(1)}, u32[]{:S(2)}, u32[]{:S(2)}) collective-permute-start(bf16[64,1024]{1,0:T(8,128)(2,1)S(1)} %get-tuple-element.31.refs_2_.na_ref), channel_id=1, source_target_pairs={{0,7},{1,0},{2,1},{3,2},{4,3},{5,4},{6,5},{7,6},{8,15},{9,8},{10,9... | collective-permute-start | bytes 393224 | tf_op jit(solution)/shard_map/ppermute | solution.py:346
  26.7 9.4 %collective-permute-start.11 = (bf16[64,1024]{1,0:T(8,128)(2,1)S(1)}, bf16[64,1024]{1,0:T(8,128)(2,1)S(1)}, u32[]{:S(2)}, u32[]{:S(2)}) collective-permute-start(bf16[64,1024]{1,0:T(8,128)(2,1)S(1)} %collective-permute-done.10.refs_14_), channel_id=1, source_target_pairs={{0,7},{1,0},{2,1},{3,2},{4,3},{5,4},{6,5},{7,6},{8,15},{9,8},{10,9... | collective-permute-start | bytes 393224 | tf_op jit(solution)/shard_map/ppermute | solution.py:346
  31.0 8.3 %collective-permute-start.1 = (bf16[64,1024]{1,0:T(8,128)(2,1)S(1)}, bf16[64,1024]{1,0:T(8,128)(2,1)S(1)}, u32[]{:S(2)}, u32[]{:S(2)}) collective-permute-start(bf16[64,1024]{1,0:T(8,128)(2,1)S(1)} %collective-permute-done.refs_4_), channel_id=1, source_target_pairs={{0,1},{1,2},{2,3},{3,4},{4,5},{5,6},{6,7},{7,0},{8,9},{9,10},{10,1... | collective-permute-start | bytes 393224 | tf_op jit(solution)/shard_map/ppermute | solution.py:346
  33.2 6.9 %collective-permute-start.5 = (bf16[64,1024]{1,0:T(8,128)(2,1)S(1)}, bf16[64,1024]{1,0:T(8,128)(2,1)S(1)}, u32[]{:S(2)}, u32[]{:S(2)}) collective-permute-start(bf16[64,1024]{1,0:T(8,128)(2,1)S(1)} %collective-permute-done.4.refs_8_), channel_id=1, source_target_pairs={{0,1},{1,2},{2,3},{3,4},{4,5},{5,6},{6,7},{7,0},{8,9},{9,10},{10,1... | collective-permute-start | bytes 393224 | tf_op jit(solution)/shard_map/ppermute | solution.py:346
  33.2 6.9 %collective-permute-start.8 = (bf16[64,1024]{1,0:T(8,128)(2,1)S(1)}, bf16[64,1024]{1,0:T(8,128)(2,1)S(1)}, u32[]{:S(2)}, u32[]{:S(2)}) collective-permute-start(bf16[64,1024]{1,0:T(8,128)(2,1)S(1)} %collective-permute-done.7.refs_11_), channel_id=1, source_target_pairs={{0,7},{1,0},{2,1},{3,2},{4,3},{5,4},{6,5},{7,6},{8,15},{9,8},{10,9... | collective-permute-start | bytes 393224 | tf_op jit(solution)/shard_map/ppermute | solution.py:346
  36.1 8.4 %collective-permute-start.12 = (bf16[64,1024]{1,0:T(8,128)(2,1)S(1)}, bf16[64,1024]{1,0:T(8,128)(2,1)S(1)}, u32[]{:S(2)}, u32[]{:S(2)}) collective-permute-start(bf16[64,1024]{1,0:T(8,128)(2,1)S(1)} %collective-permute-done.11.refs_15_), channel_id=1, source_target_pairs={{0,7},{1,0},{2,1},{3,2},{4,3},{5,4},{6,5},{7,6},{8,15},{9,8},{10,9... | collective-permute-start | bytes 393224 | tf_op jit(solution)/shard_map/ppermute | solution.py:346
  39.4 8.4 %collective-permute-start.2 = (bf16[64,1024]{1,0:T(8,128)(2,1)S(1)}, bf16[64,1024]{1,0:T(8,128)(2,1)S(1)}, u32[]{:S(2)}, u32[]{:S(2)}) collective-permute-start(bf16[64,1024]{1,0:T(8,128)(2,1)S(1)} %collective-permute-done.1.refs_5_), channel_id=1, source_target_pairs={{0,1},{1,2},{2,3},{3,4},{4,5},{5,6},{6,7},{7,0},{8,9},{9,10},{10,1... | collective-permute-start | bytes 393224 | tf_op jit(solution)/shard_map/ppermute | solution.py:346
  40.0 8.5 %collective-permute-start.6 = (bf16[64,1024]{1,0:T(8,128)(2,1)S(1)}, bf16[64,1024]{1,0:T(8,128)(2,1)S(1)}, u32[]{:S(2)}, u32[]{:S(2)}) collective-permute-start(bf16[64,1024]{1,0:T(8,128)(2,1)S(1)} %collective-permute-done.5.refs_9_), channel_id=1, source_target_pairs={{0,1},{1,2},{2,3},{3,4},{4,5},{5,6},{6,7},{7,0},{8,9},{9,10},{10,1... | collective-permute-start | bytes 393224 | tf_op jit(solution)/shard_map/ppermute | solution.py:346
  40.0 8.5 %collective-permute-start.9 = (bf16[64,1024]{1,0:T(8,128)(2,1)S(1)}, bf16[64,1024]{1,0:T(8,128)(2,1)S(1)}, u32[]{:S(2)}, u32[]{:S(2)}) collective-permute-start(bf16[64,1024]{1,0:T(8,128)(2,1)S(1)} %collective-permute-done.8.refs_12_), channel_id=1, source_target_pairs={{0,7},{1,0},{2,1},{3,2},{4,3},{5,4},{6,5},{7,6},{8,15},{9,8},{10,9... | collective-permute-start | bytes 393224 | tf_op jit(solution)/shard_map/ppermute | solution.py:346
  44.6 5.8 %collective-permute-start.13 = (bf16[64,1024]{1,0:T(8,128)(2,1)S(1)}, bf16[64,1024]{1,0:T(8,128)(2,1)S(1)}, u32[]{:S(2)}, u32[]{:S(2)}) collective-permute-start(bf16[64,1024]{1,0:T(8,128)(2,1)S(1)} %collective-permute-done.12.refs_16_), channel_id=1, source_target_pairs={{0,7},{1,0},{2,1},{3,2},{4,3},{5,4},{6,5},{7,6},{8,15},{9,8},{10,9... | collective-permute-start | bytes 393224 | tf_op jit(solution)/shard_map/ppermute | solution.py:346
  47.8 5.0 %collective-permute-start.3 = (bf16[64,1024]{1,0:T(8,128)(2,1)S(1)}, bf16[64,1024]{1,0:T(8,128)(2,1)S(1)}, u32[]{:S(2)}, u32[]{:S(2)}) collective-permute-start(bf16[64,1024]{1,0:T(8,128)(2,1)S(1)} %collective-permute-done.2.refs_6_), channel_id=1, source_target_pairs={{0,1},{1,2},{2,3},{3,4},{4,5},{5,6},{6,7},{7,0},{8,9},{9,10},{10,1... | collective-permute-start | bytes 393224 | tf_op jit(solution)/shard_map/ppermute | solution.py:346
  87.3 18.9 %collective-permute-start.14 = (bf16[512,1024]{1,0:T(8,128)(2,1)}, bf16[512,1024]{1,0:T(8,128)(2,1)S(1)}, u32[]{:S(2)}, u32[]{:S(2)}) collective-permute-start(bf16[512,1024]{1,0:T(8,128)(2,1)} %get-tuple-element.36), channel_id=1, source_target_pairs={{0,8},{8,0},{1,9},{9,1},{2,10},{10,2},{3,11},{11,3},{4,12},{12,4},... | collective-permute-start | bytes 3145736 | tf_op jit(solution)/shard_map/ppermute | solution.py:342
  87.3 7.1 %collective-permute-start.15 = (bf16[128,128]{1,0:T(8,128)(2,1)S(1)}, bf16[128,128]{1,0:T(8,128)(2,1)S(1)}, u32[]{:S(2)}, u32[]{:S(2)}) collective-permute-start(bf16[128,128]{1,0:T(8,128)(2,1)S(1)} %get-tuple-element.38), channel_id=1, source_target_pairs={{0,1},{1,2},{2,3},{3,4},{4,5},{5,6},{6,7},{7,0},{8,9},{9,10},{10,1... | collective-permute-start | bytes 98312 | tf_op jit(solution)/shard_map/ppermute | solution.py:346
  87.9 11.0 %collective-permute-start.16 = (bf16[128,128]{1,0:T(8,128)(2,1)S(1)}, bf16[128,128]{1,0:T(8,128)(2,1)S(1)}, u32[]{:S(2)}, u32[]{:S(2)}) collective-permute-start(bf16[128,128]{1,0:T(8,128)(2,1)S(1)} %get-tuple-element.39), channel_id=1, source_target_pairs={{0,2},{1,3},{2,4},{3,5},{4,6},{5,7},{6,0},{7,1},{8,10},{9,11},{10,... | collective-permute-start | bytes 98312 | tf_op jit(solution)/shard_map/ppermute | solution.py:346
  88.5 10.4 %collective-permute-start.17 = (bf16[128,128]{1,0:T(8,128)(2,1)S(1)}, bf16[128,128]{1,0:T(8,128)(2,1)S(1)}, u32[]{:S(2)}, u32[]{:S(2)}) collective-permute-start(bf16[128,128]{1,0:T(8,128)(2,1)S(1)} %get-tuple-element.40), channel_id=1, source_target_pairs={{0,3},{1,4},{2,5},{3,6},{4,7},{5,0},{6,1},{7,2},{8,11},{9,12},{10,... | collective-permute-start | bytes 98312 | tf_op jit(solution)/shard_map/ppermute | solution.py:346
  91.5 8.5 %collective-permute-start.18 = (bf16[128,128]{1,0:T(8,128)(2,1)S(1)}, bf16[128,128]{1,0:T(8,128)(2,1)S(1)}, u32[]{:S(2)}, u32[]{:S(2)}) collective-permute-start(bf16[128,128]{1,0:T(8,128)(2,1)S(1)} %get-tuple-element.41), channel_id=1, source_target_pairs={{0,4},{1,5},{2,6},{3,7},{4,0},{5,1},{6,2},{7,3},{8,12},{9,13},{10,... | collective-permute-start | bytes 98312 | tf_op jit(solution)/shard_map/ppermute | solution.py:346
  94.5 8.2 %collective-permute-start.19 = (bf16[128,128]{1,0:T(8,128)(2,1)S(1)}, bf16[128,128]{1,0:T(8,128)(2,1)S(1)}, u32[]{:S(2)}, u32[]{:S(2)}) collective-permute-start(bf16[128,128]{1,0:T(8,128)(2,1)S(1)} %get-tuple-element.42), channel_id=1, source_target_pairs={{0,5},{1,6},{2,7},{3,0},{4,1},{5,2},{6,3},{7,4},{8,13},{9,14},{10,... | collective-permute-start | bytes 98312 | tf_op jit(solution)/shard_map/ppermute | solution.py:346
  139.7 6.2 %collective-permute-start.30 = (bf16[32,1024]{1,0:T(8,128)(2,1)S(1)}, bf16[32,1024]{1,0:T(8,128)(2,1)S(1)}, u32[]{:S(2)}, u32[]{:S(2)}) collective-permute-start(bf16[32,1024]{1,0:T(8,128)(2,1)S(1)} %add_convert_fusion.2), channel_id=1, source_target_pairs={{0,3},{1,2},{2,1},{3,0},{4,7},{5,6},{6,5},{7,4},{8,11},{9,10},{10,... | collective-permute-start | bytes 196616 | tf_op jit(solution)/shard_map/ppermute | solution.py:342
  141.3 17.2 %collective-permute-start.22 = (bf16[128,384]{1,0:T(8,128)(2,1)S(1)}, bf16[128,384]{1,0:T(8,128)(2,1)S(1)}, u32[]{:S(2)}, u32[]{:S(2)}) collective-permute-start(bf16[128,384]{1,0:T(8,128)(2,1)S(1)} %get-tuple-element.50), channel_id=1, source_target_pairs={{0,1},{1,2},{2,3},{3,4},{4,5},{5,6},{6,7},{7,0},{8,9},{9,10},{10,1... | collective-permute-start | bytes 294920 | tf_op jit(solution)/shard_map/ppermute | solution.py:346
  141.8 17.9 %collective-permute-start.23 = (bf16[128,384]{1,0:T(8,128)(2,1)S(1)}, bf16[128,384]{1,0:T(8,128)(2,1)S(1)}, u32[]{:S(2)}, u32[]{:S(2)}) collective-permute-start(bf16[128,384]{1,0:T(8,128)(2,1)S(1)} %get-tuple-element.51), channel_id=1, source_target_pairs={{0,2},{1,3},{2,4},{3,5},{4,6},{5,7},{6,0},{7,1},{8,10},{9,11},{10,... | collective-permute-start | bytes 294920 | tf_op jit(solution)/shard_map/ppermute | solution.py:346
  146.0 15.7 %collective-permute-start.31 = (bf16[32,1024]{1,0:T(8,128)(2,1)S(1)}, bf16[32,1024]{1,0:T(8,128)(2,1)S(1)}, u32[]{:S(2)}, u32[]{:S(2)}) collective-permute-start(bf16[32,1024]{1,0:T(8,128)(2,1)S(1)} %add_convert_fusion.1), channel_id=1, source_target_pairs={{0,7},{1,6},{2,5},{3,4},{4,3},{5,2},{6,1},{7,0},{8,15},{9,14},{10,... | collective-permute-start | bytes 196616 | tf_op jit(solution)/shard_map/ppermute | solution.py:342
  153.3 9.9 %collective-permute-start.24 = (bf16[128,384]{1,0:T(8,128)(2,1)S(1)}, bf16[128,384]{1,0:T(8,128)(2,1)S(1)}, u32[]{:S(2)}, u32[]{:S(2)}) collective-permute-start(bf16[128,384]{1,0:T(8,128)(2,1)S(1)} %get-tuple-element.52), channel_id=1, source_target_pairs={{0,3},{1,4},{2,5},{3,6},{4,7},{5,0},{6,1},{7,2},{8,11},{9,12},{10,... | collective-permute-start | bytes 294920 | tf_op jit(solution)/shard_map/ppermute | solution.py:346
  155.2 10.6 %collective-permute-start.25 = (bf16[128,384]{1,0:T(8,128)(2,1)S(1)}, bf16[128,384]{1,0:T(8,128)(2,1)S(1)}, u32[]{:S(2)}, u32[]{:S(2)}) collective-permute-start(bf16[128,384]{1,0:T(8,128)(2,1)S(1)} %get-tuple-element.53), channel_id=1, source_target_pairs={{0,4},{1,5},{2,6},{3,7},{4,0},{5,1},{6,2},{7,3},{8,12},{9,13},{10,... | collective-permute-start | bytes 294920 | tf_op jit(solution)/shard_map/ppermute | solution.py:346
  158.5 10.4 %collective-permute-start.26 = (bf16[128,384]{1,0:T(8,128)(2,1)S(1)}, bf16[128,384]{1,0:T(8,128)(2,1)S(1)}, u32[]{:S(2)}, u32[]{:S(2)}) collective-permute-start(bf16[128,384]{1,0:T(8,128)(2,1)S(1)} %get-tuple-element.54), channel_id=1, source_target_pairs={{0,5},{1,6},{2,7},{3,0},{4,1},{5,2},{6,3},{7,4},{8,13},{9,14},{10,... | collective-permute-start | bytes 294920 | tf_op jit(solution)/shard_map/ppermute | solution.py:346
  159.7 10.9 %collective-permute-start.27 = (bf16[128,384]{1,0:T(8,128)(2,1)S(1)}, bf16[128,384]{1,0:T(8,128)(2,1)S(1)}, u32[]{:S(2)}, u32[]{:S(2)}) collective-permute-start(bf16[128,384]{1,0:T(8,128)(2,1)S(1)} %get-tuple-element.55), channel_id=1, source_target_pairs={{0,6},{1,7},{2,0},{3,1},{4,2},{5,3},{6,4},{7,5},{8,14},{9,15},{10,... | collective-permute-start | bytes 294920 | tf_op jit(solution)/shard_map/ppermute | solution.py:346
  161.6 10.7 %collective-permute-start.28 = (bf16[128,384]{1,0:T(8,128)(2,1)S(1)}, bf16[128,384]{1,0:T(8,128)(2,1)S(1)}, u32[]{:S(2)}, u32[]{:S(2)}) collective-permute-start(bf16[128,384]{1,0:T(8,128)(2,1)S(1)} %get-tuple-element.56), channel_id=1, source_target_pairs={{0,7},{1,0},{2,1},{3,2},{4,3},{5,4},{6,5},{7,6},{8,15},{9,8},{10,9... | collective-permute-start | bytes 294920 | tf_op jit(solution)/shard_map/ppermute | solution.py:346
  (12 other events, 249.6 us)
Sparse Core Ops, SparseCore 0:
  11.1 56.5 all-gather.2
  70.9 64.0 all-gather.4

commit v2 on v1

--- a/solution.py
+++ b/solution.py
@@ -19,6 +19,7 @@
 EPS = 1e-05
 MSG = 144
 LIMIT = 52000
+UNROLL = 8
 F32 = jnp.float32
 BF16 = jnp.bfloat16
 
@@ -44,13 +45,24 @@
     return jnp.dot(a, b, preferred_element_type=F32)
 
 
-def norm_kernel(x_ref, gain_ref, a_ref, b_ref):
+def prep_kernel(
+    x_ref, gain_ref, w_ref, wout_ref, a_ref, b_ref, early_ref, late_ref, copies_ref
+):
+    me = lax.axis_index("seq")
     x = x_ref[...].astype(F32)
     c = x - jnp.mean(x, axis=-1, keepdims=True)
     var = jnp.mean(c * c, axis=-1, keepdims=True)
     n = (c * lax.rsqrt(var + EPS) * gain_ref[...]).astype(BF16)
     a_ref[...] = n[:64]
     b_ref[...] = n[64:]
+    early_ref[:, :D] = w_ref[:, :D]
+    early_ref[:, D:] = wout_ref[...]
+    late_ref[...] = w_ref[:, D:]
+    for part in range(3):
+        at = pl.multiple_of((part + 1) * D + me * DH, DH)
+        own = w_ref[:, pl.ds(at, DH)]
+        for n in range(32):
+            copies_ref[n, :, part * DH : (part + 1) * DH] = own
 
 
 ARRIVALS = (
@@ -63,25 +75,20 @@
 
 
 def forward_kernel(*refs):
-    meta, bias_ref = refs[0], refs[1]
+    length_ref, bias_ref = refs[0], refs[1]
     blocks = refs[2:18]
     ws_ref, row_ref = refs[18:20]
     msg_ref, proj_ref, w_ref, g_ref = refs[20:24]
     x_all, col_sc, q_sc, k_sc, vt_sc, s_sc = refs[24:]
-    me, length = meta[0], meta[1]
+    me, length = lax.axis_index("seq"), length_ref[0]
     for (far, half), blk in zip(ARRIVALS, blocks):
         at = lax.rem(me + far + H, H) * T + half * 64
         x_all[pl.ds(pl.multiple_of(at, 64), 64), :] = blk[...]
 
-    def project(c, carry):
-        rows = pl.ds(pl.multiple_of(c * TI, TI), TI)
-        proj_ref[rows, :] = mm(x_all[rows, :], ws_ref[...])
-        return carry
-
-    lax.fori_loop(0, S // TI, project, 0)
+    proj_ref[...] = mm(x_all[...], ws_ref[...])
     for c in range(8):
         cols = slice(c * T, (c + 1) * T)
-        col_sc[cols, :] = jnp.broadcast_to(row_ref[:, cols], (T, T)).T
+        col_sc[cols, :] = jnp.broadcast_to(row_ref[:, cols].astype(F32), (T, T)).T
     for c in range(8):
         rows = slice(c * T, (c + 1) * T)
         p = proj_ref[rows, :]
@@ -99,7 +106,7 @@
             at = pl.multiple_of(c * CH, CH)
             rows = pl.ds(pl.multiple_of(j0 + at, CH), CH)
             col = col_sc[rows, :]
-            e = row_ref[:, i0 : i0 + TI] - jnp.concatenate([col, col], axis=1)
+            e = row_ref[:, i0 : i0 + TI].astype(F32) - jnp.concatenate([col, col], axis=1)
             bias = jnp.full((CH, TI), levels[0], F32)
             for b in range(1, NB):
                 bias = jnp.where(e >= float(2**b - 1), levels[b], bias)
@@ -117,7 +124,7 @@
             g_ref[rows, i0 : i0 + TI] = g.astype(BF16)
             return carry
 
-        lax.fori_loop(0, TI // CH, chunk, 0, unroll=2)
+        lax.fori_loop(0, TI // CH, chunk, 0, unroll=UNROLL)
 
     for bi in range(S // TI):
         i0 = bi * TI
@@ -152,7 +159,7 @@
 
 
 def tail_kernel(
-    meta,
+    length_ref,
     msg_ref,
     na_ref,
     nb_ref,
@@ -168,7 +175,7 @@
     *more,
 ):
     datt_out, (att_sc, datt_ref, rows_sc, pg_sc, dmix_sc) = more[:H], more[H:]
-    me, length, core = meta[0], meta[1], meta[2]
+    me, core, length = lax.axis_index("seq"), lax.axis_index("dp_2"), length_ref[0]
     for h in range(H):
         blk = msg_ref[h].astype(F32)
         att_t = blk[:DH] + (blk[DH : DH + 1] + blk[DH + 1 : DH + 2] + blk[DH + 2 : DH + 3])
@@ -178,12 +185,12 @@
     cot = cot_ref[...]
 
     def columns(n, carry):
-        at = pl.ds(pl.multiple_of(n * 256, 256), 256)
+        at = pl.ds(pl.multiple_of(n * 512, 512), 512)
         pg_sc[:, at] = mm(rows_sc[...], wg_ref[:, at])
         dmix_sc[:, at] = nt(cot, wo_ref[at, :])
         return carry
 
-    lax.fori_loop(0, D // 256, columns, 0)
+    lax.fori_loop(0, D // 512, columns, 0)
     pg = pg_sc[...]
     d_mix = dmix_sc[...]
     att = att_sc[...]
@@ -209,25 +216,14 @@
     for h in range(H):
         datt_ref[h] = d_att[:, h * DH : (h + 1) * DH]
 
-    def head(h, carry):
-        part = tn(rows_sc[:, pl.ds(pl.multiple_of(h * DH, DH), DH)], cot).astype(BF16)
+    for h in range(H):
+        part = tn(rows_sc[:, h * DH : (h + 1) * DH], cot).astype(BF16)
         for t in range(2):
-            at = pl.ds(pl.multiple_of((2 * h + t) * 32, 32), 32)
+            at = slice((2 * h + t) * 32, (2 * h + t + 1) * 32)
             even, odd = part[t * 64 : t * 64 + 32], part[t * 64 + 32 : t * 64 + 64]
             own_ref[at, :] = jnp.where(core == 0, even, odd)
             send_ref[at, :] = jnp.where(core == 0, odd, even)
-        return carry
-
-    lax.fori_loop(0, H, head, 0)
-
-    def mix(n, carry):
-        at = pl.ds(pl.multiple_of(n * 256, 256), 256)
-        mixed_ref[:, at] = (
-            x_ref[:, at].astype(F32) + mm(rows_sc[...], wo_ref[:, at])
-        ).astype(BF16)
-        return carry
-
-    lax.fori_loop(0, D // 256, mix, 0)
+    mixed_ref[...] = (x_ref[...].astype(F32) + mm(rows_sc[...], wo_ref[...])).astype(BF16)
     for k in range(H):
         datt_out[k][...] = datt_ref[lax.rem(me + k, H)]
 
@@ -242,12 +238,13 @@
 
 
 def backward_kernel(*refs):
-    meta, blocks = refs[0], refs[1:9]
-    proj_ref, w_ref, g_ref = refs[9:12]
-    outs = refs[12:20]
-    q_sc, k_sc, kt_sc, v_sc, ds_sc, dqt_sc, out_ref, d_ref = refs[20:]
+    blocks = refs[:8]
+    proj_ref, w_ref, g_ref = refs[8:11]
+    outs = refs[11:19]
+    me = lax.axis_index("seq")
+    q_sc, k_sc, kt_sc, v_sc, ds_sc, dqt_sc, out_ref, d_ref = refs[19:]
     for k in range(H):
-        d_ref[lax.rem(meta[0] - k + H, H)] = blocks[k][...]
+        d_ref[lax.rem(me - k + H, H)] = blocks[k][...]
     for c in range(8):
         rows = slice(c * T, (c + 1) * T)
         p = proj_ref[rows, :]
@@ -287,19 +284,19 @@
         slope = sg * (1.0 + p * (1.0 - sg))
         out_ref[t, :, DH : 2 * DH] = (dqt_sc[:, at].T * slope).astype(BF16)
     for k in range(H):
-        outs[k][...] = out_ref[lax.rem(meta[0] + k, H)]
+        outs[k][...] = out_ref[lax.rem(me + k, H)]
 
 
 def final_kernel(*refs):
-    meta = refs[0]
-    blocks = refs[1:9]
-    back_ref, w_ref, x_ref, cot_ref, gain_ref, out_ref, msg_ref, lhs, acc = refs[9:]
+    blocks = refs[:8]
+    back_ref, w_ref, x_ref, cot_ref, gain_ref, out_ref, msg_ref, lhs, acc = refs[8:]
+    me = lax.axis_index("seq")
     b = pl.program_id(0)
 
     @pl.when(b == 0)
     def _():
         for k in range(H):
-            msg_ref[lax.rem(meta[0] - k + H, H)] = blocks[k][...]
+            msg_ref[lax.rem(me - k + H, H)] = blocks[k][...]
         for n in range(3):
             for h in range(H):
                 lhs[n, :, h * DH : (h + 1) * DH] = msg_ref[h, :, n * DH : (n + 1) * DH]
@@ -349,36 +346,26 @@
 def layer(tokens, cotangent, stamps, lengths, w_qkvu, w_out, gain_in, gain_out, bias_table):
     x = tokens[0]
     cot = cotangent[0]
-    me = lax.axis_index("seq")
-    core = lax.axis_index("dp_2")
-    meta = jnp.stack([me, lengths[0], core]).astype(jnp.int32)
     gain_in = gain_in.reshape(1, D)
     gain_out = gain_out.reshape(1, D)
-    stamp_row = stamps.astype(F32)
-
-    na, nb = pl.pallas_call(
-        norm_kernel,
-        out_shape=[jax.ShapeDtypeStruct((64, D), BF16)] * 2,
-        in_specs=[VMEM, VMEM],
-        out_specs=[VMEM, VMEM],
-        compiler_params=params(),
-        cost_estimate=cost(1),
-        name="norm",
-    )(x, gain_in)
-
-    w_early = lax.all_gather(
-        jnp.concatenate([w_qkvu[:, :D], w_out], axis=1), DP, axis=0, tiled=True
-    )
-    w_late = lax.all_gather(w_qkvu[:, D:], DP, axis=0, tiled=True)
-
-    head_w = jnp.concatenate(
-        [
-            lax.dynamic_slice_in_dim(w_qkvu, part * D + me * DH, DH, axis=1)
-            for part in (1, 2, 3)
-        ],
-        axis=1,
-    )
-    copies = jnp.broadcast_to(head_w[None], (32, *head_w.shape))
+
+    na, nb, early, late, copies = pl.pallas_call(
+        prep_kernel,
+        out_shape=[
+            jax.ShapeDtypeStruct((64, D), BF16),
+            jax.ShapeDtypeStruct((64, D), BF16),
+            jax.ShapeDtypeStruct((32, 2 * D), BF16),
+            jax.ShapeDtypeStruct((32, 3 * D), BF16),
+            jax.ShapeDtypeStruct((32, 32, 3 * DH), BF16),
+        ],
+        in_specs=[VMEM] * 4,
+        out_specs=[VMEM] * 5,
+        compiler_params=params(61500),
+        cost_estimate=cost(2),
+        name="prep",
+    )(x, gain_in, w_qkvu, w_out)
+    w_early = lax.all_gather(early, DP, axis=0, tiled=True)
+    w_late = lax.all_gather(late, DP, axis=0, tiled=True)
     ws = lax.all_to_all(copies, DP, 0, 0, tiled=True)
     ws = ws.reshape(D, 3 * DH)
 
@@ -411,7 +398,7 @@
         compiler_params=params(),
         cost_estimate=cost(10),
         name="attend",
-    )(meta, bias_table, *[arrived[a] for a in ARRIVALS], ws, stamp_row)
+    )(lengths, bias_table, *[arrived[a] for a in ARRIVALS], ws, stamps)
 
     att_msg = lax.all_to_all(msg, "seq", 0, 0, tiled=True)
 
@@ -443,7 +430,7 @@
         compiler_params=params(),
         cost_estimate=cost(5),
         name="tail",
-    )(meta, att_msg, na, nb, x, cot, w_early, w_early, gain_out)
+    )(lengths, att_msg, na, nb, x, cot, w_early, w_early, gain_out)
 
     d_all = {0: d_att[0]}
     for k in ORDER:
@@ -467,7 +454,7 @@
     attend_back = pl.pallas_call(
         backward_kernel,
         out_shape=[jax.ShapeDtypeStruct((T, 3 * DH), BF16)] * H,
-        in_specs=[SMEM] + [VMEM] * (3 + H),
+        in_specs=[VMEM] * (3 + H),
         out_specs=[VMEM] * H,
         scratch_shapes=[
             pltpu.VMEM((S, DH), BF16),
@@ -483,7 +470,7 @@
         cost_estimate=cost(6),
         name="attend_back",
     )
-    d_proj = attend_back(meta, *[d_all[k] for k in range(H)], proj, weight, slope)
+    d_proj = attend_back(*[d_all[k] for k in range(H)], proj, weight, slope)
 
     pair, first = lax.optimization_barrier((pair, d_proj[0]))
     d_proj = [first, *d_proj[1:]]
@@ -504,8 +491,7 @@
         final_kernel,
         grid=(3,),
         out_shape=jax.ShapeDtypeStruct((T, D), BF16),
-        in_specs=[SMEM]
-        + [VMEM] * (H + 1)
+        in_specs=[VMEM] * (H + 1)
         + [pl.BlockSpec((D, D), lambda b: (0, b)), VMEM, VMEM, VMEM],
         out_specs=VMEM,
         scratch_shapes=[
@@ -518,7 +504,7 @@
         name="final",
     )
     input_grad = final(
-        meta, *[d_rows[k] for k in range(H)], gate_back, w_late, x, cot, gain_in
+        *[d_rows[k] for k in range(H)], gate_back, w_late, x, cot, gain_in
     )
 
     return (mixed[None], input_grad[None], w_grad)

time: 187 us -> 184 us (0.984)
  the two profiles are of different devices: /device:TPU:32 before, /device:TPU:22 now
where the time goes in v2:
time: 184 us; the launch traced here: 180 us
  starting transfers between devices  61.7 us (34%)
  blocking collectives  43.5 us (24%)
  Pallas kernels  29.1 us (16%)
  waiting for transfers between devices  28.1 us (15%)
  between operations  14.9 us (8%)
  local copies, waits for them, and re-layouts  1.85 us (1%)
    ppermute x28, starting transfers between devices, shifted(): return lax.ppermute(value, 'seq', [(i, (i + by) % H) for i in range(H)])  45 us
    all_to_all x1, blocking collectives, layer(): lax.all_to_all(pair.reshape(16, 32, D), ('dp_0', 'dp_1'), 0, 0, tiled=True)  29.2 us
    ppermute x28, waiting for transfers between devices, shifted(): return lax.ppermute(value, 'seq', [(i, (i + by) % H) for i in range(H)])  23 us
    all_to_all x1, blocking collectives, layer(): att_msg = lax.all_to_all(msg, 'seq', 0, 0, tiled=True)  14.3 us
    ppermute x4, starting transfers between devices, paired(): return lax.ppermute(value, axis, [(i, i ^ mask) for i in range(count)])  9.22 us
    pallas_call x1, Pallas kernels, layer(): pl.pallas_call(forward_kernel, out_shape=[jax.ShapeDtypeStruct((H, MSG, T...  8.65 us
    all_to_all x1, starting transfers between devices, layer(): ws = lax.all_to_all(copies, DP, 0, 0, tiled=True)  7.38 us
    pallas_call x1, Pallas kernels, layer(): final(*[d_rows[k] for k in range(H)], gate_back, w_late, x, cot, gain_in)  7.11 us
  transfers between devices with their start and end apart: 35, of which 18 were waited for; matrix products, arithmetic and copies ran while one was open for 1% of the time, Pallas kernels for 11%

profile of v2, /device:TPU:22, one launch (start us, length us, event | category | flops | bytes accessed | tf_op | source)
XLA Modules:
  0.0 180.4 jit_solution(9126061188049614926)
XLA Ops:
  7.2 2.3 %prep.1 = (bf16[64,1024]{1,0:T(8,128)(2,1)}, bf16[64,1024]{1,0:T(8,128)(2,1)}, bf16[32,2048]{1,0:T(8,128)(2,1)}, bf16[32,3072]{1,0:T(8,128)(2,1)}, bf16[32,32,384]{2,1,0:T(8,128)(2,1)}) custom-call(bf16[128,1024]{1,0:T(8,128)(2,1)} %bitcast.8, f32[1,1024]{1,0:T(1,128)} %bitcast.15, bf16[32,4096]{1,0:T(8,128)(2,1)} %w_ref.1, bf16[32,1024]{1,0:T(8,128)(2,1)} %wout_ref.1), custom_call_target="tpu_custom_call" | custom-call | flops 600000000 | bytes 1048576 | tf_op jit(solution)/shard_map/prep/pallas_call | solution.py:352
  10.3 7.4 %all-to-all-start = ((bf16[32,32,384]{2,1,0:T(8,128)(2,1)}), bf16[32,32,384]{2,1,0:T(8,128)(2,1)S(1)}, u32[]{:S(2)}, u32[]{:S(2)}) async-start(bf16[32,32,384]{2,1,0:T(8,128)(2,1)} %get-tuple-element.36), calls=%async_computation | async-start | bytes 1572864 | tf_op jit(solution)/shard_map/all_to_all | solution.py:369
  17.7 5.9 %collective-permute-start.10 = (bf16[64,1024]{1,0:T(8,128)(2,1)}, bf16[64,1024]{1,0:T(8,128)(2,1)S(1)}, u32[]{:S(2)}, u32[]{:S(2)}) collective-permute-start(bf16[64,1024]{1,0:T(8,128)(2,1)} %get-tuple-element.35.refs_3_.nb_ref), channel_id=1, source_target_pairs={{0,7},{1,0},{2,1},{3,2},{4,3},{5,4},{6,5},{7,6},{8,15},{9,8},{10,9... | collective-permute-start | bytes 393224 | tf_op jit(solution)/shard_map/ppermute | solution.py:343
  23.7 3.3 %collective-permute-start.7 = (bf16[64,1024]{1,0:T(8,128)(2,1)}, bf16[64,1024]{1,0:T(8,128)(2,1)S(1)}, u32[]{:S(2)}, u32[]{:S(2)}) collective-permute-start(bf16[64,1024]{1,0:T(8,128)(2,1)} %get-tuple-element.34.refs_2_.na_ref), channel_id=1, source_target_pairs={{0,7},{1,0},{2,1},{3,2},{4,3},{5,4},{6,5},{7,6},{8,15},{9,8},{10,9... | collective-permute-start | bytes 393224 | tf_op jit(solution)/shard_map/ppermute | solution.py:343
  27.1 3.6 %collective-permute-start.11 = (bf16[64,1024]{1,0:T(8,128)(2,1)S(1)}, bf16[64,1024]{1,0:T(8,128)(2,1)S(1)}, u32[]{:S(2)}, u32[]{:S(2)}) collective-permute-start(bf16[64,1024]{1,0:T(8,128)(2,1)S(1)} %collective-permute-done.10.refs_14_), channel_id=1, source_target_pairs={{0,7},{1,0},{2,1},{3,2},{4,3},{5,4},{6,5},{7,6},{8,15},{9,8},{10,9... | collective-permute-start | bytes 393224 | tf_op jit(solution)/shard_map/ppermute | solution.py:343
  31.5 1.7 collective-permute-done.4.refs_8_
  33.2 3.2 %collective-permute-start.8 = (bf16[64,1024]{1,0:T(8,128)(2,1)S(1)}, bf16[64,1024]{1,0:T(8,128)(2,1)S(1)}, u32[]{:S(2)}, u32[]{:S(2)}) collective-permute-start(bf16[64,1024]{1,0:T(8,128)(2,1)S(1)} %collective-permute-done.7.refs_11_), channel_id=1, source_target_pairs={{0,7},{1,0},{2,1},{3,2},{4,3},{5,4},{6,5},{7,6},{8,15},{9,8},{10,9... | collective-permute-start | bytes 393224 | tf_op jit(solution)/shard_map/ppermute | solution.py:343
  36.9 1.9 %collective-permute-done.1.refs_5_ = bf16[64,1024]{1,0:T(8,128)(2,1)S(1)} collective-permute-done((bf16[64,1024]{1,0:T(8,128)(2,1)S(1)}, bf16[64,1024]{1,0:T(8,128)(2,1)S(1)}, u32[]{:S(2)}, u32[]{:S(2)}) %collective-permute-start.1) | collective-permute-done | bytes 131104 | tf_op jit(solution)/shard_map/ppermute | solution.py:343
  38.8 2.8 %collective-permute-done.5.refs_9_ = bf16[64,1024]{1,0:T(8,128)(2,1)S(1)} collective-permute-done((bf16[64,1024]{1,0:T(8,128)(2,1)S(1)}, bf16[64,1024]{1,0:T(8,128)(2,1)S(1)}, u32[]{:S(2)}, u32[]{:S(2)}) %collective-permute-start.5) | collective-permute-done | bytes 131104 | tf_op jit(solution)/shard_map/ppermute | solution.py:343
  41.6 3.2 %collective-permute-start.9 = (bf16[64,1024]{1,0:T(8,128)(2,1)S(1)}, bf16[64,1024]{1,0:T(8,128)(2,1)S(1)}, u32[]{:S(2)}, u32[]{:S(2)}) collective-permute-start(bf16[64,1024]{1,0:T(8,128)(2,1)S(1)} %collective-permute-done.8.refs_12_), channel_id=1, source_target_pairs={{0,7},{1,0},{2,1},{3,2},{4,3},{5,4},{6,5},{7,6},{8,15},{9,8},{10,9... | collective-permute-start | bytes 393224 | tf_op jit(solution)/shard_map/ppermute | solution.py:343
  45.2 1.7 collective-permute-start.3
  53.2 8.6 %attend.1 = (bf16[8,144,128]{2,1,0:T(8,128)(2,1)S(1)}, f32[1024,384]{1,0:T(8,128)}, bf16[1024,1024]{1,0:T(8,128)(2,1)}, bf16[1024,1024]{1,0:T(8,128)(2,1)}) custom-call(s32[1]{0:T(128)S(6)} %copy.12.refs_0_.length_ref, f32[8,16]{1,0:T(8,128)S(1)} %copy-done.8, bf16[64,1024]{1,0:T(8,128)(2,1)S(1)} %copy-done.2, bf16[64,1024]{1,0:T(8,128)(2,1)S(1)} %copy-done.4, ...), custom_call_target="tpu_custom_call" | custom-call | flops 3000000000 | bytes 1048576 | tf_op jit(solution)/shard_map/attend/pallas_call | solution.py:380
  61.8 14.3 %all_to_all.15.msg_ref = bf16[8,144,128]{2,1,0:T(8,128)(2,1)S(1)} all-to-all(bf16[8,144,128]{2,1,0:T(8,128)(2,1)S(1)} %get-tuple-element.37), channel_id=1, replica_groups=mesh['dp_0'=4,'dp_1'=4,'dp_2'=2,'seq'=8] {'seq'}, dimensions={0} | all-to-all | bytes 589824 | tf_op jit(solution)/shard_map/all_to_all | solution.py:403
  76.2 6.3 %tail.1 = (bf16[128,1024]{1,0:T(8,128)(2,1)}, bf16[128,1024]{1,0:T(8,128)(2,1)S(1)}, bf16[512,1024]{1,0:T(8,128)(2,1)S(1)}, bf16[512,1024]{1,0:T(8,128)(2,1)}, b...) custom-call(s32[1]{0:T(128)S(6)} %copy.12.refs_0_.length_ref, ...), custom_call_target="tpu_custom_call" | custom-call | flops 1500000000 | bytes 1048576 | tf_op jit(solution)/shard_map/tail/pallas_call | solution.py:405
  83.6 2.3 %collective-permute-start.17 = (bf16[128,128]{1,0:T(8,128)(2,1)S(1)}, bf16[128,128]{1,0:T(8,128)(2,1)S(1)}, u32[]{:S(2)}, u32[]{:S(2)}) collective-permute-start(bf16[128,128]{1,0:T(8,128)(2,1)S(1)} %get-tuple-element.45), channel_id=1, source_target_pairs={{0,3},{1,4},{2,5},{3,6},{4,7},{5,0},{6,1},{7,2},{8,11},{9,12},{10,... | collective-permute-start | bytes 98312 | tf_op jit(solution)/shard_map/ppermute | solution.py:343
  85.9 3.5 %collective-permute-start.18 = (bf16[128,128]{1,0:T(8,128)(2,1)S(1)}, bf16[128,128]{1,0:T(8,128)(2,1)S(1)}, u32[]{:S(2)}, u32[]{:S(2)}) collective-permute-start(bf16[128,128]{1,0:T(8,128)(2,1)S(1)} %get-tuple-element.46), channel_id=1, source_target_pairs={{0,4},{1,5},{2,6},{3,7},{4,0},{5,1},{6,2},{7,3},{8,12},{9,13},{10,... | collective-permute-start | bytes 98312 | tf_op jit(solution)/shard_map/ppermute | solution.py:343
  89.3 2.3 %collective-permute-start.19 = (bf16[128,128]{1,0:T(8,128)(2,1)S(1)}, bf16[128,128]{1,0:T(8,128)(2,1)S(1)}, u32[]{:S(2)}, u32[]{:S(2)}) collective-permute-start(bf16[128,128]{1,0:T(8,128)(2,1)S(1)} %get-tuple-element.47), channel_id=1, source_target_pairs={{0,5},{1,6},{2,7},{3,0},{4,1},{5,2},{6,3},{7,4},{8,13},{9,14},{10,... | collective-permute-start | bytes 98312 | tf_op jit(solution)/shard_map/ppermute | solution.py:343
  91.7 2.0 %collective-permute-start.20 = (bf16[128,128]{1,0:T(8,128)(2,1)S(1)}, bf16[128,128]{1,0:T(8,128)(2,1)S(1)}, u32[]{:S(2)}, u32[]{:S(2)}) collective-permute-start(bf16[128,128]{1,0:T(8,128)(2,1)S(1)} %get-tuple-element.48), channel_id=1, source_target_pairs={{0,6},{1,7},{2,0},{3,1},{4,2},{5,3},{6,4},{7,5},{8,14},{9,15},{10,... | collective-permute-start | bytes 98312 | tf_op jit(solution)/shard_map/ppermute | solution.py:343
  95.6 2.2 %collective-permute-done.20.refs_6_ = bf16[128,128]{1,0:T(8,128)(2,1)S(1)} collective-permute-done((bf16[128,128]{1,0:T(8,128)(2,1)S(1)}, bf16[128,128]{1,0:T(8,128)(2,1)S(1)}, u32[]{:S(2)}, u32[]{:S(2)}) %collective-permute-start.20) | collective-permute-done | bytes 32800 | tf_op jit(solution)/shard_map/ppermute | solution.py:343
  98.3 1.9 %attend_back.1 = (bf16[128,384]{1,0:T(8,128)(2,1)S(1)}, bf16[128,384]{1,0:T(8,128)(2,1)S(1)}, bf16[128,384]{1,0:T(8,128)(2,1)S(1)}, bf16[128,384]{1,0:T(8,128)(2...) custom-call(bf16[128,128]{1,0:T(8,128)(2,1)S(1)} %get-tuple-element., ...), custom_call_target="tpu_custom_call" | custom-call | flops 1800000000 | bytes 1048576 | tf_op jit(solution)/shard_map/attend_back/pallas_call | solution.py:473
  100.6 29.2 %all_to_all.16 = bf16[16,32,1024]{2,1,0:T(8,128)(2,1)S(1)} all-to-all(bf16[16,32,1024]{2,1,0:T(8,128)(2,1)S(1)} %bitcast.17), channel_id=1, replica_groups=mesh['dp_0'=4,'dp_1'=4,'dp_2'=2,'seq'=8] {'dp_0','dp_1'}, dimensions={0} | all-to-all | bytes 2097152 | tf_op jit(solution)/shard_map/all_to_all | solution.py:477
  131.7 2.7 %collective-permute-done.29 = bf16[32,1024]{1,0:T(8,128)(2,1)S(1)} collective-permute-done((bf16[32,1024]{1,0:T(8,128)(2,1)S(1)}, bf16[32,1024]{1,0:T(8,128)(2,1)S(1)}, u32[]{:S(2)}, u32[]{:S(2)}) %collective-permute-start.29) | collective-permute-done | bytes 65568 | tf_op jit(solution)/shard_map/ppermute | solution.py:339
  134.4 3.6 %collective-permute-start.30 = (bf16[32,1024]{1,0:T(8,128)(2,1)S(1)}, bf16[32,1024]{1,0:T(8,128)(2,1)S(1)}, u32[]{:S(2)}, u32[]{:S(2)}) collective-permute-start(bf16[32,1024]{1,0:T(8,128)(2,1)S(1)} %add_convert_fusion.2), channel_id=1, source_target_pairs={{0,3},{1,2},{2,1},{3,0},{4,7},{5,6},{6,5},{7,4},{8,11},{9,10},{10,... | collective-permute-start | bytes 196616 | tf_op jit(solution)/shard_map/ppermute | solution.py:339
  138.9 1.7 collective-permute-done.30
  140.6 4.0 %collective-permute-start.31 = (bf16[32,1024]{1,0:T(8,128)(2,1)S(1)}, bf16[32,1024]{1,0:T(8,128)(2,1)S(1)}, u32[]{:S(2)}, u32[]{:S(2)}) collective-permute-start(bf16[32,1024]{1,0:T(8,128)(2,1)S(1)} %add_convert_fusion.1), channel_id=1, source_target_pairs={{0,7},{1,6},{2,5},{3,4},{4,3},{5,2},{6,1},{7,0},{8,15},{9,14},{10,... | collective-permute-start | bytes 196616 | tf_op jit(solution)/shard_map/ppermute | solution.py:339
  144.6 2.8 %gate.1.refs_8_ = f32[128,1024]{1,0:T(8,128)S(1)} custom-call(bf16[128,1024]{1,0:T(8,128)(2,1)S(1)} %get-tuple-element.62.dpg_ref, bf16[1024,2048]{1,0:T(8,128)(2,1)} %all-gather.3.cloned.1.call-done.wg_ref.wo_ref), custom_call_target="tpu_custom_call" | custom-call | flops 600000000 | bytes 1048576 | tf_op jit(solution)/shard_map/gate/pallas_call | solution.py:449
  147.4 1.9 %collective-permute-start.24 = (bf16[128,384]{1,0:T(8,128)(2,1)S(1)}, bf16[128,384]{1,0:T(8,128)(2,1)S(1)}, u32[]{:S(2)}, u32[]{:S(2)}) collective-permute-start(bf16[128,384]{1,0:T(8,128)(2,1)S(1)} %get-tuple-element.57), channel_id=1, source_target_pairs={{0,3},{1,4},{2,5},{3,6},{4,7},{5,0},{6,1},{7,2},{8,11},{9,12},{10,... | collective-permute-start | bytes 294920 | tf_op jit(solution)/shard_map/ppermute | solution.py:343
  150.8 4.3 %collective-permute-start.26 = (bf16[128,384]{1,0:T(8,128)(2,1)S(1)}, bf16[128,384]{1,0:T(8,128)(2,1)S(1)}, u32[]{:S(2)}, u32[]{:S(2)}) collective-permute-start(bf16[128,384]{1,0:T(8,128)(2,1)S(1)} %get-tuple-element.59), channel_id=1, source_target_pairs={{0,5},{1,6},{2,7},{3,0},{4,1},{5,2},{6,3},{7,4},{8,13},{9,14},{10,... | collective-permute-start | bytes 294920 | tf_op jit(solution)/shard_map/ppermute | solution.py:343
  155.0 1.7 collective-permute-start.27
  159.5 3.1 %collective-permute-done.26.refs_5_ = bf16[128,384]{1,0:T(8,128)(2,1)S(1)} collective-permute-done((bf16[128,384]{1,0:T(8,128)(2,1)S(1)}, bf16[128,384]{1,0:T(8,128)(2,1)S(1)}, u32[]{:S(2)}, u32[]{:S(2)}) %collective-permute-start.26) | collective-permute-done | bytes 98336 | tf_op jit(solution)/shard_map/ppermute | solution.py:343
  162.6 3.8 %collective-permute-done.27.refs_6_ = bf16[128,384]{1,0:T(8,128)(2,1)S(1)} collective-permute-done((bf16[128,384]{1,0:T(8,128)(2,1)S(1)}, bf16[128,384]{1,0:T(8,128)(2,1)S(1)}, u32[]{:S(2)}, u32[]{:S(2)}) %collective-permute-start.27) | collective-permute-done | bytes 98336 | tf_op jit(solution)/shard_map/ppermute | solution.py:343
  166.4 7.1 %final.1 = bf16[128,1024]{1,0:T(8,128)(2,1)} custom-call(bf16[128,384]{1,0:T(8,128)(2,1)S(1)} %get-tuple-element.54.refs_0_, bf16[128,384]{1,0:T(8,128)(2,1)S(1)} %collective-permute-done.22.refs_1_, bf16[128,384]{1,0:T(8,128)(2,1)S(1)} %collective-permute-done.23.refs_2_, bf16[128,384]{1,0:T(8,128)(2,1)S(1)} %collective-permute-done.24.refs_3_, ...), custom_call_target="tpu_custom_call" | custom-call | flops 1500000000 | bytes 1048576 | tf_op jit(solution)/shard_map/final/pallas_call | solution.py:506
  (79 shorter events, 19.4 us)
Async XLA Ops:
  7.2 68.9 %all-gather.3.cloned.1.call-start = ((), (), s32[]{:S(2)}) async-start(), calls=%async_computation.3 | async-start | bytes 4325376 | tf_op jit(solution)/shard_map/all_gather | solution.py:367
  9.6 156.8 %all-gather.5.cloned.1.call-start = ((), (), s32[]{:S(2)}) async-start(), calls=%async_computation.4 | async-start | bytes 6488064 | tf_op jit(solution)/shard_map/all_gather | solution.py:368
  10.3 41.0 %all-to-all-start = ((bf16[32,32,384]{2,1,0:T(8,128)(2,1)}), bf16[32,32,384]{2,1,0:T(8,128)(2,1)S(1)}, u32[]{:S(2)}, u32[]{:S(2)}) async-start(bf16[32,32,384]{2,1,0:T(8,128)(2,1)} %get-tuple-element.36), calls=%async_computation | async-start | bytes 1572864 | tf_op jit(solution)/shard_map/all_to_all | solution.py:369
  17.7 9.4 %collective-permute-start.10 = (bf16[64,1024]{1,0:T(8,128)(2,1)}, bf16[64,1024]{1,0:T(8,128)(2,1)S(1)}, u32[]{:S(2)}, u32[]{:S(2)}) collective-permute-start(bf16[64,1024]{1,0:T(8,128)(2,1)} %get-tuple-element.35.refs_3_.nb_ref), channel_id=1, source_target_pairs={{0,7},{1,0},{2,1},{3,2},{4,3},{5,4},{6,5},{7,6},{8,15},{9,8},{10,9... | collective-permute-start | bytes 393224 | tf_op jit(solution)/shard_map/ppermute | solution.py:343
  23.7 7.8 %collective-permute-start = (bf16[64,1024]{1,0:T(8,128)(2,1)}, bf16[64,1024]{1,0:T(8,128)(2,1)S(1)}, u32[]{:S(2)}, u32[]{:S(2)}) collective-permute-start(bf16[64,1024]{1,0:T(8,128)(2,1)} %get-tuple-element.34.refs_2_.na_ref), channel_id=1, source_target_pairs={{0,1},{1,2},{2,3},{3,4},{4,5},{5,6},{6,7},{7,0},{8,9},{9,10},{10,1... | collective-permute-start | bytes 393224 | tf_op jit(solution)/shard_map/ppermute | solution.py:343
  23.7 9.5 %collective-permute-start.4 = (bf16[64,1024]{1,0:T(8,128)(2,1)}, bf16[64,1024]{1,0:T(8,128)(2,1)S(1)}, u32[]{:S(2)}, u32[]{:S(2)}) collective-permute-start(bf16[64,1024]{1,0:T(8,128)(2,1)} %get-tuple-element.35.refs_3_.nb_ref), channel_id=1, source_target_pairs={{0,1},{1,2},{2,3},{3,4},{4,5},{5,6},{6,7},{7,0},{8,9},{9,10},{10,1... | collective-permute-start | bytes 393224 | tf_op jit(solution)/shard_map/ppermute | solution.py:343
  23.7 9.5 %collective-permute-start.7 = (bf16[64,1024]{1,0:T(8,128)(2,1)}, bf16[64,1024]{1,0:T(8,128)(2,1)S(1)}, u32[]{:S(2)}, u32[]{:S(2)}) collective-permute-start(bf16[64,1024]{1,0:T(8,128)(2,1)} %get-tuple-element.34.refs_2_.na_ref), channel_id=1, source_target_pairs={{0,7},{1,0},{2,1},{3,2},{4,3},{5,4},{6,5},{7,6},{8,15},{9,8},{10,9... | collective-permute-start | bytes 393224 | tf_op jit(solution)/shard_map/ppermute | solution.py:343
  27.1 9.2 %collective-permute-start.11 = (bf16[64,1024]{1,0:T(8,128)(2,1)S(1)}, bf16[64,1024]{1,0:T(8,128)(2,1)S(1)}, u32[]{:S(2)}, u32[]{:S(2)}) collective-permute-start(bf16[64,1024]{1,0:T(8,128)(2,1)S(1)} %collective-permute-done.10.refs_14_), channel_id=1, source_target_pairs={{0,7},{1,0},{2,1},{3,2},{4,3},{5,4},{6,5},{7,6},{8,15},{9,8},{10,9... | collective-permute-start | bytes 393224 | tf_op jit(solution)/shard_map/ppermute | solution.py:343
  31.5 7.3 %collective-permute-start.1 = (bf16[64,1024]{1,0:T(8,128)(2,1)S(1)}, bf16[64,1024]{1,0:T(8,128)(2,1)S(1)}, u32[]{:S(2)}, u32[]{:S(2)}) collective-permute-start(bf16[64,1024]{1,0:T(8,128)(2,1)S(1)} %collective-permute-done.refs_4_), channel_id=1, source_target_pairs={{0,1},{1,2},{2,3},{3,4},{4,5},{5,6},{6,7},{7,0},{8,9},{9,10},{10,1... | collective-permute-start | bytes 393224 | tf_op jit(solution)/shard_map/ppermute | solution.py:343
  33.1 8.4 %collective-permute-start.5 = (bf16[64,1024]{1,0:T(8,128)(2,1)S(1)}, bf16[64,1024]{1,0:T(8,128)(2,1)S(1)}, u32[]{:S(2)}, u32[]{:S(2)}) collective-permute-start(bf16[64,1024]{1,0:T(8,128)(2,1)S(1)} %collective-permute-done.4.refs_8_), channel_id=1, source_target_pairs={{0,1},{1,2},{2,3},{3,4},{4,5},{5,6},{6,7},{7,0},{8,9},{9,10},{10,1... | collective-permute-start | bytes 393224 | tf_op jit(solution)/shard_map/ppermute | solution.py:343
  33.2 8.4 %collective-permute-start.8 = (bf16[64,1024]{1,0:T(8,128)(2,1)S(1)}, bf16[64,1024]{1,0:T(8,128)(2,1)S(1)}, u32[]{:S(2)}, u32[]{:S(2)}) collective-permute-start(bf16[64,1024]{1,0:T(8,128)(2,1)S(1)} %collective-permute-done.7.refs_11_), channel_id=1, source_target_pairs={{0,7},{1,0},{2,1},{3,2},{4,3},{5,4},{6,5},{7,6},{8,15},{9,8},{10,9... | collective-permute-start | bytes 393224 | tf_op jit(solution)/shard_map/ppermute | solution.py:343
  36.4 8.4 %collective-permute-start.12 = (bf16[64,1024]{1,0:T(8,128)(2,1)S(1)}, bf16[64,1024]{1,0:T(8,128)(2,1)S(1)}, u32[]{:S(2)}, u32[]{:S(2)}) collective-permute-start(bf16[64,1024]{1,0:T(8,128)(2,1)S(1)} %collective-permute-done.11.refs_15_), channel_id=1, source_target_pairs={{0,7},{1,0},{2,1},{3,2},{4,3},{5,4},{6,5},{7,6},{8,15},{9,8},{10,9... | collective-permute-start | bytes 393224 | tf_op jit(solution)/shard_map/ppermute | solution.py:343
  38.8 6.4 %collective-permute-start.2 = (bf16[64,1024]{1,0:T(8,128)(2,1)S(1)}, bf16[64,1024]{1,0:T(8,128)(2,1)S(1)}, u32[]{:S(2)}, u32[]{:S(2)}) collective-permute-start(bf16[64,1024]{1,0:T(8,128)(2,1)S(1)} %collective-permute-done.1.refs_5_), channel_id=1, source_target_pairs={{0,1},{1,2},{2,3},{3,4},{4,5},{5,6},{6,7},{7,0},{8,9},{9,10},{10,1... | collective-permute-start | bytes 393224 | tf_op jit(solution)/shard_map/ppermute | solution.py:343
  41.6 7.1 %collective-permute-start.6 = (bf16[64,1024]{1,0:T(8,128)(2,1)S(1)}, bf16[64,1024]{1,0:T(8,128)(2,1)S(1)}, u32[]{:S(2)}, u32[]{:S(2)}) collective-permute-start(bf16[64,1024]{1,0:T(8,128)(2,1)S(1)} %collective-permute-done.5.refs_9_), channel_id=1, source_target_pairs={{0,1},{1,2},{2,3},{3,4},{4,5},{5,6},{6,7},{7,0},{8,9},{9,10},{10,1... | collective-permute-start | bytes 393224 | tf_op jit(solution)/shard_map/ppermute | solution.py:343
  41.6 7.1 %collective-permute-start.9 = (bf16[64,1024]{1,0:T(8,128)(2,1)S(1)}, bf16[64,1024]{1,0:T(8,128)(2,1)S(1)}, u32[]{:S(2)}, u32[]{:S(2)}) collective-permute-start(bf16[64,1024]{1,0:T(8,128)(2,1)S(1)} %collective-permute-done.8.refs_12_), channel_id=1, source_target_pairs={{0,7},{1,0},{2,1},{3,2},{4,3},{5,4},{6,5},{7,6},{8,15},{9,8},{10,9... | collective-permute-start | bytes 393224 | tf_op jit(solution)/shard_map/ppermute | solution.py:343
  45.2 6.2 %collective-permute-start.3 = (bf16[64,1024]{1,0:T(8,128)(2,1)S(1)}, bf16[64,1024]{1,0:T(8,128)(2,1)S(1)}, u32[]{:S(2)}, u32[]{:S(2)}) collective-permute-start(bf16[64,1024]{1,0:T(8,128)(2,1)S(1)} %collective-permute-done.2.refs_6_), channel_id=1, source_target_pairs={{0,1},{1,2},{2,3},{3,4},{4,5},{5,6},{6,7},{7,0},{8,9},{9,10},{10,1... | collective-permute-start | bytes 393224 | tf_op jit(solution)/shard_map/ppermute | solution.py:343
  82.4 17.8 %collective-permute-start.14 = (bf16[512,1024]{1,0:T(8,128)(2,1)}, bf16[512,1024]{1,0:T(8,128)(2,1)S(1)}, u32[]{:S(2)}, u32[]{:S(2)}) collective-permute-start(bf16[512,1024]{1,0:T(8,128)(2,1)} %get-tuple-element.41), channel_id=1, source_target_pairs={{0,8},{8,0},{1,9},{9,1},{2,10},{10,2},{3,11},{11,3},{4,12},{12,4},... | collective-permute-start | bytes 3145736 | tf_op jit(solution)/shard_map/ppermute | solution.py:339
  82.4 6.9 %collective-permute-start.15 = (bf16[128,128]{1,0:T(8,128)(2,1)S(1)}, bf16[128,128]{1,0:T(8,128)(2,1)S(1)}, u32[]{:S(2)}, u32[]{:S(2)}) collective-permute-start(bf16[128,128]{1,0:T(8,128)(2,1)S(1)} %get-tuple-element.43), channel_id=1, source_target_pairs={{0,1},{1,2},{2,3},{3,4},{4,5},{5,6},{6,7},{7,0},{8,9},{9,10},{10,1... | collective-permute-start | bytes 98312 | tf_op jit(solution)/shard_map/ppermute | solution.py:343
  83.0 8.7 %collective-permute-start.16 = (bf16[128,128]{1,0:T(8,128)(2,1)S(1)}, bf16[128,128]{1,0:T(8,128)(2,1)S(1)}, u32[]{:S(2)}, u32[]{:S(2)}) collective-permute-start(bf16[128,128]{1,0:T(8,128)(2,1)S(1)} %get-tuple-element.44), channel_id=1, source_target_pairs={{0,2},{1,3},{2,4},{3,5},{4,6},{5,7},{6,0},{7,1},{8,10},{9,11},{10,... | collective-permute-start | bytes 98312 | tf_op jit(solution)/shard_map/ppermute | solution.py:343
  83.6 10.0 %collective-permute-start.17 = (bf16[128,128]{1,0:T(8,128)(2,1)S(1)}, bf16[128,128]{1,0:T(8,128)(2,1)S(1)}, u32[]{:S(2)}, u32[]{:S(2)}) collective-permute-start(bf16[128,128]{1,0:T(8,128)(2,1)S(1)} %get-tuple-element.45), channel_id=1, source_target_pairs={{0,3},{1,4},{2,5},{3,6},{4,7},{5,0},{6,1},{7,2},{8,11},{9,12},{10,... | collective-permute-start | bytes 98312 | tf_op jit(solution)/shard_map/ppermute | solution.py:343
  85.9 9.4 %collective-permute-start.18 = (bf16[128,128]{1,0:T(8,128)(2,1)S(1)}, bf16[128,128]{1,0:T(8,128)(2,1)S(1)}, u32[]{:S(2)}, u32[]{:S(2)}) collective-permute-start(bf16[128,128]{1,0:T(8,128)(2,1)S(1)} %get-tuple-element.46), channel_id=1, source_target_pairs={{0,4},{1,5},{2,6},{3,7},{4,0},{5,1},{6,2},{7,3},{8,12},{9,13},{10,... | collective-permute-start | bytes 98312 | tf_op jit(solution)/shard_map/ppermute | solution.py:343
  89.3 6.3 %collective-permute-start.19 = (bf16[128,128]{1,0:T(8,128)(2,1)S(1)}, bf16[128,128]{1,0:T(8,128)(2,1)S(1)}, u32[]{:S(2)}, u32[]{:S(2)}) collective-permute-start(bf16[128,128]{1,0:T(8,128)(2,1)S(1)} %get-tuple-element.47), channel_id=1, source_target_pairs={{0,5},{1,6},{2,7},{3,0},{4,1},{5,2},{6,3},{7,4},{8,13},{9,14},{10,... | collective-permute-start | bytes 98312 | tf_op jit(solution)/shard_map/ppermute | solution.py:343
  91.7 6.1 %collective-permute-start.20 = (bf16[128,128]{1,0:T(8,128)(2,1)S(1)}, bf16[128,128]{1,0:T(8,128)(2,1)S(1)}, u32[]{:S(2)}, u32[]{:S(2)}) collective-permute-start(bf16[128,128]{1,0:T(8,128)(2,1)S(1)} %get-tuple-element.48), channel_id=1, source_target_pairs={{0,6},{1,7},{2,0},{3,1},{4,2},{5,3},{6,4},{7,5},{8,14},{9,15},{10,... | collective-permute-start | bytes 98312 | tf_op jit(solution)/shard_map/ppermute | solution.py:343
  134.4 6.2 %collective-permute-start.30 = (bf16[32,1024]{1,0:T(8,128)(2,1)S(1)}, bf16[32,1024]{1,0:T(8,128)(2,1)S(1)}, u32[]{:S(2)}, u32[]{:S(2)}) collective-permute-start(bf16[32,1024]{1,0:T(8,128)(2,1)S(1)} %add_convert_fusion.2), channel_id=1, source_target_pairs={{0,3},{1,2},{2,1},{3,0},{4,7},{5,6},{6,5},{7,4},{8,11},{9,10},{10,... | collective-permute-start | bytes 196616 | tf_op jit(solution)/shard_map/ppermute | solution.py:339
  138.1 12.7 %collective-permute-start.22 = (bf16[128,384]{1,0:T(8,128)(2,1)S(1)}, bf16[128,384]{1,0:T(8,128)(2,1)S(1)}, u32[]{:S(2)}, u32[]{:S(2)}) collective-permute-start(bf16[128,384]{1,0:T(8,128)(2,1)S(1)} %get-tuple-element.55), channel_id=1, source_target_pairs={{0,1},{1,2},{2,3},{3,4},{4,5},{5,6},{6,7},{7,0},{8,9},{9,10},{10,1... | collective-permute-start | bytes 294920 | tf_op jit(solution)/shard_map/ppermute | solution.py:343
  138.1 17.0 %collective-permute-start.23 = (bf16[128,384]{1,0:T(8,128)(2,1)S(1)}, bf16[128,384]{1,0:T(8,128)(2,1)S(1)}, u32[]{:S(2)}, u32[]{:S(2)}) collective-permute-start(bf16[128,384]{1,0:T(8,128)(2,1)S(1)} %get-tuple-element.56), channel_id=1, source_target_pairs={{0,2},{1,3},{2,4},{3,5},{4,6},{5,7},{6,0},{7,1},{8,10},{9,11},{10,... | collective-permute-start | bytes 294920 | tf_op jit(solution)/shard_map/ppermute | solution.py:343
  140.6 16.1 %collective-permute-start.31 = (bf16[32,1024]{1,0:T(8,128)(2,1)S(1)}, bf16[32,1024]{1,0:T(8,128)(2,1)S(1)}, u32[]{:S(2)}, u32[]{:S(2)}) collective-permute-start(bf16[32,1024]{1,0:T(8,128)(2,1)S(1)} %add_convert_fusion.1), channel_id=1, source_target_pairs={{0,7},{1,6},{2,5},{3,4},{4,3},{5,2},{6,1},{7,0},{8,15},{9,14},{10,... | collective-permute-start | bytes 196616 | tf_op jit(solution)/shard_map/ppermute | solution.py:339
  147.4 11.6 %collective-permute-start.24 = (bf16[128,384]{1,0:T(8,128)(2,1)S(1)}, bf16[128,384]{1,0:T(8,128)(2,1)S(1)}, u32[]{:S(2)}, u32[]{:S(2)}) collective-permute-start(bf16[128,384]{1,0:T(8,128)(2,1)S(1)} %get-tuple-element.57), channel_id=1, source_target_pairs={{0,3},{1,4},{2,5},{3,6},{4,7},{5,0},{6,1},{7,2},{8,11},{9,12},{10,... | collective-permute-start | bytes 294920 | tf_op jit(solution)/shard_map/ppermute | solution.py:343
  149.3 10.2 %collective-permute-start.25 = (bf16[128,384]{1,0:T(8,128)(2,1)S(1)}, bf16[128,384]{1,0:T(8,128)(2,1)S(1)}, u32[]{:S(2)}, u32[]{:S(2)}) collective-permute-start(bf16[128,384]{1,0:T(8,128)(2,1)S(1)} %get-tuple-element.58), channel_id=1, source_target_pairs={{0,4},{1,5},{2,6},{3,7},{4,0},{5,1},{6,2},{7,3},{8,12},{9,13},{10,... | collective-permute-start | bytes 294920 | tf_op jit(solution)/shard_map/ppermute | solution.py:343
  150.8 11.8 %collective-permute-start.26 = (bf16[128,384]{1,0:T(8,128)(2,1)S(1)}, bf16[128,384]{1,0:T(8,128)(2,1)S(1)}, u32[]{:S(2)}, u32[]{:S(2)}) collective-permute-start(bf16[128,384]{1,0:T(8,128)(2,1)S(1)} %get-tuple-element.59), channel_id=1, source_target_pairs={{0,5},{1,6},{2,7},{3,0},{4,1},{5,2},{6,3},{7,4},{8,13},{9,14},{10,... | collective-permute-start | bytes 294920 | tf_op jit(solution)/shard_map/ppermute | solution.py:343
  155.0 11.4 %collective-permute-start.27 = (bf16[128,384]{1,0:T(8,128)(2,1)S(1)}, bf16[128,384]{1,0:T(8,128)(2,1)S(1)}, u32[]{:S(2)}, u32[]{:S(2)}) collective-permute-start(bf16[128,384]{1,0:T(8,128)(2,1)S(1)} %get-tuple-element.60), channel_id=1, source_target_pairs={{0,6},{1,7},{2,0},{3,1},{4,2},{5,3},{6,4},{7,5},{8,14},{9,15},{10,... | collective-permute-start | bytes 294920 | tf_op jit(solution)/shard_map/ppermute | solution.py:343
  156.8 9.7 %collective-permute-start.28 = (bf16[128,384]{1,0:T(8,128)(2,1)S(1)}, bf16[128,384]{1,0:T(8,128)(2,1)S(1)}, u32[]{:S(2)}, u32[]{:S(2)}) collective-permute-start(bf16[128,384]{1,0:T(8,128)(2,1)S(1)} %get-tuple-element.61), channel_id=1, source_target_pairs={{0,7},{1,0},{2,1},{3,2},{4,3},{5,4},{6,5},{7,6},{8,15},{9,8},{10,9... | collective-permute-start | bytes 294920 | tf_op jit(solution)/shard_map/ppermute | solution.py:343
  (16 other events, 307.4 us)
Sparse Core Ops, SparseCore 0:
  10.5 53.7 all-gather.2
  67.4 63.7 all-gather.4

commit v3 on v2

--- a/solution.py
+++ b/solution.py
@@ -46,7 +46,7 @@
 
 
 def prep_kernel(
-    x_ref, gain_ref, w_ref, wout_ref, a_ref, b_ref, early_ref, late_ref, copies_ref
+    x_ref, gain_ref, w_ref, wout_ref, a_ref, b_ref, all_ref, copies_ref
 ):
     me = lax.axis_index("seq")
     x = x_ref[...].astype(F32)
@@ -55,9 +55,8 @@
     n = (c * lax.rsqrt(var + EPS) * gain_ref[...]).astype(BF16)
     a_ref[...] = n[:64]
     b_ref[...] = n[64:]
-    early_ref[:, :D] = w_ref[:, :D]
-    early_ref[:, D:] = wout_ref[...]
-    late_ref[...] = w_ref[:, D:]
+    all_ref[:, : 4 * D] = w_ref[...]
+    all_ref[:, 4 * D :] = wout_ref[...]
     for part in range(3):
         at = pl.multiple_of((part + 1) * D + me * DH, DH)
         own = w_ref[:, pl.ds(at, DH)]
@@ -303,11 +302,11 @@
         acc[...] = back_ref[...]
 
     def columns(n, carry):
-        at = pl.ds(pl.multiple_of(n * 256, 256), 256)
+        at = pl.ds(pl.multiple_of(n * 512, 512), 512)
         acc[:, at] += nt(lhs[b], w_ref[at, :])
         return carry
 
-    lax.fori_loop(0, D // 256, columns, 0)
+    lax.fori_loop(0, D // 512, columns, 0)
 
     @pl.when(b == 2)
     def _():
@@ -349,23 +348,21 @@
     gain_in = gain_in.reshape(1, D)
     gain_out = gain_out.reshape(1, D)
 
-    na, nb, early, late, copies = pl.pallas_call(
+    na, nb, w_rows, copies = pl.pallas_call(
         prep_kernel,
         out_shape=[
             jax.ShapeDtypeStruct((64, D), BF16),
             jax.ShapeDtypeStruct((64, D), BF16),
-            jax.ShapeDtypeStruct((32, 2 * D), BF16),
-            jax.ShapeDtypeStruct((32, 3 * D), BF16),
+            jax.ShapeDtypeStruct((32, 5 * D), BF16),
             jax.ShapeDtypeStruct((32, 32, 3 * DH), BF16),
         ],
         in_specs=[VMEM] * 4,
-        out_specs=[VMEM] * 5,
+        out_specs=[VMEM] * 4,
         compiler_params=params(61500),
         cost_estimate=cost(2),
         name="prep",
     )(x, gain_in, w_qkvu, w_out)
-    w_early = lax.all_gather(early, DP, axis=0, tiled=True)
-    w_late = lax.all_gather(late, DP, axis=0, tiled=True)
+    w_full = lax.all_gather(w_rows, DP, axis=0, tiled=True)
     ws = lax.all_to_all(copies, DP, 0, 0, tiled=True)
     ws = ws.reshape(D, 3 * DH)
 
@@ -416,7 +413,7 @@
         + [VMEM] * 5
         + [
             pl.BlockSpec((D, D), lambda i: (0, 0)),
-            pl.BlockSpec((D, D), lambda i: (0, 1)),
+            pl.BlockSpec((D, D), lambda i: (0, 4)),
             VMEM,
         ],
         out_specs=[VMEM] * (4 + H),
@@ -427,10 +424,10 @@
             pltpu.VMEM((T, D), F32),
             pltpu.VMEM((T, D), F32),
         ],
-        compiler_params=params(),
+        compiler_params=params(61500),
         cost_estimate=cost(5),
         name="tail",
-    )(lengths, att_msg, na, nb, x, cot, w_early, w_early, gain_out)
+    )(lengths, att_msg, na, nb, x, cot, w_full, w_full, gain_out)
 
     d_all = {0: d_att[0]}
     for k in ORDER:
@@ -446,7 +443,7 @@
         cost_estimate=cost(2),
         name="gate",
     )
-    gate_back = gate_call(d_pg, w_early)
+    gate_back = gate_call(d_pg, w_full)
 
     other = paired(w_send, "dp_2", 1)
     pair = (w_own.astype(F32) + other.astype(F32)).astype(BF16)
@@ -492,7 +489,7 @@
         grid=(3,),
         out_shape=jax.ShapeDtypeStruct((T, D), BF16),
         in_specs=[VMEM] * (H + 1)
-        + [pl.BlockSpec((D, D), lambda b: (0, b)), VMEM, VMEM, VMEM],
+        + [pl.BlockSpec((D, D), lambda b: (0, b + 1)), VMEM, VMEM, VMEM],
         out_specs=VMEM,
         scratch_shapes=[
             pltpu.VMEM((H, T, 3 * DH), BF16),
@@ -504,7 +501,7 @@
         name="final",
     )
     input_grad = final(
-        *[d_rows[k] for k in range(H)], gate_back, w_late, x, cot, gain_in
+        *[d_rows[k] for k in range(H)], gate_back, w_full, x, cot, gain_in
     )
 
     return (mixed[None], input_grad[None], w_grad)

time: 184 us -> 176 us (0.957)
  the two profiles are of different devices: /device:TPU:22 before, /device:TPU:2 now
where the time goes in v3:
time: 176 us; the launch traced here: 175 us
  starting transfers between devices  62.1 us (35%)
  blocking collectives  36.9 us (21%)
  Pallas kernels  29.4 us (17%)
  waiting for transfers between devices  24.9 us (14%)
  between operations  14.8 us (8%)
  local copies, waits for them, and re-layouts  5.59 us (3%)
    ppermute x28, starting transfers between devices, shifted(): return lax.ppermute(value, 'seq', [(i, (i + by) % H) for i in range(H)])  50.8 us
    ppermute x28, waiting for transfers between devices, shifted(): return lax.ppermute(value, 'seq', [(i, (i + by) % H) for i in range(H)])  21.2 us
    all_to_all x1, blocking collectives, layer(): lax.all_to_all(pair.reshape(16, 32, D), ('dp_0', 'dp_1'), 0, 0, tiled=True)  20 us
    all_to_all x1, blocking collectives, layer(): att_msg = lax.all_to_all(msg, 'seq', 0, 0, tiled=True)  17 us
    pallas_call x1, Pallas kernels, layer(): pl.pallas_call(forward_kernel, out_shape=[jax.ShapeDtypeStruct((H, MSG, T...  8.7 us
    all_to_all x1, starting transfers between devices, layer(): ws = lax.all_to_all(copies, DP, 0, 0, tiled=True)  7.63 us
    pallas_call x1, Pallas kernels, layer(): pl.pallas_call(tail_kernel, grid=(1,), out_shape=[jax.ShapeDtypeStruct((T...  7.02 us
    pallas_call x1, Pallas kernels, layer(): final(*[d_rows[k] for k in range(H)], gate_back, w_full, x, cot, gain_in)  6.56 us
  transfers between devices with their start and end apart: 34, of which 16 were waited for; matrix products, arithmetic and copies ran while one was open for 0% of the time, Pallas kernels for 11%

profile of v3, /device:TPU:2, one launch (start us, length us, event | category | flops | bytes accessed | tf_op | source)
XLA Modules:
  0.0 175.1 jit_solution(16810803252748999820)
XLA Ops:
  7.2 2.4 %prep.1 = (bf16[64,1024]{1,0:T(8,128)(2,1)}, bf16[64,1024]{1,0:T(8,128)(2,1)}, bf16[32,5120]{1,0:T(8,128)(2,1)}, bf16[32,32,384]{2,1,0:T(8,128)(2,1)}) custom-call(bf16[128,1024]{1,0:T(8,128)(2,1)} %bitcast.8, f32[1,1024]{1,0:T(1,128)} %bitcast.14, bf16[32,4096]{1,0:T(8,128)(2,1)} %w_ref.1, bf16[32,1024]{1,0:T(8,128)(2,1)} %wout_ref.1), custom_call_target="tpu_custom_call" | custom-call | flops 600000000 | bytes 1048576 | tf_op jit(solution)/shard_map/prep/pallas_call | solution.py:351
  9.7 7.6 %all-to-all-start = ((bf16[32,32,384]{2,1,0:T(8,128)(2,1)}), bf16[32,32,384]{2,1,0:T(8,128)(2,1)S(1)}, u32[]{:S(2)}, u32[]{:S(2)}) async-start(bf16[32,32,384]{2,1,0:T(8,128)(2,1)} %get-tuple-element.35), calls=%async_computation | async-start | bytes 1572864 | tf_op jit(solution)/shard_map/all_to_all | solution.py:366
  17.3 2.0 %collective-permute-start = (bf16[64,1024]{1,0:T(8,128)(2,1)}, bf16[64,1024]{1,0:T(8,128)(2,1)S(1)}, u32[]{:S(2)}, u32[]{:S(2)}) collective-permute-start(bf16[64,1024]{1,0:T(8,128)(2,1)} %get-tuple-element.33.refs_2_.na_ref), channel_id=1, source_target_pairs={{0,1},{1,2},{2,3},{3,4},{4,5},{5,6},{6,7},{7,0},{8,9},{9,10},{10,1... | collective-permute-start | bytes 393224 | tf_op jit(solution)/shard_map/ppermute | solution.py:342
  19.3 4.0 %collective-permute-start.10 = (bf16[64,1024]{1,0:T(8,128)(2,1)}, bf16[64,1024]{1,0:T(8,128)(2,1)S(1)}, u32[]{:S(2)}, u32[]{:S(2)}) collective-permute-start(bf16[64,1024]{1,0:T(8,128)(2,1)} %get-tuple-element.34.refs_3_.nb_ref), channel_id=1, source_target_pairs={{0,7},{1,0},{2,1},{3,2},{4,3},{5,4},{6,5},{7,6},{8,15},{9,8},{10,9... | collective-permute-start | bytes 393224 | tf_op jit(solution)/shard_map/ppermute | solution.py:342
  23.3 1.9 %collective-permute-start.7 = (bf16[64,1024]{1,0:T(8,128)(2,1)}, bf16[64,1024]{1,0:T(8,128)(2,1)S(1)}, u32[]{:S(2)}, u32[]{:S(2)}) collective-permute-start(bf16[64,1024]{1,0:T(8,128)(2,1)} %get-tuple-element.33.refs_2_.na_ref), channel_id=1, source_target_pairs={{0,7},{1,0},{2,1},{3,2},{4,3},{5,4},{6,5},{7,6},{8,15},{9,8},{10,9... | collective-permute-start | bytes 393224 | tf_op jit(solution)/shard_map/ppermute | solution.py:342
  25.4 1.9 %collective-permute-done.refs_4_ = bf16[64,1024]{1,0:T(8,128)(2,1)S(1)} collective-permute-done((bf16[64,1024]{1,0:T(8,128)(2,1)}, bf16[64,1024]{1,0:T(8,128)(2,1)S(1)}, u32[]{:S(2)}, u32[]{:S(2)}) %collective-permute-start) | collective-permute-done | bytes 131104 | tf_op jit(solution)/shard_map/ppermute | solution.py:342
  27.5 3.6 %collective-permute-start.11 = (bf16[64,1024]{1,0:T(8,128)(2,1)S(1)}, bf16[64,1024]{1,0:T(8,128)(2,1)S(1)}, u32[]{:S(2)}, u32[]{:S(2)}) collective-permute-start(bf16[64,1024]{1,0:T(8,128)(2,1)S(1)} %collective-permute-done.10.refs_14_), channel_id=1, source_target_pairs={{0,7},{1,0},{2,1},{3,2},{4,3},{5,4},{6,5},{7,6},{8,15},{9,8},{10,9... | collective-permute-start | bytes 393224 | tf_op jit(solution)/shard_map/ppermute | solution.py:342
  31.1 2.0 %collective-permute-start.8 = (bf16[64,1024]{1,0:T(8,128)(2,1)S(1)}, bf16[64,1024]{1,0:T(8,128)(2,1)S(1)}, u32[]{:S(2)}, u32[]{:S(2)}) collective-permute-start(bf16[64,1024]{1,0:T(8,128)(2,1)S(1)} %collective-permute-done.7.refs_11_), channel_id=1, source_target_pairs={{0,7},{1,0},{2,1},{3,2},{4,3},{5,4},{6,5},{7,6},{8,15},{9,8},{10,9... | collective-permute-start | bytes 393224 | tf_op jit(solution)/shard_map/ppermute | solution.py:342
  34.8 3.7 %collective-permute-start.12 = (bf16[64,1024]{1,0:T(8,128)(2,1)S(1)}, bf16[64,1024]{1,0:T(8,128)(2,1)S(1)}, u32[]{:S(2)}, u32[]{:S(2)}) collective-permute-start(bf16[64,1024]{1,0:T(8,128)(2,1)S(1)} %collective-permute-done.11.refs_15_), channel_id=1, source_target_pairs={{0,7},{1,0},{2,1},{3,2},{4,3},{5,4},{6,5},{7,6},{8,15},{9,8},{10,9... | collective-permute-start | bytes 393224 | tf_op jit(solution)/shard_map/ppermute | solution.py:342
  38.5 1.7 collective-permute-start.9
  42.0 3.7 %collective-permute-start.13 = (bf16[64,1024]{1,0:T(8,128)(2,1)S(1)}, bf16[64,1024]{1,0:T(8,128)(2,1)S(1)}, u32[]{:S(2)}, u32[]{:S(2)}) collective-permute-start(bf16[64,1024]{1,0:T(8,128)(2,1)S(1)} %collective-permute-done.12.refs_16_), channel_id=1, source_target_pairs={{0,7},{1,0},{2,1},{3,2},{4,3},{5,4},{6,5},{7,6},{8,15},{9,8},{10,9... | collective-permute-start | bytes 393224 | tf_op jit(solution)/shard_map/ppermute | solution.py:342
  50.0 8.7 %attend.1 = (bf16[8,144,128]{2,1,0:T(8,128)(2,1)S(1)}, f32[1024,384]{1,0:T(8,128)}, bf16[1024,1024]{1,0:T(8,128)(2,1)}, bf16[1024,1024]{1,0:T(8,128)(2,1)}) custom-call(s32[1]{0:T(128)S(6)} %copy.12.refs_0_.length_ref, f32[8,16]{1,0:T(8,128)S(1)} %copy-done.7, bf16[64,1024]{1,0:T(8,128)(2,1)S(1)} %copy-done.3, bf16[64,1024]{1,0:T(8,128)(2,1)S(1)} %copy-done.4, ...), custom_call_target="tpu_custom_call" | custom-call | flops 3000000000 | bytes 1048576 | tf_op jit(solution)/shard_map/attend/pallas_call | solution.py:377
  58.8 17.0 %all_to_all.15.msg_ref = bf16[8,144,128]{2,1,0:T(8,128)(2,1)} all-to-all(bf16[8,144,128]{2,1,0:T(8,128)(2,1)S(1)} %get-tuple-element.36), channel_id=1, replica_groups=mesh['dp_0'=4,'dp_1'=4,'dp_2'=2,'seq'=8] {'seq'}, dimensions={0} | all-to-all | bytes 589824 | tf_op jit(solution)/shard_map/all_to_all | solution.py:400
  77.3 7.0 %tail.1 = (bf16[128,1024]{1,0:T(8,128)(2,1)}, bf16[128,1024]{1,0:T(8,128)(2,1)}, bf16[512,1024]{1,0:T(8,128)(2,1)}, bf16[512,1024]{1,0:T(8,128)(2,1)}, bf16[128,...) custom-call(s32[1]{0:T(128)S(6)} %copy.12.refs_0_.length_ref, ...), custom_call_target="tpu_custom_call" | custom-call | flops 1500000000 | bytes 1048576 | tf_op jit(solution)/shard_map/tail/pallas_call | solution.py:402
  84.6 1.6 collective-permute-start.15
  86.2 2.5 %collective-permute-start.16 = (bf16[128,128]{1,0:T(8,128)(2,1)}, bf16[128,128]{1,0:T(8,128)(2,1)S(1)}, u32[]{:S(2)}, u32[]{:S(2)}) collective-permute-start(bf16[128,128]{1,0:T(8,128)(2,1)} %get-tuple-element.43), channel_id=1, source_target_pairs={{0,2},{1,3},{2,4},{3,5},{4,6},{5,7},{6,0},{7,1},{8,10},{9,11},{10,... | collective-permute-start | bytes 98312 | tf_op jit(solution)/shard_map/ppermute | solution.py:342
  88.7 2.9 %collective-permute-start.17 = (bf16[128,128]{1,0:T(8,128)(2,1)}, bf16[128,128]{1,0:T(8,128)(2,1)S(1)}, u32[]{:S(2)}, u32[]{:S(2)}) collective-permute-start(bf16[128,128]{1,0:T(8,128)(2,1)} %get-tuple-element.44), channel_id=1, source_target_pairs={{0,3},{1,4},{2,5},{3,6},{4,7},{5,0},{6,1},{7,2},{8,11},{9,12},{10,... | collective-permute-start | bytes 98312 | tf_op jit(solution)/shard_map/ppermute | solution.py:342
  91.7 2.0 %collective-permute-start.18 = (bf16[128,128]{1,0:T(8,128)(2,1)}, bf16[128,128]{1,0:T(8,128)(2,1)S(1)}, u32[]{:S(2)}, u32[]{:S(2)}) collective-permute-start(bf16[128,128]{1,0:T(8,128)(2,1)} %get-tuple-element.45), channel_id=1, source_target_pairs={{0,4},{1,5},{2,6},{3,7},{4,0},{5,1},{6,2},{7,3},{8,12},{9,13},{10,... | collective-permute-start | bytes 98312 | tf_op jit(solution)/shard_map/ppermute | solution.py:342
  93.7 3.1 %collective-permute-start.19 = (bf16[128,128]{1,0:T(8,128)(2,1)}, bf16[128,128]{1,0:T(8,128)(2,1)S(1)}, u32[]{:S(2)}, u32[]{:S(2)}) collective-permute-start(bf16[128,128]{1,0:T(8,128)(2,1)} %get-tuple-element.46), channel_id=1, source_target_pairs={{0,5},{1,6},{2,7},{3,0},{4,1},{5,2},{6,3},{7,4},{8,13},{9,14},{10,... | collective-permute-start | bytes 98312 | tf_op jit(solution)/shard_map/ppermute | solution.py:342
  96.8 3.4 %collective-permute-start.20 = (bf16[128,128]{1,0:T(8,128)(2,1)}, bf16[128,128]{1,0:T(8,128)(2,1)S(1)}, u32[]{:S(2)}, u32[]{:S(2)}) collective-permute-start(bf16[128,128]{1,0:T(8,128)(2,1)} %get-tuple-element.47), channel_id=1, source_target_pairs={{0,6},{1,7},{2,0},{3,1},{4,2},{5,3},{6,4},{7,5},{8,14},{9,15},{10,... | collective-permute-start | bytes 98312 | tf_op jit(solution)/shard_map/ppermute | solution.py:342
  105.1 1.6 copy-done.10
  108.1 1.8 %attend_back.1 = (bf16[128,384]{1,0:T(8,128)(2,1)S(1)}, bf16[128,384]{1,0:T(8,128)(2,1)S(1)}, bf16[128,384]{1,0:T(8,128)(2,1)S(1)}, bf16[128,384]{1,0:T(8,128)(2...) custom-call(bf16[128,128]{1,0:T(8,128)(2,1)S(1)} %copy-done.6, ...), custom_call_target="tpu_custom_call" | custom-call | flops 1800000000 | bytes 1048576 | tf_op jit(solution)/shard_map/attend_back/pallas_call | solution.py:470
  110.4 20.0 %all_to_all.16 = bf16[16,32,1024]{2,1,0:T(8,128)(2,1)S(1)} all-to-all(bf16[16,32,1024]{2,1,0:T(8,128)(2,1)S(1)} %bitcast.16), channel_id=1, replica_groups=mesh['dp_0'=4,'dp_1'=4,'dp_2'=2,'seq'=8] {'dp_0','dp_1'}, dimensions={0} | all-to-all | bytes 2097152 | tf_op jit(solution)/shard_map/all_to_all | solution.py:474
  132.8 2.1 %collective-permute-done.29 = bf16[32,1024]{1,0:T(8,128)(2,1)S(1)} collective-permute-done((bf16[32,1024]{1,0:T(8,128)(2,1)S(1)}, bf16[32,1024]{1,0:T(8,128)(2,1)S(1)}, u32[]{:S(2)}, u32[]{:S(2)}) %collective-permute-start.29) | collective-permute-done | bytes 65568 | tf_op jit(solution)/shard_map/ppermute | solution.py:338
  134.9 2.4 %collective-permute-start.30 = (bf16[32,1024]{1,0:T(8,128)(2,1)S(1)}, bf16[32,1024]{1,0:T(8,128)(2,1)S(1)}, u32[]{:S(2)}, u32[]{:S(2)}) collective-permute-start(bf16[32,1024]{1,0:T(8,128)(2,1)S(1)} %add_convert_fusion.2), channel_id=1, source_target_pairs={{0,3},{1,2},{2,1},{3,0},{4,7},{5,6},{6,5},{7,4},{8,11},{9,10},{10,... | collective-permute-start | bytes 196616 | tf_op jit(solution)/shard_map/ppermute | solution.py:338
  137.4 2.9 %gate.1.refs_8_ = f32[128,1024]{1,0:T(8,128)S(1)} custom-call(bf16[128,1024]{1,0:T(8,128)(2,1)S(1)} %copy-done.2, bf16[1024,5120]{1,0:T(8,128)(2,1)} %all-gather.2.cloned.1.call-done.wg_ref.wo_ref.refs_9_), custom_call_target="tpu_custom_call" | custom-call | flops 600000000 | bytes 1048576 | tf_op jit(solution)/shard_map/gate/pallas_call | solution.py:446
  141.8 2.2 %collective-permute-start.25 = (bf16[128,384]{1,0:T(8,128)(2,1)S(1)}, bf16[128,384]{1,0:T(8,128)(2,1)S(1)}, u32[]{:S(2)}, u32[]{:S(2)}) collective-permute-start(bf16[128,384]{1,0:T(8,128)(2,1)S(1)} %get-tuple-element.57), channel_id=1, source_target_pairs={{0,4},{1,5},{2,6},{3,7},{4,0},{5,1},{6,2},{7,3},{8,12},{9,13},{10,... | collective-permute-start | bytes 294920 | tf_op jit(solution)/shard_map/ppermute | solution.py:342
  144.1 4.9 %collective-permute-start.26 = (bf16[128,384]{1,0:T(8,128)(2,1)S(1)}, bf16[128,384]{1,0:T(8,128)(2,1)S(1)}, u32[]{:S(2)}, u32[]{:S(2)}) collective-permute-start(bf16[128,384]{1,0:T(8,128)(2,1)S(1)} %get-tuple-element.58), channel_id=1, source_target_pairs={{0,5},{1,6},{2,7},{3,0},{4,1},{5,2},{6,3},{7,4},{8,13},{9,14},{10,... | collective-permute-start | bytes 294920 | tf_op jit(solution)/shard_map/ppermute | solution.py:342
  149.7 3.5 %collective-permute-done.24.refs_3_ = bf16[128,384]{1,0:T(8,128)(2,1)S(1)} collective-permute-done((bf16[128,384]{1,0:T(8,128)(2,1)S(1)}, bf16[128,384]{1,0:T(8,128)(2,1)S(1)}, u32[]{:S(2)}, u32[]{:S(2)}) %collective-permute-start.24) | collective-permute-done | bytes 98336 | tf_op jit(solution)/shard_map/ppermute | solution.py:342
  154.1 5.2 %collective-permute-done.27.refs_6_ = bf16[128,384]{1,0:T(8,128)(2,1)S(1)} collective-permute-done((bf16[128,384]{1,0:T(8,128)(2,1)S(1)}, bf16[128,384]{1,0:T(8,128)(2,1)S(1)}, u32[]{:S(2)}, u32[]{:S(2)}) %collective-permute-start.27) | collective-permute-done | bytes 98336 | tf_op jit(solution)/shard_map/ppermute | solution.py:342
  159.2 1.7 collective-permute-done.28.refs_7_
  161.0 6.6 %final.1 = bf16[128,1024]{1,0:T(8,128)(2,1)} custom-call(bf16[128,384]{1,0:T(8,128)(2,1)S(1)} %get-tuple-element.53.refs_0_, bf16[128,384]{1,0:T(8,128)(2,1)S(1)} %collective-permute-done.22.refs_1_, bf16[128,384]{1,0:T(8,128)(2,1)S(1)} %collective-permute-done.23.refs_2_, bf16[128,384]{1,0:T(8,128)(2,1)S(1)} %collective-permute-done.24.refs_3_, ...), custom_call_target="tpu_custom_call" | custom-call | flops 1500000000 | bytes 1048576 | tf_op jit(solution)/shard_map/final/pallas_call | solution.py:503
  (76 shorter events, 22.6 us)
Async XLA Ops:
  7.2 70.1 %all-gather.2.cloned.1.call-start = ((), (), s32[]{:S(2)}) async-start(), calls=%async_computation.3 | async-start | bytes 10813440 | tf_op jit(solution)/shard_map/all_gather | solution.py:365
  9.7 38.5 %all-to-all-start = ((bf16[32,32,384]{2,1,0:T(8,128)(2,1)}), bf16[32,32,384]{2,1,0:T(8,128)(2,1)S(1)}, u32[]{:S(2)}, u32[]{:S(2)}) async-start(bf16[32,32,384]{2,1,0:T(8,128)(2,1)} %get-tuple-element.35), calls=%async_computation | async-start | bytes 1572864 | tf_op jit(solution)/shard_map/all_to_all | solution.py:366
  17.3 9.9 %collective-permute-start = (bf16[64,1024]{1,0:T(8,128)(2,1)}, bf16[64,1024]{1,0:T(8,128)(2,1)S(1)}, u32[]{:S(2)}, u32[]{:S(2)}) collective-permute-start(bf16[64,1024]{1,0:T(8,128)(2,1)} %get-tuple-element.33.refs_2_.na_ref), channel_id=1, source_target_pairs={{0,1},{1,2},{2,3},{3,4},{4,5},{5,6},{6,7},{7,0},{8,9},{9,10},{10,1... | collective-permute-start | bytes 393224 | tf_op jit(solution)/shard_map/ppermute | solution.py:342
  19.3 8.2 %collective-permute-start.10 = (bf16[64,1024]{1,0:T(8,128)(2,1)}, bf16[64,1024]{1,0:T(8,128)(2,1)S(1)}, u32[]{:S(2)}, u32[]{:S(2)}) collective-permute-start(bf16[64,1024]{1,0:T(8,128)(2,1)} %get-tuple-element.34.refs_3_.nb_ref), channel_id=1, source_target_pairs={{0,7},{1,0},{2,1},{3,2},{4,3},{5,4},{6,5},{7,6},{8,15},{9,8},{10,9... | collective-permute-start | bytes 393224 | tf_op jit(solution)/shard_map/ppermute | solution.py:342
  23.3 7.8 %collective-permute-start.7 = (bf16[64,1024]{1,0:T(8,128)(2,1)}, bf16[64,1024]{1,0:T(8,128)(2,1)S(1)}, u32[]{:S(2)}, u32[]{:S(2)}) collective-permute-start(bf16[64,1024]{1,0:T(8,128)(2,1)} %get-tuple-element.33.refs_2_.na_ref), channel_id=1, source_target_pairs={{0,7},{1,0},{2,1},{3,2},{4,3},{5,4},{6,5},{7,6},{8,15},{9,8},{10,9... | collective-permute-start | bytes 393224 | tf_op jit(solution)/shard_map/ppermute | solution.py:342
  25.3 7.8 %collective-permute-start.4 = (bf16[64,1024]{1,0:T(8,128)(2,1)}, bf16[64,1024]{1,0:T(8,128)(2,1)S(1)}, u32[]{:S(2)}, u32[]{:S(2)}) collective-permute-start(bf16[64,1024]{1,0:T(8,128)(2,1)} %get-tuple-element.34.refs_3_.nb_ref), channel_id=1, source_target_pairs={{0,1},{1,2},{2,3},{3,4},{4,5},{5,6},{6,7},{7,0},{8,9},{9,10},{10,1... | collective-permute-start | bytes 393224 | tf_op jit(solution)/shard_map/ppermute | solution.py:342
  27.2 7.2 %collective-permute-start.1 = (bf16[64,1024]{1,0:T(8,128)(2,1)S(1)}, bf16[64,1024]{1,0:T(8,128)(2,1)S(1)}, u32[]{:S(2)}, u32[]{:S(2)}) collective-permute-start(bf16[64,1024]{1,0:T(8,128)(2,1)S(1)} %collective-permute-done.refs_4_), channel_id=1, source_target_pairs={{0,1},{1,2},{2,3},{3,4},{4,5},{5,6},{6,7},{7,0},{8,9},{9,10},{10,1... | collective-permute-start | bytes 393224 | tf_op jit(solution)/shard_map/ppermute | solution.py:342
  27.5 7.2 %collective-permute-start.11 = (bf16[64,1024]{1,0:T(8,128)(2,1)S(1)}, bf16[64,1024]{1,0:T(8,128)(2,1)S(1)}, u32[]{:S(2)}, u32[]{:S(2)}) collective-permute-start(bf16[64,1024]{1,0:T(8,128)(2,1)S(1)} %collective-permute-done.10.refs_14_), channel_id=1, source_target_pairs={{0,7},{1,0},{2,1},{3,2},{4,3},{5,4},{6,5},{7,6},{8,15},{9,8},{10,9... | collective-permute-start | bytes 393224 | tf_op jit(solution)/shard_map/ppermute | solution.py:342
  31.1 7.3 %collective-permute-start.8 = (bf16[64,1024]{1,0:T(8,128)(2,1)S(1)}, bf16[64,1024]{1,0:T(8,128)(2,1)S(1)}, u32[]{:S(2)}, u32[]{:S(2)}) collective-permute-start(bf16[64,1024]{1,0:T(8,128)(2,1)S(1)} %collective-permute-done.7.refs_11_), channel_id=1, source_target_pairs={{0,7},{1,0},{2,1},{3,2},{4,3},{5,4},{6,5},{7,6},{8,15},{9,8},{10,9... | collective-permute-start | bytes 393224 | tf_op jit(solution)/shard_map/ppermute | solution.py:342
  33.1 7.0 %collective-permute-start.5 = (bf16[64,1024]{1,0:T(8,128)(2,1)S(1)}, bf16[64,1024]{1,0:T(8,128)(2,1)S(1)}, u32[]{:S(2)}, u32[]{:S(2)}) collective-permute-start(bf16[64,1024]{1,0:T(8,128)(2,1)S(1)} %collective-permute-done.4.refs_8_), channel_id=1, source_target_pairs={{0,1},{1,2},{2,3},{3,4},{4,5},{5,6},{6,7},{7,0},{8,9},{9,10},{10,1... | collective-permute-start | bytes 393224 | tf_op jit(solution)/shard_map/ppermute | solution.py:342
  34.5 7.0 %collective-permute-start.2 = (bf16[64,1024]{1,0:T(8,128)(2,1)S(1)}, bf16[64,1024]{1,0:T(8,128)(2,1)S(1)}, u32[]{:S(2)}, u32[]{:S(2)}) collective-permute-start(bf16[64,1024]{1,0:T(8,128)(2,1)S(1)} %collective-permute-done.1.refs_5_), channel_id=1, source_target_pairs={{0,1},{1,2},{2,3},{3,4},{4,5},{5,6},{6,7},{7,0},{8,9},{9,10},{10,1... | collective-permute-start | bytes 393224 | tf_op jit(solution)/shard_map/ppermute | solution.py:342
  34.8 7.2 %collective-permute-start.12 = (bf16[64,1024]{1,0:T(8,128)(2,1)S(1)}, bf16[64,1024]{1,0:T(8,128)(2,1)S(1)}, u32[]{:S(2)}, u32[]{:S(2)}) collective-permute-start(bf16[64,1024]{1,0:T(8,128)(2,1)S(1)} %collective-permute-done.11.refs_15_), channel_id=1, source_target_pairs={{0,7},{1,0},{2,1},{3,2},{4,3},{5,4},{6,5},{7,6},{8,15},{9,8},{10,9... | collective-permute-start | bytes 393224 | tf_op jit(solution)/shard_map/ppermute | solution.py:342
  38.5 7.9 %collective-permute-start.9 = (bf16[64,1024]{1,0:T(8,128)(2,1)S(1)}, bf16[64,1024]{1,0:T(8,128)(2,1)S(1)}, u32[]{:S(2)}, u32[]{:S(2)}) collective-permute-start(bf16[64,1024]{1,0:T(8,128)(2,1)S(1)} %collective-permute-done.8.refs_12_), channel_id=1, source_target_pairs={{0,7},{1,0},{2,1},{3,2},{4,3},{5,4},{6,5},{7,6},{8,15},{9,8},{10,9... | collective-permute-start | bytes 393224 | tf_op jit(solution)/shard_map/ppermute | solution.py:342
  40.1 6.7 %collective-permute-start.6 = (bf16[64,1024]{1,0:T(8,128)(2,1)S(1)}, bf16[64,1024]{1,0:T(8,128)(2,1)S(1)}, u32[]{:S(2)}, u32[]{:S(2)}) collective-permute-start(bf16[64,1024]{1,0:T(8,128)(2,1)S(1)} %collective-permute-done.5.refs_9_), channel_id=1, source_target_pairs={{0,1},{1,2},{2,3},{3,4},{4,5},{5,6},{6,7},{7,0},{8,9},{9,10},{10,1... | collective-permute-start | bytes 393224 | tf_op jit(solution)/shard_map/ppermute | solution.py:342
  41.5 6.7 %collective-permute-start.3 = (bf16[64,1024]{1,0:T(8,128)(2,1)S(1)}, bf16[64,1024]{1,0:T(8,128)(2,1)S(1)}, u32[]{:S(2)}, u32[]{:S(2)}) collective-permute-start(bf16[64,1024]{1,0:T(8,128)(2,1)S(1)} %collective-permute-done.2.refs_6_), channel_id=1, source_target_pairs={{0,1},{1,2},{2,3},{3,4},{4,5},{5,6},{6,7},{7,0},{8,9},{9,10},{10,1... | collective-permute-start | bytes 393224 | tf_op jit(solution)/shard_map/ppermute | solution.py:342
  42.0 6.2 %collective-permute-start.13 = (bf16[64,1024]{1,0:T(8,128)(2,1)S(1)}, bf16[64,1024]{1,0:T(8,128)(2,1)S(1)}, u32[]{:S(2)}, u32[]{:S(2)}) collective-permute-start(bf16[64,1024]{1,0:T(8,128)(2,1)S(1)} %collective-permute-done.12.refs_16_), channel_id=1, source_target_pairs={{0,7},{1,0},{2,1},{3,2},{4,3},{5,4},{6,5},{7,6},{8,15},{9,8},{10,9... | collective-permute-start | bytes 393224 | tf_op jit(solution)/shard_map/ppermute | solution.py:342
  84.3 25.7 %collective-permute-start.14 = (bf16[512,1024]{1,0:T(8,128)(2,1)}, bf16[512,1024]{1,0:T(8,128)(2,1)S(1)}, u32[]{:S(2)}, u32[]{:S(2)}) collective-permute-start(bf16[512,1024]{1,0:T(8,128)(2,1)} %get-tuple-element.40), channel_id=1, source_target_pairs={{0,8},{8,0},{1,9},{9,1},{2,10},{10,2},{3,11},{11,3},{4,12},{12,4},... | collective-permute-start | bytes 3145736 | tf_op jit(solution)/shard_map/ppermute | solution.py:338
  84.6 9.1 %collective-permute-start.15 = (bf16[128,128]{1,0:T(8,128)(2,1)}, bf16[128,128]{1,0:T(8,128)(2,1)S(1)}, u32[]{:S(2)}, u32[]{:S(2)}) collective-permute-start(bf16[128,128]{1,0:T(8,128)(2,1)} %get-tuple-element.42), channel_id=1, source_target_pairs={{0,1},{1,2},{2,3},{3,4},{4,5},{5,6},{6,7},{7,0},{8,9},{9,10},{10,1... | collective-permute-start | bytes 98312 | tf_op jit(solution)/shard_map/ppermute | solution.py:342
  86.2 10.6 %collective-permute-start.16 = (bf16[128,128]{1,0:T(8,128)(2,1)}, bf16[128,128]{1,0:T(8,128)(2,1)S(1)}, u32[]{:S(2)}, u32[]{:S(2)}) collective-permute-start(bf16[128,128]{1,0:T(8,128)(2,1)} %get-tuple-element.43), channel_id=1, source_target_pairs={{0,2},{1,3},{2,4},{3,5},{4,6},{5,7},{6,0},{7,1},{8,10},{9,11},{10,... | collective-permute-start | bytes 98312 | tf_op jit(solution)/shard_map/ppermute | solution.py:342
  88.7 11.5 %collective-permute-start.17 = (bf16[128,128]{1,0:T(8,128)(2,1)}, bf16[128,128]{1,0:T(8,128)(2,1)S(1)}, u32[]{:S(2)}, u32[]{:S(2)}) collective-permute-start(bf16[128,128]{1,0:T(8,128)(2,1)} %get-tuple-element.44), channel_id=1, source_target_pairs={{0,3},{1,4},{2,5},{3,6},{4,7},{5,0},{6,1},{7,2},{8,11},{9,12},{10,... | collective-permute-start | bytes 98312 | tf_op jit(solution)/shard_map/ppermute | solution.py:342
  91.7 9.9 %collective-permute-start.18 = (bf16[128,128]{1,0:T(8,128)(2,1)}, bf16[128,128]{1,0:T(8,128)(2,1)S(1)}, u32[]{:S(2)}, u32[]{:S(2)}) collective-permute-start(bf16[128,128]{1,0:T(8,128)(2,1)} %get-tuple-element.45), channel_id=1, source_target_pairs={{0,4},{1,5},{2,6},{3,7},{4,0},{5,1},{6,2},{7,3},{8,12},{9,13},{10,... | collective-permute-start | bytes 98312 | tf_op jit(solution)/shard_map/ppermute | solution.py:342
  93.7 7.9 %collective-permute-start.19 = (bf16[128,128]{1,0:T(8,128)(2,1)}, bf16[128,128]{1,0:T(8,128)(2,1)S(1)}, u32[]{:S(2)}, u32[]{:S(2)}) collective-permute-start(bf16[128,128]{1,0:T(8,128)(2,1)} %get-tuple-element.46), channel_id=1, source_target_pairs={{0,5},{1,6},{2,7},{3,0},{4,1},{5,2},{6,3},{7,4},{8,13},{9,14},{10,... | collective-permute-start | bytes 98312 | tf_op jit(solution)/shard_map/ppermute | solution.py:342
  96.8 6.1 %collective-permute-start.20 = (bf16[128,128]{1,0:T(8,128)(2,1)}, bf16[128,128]{1,0:T(8,128)(2,1)S(1)}, u32[]{:S(2)}, u32[]{:S(2)}) collective-permute-start(bf16[128,128]{1,0:T(8,128)(2,1)} %get-tuple-element.47), channel_id=1, source_target_pairs={{0,6},{1,7},{2,0},{3,1},{4,2},{5,3},{6,4},{7,5},{8,14},{9,15},{10,... | collective-permute-start | bytes 98312 | tf_op jit(solution)/shard_map/ppermute | solution.py:342
  131.4 12.7 %collective-permute-start.22 = (bf16[128,384]{1,0:T(8,128)(2,1)S(1)}, bf16[128,384]{1,0:T(8,128)(2,1)S(1)}, u32[]{:S(2)}, u32[]{:S(2)}) collective-permute-start(bf16[128,384]{1,0:T(8,128)(2,1)S(1)} %get-tuple-element.54), channel_id=1, source_target_pairs={{0,1},{1,2},{2,3},{3,4},{4,5},{5,6},{6,7},{7,0},{8,9},{9,10},{10,1... | collective-permute-start | bytes 294920 | tf_op jit(solution)/shard_map/ppermute | solution.py:342
  132.7 16.3 %collective-permute-start.23 = (bf16[128,384]{1,0:T(8,128)(2,1)S(1)}, bf16[128,384]{1,0:T(8,128)(2,1)S(1)}, u32[]{:S(2)}, u32[]{:S(2)}) collective-permute-start(bf16[128,384]{1,0:T(8,128)(2,1)S(1)} %get-tuple-element.55), channel_id=1, source_target_pairs={{0,2},{1,3},{2,4},{3,5},{4,6},{5,7},{6,0},{7,1},{8,10},{9,11},{10,... | collective-permute-start | bytes 294920 | tf_op jit(solution)/shard_map/ppermute | solution.py:342
  134.9 14.1 %collective-permute-start.30 = (bf16[32,1024]{1,0:T(8,128)(2,1)S(1)}, bf16[32,1024]{1,0:T(8,128)(2,1)S(1)}, u32[]{:S(2)}, u32[]{:S(2)}) collective-permute-start(bf16[32,1024]{1,0:T(8,128)(2,1)S(1)} %add_convert_fusion.2), channel_id=1, source_target_pairs={{0,3},{1,2},{2,1},{3,0},{4,7},{5,6},{6,5},{7,4},{8,11},{9,10},{10,... | collective-permute-start | bytes 196616 | tf_op jit(solution)/shard_map/ppermute | solution.py:338
  140.3 12.9 %collective-permute-start.24 = (bf16[128,384]{1,0:T(8,128)(2,1)S(1)}, bf16[128,384]{1,0:T(8,128)(2,1)S(1)}, u32[]{:S(2)}, u32[]{:S(2)}) collective-permute-start(bf16[128,384]{1,0:T(8,128)(2,1)S(1)} %get-tuple-element.56), channel_id=1, source_target_pairs={{0,3},{1,4},{2,5},{3,6},{4,7},{5,0},{6,1},{7,2},{8,11},{9,12},{10,... | collective-permute-start | bytes 294920 | tf_op jit(solution)/shard_map/ppermute | solution.py:342
  141.8 11.4 %collective-permute-start.25 = (bf16[128,384]{1,0:T(8,128)(2,1)S(1)}, bf16[128,384]{1,0:T(8,128)(2,1)S(1)}, u32[]{:S(2)}, u32[]{:S(2)}) collective-permute-start(bf16[128,384]{1,0:T(8,128)(2,1)S(1)} %get-tuple-element.57), channel_id=1, source_target_pairs={{0,4},{1,5},{2,6},{3,7},{4,0},{5,1},{6,2},{7,3},{8,12},{9,13},{10,... | collective-permute-start | bytes 294920 | tf_op jit(solution)/shard_map/ppermute | solution.py:342
  144.1 10.0 %collective-permute-start.26 = (bf16[128,384]{1,0:T(8,128)(2,1)S(1)}, bf16[128,384]{1,0:T(8,128)(2,1)S(1)}, u32[]{:S(2)}, u32[]{:S(2)}) collective-permute-start(bf16[128,384]{1,0:T(8,128)(2,1)S(1)} %get-tuple-element.58), channel_id=1, source_target_pairs={{0,5},{1,6},{2,7},{3,0},{4,1},{5,2},{6,3},{7,4},{8,13},{9,14},{10,... | collective-permute-start | bytes 294920 | tf_op jit(solution)/shard_map/ppermute | solution.py:342
  149.0 10.2 %collective-permute-start.27 = (bf16[128,384]{1,0:T(8,128)(2,1)S(1)}, bf16[128,384]{1,0:T(8,128)(2,1)S(1)}, u32[]{:S(2)}, u32[]{:S(2)}) collective-permute-start(bf16[128,384]{1,0:T(8,128)(2,1)S(1)} %get-tuple-element.59), channel_id=1, source_target_pairs={{0,6},{1,7},{2,0},{3,1},{4,2},{5,3},{6,4},{7,5},{8,14},{9,15},{10,... | collective-permute-start | bytes 294920 | tf_op jit(solution)/shard_map/ppermute | solution.py:342
  149.0 11.9 %collective-permute-start.28 = (bf16[128,384]{1,0:T(8,128)(2,1)S(1)}, bf16[128,384]{1,0:T(8,128)(2,1)S(1)}, u32[]{:S(2)}, u32[]{:S(2)}) collective-permute-start(bf16[128,384]{1,0:T(8,128)(2,1)S(1)} %get-tuple-element.60), channel_id=1, source_target_pairs={{0,7},{1,0},{2,1},{3,2},{4,3},{5,4},{6,5},{7,6},{8,15},{9,8},{10,9... | collective-permute-start | bytes 294920 | tf_op jit(solution)/shard_map/ppermute | solution.py:342
  153.2 14.4 %collective-permute-start.31 = (bf16[32,1024]{1,0:T(8,128)(2,1)S(1)}, bf16[32,1024]{1,0:T(8,128)(2,1)S(1)}, u32[]{:S(2)}, u32[]{:S(2)}) collective-permute-start(bf16[32,1024]{1,0:T(8,128)(2,1)S(1)} %add_convert_fusion.1), channel_id=1, source_target_pairs={{0,7},{1,6},{2,5},{3,4},{4,3},{5,2},{6,1},{7,0},{8,15},{9,14},{10,... | collective-permute-start | bytes 196616 | tf_op jit(solution)/shard_map/ppermute | solution.py:338
  (15 other events, 222.8 us)
Sparse Core Ops, SparseCore 0:
  10.5 66.6 all-gather.1

commit v4 on v3

--- a/solution.py
+++ b/solution.py
@@ -225,15 +225,6 @@
     mixed_ref[...] = (x_ref[...].astype(F32) + mm(rows_sc[...], wo_ref[...])).astype(BF16)
     for k in range(H):
         datt_out[k][...] = datt_ref[lax.rem(me + k, H)]
-
-
-def gate_kernel(dpg_ref, wg_ref, out_ref):
-    def columns(n, carry):
-        at = pl.ds(pl.multiple_of(n * 256, 256), 256)
-        out_ref[:, at] = nt(dpg_ref[...], wg_ref[at, :])
-        return carry
-
-    lax.fori_loop(0, D // 256, columns, 0)
 
 
 def backward_kernel(*refs):
@@ -288,7 +279,7 @@
 
 def final_kernel(*refs):
     blocks = refs[:8]
-    back_ref, w_ref, x_ref, cot_ref, gain_ref, out_ref, msg_ref, lhs, acc = refs[8:]
+    dpg_ref, w_ref, x_ref, cot_ref, gain_ref, out_ref, msg_ref, lhs, acc = refs[8:]
     me = lax.axis_index("seq")
     b = pl.program_id(0)
 
@@ -298,8 +289,9 @@
             msg_ref[lax.rem(me - k + H, H)] = blocks[k][...]
         for n in range(3):
             for h in range(H):
-                lhs[n, :, h * DH : (h + 1) * DH] = msg_ref[h, :, n * DH : (n + 1) * DH]
-        acc[...] = back_ref[...]
+                lhs[n + 1, :, h * DH : (h + 1) * DH] = msg_ref[h, :, n * DH : (n + 1) * DH]
+        lhs[0] = dpg_ref[...]
+        acc[...] = jnp.zeros_like(acc)
 
     def columns(n, carry):
         at = pl.ds(pl.multiple_of(n * 512, 512), 512)
@@ -308,7 +300,7 @@
 
     lax.fori_loop(0, D // 512, columns, 0)
 
-    @pl.when(b == 2)
+    @pl.when(b == 3)
     def _():
         x = x_ref[...].astype(F32)
         c = x - jnp.mean(x, axis=-1, keepdims=True)
@@ -424,7 +416,7 @@
             pltpu.VMEM((T, D), F32),
             pltpu.VMEM((T, D), F32),
         ],
-        compiler_params=params(61500),
+        compiler_params=params(),
         cost_estimate=cost(5),
         name="tail",
     )(lengths, att_msg, na, nb, x, cot, w_full, w_full, gain_out)
@@ -433,20 +425,9 @@
     for k in ORDER:
         d_all[k] = shifted(d_att[k], k)
 
-    gate_call = pl.pallas_call(
-        gate_kernel,
-        grid=(1,),
-        out_shape=jax.ShapeDtypeStruct((T, D), F32),
-        in_specs=[VMEM, pl.BlockSpec((D, D), lambda i: (0, 0))],
-        out_specs=VMEM,
-        compiler_params=params(),
-        cost_estimate=cost(2),
-        name="gate",
-    )
-    gate_back = gate_call(d_pg, w_full)
-
     other = paired(w_send, "dp_2", 1)
     pair = (w_own.astype(F32) + other.astype(F32)).astype(BF16)
+    planes = lax.all_to_all(pair.reshape(16, 32, D), ("dp_0", "dp_1"), 0, 0, tiled=True)
 
     attend_back = pl.pallas_call(
         backward_kernel,
@@ -463,15 +444,11 @@
             pltpu.VMEM((H, T, 3 * DH), BF16),
             pltpu.VMEM((H, T, DH), BF16),
         ],
-        compiler_params=params(24000),
+        compiler_params=params(63400),
         cost_estimate=cost(6),
         name="attend_back",
     )
     d_proj = attend_back(*[d_all[k] for k in range(H)], proj, weight, slope)
-
-    pair, first = lax.optimization_barrier((pair, d_proj[0]))
-    d_proj = [first, *d_proj[1:]]
-    planes = lax.all_to_all(pair.reshape(16, 32, D), ("dp_0", "dp_1"), 0, 0, tiled=True)
 
     total = jnp.sum(planes.astype(F32), axis=0)
     for mask in (1, 3, 7):
@@ -486,23 +463,21 @@
 
     final = pl.pallas_call(
         final_kernel,
-        grid=(3,),
+        grid=(4,),
         out_shape=jax.ShapeDtypeStruct((T, D), BF16),
         in_specs=[VMEM] * (H + 1)
-        + [pl.BlockSpec((D, D), lambda b: (0, b + 1)), VMEM, VMEM, VMEM],
+        + [pl.BlockSpec((D, D), lambda b: (0, b)), VMEM, VMEM, VMEM],
         out_specs=VMEM,
         scratch_shapes=[
             pltpu.VMEM((H, T, 3 * DH), BF16),
-            pltpu.VMEM((3, T, D), BF16),
+            pltpu.VMEM((4, T, D), BF16),
             pltpu.VMEM((T, D), F32),
         ],
         compiler_params=params(dimension_semantics=("arbitrary",)),
         cost_estimate=cost(5),
         name="final",
     )
-    input_grad = final(
-        *[d_rows[k] for k in range(H)], gate_back, w_full, x, cot, gain_in
-    )
+    input_grad = final(*[d_rows[k] for k in range(H)], d_pg, w_full, x, cot, gain_in)
 
     return (mixed[None], input_grad[None], w_grad)
 

time: 176 us -> 164 us (0.932)
  the two profiles are of different devices: /device:TPU:2 before, /device:TPU:22 now
where the time goes in v4:
time: 164 us; the launch traced here: 163 us
  starting transfers between devices  73.6 us (45%)
  Pallas kernels  30.4 us (19%)
  waiting for transfers between devices  18.4 us (11%)
  blocking collectives  16.8 us (10%)
  between operations  14.9 us (9%)
  local copies, waits for them, and re-layouts  6.48 us (4%)
  other arithmetic  2.29 us (1%)
    ppermute x28, starting transfers between devices, shifted(): return lax.ppermute(value, 'seq', [(i, (i + by) % H) for i in range(H)])  55.5 us
    all_to_all x1, blocking collectives, layer(): att_msg = lax.all_to_all(msg, 'seq', 0, 0, tiled=True)  16.8 us
    ppermute x28, waiting for transfers between devices, shifted(): return lax.ppermute(value, 'seq', [(i, (i + by) % H) for i in range(H)])  15.2 us
    pallas_call x1, Pallas kernels, layer(): pl.pallas_call(forward_kernel, out_shape=[jax.ShapeDtypeStruct((H, MSG, T...  8.65 us
    pallas_call x1, Pallas kernels, layer(): final(*[d_rows[k] for k in range(H)], d_pg, w_full, x, cot, gain_in)  7.73 us
    all_to_all x1, starting transfers between devices, layer(): ws = lax.all_to_all(copies, DP, 0, 0, tiled=True)  7.38 us
    all_to_all x1, starting transfers between devices, layer(): lax.all_to_all(pair.reshape(16, 32, D), ('dp_0', 'dp_1'), 0, 0, tiled=True)  7.11 us
    unnamed x46, local copies, waits for them, and re-layouts  6.48 us
  transfers between devices with their start and end apart: 35, of which 15 were waited for; matrix products, arithmetic and copies ran while one was open for 0% of the time, Pallas kernels for 13%

profile of v4, /device:TPU:22, one launch (start us, length us, event | category | flops | bytes accessed | tf_op | source)
XLA Modules:
  0.0 162.9 jit_solution(1210238959699319776)
XLA Ops:
  7.2 2.4 %prep.1 = (bf16[64,1024]{1,0:T(8,128)(2,1)}, bf16[64,1024]{1,0:T(8,128)(2,1)}, bf16[32,5120]{1,0:T(8,128)(2,1)}, bf16[32,32,384]{2,1,0:T(8,128)(2,1)}) custom-call(bf16[128,1024]{1,0:T(8,128)(2,1)} %bitcast.8, f32[1,1024]{1,0:T(1,128)} %bitcast.14, bf16[32,4096]{1,0:T(8,128)(2,1)} %w_ref.1, bf16[32,1024]{1,0:T(8,128)(2,1)} %wout_ref.1), custom_call_target="tpu_custom_call" | custom-call | flops 600000000 | bytes 1048576 | tf_op jit(solution)/shard_map/prep/pallas_call | solution.py:343
  9.7 7.4 %all-to-all-start = ((bf16[32,32,384]{2,1,0:T(8,128)(2,1)}), bf16[32,32,384]{2,1,0:T(8,128)(2,1)S(1)}, u32[]{:S(2)}, u32[]{:S(2)}) async-start(bf16[32,32,384]{2,1,0:T(8,128)(2,1)} %get-tuple-element.33), calls=%async_computation | async-start | bytes 1572864 | tf_op jit(solution)/shard_map/all_to_all | solution.py:358
  17.1 2.0 %collective-permute-start = (bf16[64,1024]{1,0:T(8,128)(2,1)}, bf16[64,1024]{1,0:T(8,128)(2,1)S(1)}, u32[]{:S(2)}, u32[]{:S(2)}) collective-permute-start(bf16[64,1024]{1,0:T(8,128)(2,1)} %get-tuple-element.31.refs_2_.na_ref), channel_id=1, source_target_pairs={{0,1},{1,2},{2,3},{3,4},{4,5},{5,6},{6,7},{7,0},{8,9},{9,10},{10,1... | collective-permute-start | bytes 393224 | tf_op jit(solution)/shard_map/ppermute | solution.py:334
  19.1 4.0 %collective-permute-start.10 = (bf16[64,1024]{1,0:T(8,128)(2,1)}, bf16[64,1024]{1,0:T(8,128)(2,1)S(1)}, u32[]{:S(2)}, u32[]{:S(2)}) collective-permute-start(bf16[64,1024]{1,0:T(8,128)(2,1)} %get-tuple-element.32.refs_3_.nb_ref), channel_id=1, source_target_pairs={{0,7},{1,0},{2,1},{3,2},{4,3},{5,4},{6,5},{7,6},{8,15},{9,8},{10,9... | collective-permute-start | bytes 393224 | tf_op jit(solution)/shard_map/ppermute | solution.py:334
  23.1 1.9 %collective-permute-start.7 = (bf16[64,1024]{1,0:T(8,128)(2,1)}, bf16[64,1024]{1,0:T(8,128)(2,1)S(1)}, u32[]{:S(2)}, u32[]{:S(2)}) collective-permute-start(bf16[64,1024]{1,0:T(8,128)(2,1)} %get-tuple-element.31.refs_2_.na_ref), channel_id=1, source_target_pairs={{0,7},{1,0},{2,1},{3,2},{4,3},{5,4},{6,5},{7,6},{8,15},{9,8},{10,9... | collective-permute-start | bytes 393224 | tf_op jit(solution)/shard_map/ppermute | solution.py:334
  25.1 1.9 %collective-permute-done.refs_4_ = bf16[64,1024]{1,0:T(8,128)(2,1)S(1)} collective-permute-done((bf16[64,1024]{1,0:T(8,128)(2,1)}, bf16[64,1024]{1,0:T(8,128)(2,1)S(1)}, u32[]{:S(2)}, u32[]{:S(2)}) %collective-permute-start) | collective-permute-done | bytes 131104 | tf_op jit(solution)/shard_map/ppermute | solution.py:334
  27.3 3.6 %collective-permute-start.11 = (bf16[64,1024]{1,0:T(8,128)(2,1)S(1)}, bf16[64,1024]{1,0:T(8,128)(2,1)S(1)}, u32[]{:S(2)}, u32[]{:S(2)}) collective-permute-start(bf16[64,1024]{1,0:T(8,128)(2,1)S(1)} %collective-permute-done.10.refs_14_), channel_id=1, source_target_pairs={{0,7},{1,0},{2,1},{3,2},{4,3},{5,4},{6,5},{7,6},{8,15},{9,8},{10,9... | collective-permute-start | bytes 393224 | tf_op jit(solution)/shard_map/ppermute | solution.py:334
  30.9 2.0 %collective-permute-start.8 = (bf16[64,1024]{1,0:T(8,128)(2,1)S(1)}, bf16[64,1024]{1,0:T(8,128)(2,1)S(1)}, u32[]{:S(2)}, u32[]{:S(2)}) collective-permute-start(bf16[64,1024]{1,0:T(8,128)(2,1)S(1)} %collective-permute-done.7.refs_11_), channel_id=1, source_target_pairs={{0,7},{1,0},{2,1},{3,2},{4,3},{5,4},{6,5},{7,6},{8,15},{9,8},{10,9... | collective-permute-start | bytes 393224 | tf_op jit(solution)/shard_map/ppermute | solution.py:334
  34.4 3.7 %collective-permute-start.12 = (bf16[64,1024]{1,0:T(8,128)(2,1)S(1)}, bf16[64,1024]{1,0:T(8,128)(2,1)S(1)}, u32[]{:S(2)}, u32[]{:S(2)}) collective-permute-start(bf16[64,1024]{1,0:T(8,128)(2,1)S(1)} %collective-permute-done.11.refs_15_), channel_id=1, source_target_pairs={{0,7},{1,0},{2,1},{3,2},{4,3},{5,4},{6,5},{7,6},{8,15},{9,8},{10,9... | collective-permute-start | bytes 393224 | tf_op jit(solution)/shard_map/ppermute | solution.py:334
  38.1 1.8 %collective-permute-start.9 = (bf16[64,1024]{1,0:T(8,128)(2,1)S(1)}, bf16[64,1024]{1,0:T(8,128)(2,1)S(1)}, u32[]{:S(2)}, u32[]{:S(2)}) collective-permute-start(bf16[64,1024]{1,0:T(8,128)(2,1)S(1)} %collective-permute-done.8.refs_12_), channel_id=1, source_target_pairs={{0,7},{1,0},{2,1},{3,2},{4,3},{5,4},{6,5},{7,6},{8,15},{9,8},{10,9... | collective-permute-start | bytes 393224 | tf_op jit(solution)/shard_map/ppermute | solution.py:334
  42.0 3.7 %collective-permute-start.13 = (bf16[64,1024]{1,0:T(8,128)(2,1)S(1)}, bf16[64,1024]{1,0:T(8,128)(2,1)S(1)}, u32[]{:S(2)}, u32[]{:S(2)}) collective-permute-start(bf16[64,1024]{1,0:T(8,128)(2,1)S(1)} %collective-permute-done.12.refs_16_), channel_id=1, source_target_pairs={{0,7},{1,0},{2,1},{3,2},{4,3},{5,4},{6,5},{7,6},{8,15},{9,8},{10,9... | collective-permute-start | bytes 393224 | tf_op jit(solution)/shard_map/ppermute | solution.py:334
  53.2 8.7 %attend.1 = (bf16[8,144,128]{2,1,0:T(8,128)(2,1)S(1)}, f32[1024,384]{1,0:T(8,128)}, bf16[1024,1024]{1,0:T(8,128)(2,1)}, bf16[1024,1024]{1,0:T(8,128)(2,1)}) custom-call(s32[1]{0:T(128)S(6)} %copy.12.refs_0_.length_ref, f32[8,16]{1,0:T(8,128)S(1)} %copy-done.14, bf16[64,1024]{1,0:T(8,128)(2,1)S(1)} %copy-done.2, bf16[64,1024]{1,0:T(8,128)(2,1)S(1)} %copy-done.4, ...), custom_call_target="tpu_custom_call" | custom-call | flops 3000000000 | bytes 1048576 | tf_op jit(solution)/shard_map/attend/pallas_call | solution.py:369
  61.9 16.8 %all_to_all.15.msg_ref = bf16[8,144,128]{2,1,0:T(8,128)(2,1)S(1)} all-to-all(bf16[8,144,128]{2,1,0:T(8,128)(2,1)S(1)} %get-tuple-element.34), channel_id=1, replica_groups=mesh['dp_0'=4,'dp_1'=4,'dp_2'=2,'seq'=8] {'seq'}, dimensions={0} | all-to-all | bytes 589824 | tf_op jit(solution)/shard_map/all_to_all | solution.py:392
  78.7 6.1 %tail.1 = (bf16[128,1024]{1,0:T(8,128)(2,1)}, bf16[128,1024]{1,0:T(8,128)(2,1)S(1)}, bf16[512,1024]{1,0:T(8,128)(2,1)S(1)}, bf16[512,1024]{1,0:T(8,128)(2,1)}, b...) custom-call(s32[1]{0:T(128)S(6)} %copy.12.refs_0_.length_ref, ...), custom_call_target="tpu_custom_call" | custom-call | flops 1500000000 | bytes 1048576 | tf_op jit(solution)/shard_map/tail/pallas_call | solution.py:394
  84.9 2.9 %collective-permute-done.28 = bf16[512,1024]{1,0:T(8,128)(2,1)S(1)} collective-permute-done((bf16[512,1024]{1,0:T(8,128)(2,1)}, bf16[512,1024]{1,0:T(8,128)(2,1)S(1)}, u32[]{:S(2)}, u32[]{:S(2)}) %collective-permute-start.28) | collective-permute-done | bytes 1048608 | tf_op jit(solution)/shard_map/ppermute | solution.py:330
  89.1 7.1 %all-to-all-start.2 = ((bf16[16,32,1024]{2,1,0:T(8,128)(2,1)}), bf16[16,32,1024]{2,1,0:T(8,128)(2,1)S(1)}, u32[]{:S(2)}, u32[]{:S(2)}) async-start(bf16[16,32,1024]{2,1,0:T(8,128)(2,1)} %bitcast.7), calls=%async_computation.2 | async-start | bytes 2097152 | tf_op jit(solution)/shard_map/all_to_all | solution.py:430
  97.3 2.7 %collective-permute-start.16 = (bf16[128,128]{1,0:T(8,128)(2,1)S(1)}, bf16[128,128]{1,0:T(8,128)(2,1)S(1)}, u32[]{:S(2)}, u32[]{:S(2)}) collective-permute-start(bf16[128,128]{1,0:T(8,128)(2,1)S(1)} %get-tuple-element.40), channel_id=1, source_target_pairs={{0,3},{1,4},{2,5},{3,6},{4,7},{5,0},{6,1},{7,2},{8,11},{9,12},{10,... | collective-permute-start | bytes 98312 | tf_op jit(solution)/shard_map/ppermute | solution.py:334
  100.1 3.1 %collective-permute-start.17 = (bf16[128,128]{1,0:T(8,128)(2,1)S(1)}, bf16[128,128]{1,0:T(8,128)(2,1)S(1)}, u32[]{:S(2)}, u32[]{:S(2)}) collective-permute-start(bf16[128,128]{1,0:T(8,128)(2,1)S(1)} %get-tuple-element.41), channel_id=1, source_target_pairs={{0,4},{1,5},{2,6},{3,7},{4,0},{5,1},{6,2},{7,3},{8,12},{9,13},{10,... | collective-permute-start | bytes 98312 | tf_op jit(solution)/shard_map/ppermute | solution.py:334
  103.2 2.3 %collective-permute-start.18 = (bf16[128,128]{1,0:T(8,128)(2,1)S(1)}, bf16[128,128]{1,0:T(8,128)(2,1)S(1)}, u32[]{:S(2)}, u32[]{:S(2)}) collective-permute-start(bf16[128,128]{1,0:T(8,128)(2,1)S(1)} %get-tuple-element.42), channel_id=1, source_target_pairs={{0,5},{1,6},{2,7},{3,0},{4,1},{5,2},{6,3},{7,4},{8,13},{9,14},{10,... | collective-permute-start | bytes 98312 | tf_op jit(solution)/shard_map/ppermute | solution.py:334
  105.4 3.2 %collective-permute-start.19 = (bf16[128,128]{1,0:T(8,128)(2,1)S(1)}, bf16[128,128]{1,0:T(8,128)(2,1)S(1)}, u32[]{:S(2)}, u32[]{:S(2)}) collective-permute-start(bf16[128,128]{1,0:T(8,128)(2,1)S(1)} %get-tuple-element.43), channel_id=1, source_target_pairs={{0,6},{1,7},{2,0},{3,1},{4,2},{5,3},{6,4},{7,5},{8,14},{9,15},{10,... | collective-permute-start | bytes 98312 | tf_op jit(solution)/shard_map/ppermute | solution.py:334
  111.0 1.5 collective-permute-done.20.refs_7_
  113.1 5.5 %attend_back.1 = (bf16[128,384]{1,0:T(8,128)(2,1)}, bf16[128,384]{1,0:T(8,128)(2,1)}, bf16[128,384]{1,0:T(8,128)(2,1)}, bf16[128,384]{1,0:T(8,128)(2,1)}, bf16[1...) custom-call(bf16[128,128]{1,0:T(8,128)(2,1)} %copy-done.13, ...), custom_call_target="tpu_custom_call" | custom-call | flops 1800000000 | bytes 1048576 | tf_op jit(solution)/shard_map/attend_back/pallas_call | solution.py:451
  119.5 3.0 %collective-permute-start.22 = (bf16[128,384]{1,0:T(8,128)(2,1)}, bf16[128,384]{1,0:T(8,128)(2,1)S(1)}, u32[]{:S(2)}, u32[]{:S(2)}) collective-permute-start(bf16[128,384]{1,0:T(8,128)(2,1)} %get-tuple-element.50), channel_id=1, source_target_pairs={{0,2},{1,3},{2,4},{3,5},{4,6},{5,7},{6,0},{7,1},{8,10},{9,11},{10,... | collective-permute-start | bytes 294920 | tf_op jit(solution)/shard_map/ppermute | solution.py:334
  122.5 1.5 collective-permute-start.30
  124.1 2.4 %collective-permute-start.23 = (bf16[128,384]{1,0:T(8,128)(2,1)}, bf16[128,384]{1,0:T(8,128)(2,1)S(1)}, u32[]{:S(2)}, u32[]{:S(2)}) collective-permute-start(bf16[128,384]{1,0:T(8,128)(2,1)} %get-tuple-element.51), channel_id=1, source_target_pairs={{0,3},{1,4},{2,5},{3,6},{4,7},{5,0},{6,1},{7,2},{8,11},{9,12},{10,... | collective-permute-start | bytes 294920 | tf_op jit(solution)/shard_map/ppermute | solution.py:334
  126.4 2.5 %collective-permute-start.24 = (bf16[128,384]{1,0:T(8,128)(2,1)}, bf16[128,384]{1,0:T(8,128)(2,1)S(1)}, u32[]{:S(2)}, u32[]{:S(2)}) collective-permute-start(bf16[128,384]{1,0:T(8,128)(2,1)} %get-tuple-element.52), channel_id=1, source_target_pairs={{0,4},{1,5},{2,6},{3,7},{4,0},{5,1},{6,2},{7,3},{8,12},{9,13},{10,... | collective-permute-start | bytes 294920 | tf_op jit(solution)/shard_map/ppermute | solution.py:334
  129.0 3.4 %collective-permute-start.25 = (bf16[128,384]{1,0:T(8,128)(2,1)}, bf16[128,384]{1,0:T(8,128)(2,1)S(1)}, u32[]{:S(2)}, u32[]{:S(2)}) collective-permute-start(bf16[128,384]{1,0:T(8,128)(2,1)} %get-tuple-element.53), channel_id=1, source_target_pairs={{0,5},{1,6},{2,7},{3,0},{4,1},{5,2},{6,3},{7,4},{8,13},{9,14},{10,... | collective-permute-start | bytes 294920 | tf_op jit(solution)/shard_map/ppermute | solution.py:334
  132.4 2.3 %collective-permute-start.26 = (bf16[128,384]{1,0:T(8,128)(2,1)}, bf16[128,384]{1,0:T(8,128)(2,1)S(1)}, u32[]{:S(2)}, u32[]{:S(2)}) collective-permute-start(bf16[128,384]{1,0:T(8,128)(2,1)} %get-tuple-element.54), channel_id=1, source_target_pairs={{0,6},{1,7},{2,0},{3,1},{4,2},{5,3},{6,4},{7,5},{8,14},{9,15},{10,... | collective-permute-start | bytes 294920 | tf_op jit(solution)/shard_map/ppermute | solution.py:334
  134.9 4.3 %collective-permute-start.27 = (bf16[128,384]{1,0:T(8,128)(2,1)}, bf16[128,384]{1,0:T(8,128)(2,1)S(1)}, u32[]{:S(2)}, u32[]{:S(2)}) collective-permute-start(bf16[128,384]{1,0:T(8,128)(2,1)} %get-tuple-element.55), channel_id=1, source_target_pairs={{0,7},{1,0},{2,1},{3,2},{4,3},{5,4},{6,5},{7,6},{8,15},{9,8},{10,9... | collective-permute-start | bytes 294920 | tf_op jit(solution)/shard_map/ppermute | solution.py:334
  141.1 2.6 %collective-permute-done.26.refs_6_ = bf16[128,384]{1,0:T(8,128)(2,1)S(1)} collective-permute-done((bf16[128,384]{1,0:T(8,128)(2,1)}, bf16[128,384]{1,0:T(8,128)(2,1)S(1)}, u32[]{:S(2)}, u32[]{:S(2)}) %collective-permute-start.26) | collective-permute-done | bytes 98336 | tf_op jit(solution)/shard_map/ppermute | solution.py:334
  143.8 3.0 %collective-permute-done.27.refs_7_ = bf16[128,384]{1,0:T(8,128)(2,1)S(1)} collective-permute-done((bf16[128,384]{1,0:T(8,128)(2,1)}, bf16[128,384]{1,0:T(8,128)(2,1)S(1)}, u32[]{:S(2)}, u32[]{:S(2)}) %collective-permute-start.27) | collective-permute-done | bytes 98336 | tf_op jit(solution)/shard_map/ppermute | solution.py:334
  147.7 7.7 %final.1 = bf16[128,1024]{1,0:T(8,128)(2,1)} custom-call(bf16[128,384]{1,0:T(8,128)(2,1)S(1)} %copy-done.6, bf16[128,384]{1,0:T(8,128)(2,1)S(1)} %collective-permute-done.21.refs_1_, bf16[128,384]{1,0:T(8,128)(2,1)S(1)} %collective-permute-done.22.refs_2_, bf16[128,384]{1,0:T(8,128)(2,1)S(1)} %collective-permute-done.23.refs_3_, ...), custom_call_target="tpu_custom_call" | custom-call | flops 1500000000 | bytes 1048576 | tf_op jit(solution)/shard_map/final/pallas_call | solution.py:480
  (96 shorter events, 21.0 us)
Async XLA Ops:
  7.2 71.5 %all-gather.2.cloned.1.call-start = ((), (), s32[]{:S(2)}) async-start(), calls=%async_computation.3 | async-start | bytes 10813440 | tf_op jit(solution)/shard_map/all_gather | solution.py:357
  9.7 39.8 %all-to-all-start = ((bf16[32,32,384]{2,1,0:T(8,128)(2,1)}), bf16[32,32,384]{2,1,0:T(8,128)(2,1)S(1)}, u32[]{:S(2)}, u32[]{:S(2)}) async-start(bf16[32,32,384]{2,1,0:T(8,128)(2,1)} %get-tuple-element.33), calls=%async_computation | async-start | bytes 1572864 | tf_op jit(solution)/shard_map/all_to_all | solution.py:358
  17.1 9.9 %collective-permute-start = (bf16[64,1024]{1,0:T(8,128)(2,1)}, bf16[64,1024]{1,0:T(8,128)(2,1)S(1)}, u32[]{:S(2)}, u32[]{:S(2)}) collective-permute-start(bf16[64,1024]{1,0:T(8,128)(2,1)} %get-tuple-element.31.refs_2_.na_ref), channel_id=1, source_target_pairs={{0,1},{1,2},{2,3},{3,4},{4,5},{5,6},{6,7},{7,0},{8,9},{9,10},{10,1... | collective-permute-start | bytes 393224 | tf_op jit(solution)/shard_map/ppermute | solution.py:334
  19.1 8.2 %collective-permute-start.10 = (bf16[64,1024]{1,0:T(8,128)(2,1)}, bf16[64,1024]{1,0:T(8,128)(2,1)S(1)}, u32[]{:S(2)}, u32[]{:S(2)}) collective-permute-start(bf16[64,1024]{1,0:T(8,128)(2,1)} %get-tuple-element.32.refs_3_.nb_ref), channel_id=1, source_target_pairs={{0,7},{1,0},{2,1},{3,2},{4,3},{5,4},{6,5},{7,6},{8,15},{9,8},{10,9... | collective-permute-start | bytes 393224 | tf_op jit(solution)/shard_map/ppermute | solution.py:334
  23.1 7.8 %collective-permute-start.7 = (bf16[64,1024]{1,0:T(8,128)(2,1)}, bf16[64,1024]{1,0:T(8,128)(2,1)S(1)}, u32[]{:S(2)}, u32[]{:S(2)}) collective-permute-start(bf16[64,1024]{1,0:T(8,128)(2,1)} %get-tuple-element.31.refs_2_.na_ref), channel_id=1, source_target_pairs={{0,7},{1,0},{2,1},{3,2},{4,3},{5,4},{6,5},{7,6},{8,15},{9,8},{10,9... | collective-permute-start | bytes 393224 | tf_op jit(solution)/shard_map/ppermute | solution.py:334
  25.0 7.8 %collective-permute-start.4 = (bf16[64,1024]{1,0:T(8,128)(2,1)}, bf16[64,1024]{1,0:T(8,128)(2,1)S(1)}, u32[]{:S(2)}, u32[]{:S(2)}) collective-permute-start(bf16[64,1024]{1,0:T(8,128)(2,1)} %get-tuple-element.32.refs_3_.nb_ref), channel_id=1, source_target_pairs={{0,1},{1,2},{2,3},{3,4},{4,5},{5,6},{6,7},{7,0},{8,9},{9,10},{10,1... | collective-permute-start | bytes 393224 | tf_op jit(solution)/shard_map/ppermute | solution.py:334
  27.0 7.2 %collective-permute-start.1 = (bf16[64,1024]{1,0:T(8,128)(2,1)S(1)}, bf16[64,1024]{1,0:T(8,128)(2,1)S(1)}, u32[]{:S(2)}, u32[]{:S(2)}) collective-permute-start(bf16[64,1024]{1,0:T(8,128)(2,1)S(1)} %collective-permute-done.refs_4_), channel_id=1, source_target_pairs={{0,1},{1,2},{2,3},{3,4},{4,5},{5,6},{6,7},{7,0},{8,9},{9,10},{10,1... | collective-permute-start | bytes 393224 | tf_op jit(solution)/shard_map/ppermute | solution.py:334
  27.3 7.1 %collective-permute-start.11 = (bf16[64,1024]{1,0:T(8,128)(2,1)S(1)}, bf16[64,1024]{1,0:T(8,128)(2,1)S(1)}, u32[]{:S(2)}, u32[]{:S(2)}) collective-permute-start(bf16[64,1024]{1,0:T(8,128)(2,1)S(1)} %collective-permute-done.10.refs_14_), channel_id=1, source_target_pairs={{0,7},{1,0},{2,1},{3,2},{4,3},{5,4},{6,5},{7,6},{8,15},{9,8},{10,9... | collective-permute-start | bytes 393224 | tf_op jit(solution)/shard_map/ppermute | solution.py:334
  30.9 7.2 %collective-permute-start.8 = (bf16[64,1024]{1,0:T(8,128)(2,1)S(1)}, bf16[64,1024]{1,0:T(8,128)(2,1)S(1)}, u32[]{:S(2)}, u32[]{:S(2)}) collective-permute-start(bf16[64,1024]{1,0:T(8,128)(2,1)S(1)} %collective-permute-done.7.refs_11_), channel_id=1, source_target_pairs={{0,7},{1,0},{2,1},{3,2},{4,3},{5,4},{6,5},{7,6},{8,15},{9,8},{10,9... | collective-permute-start | bytes 393224 | tf_op jit(solution)/shard_map/ppermute | solution.py:334
  32.8 7.1 %collective-permute-start.5 = (bf16[64,1024]{1,0:T(8,128)(2,1)S(1)}, bf16[64,1024]{1,0:T(8,128)(2,1)S(1)}, u32[]{:S(2)}, u32[]{:S(2)}) collective-permute-start(bf16[64,1024]{1,0:T(8,128)(2,1)S(1)} %collective-permute-done.4.refs_8_), channel_id=1, source_target_pairs={{0,1},{1,2},{2,3},{3,4},{4,5},{5,6},{6,7},{7,0},{8,9},{9,10},{10,1... | collective-permute-start | bytes 393224 | tf_op jit(solution)/shard_map/ppermute | solution.py:334
  34.2 7.2 %collective-permute-start.2 = (bf16[64,1024]{1,0:T(8,128)(2,1)S(1)}, bf16[64,1024]{1,0:T(8,128)(2,1)S(1)}, u32[]{:S(2)}, u32[]{:S(2)}) collective-permute-start(bf16[64,1024]{1,0:T(8,128)(2,1)S(1)} %collective-permute-done.1.refs_5_), channel_id=1, source_target_pairs={{0,1},{1,2},{2,3},{3,4},{4,5},{5,6},{6,7},{7,0},{8,9},{9,10},{10,1... | collective-permute-start | bytes 393224 | tf_op jit(solution)/shard_map/ppermute | solution.py:334
  34.4 7.6 %collective-permute-start.12 = (bf16[64,1024]{1,0:T(8,128)(2,1)S(1)}, bf16[64,1024]{1,0:T(8,128)(2,1)S(1)}, u32[]{:S(2)}, u32[]{:S(2)}) collective-permute-start(bf16[64,1024]{1,0:T(8,128)(2,1)S(1)} %collective-permute-done.11.refs_15_), channel_id=1, source_target_pairs={{0,7},{1,0},{2,1},{3,2},{4,3},{5,4},{6,5},{7,6},{8,15},{9,8},{10,9... | collective-permute-start | bytes 393224 | tf_op jit(solution)/shard_map/ppermute | solution.py:334
  38.1 8.2 %collective-permute-start.9 = (bf16[64,1024]{1,0:T(8,128)(2,1)S(1)}, bf16[64,1024]{1,0:T(8,128)(2,1)S(1)}, u32[]{:S(2)}, u32[]{:S(2)}) collective-permute-start(bf16[64,1024]{1,0:T(8,128)(2,1)S(1)} %collective-permute-done.8.refs_12_), channel_id=1, source_target_pairs={{0,7},{1,0},{2,1},{3,2},{4,3},{5,4},{6,5},{7,6},{8,15},{9,8},{10,9... | collective-permute-start | bytes 393224 | tf_op jit(solution)/shard_map/ppermute | solution.py:334
  40.0 6.8 %collective-permute-start.6 = (bf16[64,1024]{1,0:T(8,128)(2,1)S(1)}, bf16[64,1024]{1,0:T(8,128)(2,1)S(1)}, u32[]{:S(2)}, u32[]{:S(2)}) collective-permute-start(bf16[64,1024]{1,0:T(8,128)(2,1)S(1)} %collective-permute-done.5.refs_9_), channel_id=1, source_target_pairs={{0,1},{1,2},{2,3},{3,4},{4,5},{5,6},{6,7},{7,0},{8,9},{9,10},{10,1... | collective-permute-start | bytes 393224 | tf_op jit(solution)/shard_map/ppermute | solution.py:334
  41.4 6.8 %collective-permute-start.3 = (bf16[64,1024]{1,0:T(8,128)(2,1)S(1)}, bf16[64,1024]{1,0:T(8,128)(2,1)S(1)}, u32[]{:S(2)}, u32[]{:S(2)}) collective-permute-start(bf16[64,1024]{1,0:T(8,128)(2,1)S(1)} %collective-permute-done.2.refs_6_), channel_id=1, source_target_pairs={{0,1},{1,2},{2,3},{3,4},{4,5},{5,6},{6,7},{7,0},{8,9},{9,10},{10,1... | collective-permute-start | bytes 393224 | tf_op jit(solution)/shard_map/ppermute | solution.py:334
  42.0 6.9 %collective-permute-start.13 = (bf16[64,1024]{1,0:T(8,128)(2,1)S(1)}, bf16[64,1024]{1,0:T(8,128)(2,1)S(1)}, u32[]{:S(2)}, u32[]{:S(2)}) collective-permute-start(bf16[64,1024]{1,0:T(8,128)(2,1)S(1)} %collective-permute-done.12.refs_16_), channel_id=1, source_target_pairs={{0,7},{1,0},{2,1},{3,2},{4,3},{5,4},{6,5},{7,6},{8,15},{9,8},{10,9... | collective-permute-start | bytes 393224 | tf_op jit(solution)/shard_map/ppermute | solution.py:334
  89.1 20.8 %all-to-all-start.2 = ((bf16[16,32,1024]{2,1,0:T(8,128)(2,1)}), bf16[16,32,1024]{2,1,0:T(8,128)(2,1)S(1)}, u32[]{:S(2)}, u32[]{:S(2)}) async-start(bf16[16,32,1024]{2,1,0:T(8,128)(2,1)} %bitcast.7), calls=%async_computation.2 | async-start | bytes 2097152 | tf_op jit(solution)/shard_map/all_to_all | solution.py:430
  96.2 9.2 %collective-permute-start.14 = (bf16[128,128]{1,0:T(8,128)(2,1)S(1)}, bf16[128,128]{1,0:T(8,128)(2,1)S(1)}, u32[]{:S(2)}, u32[]{:S(2)}) collective-permute-start(bf16[128,128]{1,0:T(8,128)(2,1)S(1)} %get-tuple-element.38), channel_id=1, source_target_pairs={{0,1},{1,2},{2,3},{3,4},{4,5},{5,6},{6,7},{7,0},{8,9},{9,10},{10,1... | collective-permute-start | bytes 98312 | tf_op jit(solution)/shard_map/ppermute | solution.py:334
  96.8 11.8 %collective-permute-start.15 = (bf16[128,128]{1,0:T(8,128)(2,1)S(1)}, bf16[128,128]{1,0:T(8,128)(2,1)S(1)}, u32[]{:S(2)}, u32[]{:S(2)}) collective-permute-start(bf16[128,128]{1,0:T(8,128)(2,1)S(1)} %get-tuple-element.39), channel_id=1, source_target_pairs={{0,2},{1,3},{2,4},{3,5},{4,6},{5,7},{6,0},{7,1},{8,10},{9,11},{10,... | collective-permute-start | bytes 98312 | tf_op jit(solution)/shard_map/ppermute | solution.py:334
  97.3 12.8 %collective-permute-start.16 = (bf16[128,128]{1,0:T(8,128)(2,1)S(1)}, bf16[128,128]{1,0:T(8,128)(2,1)S(1)}, u32[]{:S(2)}, u32[]{:S(2)}) collective-permute-start(bf16[128,128]{1,0:T(8,128)(2,1)S(1)} %get-tuple-element.40), channel_id=1, source_target_pairs={{0,3},{1,4},{2,5},{3,6},{4,7},{5,0},{6,1},{7,2},{8,11},{9,12},{10,... | collective-permute-start | bytes 98312 | tf_op jit(solution)/shard_map/ppermute | solution.py:334
  100.1 10.9 %collective-permute-start.17 = (bf16[128,128]{1,0:T(8,128)(2,1)S(1)}, bf16[128,128]{1,0:T(8,128)(2,1)S(1)}, u32[]{:S(2)}, u32[]{:S(2)}) collective-permute-start(bf16[128,128]{1,0:T(8,128)(2,1)S(1)} %get-tuple-element.41), channel_id=1, source_target_pairs={{0,4},{1,5},{2,6},{3,7},{4,0},{5,1},{6,2},{7,3},{8,12},{9,13},{10,... | collective-permute-start | bytes 98312 | tf_op jit(solution)/shard_map/ppermute | solution.py:334
  103.2 7.8 %collective-permute-start.18 = (bf16[128,128]{1,0:T(8,128)(2,1)S(1)}, bf16[128,128]{1,0:T(8,128)(2,1)S(1)}, u32[]{:S(2)}, u32[]{:S(2)}) collective-permute-start(bf16[128,128]{1,0:T(8,128)(2,1)S(1)} %get-tuple-element.42), channel_id=1, source_target_pairs={{0,5},{1,6},{2,7},{3,0},{4,1},{5,2},{6,3},{7,4},{8,13},{9,14},{10,... | collective-permute-start | bytes 98312 | tf_op jit(solution)/shard_map/ppermute | solution.py:334
  110.2 12.3 %collective-permute-start.29 = (bf16[32,1024]{1,0:T(8,128)(2,1)S(1)}, bf16[32,1024]{1,0:T(8,128)(2,1)S(1)}, u32[]{:S(2)}, u32[]{:S(2)}) collective-permute-start(bf16[32,1024]{1,0:T(8,128)(2,1)S(1)} %reduce_sum.12), channel_id=1, source_target_pairs={{0,1},{1,0},{2,3},{3,2},{4,5},{5,4},{6,7},{7,6},{8,9},{9,8},{10,11... | collective-permute-start | bytes 196616 | tf_op jit(solution)/shard_map/ppermute | solution.py:330
  118.6 10.3 %collective-permute-start.21 = (bf16[128,384]{1,0:T(8,128)(2,1)}, bf16[128,384]{1,0:T(8,128)(2,1)S(1)}, u32[]{:S(2)}, u32[]{:S(2)}) collective-permute-start(bf16[128,384]{1,0:T(8,128)(2,1)} %get-tuple-element.49), channel_id=1, source_target_pairs={{0,1},{1,2},{2,3},{3,4},{4,5},{5,6},{6,7},{7,0},{8,9},{9,10},{10,1... | collective-permute-start | bytes 294920 | tf_op jit(solution)/shard_map/ppermute | solution.py:334
  119.5 12.9 %collective-permute-start.22 = (bf16[128,384]{1,0:T(8,128)(2,1)}, bf16[128,384]{1,0:T(8,128)(2,1)S(1)}, u32[]{:S(2)}, u32[]{:S(2)}) collective-permute-start(bf16[128,384]{1,0:T(8,128)(2,1)} %get-tuple-element.50), channel_id=1, source_target_pairs={{0,2},{1,3},{2,4},{3,5},{4,6},{5,7},{6,0},{7,1},{8,10},{9,11},{10,... | collective-permute-start | bytes 294920 | tf_op jit(solution)/shard_map/ppermute | solution.py:334
  122.5 12.4 %collective-permute-start.30 = (bf16[32,1024]{1,0:T(8,128)(2,1)S(1)}, bf16[32,1024]{1,0:T(8,128)(2,1)S(1)}, u32[]{:S(2)}, u32[]{:S(2)}) collective-permute-start(bf16[32,1024]{1,0:T(8,128)(2,1)S(1)} %add_convert_fusion.2), channel_id=1, source_target_pairs={{0,3},{1,2},{2,1},{3,0},{4,7},{5,6},{6,5},{7,4},{8,11},{9,10},{10,... | collective-permute-start | bytes 196616 | tf_op jit(solution)/shard_map/ppermute | solution.py:330
  124.1 15.3 %collective-permute-start.23 = (bf16[128,384]{1,0:T(8,128)(2,1)}, bf16[128,384]{1,0:T(8,128)(2,1)S(1)}, u32[]{:S(2)}, u32[]{:S(2)}) collective-permute-start(bf16[128,384]{1,0:T(8,128)(2,1)} %get-tuple-element.51), channel_id=1, source_target_pairs={{0,3},{1,4},{2,5},{3,6},{4,7},{5,0},{6,1},{7,2},{8,11},{9,12},{10,... | collective-permute-start | bytes 294920 | tf_op jit(solution)/shard_map/ppermute | solution.py:334
  126.4 14.7 %collective-permute-start.24 = (bf16[128,384]{1,0:T(8,128)(2,1)}, bf16[128,384]{1,0:T(8,128)(2,1)S(1)}, u32[]{:S(2)}, u32[]{:S(2)}) collective-permute-start(bf16[128,384]{1,0:T(8,128)(2,1)} %get-tuple-element.52), channel_id=1, source_target_pairs={{0,4},{1,5},{2,6},{3,7},{4,0},{5,1},{6,2},{7,3},{8,12},{9,13},{10,... | collective-permute-start | bytes 294920 | tf_op jit(solution)/shard_map/ppermute | solution.py:334
  129.0 12.2 %collective-permute-start.25 = (bf16[128,384]{1,0:T(8,128)(2,1)}, bf16[128,384]{1,0:T(8,128)(2,1)S(1)}, u32[]{:S(2)}, u32[]{:S(2)}) collective-permute-start(bf16[128,384]{1,0:T(8,128)(2,1)} %get-tuple-element.53), channel_id=1, source_target_pairs={{0,5},{1,6},{2,7},{3,0},{4,1},{5,2},{6,3},{7,4},{8,13},{9,14},{10,... | collective-permute-start | bytes 294920 | tf_op jit(solution)/shard_map/ppermute | solution.py:334
  132.4 11.4 %collective-permute-start.26 = (bf16[128,384]{1,0:T(8,128)(2,1)}, bf16[128,384]{1,0:T(8,128)(2,1)S(1)}, u32[]{:S(2)}, u32[]{:S(2)}) collective-permute-start(bf16[128,384]{1,0:T(8,128)(2,1)} %get-tuple-element.54), channel_id=1, source_target_pairs={{0,6},{1,7},{2,0},{3,1},{4,2},{5,3},{6,4},{7,5},{8,14},{9,15},{10,... | collective-permute-start | bytes 294920 | tf_op jit(solution)/shard_map/ppermute | solution.py:334
  134.9 11.8 %collective-permute-start.27 = (bf16[128,384]{1,0:T(8,128)(2,1)}, bf16[128,384]{1,0:T(8,128)(2,1)S(1)}, u32[]{:S(2)}, u32[]{:S(2)}) collective-permute-start(bf16[128,384]{1,0:T(8,128)(2,1)} %get-tuple-element.55), channel_id=1, source_target_pairs={{0,7},{1,0},{2,1},{3,2},{4,3},{5,4},{6,5},{7,6},{8,15},{9,8},{10,9... | collective-permute-start | bytes 294920 | tf_op jit(solution)/shard_map/ppermute | solution.py:334
  139.3 16.1 %collective-permute-start.31 = (bf16[32,1024]{1,0:T(8,128)(2,1)S(1)}, bf16[32,1024]{1,0:T(8,128)(2,1)S(1)}, u32[]{:S(2)}, u32[]{:S(2)}) collective-permute-start(bf16[32,1024]{1,0:T(8,128)(2,1)S(1)} %add_convert_fusion.1), channel_id=1, source_target_pairs={{0,7},{1,6},{2,5},{3,4},{4,3},{5,2},{6,1},{7,0},{8,15},{9,14},{10,... | collective-permute-start | bytes 196616 | tf_op jit(solution)/shard_map/ppermute | solution.py:330
  (26 other events, 287.2 us)
Sparse Core Ops, SparseCore 0:
  10.5 64.8 all-gather.1

commit v5 on v4

--- a/solution.py
+++ b/solution.py
@@ -46,7 +46,7 @@
 
 
 def prep_kernel(
-    x_ref, gain_ref, w_ref, wout_ref, a_ref, b_ref, all_ref, copies_ref
+    x_ref, gain_ref, w_ref, wout_ref, a_ref, b_ref, early_ref, late_ref, copies_ref
 ):
     me = lax.axis_index("seq")
     x = x_ref[...].astype(F32)
@@ -55,8 +55,9 @@
     n = (c * lax.rsqrt(var + EPS) * gain_ref[...]).astype(BF16)
     a_ref[...] = n[:64]
     b_ref[...] = n[64:]
-    all_ref[:, : 4 * D] = w_ref[...]
-    all_ref[:, 4 * D :] = wout_ref[...]
+    early_ref[:, :D] = w_ref[:, :D]
+    early_ref[:, D:] = wout_ref[...]
+    late_ref[...] = w_ref[:, D:]
     for part in range(3):
         at = pl.multiple_of((part + 1) * D + me * DH, DH)
         own = w_ref[:, pl.ds(at, DH)]
@@ -279,7 +280,7 @@
 
 def final_kernel(*refs):
     blocks = refs[:8]
-    dpg_ref, w_ref, x_ref, cot_ref, gain_ref, out_ref, msg_ref, lhs, acc = refs[8:]
+    dpg_ref, early_ref, w_ref, x_ref, cot_ref, gain_ref, out_ref, msg_ref, lhs, acc = refs[8:]
     me = lax.axis_index("seq")
     b = pl.program_id(0)
 
@@ -293,14 +294,21 @@
         lhs[0] = dpg_ref[...]
         acc[...] = jnp.zeros_like(acc)
 
+        def gate(n, carry):
+            at = pl.ds(pl.multiple_of(n * 512, 512), 512)
+            acc[:, at] += nt(lhs[0], early_ref[at, :])
+            return carry
+
+        lax.fori_loop(0, D // 512, gate, 0)
+
     def columns(n, carry):
         at = pl.ds(pl.multiple_of(n * 512, 512), 512)
-        acc[:, at] += nt(lhs[b], w_ref[at, :])
+        acc[:, at] += nt(lhs[b + 1], w_ref[at, :])
         return carry
 
     lax.fori_loop(0, D // 512, columns, 0)
 
-    @pl.when(b == 3)
+    @pl.when(b == 2)
     def _():
         x = x_ref[...].astype(F32)
         c = x - jnp.mean(x, axis=-1, keepdims=True)
@@ -340,21 +348,23 @@
     gain_in = gain_in.reshape(1, D)
     gain_out = gain_out.reshape(1, D)
 
-    na, nb, w_rows, copies = pl.pallas_call(
+    na, nb, early, late, copies = pl.pallas_call(
         prep_kernel,
         out_shape=[
             jax.ShapeDtypeStruct((64, D), BF16),
             jax.ShapeDtypeStruct((64, D), BF16),
-            jax.ShapeDtypeStruct((32, 5 * D), BF16),
+            jax.ShapeDtypeStruct((32, 2 * D), BF16),
+            jax.ShapeDtypeStruct((32, 3 * D), BF16),
             jax.ShapeDtypeStruct((32, 32, 3 * DH), BF16),
         ],
         in_specs=[VMEM] * 4,
-        out_specs=[VMEM] * 4,
+        out_specs=[VMEM] * 5,
         compiler_params=params(61500),
         cost_estimate=cost(2),
         name="prep",
     )(x, gain_in, w_qkvu, w_out)
-    w_full = lax.all_gather(w_rows, DP, axis=0, tiled=True)
+    w_early = lax.all_gather(early, DP, axis=0, tiled=True)
+    w_late = lax.all_gather(late, DP, axis=0, tiled=True)
     ws = lax.all_to_all(copies, DP, 0, 0, tiled=True)
     ws = ws.reshape(D, 3 * DH)
 
@@ -405,7 +415,7 @@
         + [VMEM] * 5
         + [
             pl.BlockSpec((D, D), lambda i: (0, 0)),
-            pl.BlockSpec((D, D), lambda i: (0, 4)),
+            pl.BlockSpec((D, D), lambda i: (0, 1)),
             VMEM,
         ],
         out_specs=[VMEM] * (4 + H),
@@ -419,7 +429,7 @@
         compiler_params=params(),
         cost_estimate=cost(5),
         name="tail",
-    )(lengths, att_msg, na, nb, x, cot, w_full, w_full, gain_out)
+    )(lengths, att_msg, na, nb, x, cot, w_early, w_early, gain_out)
 
     d_all = {0: d_att[0]}
     for k in ORDER:
@@ -444,7 +454,7 @@
             pltpu.VMEM((H, T, 3 * DH), BF16),
             pltpu.VMEM((H, T, DH), BF16),
         ],
-        compiler_params=params(63400),
+        compiler_params=params(52000),
         cost_estimate=cost(6),
         name="attend_back",
     )
@@ -463,10 +473,16 @@
 
     final = pl.pallas_call(
         final_kernel,
-        grid=(4,),
+        grid=(3,),
         out_shape=jax.ShapeDtypeStruct((T, D), BF16),
         in_specs=[VMEM] * (H + 1)
-        + [pl.BlockSpec((D, D), lambda b: (0, b)), VMEM, VMEM, VMEM],
+        + [
+            pl.BlockSpec((D, D), lambda b: (0, 0)),
+            pl.BlockSpec((D, D), lambda b: (0, b)),
+            VMEM,
+            VMEM,
+            VMEM,
+        ],
         out_specs=VMEM,
         scratch_shapes=[
             pltpu.VMEM((H, T, 3 * DH), BF16),
@@ -477,7 +493,9 @@
         cost_estimate=cost(5),
         name="final",
     )
-    input_grad = final(*[d_rows[k] for k in range(H)], d_pg, w_full, x, cot, gain_in)
+    input_grad = final(
+        *[d_rows[k] for k in range(H)], d_pg, w_early, w_late, x, cot, gain_in
+    )
 
     return (mixed[None], input_grad[None], w_grad)
 

time: 164 us -> 174 us (1.061); the launches traced: 163 us -> 171 us
  blocking collectives: 16.8 us -> 34.8 us
  starting transfers between devices: 73.6 us -> 61.7 us
  waiting for transfers between devices: 18.4 us -> 25.6 us
  local copies, waits for them, and re-layouts: 6.48 us -> 1.84 us
    all_to_all x0 -> x1, blocking collectives: none -> 20.5 us  [layer(): lax.all_to_all(pair.reshape(16, 32, D), ('dp_0', 'dp_1'), 0, 0, tiled=True)]
    all_to_all x1 -> x0, starting transfers between devices: 7.11 us -> none  [layer(): lax.all_to_all(pair.reshape(16, 32, D), ('dp_0', 'dp_1'), 0, 0, tiled=True)]
    ppermute x28, waiting for transfers between devices: 15.2 us -> 22 us  [shifted(): return lax.ppermute(value, 'seq', [(i, (i + by) % H) for i in range(H)])]
    ppermute x28, starting transfers between devices: 55.5 us -> 50.2 us  [shifted(): return lax.ppermute(value, 'seq', [(i, (i + by) % H) for i in range(H)])]
    unnamed x46 -> x22, local copies, waits for them, and re-layouts: 6.48 us -> 1.84 us
    all_to_all x1, blocking collectives: 16.8 us -> 14.3 us  [layer(): att_msg = lax.all_to_all(msg, 'seq', 0, 0, tiled=True)]
  transfers between devices with their start and end apart: 35 -> 35, of which waited for: 15 -> 14; matrix products, arithmetic and copies ran while one was open for 0% -> 1% of each run, Pallas kernels for 13% -> 11%
where the time goes in v5:
time: 174 us; the launch traced here: 171 us
  starting transfers between devices  61.7 us (35%)
  blocking collectives  34.8 us (20%)
  Pallas kernels  29.5 us (17%)
  waiting for transfers between devices  25.6 us (15%)
  between operations  14.8 us (9%)
  other arithmetic  2.52 us (1%)
  local copies, waits for them, and re-layouts  1.84 us (1%)
    ppermute x28, starting transfers between devices, shifted(): return lax.ppermute(value, 'seq', [(i, (i + by) % H) for i in range(H)])  50.2 us
    ppermute x28, waiting for transfers between devices, shifted(): return lax.ppermute(value, 'seq', [(i, (i + by) % H) for i in range(H)])  22 us
    all_to_all x1, blocking collectives, layer(): lax.all_to_all(pair.reshape(16, 32, D), ('dp_0', 'dp_1'), 0, 0, tiled=True)  20.5 us
    all_to_all x1, blocking collectives, layer(): att_msg = lax.all_to_all(msg, 'seq', 0, 0, tiled=True)  14.3 us
    pallas_call x1, Pallas kernels, layer(): pl.pallas_call(forward_kernel, out_shape=[jax.ShapeDtypeStruct((H, MSG, T...  8.66 us
    pallas_call x1, Pallas kernels, layer(): final(*[d_rows[k] for k in range(H)], d_pg, w_early, w_late, x, cot, gain...  8.2 us
    all_to_all x1, starting transfers between devices, layer(): ws = lax.all_to_all(copies, DP, 0, 0, tiled=True)  7.38 us
    pallas_call x1, Pallas kernels, layer(): pl.pallas_call(tail_kernel, grid=(1,), out_shape=[jax.ShapeDtypeStruct((T...  6.12 us
  transfers between devices with their start and end apart: 35, of which 14 were waited for; matrix products, arithmetic and copies ran while one was open for 1% of the time, Pallas kernels for 11%

profile of v5, /device:TPU:22, one launch (start us, length us, event | category | flops | bytes accessed | tf_op | source)
XLA Modules:
  0.0 170.8 jit_solution(1928586767372091954)
XLA Ops:
  7.2 2.3 %prep.1 = (bf16[64,1024]{1,0:T(8,128)(2,1)}, bf16[64,1024]{1,0:T(8,128)(2,1)}, bf16[32,2048]{1,0:T(8,128)(2,1)}, bf16[32,3072]{1,0:T(8,128)(2,1)}, bf16[32,32,384]{2,1,0:T(8,128)(2,1)}) custom-call(bf16[128,1024]{1,0:T(8,128)(2,1)} %bitcast.8, f32[1,1024]{1,0:T(1,128)} %bitcast.15, bf16[32,4096]{1,0:T(8,128)(2,1)} %w_ref.1, bf16[32,1024]{1,0:T(8,128)(2,1)} %wout_ref.1), custom_call_target="tpu_custom_call" | custom-call | flops 600000000 | bytes 1048576 | tf_op jit(solution)/shard_map/prep/pallas_call | solution.py:351
  10.3 7.4 %all-to-all-start = ((bf16[32,32,384]{2,1,0:T(8,128)(2,1)}), bf16[32,32,384]{2,1,0:T(8,128)(2,1)S(1)}, u32[]{:S(2)}, u32[]{:S(2)}) async-start(bf16[32,32,384]{2,1,0:T(8,128)(2,1)} %get-tuple-element.34), calls=%async_computation | async-start | bytes 1572864 | tf_op jit(solution)/shard_map/all_to_all | solution.py:368
  17.7 5.9 %collective-permute-start.10 = (bf16[64,1024]{1,0:T(8,128)(2,1)}, bf16[64,1024]{1,0:T(8,128)(2,1)S(1)}, u32[]{:S(2)}, u32[]{:S(2)}) collective-permute-start(bf16[64,1024]{1,0:T(8,128)(2,1)} %get-tuple-element.33.refs_3_.nb_ref), channel_id=1, source_target_pairs={{0,7},{1,0},{2,1},{3,2},{4,3},{5,4},{6,5},{7,6},{8,15},{9,8},{10,9... | collective-permute-start | bytes 393224 | tf_op jit(solution)/shard_map/ppermute | solution.py:342
  23.7 3.3 %collective-permute-start.7 = (bf16[64,1024]{1,0:T(8,128)(2,1)}, bf16[64,1024]{1,0:T(8,128)(2,1)S(1)}, u32[]{:S(2)}, u32[]{:S(2)}) collective-permute-start(bf16[64,1024]{1,0:T(8,128)(2,1)} %get-tuple-element.32.refs_2_.na_ref), channel_id=1, source_target_pairs={{0,7},{1,0},{2,1},{3,2},{4,3},{5,4},{6,5},{7,6},{8,15},{9,8},{10,9... | collective-permute-start | bytes 393224 | tf_op jit(solution)/shard_map/ppermute | solution.py:342
  27.1 3.6 %collective-permute-start.11 = (bf16[64,1024]{1,0:T(8,128)(2,1)S(1)}, bf16[64,1024]{1,0:T(8,128)(2,1)S(1)}, u32[]{:S(2)}, u32[]{:S(2)}) collective-permute-start(bf16[64,1024]{1,0:T(8,128)(2,1)S(1)} %collective-permute-done.10.refs_14_), channel_id=1, source_target_pairs={{0,7},{1,0},{2,1},{3,2},{4,3},{5,4},{6,5},{7,6},{8,15},{9,8},{10,9... | collective-permute-start | bytes 393224 | tf_op jit(solution)/shard_map/ppermute | solution.py:342
  31.5 1.7 collective-permute-done.4.refs_8_
  33.2 3.2 %collective-permute-start.8 = (bf16[64,1024]{1,0:T(8,128)(2,1)S(1)}, bf16[64,1024]{1,0:T(8,128)(2,1)S(1)}, u32[]{:S(2)}, u32[]{:S(2)}) collective-permute-start(bf16[64,1024]{1,0:T(8,128)(2,1)S(1)} %collective-permute-done.7.refs_11_), channel_id=1, source_target_pairs={{0,7},{1,0},{2,1},{3,2},{4,3},{5,4},{6,5},{7,6},{8,15},{9,8},{10,9... | collective-permute-start | bytes 393224 | tf_op jit(solution)/shard_map/ppermute | solution.py:342
  36.9 1.9 %collective-permute-done.1.refs_5_ = bf16[64,1024]{1,0:T(8,128)(2,1)S(1)} collective-permute-done((bf16[64,1024]{1,0:T(8,128)(2,1)S(1)}, bf16[64,1024]{1,0:T(8,128)(2,1)S(1)}, u32[]{:S(2)}, u32[]{:S(2)}) %collective-permute-start.1) | collective-permute-done | bytes 131104 | tf_op jit(solution)/shard_map/ppermute | solution.py:342
  38.8 2.8 %collective-permute-done.5.refs_9_ = bf16[64,1024]{1,0:T(8,128)(2,1)S(1)} collective-permute-done((bf16[64,1024]{1,0:T(8,128)(2,1)S(1)}, bf16[64,1024]{1,0:T(8,128)(2,1)S(1)}, u32[]{:S(2)}, u32[]{:S(2)}) %collective-permute-start.5) | collective-permute-done | bytes 131104 | tf_op jit(solution)/shard_map/ppermute | solution.py:342
  41.6 3.2 %collective-permute-start.9 = (bf16[64,1024]{1,0:T(8,128)(2,1)S(1)}, bf16[64,1024]{1,0:T(8,128)(2,1)S(1)}, u32[]{:S(2)}, u32[]{:S(2)}) collective-permute-start(bf16[64,1024]{1,0:T(8,128)(2,1)S(1)} %collective-permute-done.8.refs_12_), channel_id=1, source_target_pairs={{0,7},{1,0},{2,1},{3,2},{4,3},{5,4},{6,5},{7,6},{8,15},{9,8},{10,9... | collective-permute-start | bytes 393224 | tf_op jit(solution)/shard_map/ppermute | solution.py:342
  45.2 1.7 collective-permute-start.3
  49.8 1.6 collective-permute-done.3.refs_7_
  53.2 8.7 %attend.1 = (bf16[8,144,128]{2,1,0:T(8,128)(2,1)S(1)}, f32[1024,384]{1,0:T(8,128)}, bf16[1024,1024]{1,0:T(8,128)(2,1)}, bf16[1024,1024]{1,0:T(8,128)(2,1)}) custom-call(s32[1]{0:T(128)S(6)} %copy.12.refs_0_.length_ref, f32[8,16]{1,0:T(8,128)S(1)} %copy-done.8, bf16[64,1024]{1,0:T(8,128)(2,1)S(1)} %copy-done.2, bf16[64,1024]{1,0:T(8,128)(2,1)S(1)} %copy-done.4, ...), custom_call_target="tpu_custom_call" | custom-call | flops 3000000000 | bytes 1048576 | tf_op jit(solution)/shard_map/attend/pallas_call | solution.py:379
  61.9 14.3 %all_to_all.15.msg_ref = bf16[8,144,128]{2,1,0:T(8,128)(2,1)S(1)} all-to-all(bf16[8,144,128]{2,1,0:T(8,128)(2,1)S(1)} %get-tuple-element.35), channel_id=1, replica_groups=mesh['dp_0'=4,'dp_1'=4,'dp_2'=2,'seq'=8] {'seq'}, dimensions={0} | all-to-all | bytes 589824 | tf_op jit(solution)/shard_map/all_to_all | solution.py:402
  76.2 6.1 %tail.1 = (bf16[128,1024]{1,0:T(8,128)(2,1)}, bf16[128,1024]{1,0:T(8,128)(2,1)S(1)}, bf16[512,1024]{1,0:T(8,128)(2,1)S(1)}, bf16[512,1024]{1,0:T(8,128)(2,1)}, b...) custom-call(s32[1]{0:T(128)S(6)} %copy.12.refs_0_.length_ref, ...), custom_call_target="tpu_custom_call" | custom-call | flops 1500000000 | bytes 1048576 | tf_op jit(solution)/shard_map/tail/pallas_call | solution.py:404
  82.3 2.9 %collective-permute-done.28 = bf16[512,1024]{1,0:T(8,128)(2,1)S(1)} collective-permute-done((bf16[512,1024]{1,0:T(8,128)(2,1)}, bf16[512,1024]{1,0:T(8,128)(2,1)S(1)}, u32[]{:S(2)}, u32[]{:S(2)}) %collective-permute-start.28) | collective-permute-done | bytes 1048608 | tf_op jit(solution)/shard_map/ppermute | solution.py:338
  85.6 20.5 %all_to_all.16 = bf16[16,32,1024]{2,1,0:T(8,128)(2,1)} all-to-all(bf16[16,32,1024]{2,1,0:T(8,128)(2,1)S(1)} %bitcast.17), channel_id=1, replica_groups=mesh['dp_0'=4,'dp_1'=4,'dp_2'=2,'seq'=8] {'dp_0','dp_1'}, dimensions={0} | all-to-all | bytes 2097152 | tf_op jit(solution)/shard_map/all_to_all | solution.py:440
  110.0 2.8 %collective-permute-start.16 = (bf16[128,128]{1,0:T(8,128)(2,1)S(1)}, bf16[128,128]{1,0:T(8,128)(2,1)S(1)}, u32[]{:S(2)}, u32[]{:S(2)}) collective-permute-start(bf16[128,128]{1,0:T(8,128)(2,1)S(1)} %get-tuple-element.41), channel_id=1, source_target_pairs={{0,3},{1,4},{2,5},{3,6},{4,7},{5,0},{6,1},{7,2},{8,11},{9,12},{10,... | collective-permute-start | bytes 98312 | tf_op jit(solution)/shard_map/ppermute | solution.py:342
  112.8 2.9 %collective-permute-start.17 = (bf16[128,128]{1,0:T(8,128)(2,1)S(1)}, bf16[128,128]{1,0:T(8,128)(2,1)S(1)}, u32[]{:S(2)}, u32[]{:S(2)}) collective-permute-start(bf16[128,128]{1,0:T(8,128)(2,1)S(1)} %get-tuple-element.42), channel_id=1, source_target_pairs={{0,4},{1,5},{2,6},{3,7},{4,0},{5,1},{6,2},{7,3},{8,12},{9,13},{10,... | collective-permute-start | bytes 98312 | tf_op jit(solution)/shard_map/ppermute | solution.py:342
  115.7 2.3 %collective-permute-start.18 = (bf16[128,128]{1,0:T(8,128)(2,1)S(1)}, bf16[128,128]{1,0:T(8,128)(2,1)S(1)}, u32[]{:S(2)}, u32[]{:S(2)}) collective-permute-start(bf16[128,128]{1,0:T(8,128)(2,1)S(1)} %get-tuple-element.43), channel_id=1, source_target_pairs={{0,5},{1,6},{2,7},{3,0},{4,1},{5,2},{6,3},{7,4},{8,13},{9,14},{10,... | collective-permute-start | bytes 98312 | tf_op jit(solution)/shard_map/ppermute | solution.py:342
  118.0 2.4 %collective-permute-start.19 = (bf16[128,128]{1,0:T(8,128)(2,1)S(1)}, bf16[128,128]{1,0:T(8,128)(2,1)S(1)}, u32[]{:S(2)}, u32[]{:S(2)}) collective-permute-start(bf16[128,128]{1,0:T(8,128)(2,1)S(1)} %get-tuple-element.44), channel_id=1, source_target_pairs={{0,6},{1,7},{2,0},{3,1},{4,2},{5,3},{6,4},{7,5},{8,14},{9,15},{10,... | collective-permute-start | bytes 98312 | tf_op jit(solution)/shard_map/ppermute | solution.py:342
  122.8 1.9 %collective-permute-done.19.refs_6_ = bf16[128,128]{1,0:T(8,128)(2,1)S(1)} collective-permute-done((bf16[128,128]{1,0:T(8,128)(2,1)S(1)}, bf16[128,128]{1,0:T(8,128)(2,1)S(1)}, u32[]{:S(2)}, u32[]{:S(2)}) %collective-permute-start.19) | collective-permute-done | bytes 32800 | tf_op jit(solution)/shard_map/ppermute | solution.py:342
  124.8 4.2 %attend_back.1 = (bf16[128,384]{1,0:T(8,128)(2,1)S(1)}, bf16[128,384]{1,0:T(8,128)(2,1)S(1)}, bf16[128,384]{1,0:T(8,128)(2,1)S(1)}, bf16[128,384]{1,0:T(8,128)(2...) custom-call(bf16[128,128]{1,0:T(8,128)(2,1)S(1)} %get-tuple-element., ...), custom_call_target="tpu_custom_call" | custom-call | flops 1800000000 | bytes 1048576 | tf_op jit(solution)/shard_map/attend_back/pallas_call | solution.py:461
  129.9 2.6 %collective-permute-start.22 = (bf16[128,384]{1,0:T(8,128)(2,1)S(1)}, bf16[128,384]{1,0:T(8,128)(2,1)S(1)}, u32[]{:S(2)}, u32[]{:S(2)}) collective-permute-start(bf16[128,384]{1,0:T(8,128)(2,1)S(1)} %get-tuple-element.51), channel_id=1, source_target_pairs={{0,2},{1,3},{2,4},{3,5},{4,6},{5,7},{6,0},{7,1},{8,10},{9,11},{10,... | collective-permute-start | bytes 294920 | tf_op jit(solution)/shard_map/ppermute | solution.py:342
  132.5 2.3 %collective-permute-start.31 = (bf16[32,1024]{1,0:T(8,128)(2,1)S(1)}, bf16[32,1024]{1,0:T(8,128)(2,1)S(1)}, u32[]{:S(2)}, u32[]{:S(2)}) collective-permute-start(bf16[32,1024]{1,0:T(8,128)(2,1)S(1)} %add_convert_fusion.1), channel_id=1, source_target_pairs={{0,7},{1,6},{2,5},{3,4},{4,3},{5,2},{6,1},{7,0},{8,15},{9,14},{10,... | collective-permute-start | bytes 196616 | tf_op jit(solution)/shard_map/ppermute | solution.py:338
  135.4 3.7 %collective-permute-start.24 = (bf16[128,384]{1,0:T(8,128)(2,1)S(1)}, bf16[128,384]{1,0:T(8,128)(2,1)S(1)}, u32[]{:S(2)}, u32[]{:S(2)}) collective-permute-start(bf16[128,384]{1,0:T(8,128)(2,1)S(1)} %get-tuple-element.53), channel_id=1, source_target_pairs={{0,4},{1,5},{2,6},{3,7},{4,0},{5,1},{6,2},{7,3},{8,12},{9,13},{10,... | collective-permute-start | bytes 294920 | tf_op jit(solution)/shard_map/ppermute | solution.py:342
  139.1 2.6 %collective-permute-start.25 = (bf16[128,384]{1,0:T(8,128)(2,1)S(1)}, bf16[128,384]{1,0:T(8,128)(2,1)S(1)}, u32[]{:S(2)}, u32[]{:S(2)}) collective-permute-start(bf16[128,384]{1,0:T(8,128)(2,1)S(1)} %get-tuple-element.54), channel_id=1, source_target_pairs={{0,5},{1,6},{2,7},{3,0},{4,1},{5,2},{6,3},{7,4},{8,13},{9,14},{10,... | collective-permute-start | bytes 294920 | tf_op jit(solution)/shard_map/ppermute | solution.py:342
  141.7 3.2 %collective-permute-start.26 = (bf16[128,384]{1,0:T(8,128)(2,1)S(1)}, bf16[128,384]{1,0:T(8,128)(2,1)S(1)}, u32[]{:S(2)}, u32[]{:S(2)}) collective-permute-start(bf16[128,384]{1,0:T(8,128)(2,1)S(1)} %get-tuple-element.55), channel_id=1, source_target_pairs={{0,6},{1,7},{2,0},{3,1},{4,2},{5,3},{6,4},{7,5},{8,14},{9,15},{10,... | collective-permute-start | bytes 294920 | tf_op jit(solution)/shard_map/ppermute | solution.py:342
  144.9 1.7 collective-permute-start.27
  147.2 6.1 %collective-permute-done.25.refs_5_ = bf16[128,384]{1,0:T(8,128)(2,1)S(1)} collective-permute-done((bf16[128,384]{1,0:T(8,128)(2,1)S(1)}, bf16[128,384]{1,0:T(8,128)(2,1)S(1)}, u32[]{:S(2)}, u32[]{:S(2)}) %collective-permute-start.25) | collective-permute-done | bytes 98336 | tf_op jit(solution)/shard_map/ppermute | solution.py:342
  153.3 1.9 %collective-permute-done.26.refs_6_ = bf16[128,384]{1,0:T(8,128)(2,1)S(1)} collective-permute-done((bf16[128,384]{1,0:T(8,128)(2,1)S(1)}, bf16[128,384]{1,0:T(8,128)(2,1)S(1)}, u32[]{:S(2)}, u32[]{:S(2)}) %collective-permute-start.26) | collective-permute-done | bytes 98336 | tf_op jit(solution)/shard_map/ppermute | solution.py:342
  155.8 8.2 %final.1 = bf16[128,1024]{1,0:T(8,128)(2,1)} custom-call(bf16[128,384]{1,0:T(8,128)(2,1)S(1)} %get-tuple-element.49.refs_0_, bf16[128,384]{1,0:T(8,128)(2,1)S(1)} %collective-permute-done.21.refs_1_, bf16[128,384]{1,0:T(8,128)(2,1)S(1)} %collective-permute-done.22.refs_2_, bf16[128,384]{1,0:T(8,128)(2,1)S(1)} %collective-permute-done.23.refs_3_, ...), custom_call_target="tpu_custom_call" | custom-call | flops 1500000000 | bytes 1048576 | tf_op jit(solution)/shard_map/final/pallas_call | solution.py:496
  (74 shorter events, 16.3 us)
Async XLA Ops:
  7.2 68.9 %all-gather.3.cloned.1.call-start = ((), (), s32[]{:S(2)}) async-start(), calls=%async_computation.3 | async-start | bytes 4325376 | tf_op jit(solution)/shard_map/all_gather | solution.py:366
  9.6 146.2 %all-gather.5.cloned.1.call-start = ((), (), s32[]{:S(2)}) async-start(), calls=%async_computation.4 | async-start | bytes 6488064 | tf_op jit(solution)/shard_map/all_gather | solution.py:367
  10.3 41.0 %all-to-all-start = ((bf16[32,32,384]{2,1,0:T(8,128)(2,1)}), bf16[32,32,384]{2,1,0:T(8,128)(2,1)S(1)}, u32[]{:S(2)}, u32[]{:S(2)}) async-start(bf16[32,32,384]{2,1,0:T(8,128)(2,1)} %get-tuple-element.34), calls=%async_computation | async-start | bytes 1572864 | tf_op jit(solution)/shard_map/all_to_all | solution.py:368
  17.7 9.4 %collective-permute-start.10 = (bf16[64,1024]{1,0:T(8,128)(2,1)}, bf16[64,1024]{1,0:T(8,128)(2,1)S(1)}, u32[]{:S(2)}, u32[]{:S(2)}) collective-permute-start(bf16[64,1024]{1,0:T(8,128)(2,1)} %get-tuple-element.33.refs_3_.nb_ref), channel_id=1, source_target_pairs={{0,7},{1,0},{2,1},{3,2},{4,3},{5,4},{6,5},{7,6},{8,15},{9,8},{10,9... | collective-permute-start | bytes 393224 | tf_op jit(solution)/shard_map/ppermute | solution.py:342
  23.7 7.8 %collective-permute-start = (bf16[64,1024]{1,0:T(8,128)(2,1)}, bf16[64,1024]{1,0:T(8,128)(2,1)S(1)}, u32[]{:S(2)}, u32[]{:S(2)}) collective-permute-start(bf16[64,1024]{1,0:T(8,128)(2,1)} %get-tuple-element.32.refs_2_.na_ref), channel_id=1, source_target_pairs={{0,1},{1,2},{2,3},{3,4},{4,5},{5,6},{6,7},{7,0},{8,9},{9,10},{10,1... | collective-permute-start | bytes 393224 | tf_op jit(solution)/shard_map/ppermute | solution.py:342
  23.7 9.5 %collective-permute-start.4 = (bf16[64,1024]{1,0:T(8,128)(2,1)}, bf16[64,1024]{1,0:T(8,128)(2,1)S(1)}, u32[]{:S(2)}, u32[]{:S(2)}) collective-permute-start(bf16[64,1024]{1,0:T(8,128)(2,1)} %get-tuple-element.33.refs_3_.nb_ref), channel_id=1, source_target_pairs={{0,1},{1,2},{2,3},{3,4},{4,5},{5,6},{6,7},{7,0},{8,9},{9,10},{10,1... | collective-permute-start | bytes 393224 | tf_op jit(solution)/shard_map/ppermute | solution.py:342
  23.7 9.5 %collective-permute-start.7 = (bf16[64,1024]{1,0:T(8,128)(2,1)}, bf16[64,1024]{1,0:T(8,128)(2,1)S(1)}, u32[]{:S(2)}, u32[]{:S(2)}) collective-permute-start(bf16[64,1024]{1,0:T(8,128)(2,1)} %get-tuple-element.32.refs_2_.na_ref), channel_id=1, source_target_pairs={{0,7},{1,0},{2,1},{3,2},{4,3},{5,4},{6,5},{7,6},{8,15},{9,8},{10,9... | collective-permute-start | bytes 393224 | tf_op jit(solution)/shard_map/ppermute | solution.py:342
  27.1 9.2 %collective-permute-start.11 = (bf16[64,1024]{1,0:T(8,128)(2,1)S(1)}, bf16[64,1024]{1,0:T(8,128)(2,1)S(1)}, u32[]{:S(2)}, u32[]{:S(2)}) collective-permute-start(bf16[64,1024]{1,0:T(8,128)(2,1)S(1)} %collective-permute-done.10.refs_14_), channel_id=1, source_target_pairs={{0,7},{1,0},{2,1},{3,2},{4,3},{5,4},{6,5},{7,6},{8,15},{9,8},{10,9... | collective-permute-start | bytes 393224 | tf_op jit(solution)/shard_map/ppermute | solution.py:342
  31.5 7.3 %collective-permute-start.1 = (bf16[64,1024]{1,0:T(8,128)(2,1)S(1)}, bf16[64,1024]{1,0:T(8,128)(2,1)S(1)}, u32[]{:S(2)}, u32[]{:S(2)}) collective-permute-start(bf16[64,1024]{1,0:T(8,128)(2,1)S(1)} %collective-permute-done.refs_4_), channel_id=1, source_target_pairs={{0,1},{1,2},{2,3},{3,4},{4,5},{5,6},{6,7},{7,0},{8,9},{9,10},{10,1... | collective-permute-start | bytes 393224 | tf_op jit(solution)/shard_map/ppermute | solution.py:342
  33.1 8.4 %collective-permute-start.5 = (bf16[64,1024]{1,0:T(8,128)(2,1)S(1)}, bf16[64,1024]{1,0:T(8,128)(2,1)S(1)}, u32[]{:S(2)}, u32[]{:S(2)}) collective-permute-start(bf16[64,1024]{1,0:T(8,128)(2,1)S(1)} %collective-permute-done.4.refs_8_), channel_id=1, source_target_pairs={{0,1},{1,2},{2,3},{3,4},{4,5},{5,6},{6,7},{7,0},{8,9},{9,10},{10,1... | collective-permute-start | bytes 393224 | tf_op jit(solution)/shard_map/ppermute | solution.py:342
  33.2 8.4 %collective-permute-start.8 = (bf16[64,1024]{1,0:T(8,128)(2,1)S(1)}, bf16[64,1024]{1,0:T(8,128)(2,1)S(1)}, u32[]{:S(2)}, u32[]{:S(2)}) collective-permute-start(bf16[64,1024]{1,0:T(8,128)(2,1)S(1)} %collective-permute-done.7.refs_11_), channel_id=1, source_target_pairs={{0,7},{1,0},{2,1},{3,2},{4,3},{5,4},{6,5},{7,6},{8,15},{9,8},{10,9... | collective-permute-start | bytes 393224 | tf_op jit(solution)/shard_map/ppermute | solution.py:342
  36.4 8.4 %collective-permute-start.12 = (bf16[64,1024]{1,0:T(8,128)(2,1)S(1)}, bf16[64,1024]{1,0:T(8,128)(2,1)S(1)}, u32[]{:S(2)}, u32[]{:S(2)}) collective-permute-start(bf16[64,1024]{1,0:T(8,128)(2,1)S(1)} %collective-permute-done.11.refs_15_), channel_id=1, source_target_pairs={{0,7},{1,0},{2,1},{3,2},{4,3},{5,4},{6,5},{7,6},{8,15},{9,8},{10,9... | collective-permute-start | bytes 393224 | tf_op jit(solution)/shard_map/ppermute | solution.py:342
  38.8 6.4 %collective-permute-start.2 = (bf16[64,1024]{1,0:T(8,128)(2,1)S(1)}, bf16[64,1024]{1,0:T(8,128)(2,1)S(1)}, u32[]{:S(2)}, u32[]{:S(2)}) collective-permute-start(bf16[64,1024]{1,0:T(8,128)(2,1)S(1)} %collective-permute-done.1.refs_5_), channel_id=1, source_target_pairs={{0,1},{1,2},{2,3},{3,4},{4,5},{5,6},{6,7},{7,0},{8,9},{9,10},{10,1... | collective-permute-start | bytes 393224 | tf_op jit(solution)/shard_map/ppermute | solution.py:342
  41.6 7.1 %collective-permute-start.6 = (bf16[64,1024]{1,0:T(8,128)(2,1)S(1)}, bf16[64,1024]{1,0:T(8,128)(2,1)S(1)}, u32[]{:S(2)}, u32[]{:S(2)}) collective-permute-start(bf16[64,1024]{1,0:T(8,128)(2,1)S(1)} %collective-permute-done.5.refs_9_), channel_id=1, source_target_pairs={{0,1},{1,2},{2,3},{3,4},{4,5},{5,6},{6,7},{7,0},{8,9},{9,10},{10,1... | collective-permute-start | bytes 393224 | tf_op jit(solution)/shard_map/ppermute | solution.py:342
  41.6 7.1 %collective-permute-start.9 = (bf16[64,1024]{1,0:T(8,128)(2,1)S(1)}, bf16[64,1024]{1,0:T(8,128)(2,1)S(1)}, u32[]{:S(2)}, u32[]{:S(2)}) collective-permute-start(bf16[64,1024]{1,0:T(8,128)(2,1)S(1)} %collective-permute-done.8.refs_12_), channel_id=1, source_target_pairs={{0,7},{1,0},{2,1},{3,2},{4,3},{5,4},{6,5},{7,6},{8,15},{9,8},{10,9... | collective-permute-start | bytes 393224 | tf_op jit(solution)/shard_map/ppermute | solution.py:342
  45.2 6.2 %collective-permute-start.3 = (bf16[64,1024]{1,0:T(8,128)(2,1)S(1)}, bf16[64,1024]{1,0:T(8,128)(2,1)S(1)}, u32[]{:S(2)}, u32[]{:S(2)}) collective-permute-start(bf16[64,1024]{1,0:T(8,128)(2,1)S(1)} %collective-permute-done.2.refs_6_), channel_id=1, source_target_pairs={{0,1},{1,2},{2,3},{3,4},{4,5},{5,6},{6,7},{7,0},{8,9},{9,10},{10,1... | collective-permute-start | bytes 393224 | tf_op jit(solution)/shard_map/ppermute | solution.py:342
  107.5 12.9 %collective-permute-start.29 = (bf16[32,1024]{1,0:T(8,128)(2,1)S(1)}, bf16[32,1024]{1,0:T(8,128)(2,1)S(1)}, u32[]{:S(2)}, u32[]{:S(2)}) collective-permute-start(bf16[32,1024]{1,0:T(8,128)(2,1)S(1)} %reduce_sum.12), channel_id=1, source_target_pairs={{0,1},{1,0},{2,3},{3,2},{4,5},{5,4},{6,7},{7,6},{8,9},{9,8},{10,11... | collective-permute-start | bytes 196616 | tf_op jit(solution)/shard_map/ppermute | solution.py:338
  108.1 7.6 %collective-permute-start.14 = (bf16[128,128]{1,0:T(8,128)(2,1)S(1)}, bf16[128,128]{1,0:T(8,128)(2,1)S(1)}, u32[]{:S(2)}, u32[]{:S(2)}) collective-permute-start(bf16[128,128]{1,0:T(8,128)(2,1)S(1)} %get-tuple-element.39), channel_id=1, source_target_pairs={{0,1},{1,2},{2,3},{3,4},{4,5},{5,6},{6,7},{7,0},{8,9},{9,10},{10,1... | collective-permute-start | bytes 98312 | tf_op jit(solution)/shard_map/ppermute | solution.py:342
  109.6 8.4 %collective-permute-start.15 = (bf16[128,128]{1,0:T(8,128)(2,1)S(1)}, bf16[128,128]{1,0:T(8,128)(2,1)S(1)}, u32[]{:S(2)}, u32[]{:S(2)}) collective-permute-start(bf16[128,128]{1,0:T(8,128)(2,1)S(1)} %get-tuple-element.40), channel_id=1, source_target_pairs={{0,2},{1,3},{2,4},{3,5},{4,6},{5,7},{6,0},{7,1},{8,10},{9,11},{10,... | collective-permute-start | bytes 98312 | tf_op jit(solution)/shard_map/ppermute | solution.py:342
  110.0 11.6 %collective-permute-start.16 = (bf16[128,128]{1,0:T(8,128)(2,1)S(1)}, bf16[128,128]{1,0:T(8,128)(2,1)S(1)}, u32[]{:S(2)}, u32[]{:S(2)}) collective-permute-start(bf16[128,128]{1,0:T(8,128)(2,1)S(1)} %get-tuple-element.41), channel_id=1, source_target_pairs={{0,3},{1,4},{2,5},{3,6},{4,7},{5,0},{6,1},{7,2},{8,11},{9,12},{10,... | collective-permute-start | bytes 98312 | tf_op jit(solution)/shard_map/ppermute | solution.py:342
  112.8 10.0 %collective-permute-start.17 = (bf16[128,128]{1,0:T(8,128)(2,1)S(1)}, bf16[128,128]{1,0:T(8,128)(2,1)S(1)}, u32[]{:S(2)}, u32[]{:S(2)}) collective-permute-start(bf16[128,128]{1,0:T(8,128)(2,1)S(1)} %get-tuple-element.42), channel_id=1, source_target_pairs={{0,4},{1,5},{2,6},{3,7},{4,0},{5,1},{6,2},{7,3},{8,12},{9,13},{10,... | collective-permute-start | bytes 98312 | tf_op jit(solution)/shard_map/ppermute | solution.py:342
  115.7 7.1 %collective-permute-start.18 = (bf16[128,128]{1,0:T(8,128)(2,1)S(1)}, bf16[128,128]{1,0:T(8,128)(2,1)S(1)}, u32[]{:S(2)}, u32[]{:S(2)}) collective-permute-start(bf16[128,128]{1,0:T(8,128)(2,1)S(1)} %get-tuple-element.43), channel_id=1, source_target_pairs={{0,5},{1,6},{2,7},{3,0},{4,1},{5,2},{6,3},{7,4},{8,13},{9,14},{10,... | collective-permute-start | bytes 98312 | tf_op jit(solution)/shard_map/ppermute | solution.py:342
  118.0 6.8 %collective-permute-start.19 = (bf16[128,128]{1,0:T(8,128)(2,1)S(1)}, bf16[128,128]{1,0:T(8,128)(2,1)S(1)}, u32[]{:S(2)}, u32[]{:S(2)}) collective-permute-start(bf16[128,128]{1,0:T(8,128)(2,1)S(1)} %get-tuple-element.44), channel_id=1, source_target_pairs={{0,6},{1,7},{2,0},{3,1},{4,2},{5,3},{6,4},{7,5},{8,14},{9,15},{10,... | collective-permute-start | bytes 98312 | tf_op jit(solution)/shard_map/ppermute | solution.py:342
  121.6 10.9 %collective-permute-start.30 = (bf16[32,1024]{1,0:T(8,128)(2,1)S(1)}, bf16[32,1024]{1,0:T(8,128)(2,1)S(1)}, u32[]{:S(2)}, u32[]{:S(2)}) collective-permute-start(bf16[32,1024]{1,0:T(8,128)(2,1)S(1)} %add_convert_fusion.2), channel_id=1, source_target_pairs={{0,3},{1,2},{2,1},{3,0},{4,7},{5,6},{6,5},{7,4},{8,11},{9,10},{10,... | collective-permute-start | bytes 196616 | tf_op jit(solution)/shard_map/ppermute | solution.py:338
  129.0 10.1 %collective-permute-start.21 = (bf16[128,384]{1,0:T(8,128)(2,1)S(1)}, bf16[128,384]{1,0:T(8,128)(2,1)S(1)}, u32[]{:S(2)}, u32[]{:S(2)}) collective-permute-start(bf16[128,384]{1,0:T(8,128)(2,1)S(1)} %get-tuple-element.50), channel_id=1, source_target_pairs={{0,1},{1,2},{2,3},{3,4},{4,5},{5,6},{6,7},{7,0},{8,9},{9,10},{10,1... | collective-permute-start | bytes 294920 | tf_op jit(solution)/shard_map/ppermute | solution.py:342
  129.9 11.8 %collective-permute-start.22 = (bf16[128,384]{1,0:T(8,128)(2,1)S(1)}, bf16[128,384]{1,0:T(8,128)(2,1)S(1)}, u32[]{:S(2)}, u32[]{:S(2)}) collective-permute-start(bf16[128,384]{1,0:T(8,128)(2,1)S(1)} %get-tuple-element.51), channel_id=1, source_target_pairs={{0,2},{1,3},{2,4},{3,5},{4,6},{5,7},{6,0},{7,1},{8,10},{9,11},{10,... | collective-permute-start | bytes 294920 | tf_op jit(solution)/shard_map/ppermute | solution.py:342
  132.5 12.3 %collective-permute-start.31 = (bf16[32,1024]{1,0:T(8,128)(2,1)S(1)}, bf16[32,1024]{1,0:T(8,128)(2,1)S(1)}, u32[]{:S(2)}, u32[]{:S(2)}) collective-permute-start(bf16[32,1024]{1,0:T(8,128)(2,1)S(1)} %add_convert_fusion.1), channel_id=1, source_target_pairs={{0,7},{1,6},{2,5},{3,4},{4,3},{5,2},{6,1},{7,0},{8,15},{9,14},{10,... | collective-permute-start | bytes 196616 | tf_op jit(solution)/shard_map/ppermute | solution.py:338
  134.8 12.4 %collective-permute-start.23 = (bf16[128,384]{1,0:T(8,128)(2,1)S(1)}, bf16[128,384]{1,0:T(8,128)(2,1)S(1)}, u32[]{:S(2)}, u32[]{:S(2)}) collective-permute-start(bf16[128,384]{1,0:T(8,128)(2,1)S(1)} %get-tuple-element.52), channel_id=1, source_target_pairs={{0,3},{1,4},{2,5},{3,6},{4,7},{5,0},{6,1},{7,2},{8,11},{9,12},{10,... | collective-permute-start | bytes 294920 | tf_op jit(solution)/shard_map/ppermute | solution.py:342
  135.4 11.8 %collective-permute-start.24 = (bf16[128,384]{1,0:T(8,128)(2,1)S(1)}, bf16[128,384]{1,0:T(8,128)(2,1)S(1)}, u32[]{:S(2)}, u32[]{:S(2)}) collective-permute-start(bf16[128,384]{1,0:T(8,128)(2,1)S(1)} %get-tuple-element.53), channel_id=1, source_target_pairs={{0,4},{1,5},{2,6},{3,7},{4,0},{5,1},{6,2},{7,3},{8,12},{9,13},{10,... | collective-permute-start | bytes 294920 | tf_op jit(solution)/shard_map/ppermute | solution.py:342
  139.1 14.2 %collective-permute-start.25 = (bf16[128,384]{1,0:T(8,128)(2,1)S(1)}, bf16[128,384]{1,0:T(8,128)(2,1)S(1)}, u32[]{:S(2)}, u32[]{:S(2)}) collective-permute-start(bf16[128,384]{1,0:T(8,128)(2,1)S(1)} %get-tuple-element.54), channel_id=1, source_target_pairs={{0,5},{1,6},{2,7},{3,0},{4,1},{5,2},{6,3},{7,4},{8,13},{9,14},{10,... | collective-permute-start | bytes 294920 | tf_op jit(solution)/shard_map/ppermute | solution.py:342
  141.7 13.5 %collective-permute-start.26 = (bf16[128,384]{1,0:T(8,128)(2,1)S(1)}, bf16[128,384]{1,0:T(8,128)(2,1)S(1)}, u32[]{:S(2)}, u32[]{:S(2)}) collective-permute-start(bf16[128,384]{1,0:T(8,128)(2,1)S(1)} %get-tuple-element.55), channel_id=1, source_target_pairs={{0,6},{1,7},{2,0},{3,1},{4,2},{5,3},{6,4},{7,5},{8,14},{9,15},{10,... | collective-permute-start | bytes 294920 | tf_op jit(solution)/shard_map/ppermute | solution.py:342
  144.9 10.9 %collective-permute-start.27 = (bf16[128,384]{1,0:T(8,128)(2,1)S(1)}, bf16[128,384]{1,0:T(8,128)(2,1)S(1)}, u32[]{:S(2)}, u32[]{:S(2)}) collective-permute-start(bf16[128,384]{1,0:T(8,128)(2,1)S(1)} %get-tuple-element.56), channel_id=1, source_target_pairs={{0,7},{1,0},{2,1},{3,2},{4,3},{5,4},{6,5},{7,6},{8,15},{9,8},{10,9... | collective-permute-start | bytes 294920 | tf_op jit(solution)/shard_map/ppermute | solution.py:342
  (14 other events, 287.4 us)
Sparse Core Ops, SparseCore 0:
  10.5 53.7 all-gather.2
  67.4 60.4 all-gather.4

commit v6 on v5

--- a/solution.py
+++ b/solution.py
@@ -20,6 +20,7 @@
 MSG = 144
 LIMIT = 52000
 UNROLL = 8
+FINAL = 52000
 F32 = jnp.float32
 BF16 = jnp.bfloat16
 
@@ -278,32 +279,33 @@
         outs[k][...] = out_ref[lax.rem(me + k, H)]
 
 
+def gate_kernel(dpg_ref, wg_ref, out_ref):
+    def columns(n, carry):
+        at = pl.ds(pl.multiple_of(n * 512, 512), 512)
+        out_ref[:, at] = nt(dpg_ref[...], wg_ref[at, :])
+        return carry
+
+    lax.fori_loop(0, D // 512, columns, 0)
+
+
 def final_kernel(*refs):
     blocks = refs[:8]
-    dpg_ref, early_ref, w_ref, x_ref, cot_ref, gain_ref, out_ref, msg_ref, lhs, acc = refs[8:]
-    me = lax.axis_index("seq")
+    back_ref, w_ref, x_ref, cot_ref, gain_ref, out_ref, lhs, acc = refs[8:]
     b = pl.program_id(0)
 
     @pl.when(b == 0)
     def _():
+        me = lax.axis_index("seq")
         for k in range(H):
-            msg_ref[lax.rem(me - k + H, H)] = blocks[k][...]
-        for n in range(3):
-            for h in range(H):
-                lhs[n + 1, :, h * DH : (h + 1) * DH] = msg_ref[h, :, n * DH : (n + 1) * DH]
-        lhs[0] = dpg_ref[...]
-        acc[...] = jnp.zeros_like(acc)
-
-        def gate(n, carry):
-            at = pl.ds(pl.multiple_of(n * 512, 512), 512)
-            acc[:, at] += nt(lhs[0], early_ref[at, :])
-            return carry
-
-        lax.fori_loop(0, D // 512, gate, 0)
+            h = lax.rem(me - k + H, H)
+            at = pl.ds(pl.multiple_of(h * DH, DH), DH)
+            for n in range(3):
+                lhs[n, :, at] = blocks[k][:, n * DH : (n + 1) * DH]
+        acc[...] = back_ref[...]
 
     def columns(n, carry):
         at = pl.ds(pl.multiple_of(n * 512, 512), 512)
-        acc[:, at] += nt(lhs[b + 1], w_ref[at, :])
+        acc[:, at] += nt(lhs[b], w_ref[at, :])
         return carry
 
     lax.fori_loop(0, D // 512, columns, 0)
@@ -471,30 +473,32 @@
     for k in ORDER:
         d_rows[k] = shifted(d_proj[k], k)
 
+    gate_call = pl.pallas_call(
+        gate_kernel,
+        grid=(1,),
+        out_shape=jax.ShapeDtypeStruct((T, D), F32),
+        in_specs=[VMEM, pl.BlockSpec((D, D), lambda i: (0, 0))],
+        out_specs=VMEM,
+        compiler_params=params(),
+        cost_estimate=cost(2),
+        name="gate",
+    )
+    gate_back = gate_call(d_pg, w_early)
+
     final = pl.pallas_call(
         final_kernel,
         grid=(3,),
         out_shape=jax.ShapeDtypeStruct((T, D), BF16),
         in_specs=[VMEM] * (H + 1)
-        + [
-            pl.BlockSpec((D, D), lambda b: (0, 0)),
-            pl.BlockSpec((D, D), lambda b: (0, b)),
-            VMEM,
-            VMEM,
-            VMEM,
-        ],
+        + [pl.BlockSpec((D, D), lambda b: (0, b)), VMEM, VMEM, VMEM],
         out_specs=VMEM,
-        scratch_shapes=[
-            pltpu.VMEM((H, T, 3 * DH), BF16),
-            pltpu.VMEM((4, T, D), BF16),
-            pltpu.VMEM((T, D), F32),
-        ],
-        compiler_params=params(dimension_semantics=("arbitrary",)),
+        scratch_shapes=[pltpu.VMEM((3, T, D), BF16), pltpu.VMEM((T, D), F32)],
+        compiler_params=params(FINAL, dimension_semantics=("arbitrary",)),
         cost_estimate=cost(5),
         name="final",
     )
     input_grad = final(
-        *[d_rows[k] for k in range(H)], d_pg, w_early, w_late, x, cot, gain_in
+        *[d_rows[k] for k in range(H)], gate_back, w_late, x, cot, gain_in
     )
 
     return (mixed[None], input_grad[None], w_grad)

time: 174 us -> 174 us (level)
  waiting for transfers between devices: 25.6 us -> 18.2 us
  starting transfers between devices: 61.7 us -> 65.4 us
  blocking collectives: 34.8 us -> 37.7 us
    ppermute x28, waiting for transfers between devices: 22 us -> 14.6 us  [shifted(): return lax.ppermute(value, 'seq', [(i, (i + by) % H) for i in range(H)])]
    ppermute x28, starting transfers between devices: 50.2 us -> 54 us  [shifted(): return lax.ppermute(value, 'seq', [(i, (i + by) % H) for i in range(H)])]
    all_to_all x1, blocking collectives: 14.3 us -> 17.3 us  [layer(): att_msg = lax.all_to_all(msg, 'seq', 0, 0, tiled=True)]
    pallas_call x1 -> x2, Pallas kernels: 8.2 us -> 9.1 us  [the longest x1 6.52 us: layer(): final(*[d_rows[k] for k in range(H)], gate_back, w_late, x, cot, gain_in)]
  transfers between devices with their start and end apart: 35 -> 35, of which waited for: 14 -> 10; matrix products, arithmetic and copies ran while one was open for 1% -> 1% of each run, Pallas kernels for 11% -> 13%
where the time goes in v6:
time: 174 us; the launch traced here: 171 us
  starting transfers between devices  65.4 us (38%)
  blocking collectives  37.7 us (22%)
  Pallas kernels  30.4 us (17%)
  waiting for transfers between devices  18.2 us (10%)
  between operations  14.9 us (9%)
  other arithmetic  2.52 us (1%)
  local copies, waits for them, and re-layouts  1.84 us (1%)
    ppermute x28, starting transfers between devices, shifted(): return lax.ppermute(value, 'seq', [(i, (i + by) % H) for i in range(H)])  54 us
    all_to_all x1, blocking collectives, layer(): lax.all_to_all(pair.reshape(16, 32, D), ('dp_0', 'dp_1'), 0, 0, tiled=True)  20.3 us
    all_to_all x1, blocking collectives, layer(): att_msg = lax.all_to_all(msg, 'seq', 0, 0, tiled=True)  17.3 us
    ppermute x28, waiting for transfers between devices, shifted(): return lax.ppermute(value, 'seq', [(i, (i + by) % H) for i in range(H)])  14.6 us
    pallas_call x1, Pallas kernels, layer(): pl.pallas_call(forward_kernel, out_shape=[jax.ShapeDtypeStruct((H, MSG, T...  8.66 us
    all_to_all x1, starting transfers between devices, layer(): ws = lax.all_to_all(copies, DP, 0, 0, tiled=True)  7.38 us
    pallas_call x1, Pallas kernels, layer(): final(*[d_rows[k] for k in range(H)], gate_back, w_late, x, cot, gain_in)  6.52 us
    pallas_call x1, Pallas kernels, layer(): pl.pallas_call(tail_kernel, grid=(1,), out_shape=[jax.ShapeDtypeStruct((T...  6.11 us
  transfers between devices with their start and end apart: 35, of which 10 were waited for; matrix products, arithmetic and copies ran while one was open for 1% of the time, Pallas kernels for 13%

profile of v6, /device:TPU:22, one launch (start us, length us, event | category | flops | bytes accessed | tf_op | source)
XLA Modules:
  0.0 170.9 jit_solution(5033250302677102439)
XLA Ops:
  7.2 2.3 %prep.1 = (bf16[64,1024]{1,0:T(8,128)(2,1)}, bf16[64,1024]{1,0:T(8,128)(2,1)}, bf16[32,2048]{1,0:T(8,128)(2,1)}, bf16[32,3072]{1,0:T(8,128)(2,1)}, bf16[32,32,384]{2,1,0:T(8,128)(2,1)}) custom-call(bf16[128,1024]{1,0:T(8,128)(2,1)} %bitcast.8, f32[1,1024]{1,0:T(1,128)} %bitcast.15, bf16[32,4096]{1,0:T(8,128)(2,1)} %w_ref.1, bf16[32,1024]{1,0:T(8,128)(2,1)} %wout_ref.1), custom_call_target="tpu_custom_call" | custom-call | flops 600000000 | bytes 1048576 | tf_op jit(solution)/shard_map/prep/pallas_call | solution.py:353
  10.3 7.4 %all-to-all-start = ((bf16[32,32,384]{2,1,0:T(8,128)(2,1)}), bf16[32,32,384]{2,1,0:T(8,128)(2,1)S(1)}, u32[]{:S(2)}, u32[]{:S(2)}) async-start(bf16[32,32,384]{2,1,0:T(8,128)(2,1)} %get-tuple-element.34), calls=%async_computation | async-start | bytes 1572864 | tf_op jit(solution)/shard_map/all_to_all | solution.py:370
  17.7 2.0 %collective-permute-start = (bf16[64,1024]{1,0:T(8,128)(2,1)}, bf16[64,1024]{1,0:T(8,128)(2,1)S(1)}, u32[]{:S(2)}, u32[]{:S(2)}) collective-permute-start(bf16[64,1024]{1,0:T(8,128)(2,1)} %get-tuple-element.32.refs_2_.na_ref), channel_id=1, source_target_pairs={{0,1},{1,2},{2,3},{3,4},{4,5},{5,6},{6,7},{7,0},{8,9},{9,10},{10,1... | collective-permute-start | bytes 393224 | tf_op jit(solution)/shard_map/ppermute | solution.py:344
  19.7 4.0 %collective-permute-start.10 = (bf16[64,1024]{1,0:T(8,128)(2,1)}, bf16[64,1024]{1,0:T(8,128)(2,1)S(1)}, u32[]{:S(2)}, u32[]{:S(2)}) collective-permute-start(bf16[64,1024]{1,0:T(8,128)(2,1)} %get-tuple-element.33.refs_3_.nb_ref), channel_id=1, source_target_pairs={{0,7},{1,0},{2,1},{3,2},{4,3},{5,4},{6,5},{7,6},{8,15},{9,8},{10,9... | collective-permute-start | bytes 393224 | tf_op jit(solution)/shard_map/ppermute | solution.py:344
  23.8 3.2 %collective-permute-start.7 = (bf16[64,1024]{1,0:T(8,128)(2,1)}, bf16[64,1024]{1,0:T(8,128)(2,1)S(1)}, u32[]{:S(2)}, u32[]{:S(2)}) collective-permute-start(bf16[64,1024]{1,0:T(8,128)(2,1)} %get-tuple-element.32.refs_2_.na_ref), channel_id=1, source_target_pairs={{0,7},{1,0},{2,1},{3,2},{4,3},{5,4},{6,5},{7,6},{8,15},{9,8},{10,9... | collective-permute-start | bytes 393224 | tf_op jit(solution)/shard_map/ppermute | solution.py:344
  27.7 3.2 %collective-permute-start.11 = (bf16[64,1024]{1,0:T(8,128)(2,1)S(1)}, bf16[64,1024]{1,0:T(8,128)(2,1)S(1)}, u32[]{:S(2)}, u32[]{:S(2)}) collective-permute-start(bf16[64,1024]{1,0:T(8,128)(2,1)S(1)} %collective-permute-done.10.refs_14_), channel_id=1, source_target_pairs={{0,7},{1,0},{2,1},{3,2},{4,3},{5,4},{6,5},{7,6},{8,15},{9,8},{10,9... | collective-permute-start | bytes 393224 | tf_op jit(solution)/shard_map/ppermute | solution.py:344
  31.0 3.2 %collective-permute-start.8 = (bf16[64,1024]{1,0:T(8,128)(2,1)S(1)}, bf16[64,1024]{1,0:T(8,128)(2,1)S(1)}, u32[]{:S(2)}, u32[]{:S(2)}) collective-permute-start(bf16[64,1024]{1,0:T(8,128)(2,1)S(1)} %collective-permute-done.7.refs_11_), channel_id=1, source_target_pairs={{0,7},{1,0},{2,1},{3,2},{4,3},{5,4},{6,5},{7,6},{8,15},{9,8},{10,9... | collective-permute-start | bytes 393224 | tf_op jit(solution)/shard_map/ppermute | solution.py:344
  34.2 3.4 %collective-permute-start.12 = (bf16[64,1024]{1,0:T(8,128)(2,1)S(1)}, bf16[64,1024]{1,0:T(8,128)(2,1)S(1)}, u32[]{:S(2)}, u32[]{:S(2)}) collective-permute-start(bf16[64,1024]{1,0:T(8,128)(2,1)S(1)} %collective-permute-done.11.refs_15_), channel_id=1, source_target_pairs={{0,7},{1,0},{2,1},{3,2},{4,3},{5,4},{6,5},{7,6},{8,15},{9,8},{10,9... | collective-permute-start | bytes 393224 | tf_op jit(solution)/shard_map/ppermute | solution.py:344
  37.9 3.5 %collective-permute-start.9 = (bf16[64,1024]{1,0:T(8,128)(2,1)S(1)}, bf16[64,1024]{1,0:T(8,128)(2,1)S(1)}, u32[]{:S(2)}, u32[]{:S(2)}) collective-permute-start(bf16[64,1024]{1,0:T(8,128)(2,1)S(1)} %collective-permute-done.8.refs_12_), channel_id=1, source_target_pairs={{0,7},{1,0},{2,1},{3,2},{4,3},{5,4},{6,5},{7,6},{8,15},{9,8},{10,9... | collective-permute-start | bytes 393224 | tf_op jit(solution)/shard_map/ppermute | solution.py:344
  41.7 3.3 %collective-permute-start.13 = (bf16[64,1024]{1,0:T(8,128)(2,1)S(1)}, bf16[64,1024]{1,0:T(8,128)(2,1)S(1)}, u32[]{:S(2)}, u32[]{:S(2)}) collective-permute-start(bf16[64,1024]{1,0:T(8,128)(2,1)S(1)} %collective-permute-done.12.refs_16_), channel_id=1, source_target_pairs={{0,7},{1,0},{2,1},{3,2},{4,3},{5,4},{6,5},{7,6},{8,15},{9,8},{10,9... | collective-permute-start | bytes 393224 | tf_op jit(solution)/shard_map/ppermute | solution.py:344
  45.6 2.2 %collective-permute-done.3.refs_7_ = bf16[64,1024]{1,0:T(8,128)(2,1)S(1)} collective-permute-done((bf16[64,1024]{1,0:T(8,128)(2,1)S(1)}, bf16[64,1024]{1,0:T(8,128)(2,1)S(1)}, u32[]{:S(2)}, u32[]{:S(2)}) %collective-permute-start.3) | collective-permute-done | bytes 131104 | tf_op jit(solution)/shard_map/ppermute | solution.py:344
  49.7 8.7 %attend.1 = (bf16[8,144,128]{2,1,0:T(8,128)(2,1)S(1)}, f32[1024,384]{1,0:T(8,128)}, bf16[1024,1024]{1,0:T(8,128)(2,1)}, bf16[1024,1024]{1,0:T(8,128)(2,1)}) custom-call(s32[1]{0:T(128)S(6)} %copy.12.refs_0_.length_ref, f32[8,16]{1,0:T(8,128)S(1)} %copy-done.8, bf16[64,1024]{1,0:T(8,128)(2,1)S(1)} %copy-done.2, bf16[64,1024]{1,0:T(8,128)(2,1)S(1)} %copy-done.4, ...), custom_call_target="tpu_custom_call" | custom-call | flops 3000000000 | bytes 1048576 | tf_op jit(solution)/shard_map/attend/pallas_call | solution.py:381
  58.4 17.3 %all_to_all.15.msg_ref = bf16[8,144,128]{2,1,0:T(8,128)(2,1)S(1)} all-to-all(bf16[8,144,128]{2,1,0:T(8,128)(2,1)S(1)} %get-tuple-element.35), channel_id=1, replica_groups=mesh['dp_0'=4,'dp_1'=4,'dp_2'=2,'seq'=8] {'seq'}, dimensions={0} | all-to-all | bytes 589824 | tf_op jit(solution)/shard_map/all_to_all | solution.py:404
  75.7 6.1 %tail.1 = (bf16[128,1024]{1,0:T(8,128)(2,1)}, bf16[128,1024]{1,0:T(8,128)(2,1)S(1)}, bf16[512,1024]{1,0:T(8,128)(2,1)S(1)}, bf16[512,1024]{1,0:T(8,128)(2,1)}, b...) custom-call(s32[1]{0:T(128)S(6)} %copy.12.refs_0_.length_ref, ...), custom_call_target="tpu_custom_call" | custom-call | flops 1500000000 | bytes 1048576 | tf_op jit(solution)/shard_map/tail/pallas_call | solution.py:406
  81.9 2.9 %collective-permute-done.28 = bf16[512,1024]{1,0:T(8,128)(2,1)S(1)} collective-permute-done((bf16[512,1024]{1,0:T(8,128)(2,1)}, bf16[512,1024]{1,0:T(8,128)(2,1)S(1)}, u32[]{:S(2)}, u32[]{:S(2)}) %collective-permute-start.28) | collective-permute-done | bytes 1048608 | tf_op jit(solution)/shard_map/ppermute | solution.py:340
  85.1 20.3 %all_to_all.16 = bf16[16,32,1024]{2,1,0:T(8,128)(2,1)} all-to-all(bf16[16,32,1024]{2,1,0:T(8,128)(2,1)S(1)} %bitcast.17), channel_id=1, replica_groups=mesh['dp_0'=4,'dp_1'=4,'dp_2'=2,'seq'=8] {'dp_0','dp_1'}, dimensions={0} | all-to-all | bytes 2097152 | tf_op jit(solution)/shard_map/all_to_all | solution.py:442
  105.5 1.4 reduce_sum.12
  107.5 1.5 collective-permute-start.14
  109.7 2.6 %collective-permute-start.16 = (bf16[128,128]{1,0:T(8,128)(2,1)S(1)}, bf16[128,128]{1,0:T(8,128)(2,1)S(1)}, u32[]{:S(2)}, u32[]{:S(2)}) collective-permute-start(bf16[128,128]{1,0:T(8,128)(2,1)S(1)} %get-tuple-element.41), channel_id=1, source_target_pairs={{0,3},{1,4},{2,5},{3,6},{4,7},{5,0},{6,1},{7,2},{8,11},{9,12},{10,... | collective-permute-start | bytes 98312 | tf_op jit(solution)/shard_map/ppermute | solution.py:344
  112.2 2.9 %collective-permute-start.17 = (bf16[128,128]{1,0:T(8,128)(2,1)S(1)}, bf16[128,128]{1,0:T(8,128)(2,1)S(1)}, u32[]{:S(2)}, u32[]{:S(2)}) collective-permute-start(bf16[128,128]{1,0:T(8,128)(2,1)S(1)} %get-tuple-element.42), channel_id=1, source_target_pairs={{0,4},{1,5},{2,6},{3,7},{4,0},{5,1},{6,2},{7,3},{8,12},{9,13},{10,... | collective-permute-start | bytes 98312 | tf_op jit(solution)/shard_map/ppermute | solution.py:344
  115.1 2.4 %collective-permute-start.18 = (bf16[128,128]{1,0:T(8,128)(2,1)S(1)}, bf16[128,128]{1,0:T(8,128)(2,1)S(1)}, u32[]{:S(2)}, u32[]{:S(2)}) collective-permute-start(bf16[128,128]{1,0:T(8,128)(2,1)S(1)} %get-tuple-element.43), channel_id=1, source_target_pairs={{0,5},{1,6},{2,7},{3,0},{4,1},{5,2},{6,3},{7,4},{8,13},{9,14},{10,... | collective-permute-start | bytes 98312 | tf_op jit(solution)/shard_map/ppermute | solution.py:344
  117.5 2.6 %collective-permute-start.19 = (bf16[128,128]{1,0:T(8,128)(2,1)S(1)}, bf16[128,128]{1,0:T(8,128)(2,1)S(1)}, u32[]{:S(2)}, u32[]{:S(2)}) collective-permute-start(bf16[128,128]{1,0:T(8,128)(2,1)S(1)} %get-tuple-element.44), channel_id=1, source_target_pairs={{0,6},{1,7},{2,0},{3,1},{4,2},{5,3},{6,4},{7,5},{8,14},{9,15},{10,... | collective-permute-start | bytes 98312 | tf_op jit(solution)/shard_map/ppermute | solution.py:344
  124.4 4.2 %attend_back.1 = (bf16[128,384]{1,0:T(8,128)(2,1)S(1)}, bf16[128,384]{1,0:T(8,128)(2,1)S(1)}, bf16[128,384]{1,0:T(8,128)(2,1)S(1)}, bf16[128,384]{1,0:T(8,128)(2...) custom-call(bf16[128,128]{1,0:T(8,128)(2,1)S(1)} %get-tuple-element., ...), custom_call_target="tpu_custom_call" | custom-call | flops 1800000000 | bytes 1048576 | tf_op jit(solution)/shard_map/attend_back/pallas_call | solution.py:463
  129.5 2.4 %collective-permute-start.22 = (bf16[128,384]{1,0:T(8,128)(2,1)S(1)}, bf16[128,384]{1,0:T(8,128)(2,1)S(1)}, u32[]{:S(2)}, u32[]{:S(2)}) collective-permute-start(bf16[128,384]{1,0:T(8,128)(2,1)S(1)} %get-tuple-element.51), channel_id=1, source_target_pairs={{0,2},{1,3},{2,4},{3,5},{4,6},{5,7},{6,0},{7,1},{8,10},{9,11},{10,... | collective-permute-start | bytes 294920 | tf_op jit(solution)/shard_map/ppermute | solution.py:344
  131.9 2.2 %collective-permute-start.31 = (bf16[32,1024]{1,0:T(8,128)(2,1)S(1)}, bf16[32,1024]{1,0:T(8,128)(2,1)S(1)}, u32[]{:S(2)}, u32[]{:S(2)}) collective-permute-start(bf16[32,1024]{1,0:T(8,128)(2,1)S(1)} %add_convert_fusion.1), channel_id=1, source_target_pairs={{0,7},{1,6},{2,5},{3,4},{4,3},{5,2},{6,1},{7,0},{8,15},{9,14},{10,... | collective-permute-start | bytes 196616 | tf_op jit(solution)/shard_map/ppermute | solution.py:340
  134.2 2.6 %gate.1.refs_8_ = f32[128,1024]{1,0:T(8,128)S(1)} custom-call(bf16[128,1024]{1,0:T(8,128)(2,1)S(1)} %get-tuple-element.57.dpg_ref, bf16[1024,2048]{1,0:T(8,128)(2,1)} %all-gather.3.cloned.1.call-done.wg_ref.wo_ref), custom_call_target="tpu_custom_call" | custom-call | flops 600000000 | bytes 1048576 | tf_op jit(solution)/shard_map/gate/pallas_call | solution.py:486
  137.6 3.6 %collective-permute-start.24 = (bf16[128,384]{1,0:T(8,128)(2,1)S(1)}, bf16[128,384]{1,0:T(8,128)(2,1)S(1)}, u32[]{:S(2)}, u32[]{:S(2)}) collective-permute-start(bf16[128,384]{1,0:T(8,128)(2,1)S(1)} %get-tuple-element.53), channel_id=1, source_target_pairs={{0,4},{1,5},{2,6},{3,7},{4,0},{5,1},{6,2},{7,3},{8,12},{9,13},{10,... | collective-permute-start | bytes 294920 | tf_op jit(solution)/shard_map/ppermute | solution.py:344
  141.2 2.8 %collective-permute-start.25 = (bf16[128,384]{1,0:T(8,128)(2,1)S(1)}, bf16[128,384]{1,0:T(8,128)(2,1)S(1)}, u32[]{:S(2)}, u32[]{:S(2)}) collective-permute-start(bf16[128,384]{1,0:T(8,128)(2,1)S(1)} %get-tuple-element.54), channel_id=1, source_target_pairs={{0,5},{1,6},{2,7},{3,0},{4,1},{5,2},{6,3},{7,4},{8,13},{9,14},{10,... | collective-permute-start | bytes 294920 | tf_op jit(solution)/shard_map/ppermute | solution.py:344
  144.0 3.1 %collective-permute-start.26 = (bf16[128,384]{1,0:T(8,128)(2,1)S(1)}, bf16[128,384]{1,0:T(8,128)(2,1)S(1)}, u32[]{:S(2)}, u32[]{:S(2)}) collective-permute-start(bf16[128,384]{1,0:T(8,128)(2,1)S(1)} %get-tuple-element.55), channel_id=1, source_target_pairs={{0,6},{1,7},{2,0},{3,1},{4,2},{5,3},{6,4},{7,5},{8,14},{9,15},{10,... | collective-permute-start | bytes 294920 | tf_op jit(solution)/shard_map/ppermute | solution.py:344
  148.7 4.0 %collective-permute-done.25.refs_5_ = bf16[128,384]{1,0:T(8,128)(2,1)S(1)} collective-permute-done((bf16[128,384]{1,0:T(8,128)(2,1)S(1)}, bf16[128,384]{1,0:T(8,128)(2,1)S(1)}, u32[]{:S(2)}, u32[]{:S(2)}) %collective-permute-start.25) | collective-permute-done | bytes 98336 | tf_op jit(solution)/shard_map/ppermute | solution.py:344
  152.7 3.8 %collective-permute-done.26.refs_6_ = bf16[128,384]{1,0:T(8,128)(2,1)S(1)} collective-permute-done((bf16[128,384]{1,0:T(8,128)(2,1)S(1)}, bf16[128,384]{1,0:T(8,128)(2,1)S(1)}, u32[]{:S(2)}, u32[]{:S(2)}) %collective-permute-start.26) | collective-permute-done | bytes 98336 | tf_op jit(solution)/shard_map/ppermute | solution.py:344
  157.5 6.5 %final.1 = bf16[128,1024]{1,0:T(8,128)(2,1)} custom-call(bf16[128,384]{1,0:T(8,128)(2,1)S(1)} %get-tuple-element.49.refs_0_, bf16[128,384]{1,0:T(8,128)(2,1)S(1)} %collective-permute-done.21.refs_1_, bf16[128,384]{1,0:T(8,128)(2,1)S(1)} %collective-permute-done.22.refs_2_, bf16[128,384]{1,0:T(8,128)(2,1)S(1)} %collective-permute-done.23.refs_3_, ...), custom_call_target="tpu_custom_call" | custom-call | flops 1500000000 | bytes 1048576 | tf_op jit(solution)/shard_map/final/pallas_call | solution.py:500
  (75 shorter events, 14.2 us)
Async XLA Ops:
  7.2 68.5 %all-gather.3.cloned.1.call-start = ((), (), s32[]{:S(2)}) async-start(), calls=%async_computation.3 | async-start | bytes 4325376 | tf_op jit(solution)/shard_map/all_gather | solution.py:368
  9.6 147.9 %all-gather.5.cloned.1.call-start = ((), (), s32[]{:S(2)}) async-start(), calls=%async_computation.4 | async-start | bytes 6488064 | tf_op jit(solution)/shard_map/all_gather | solution.py:369
  10.3 37.5 %all-to-all-start = ((bf16[32,32,384]{2,1,0:T(8,128)(2,1)}), bf16[32,32,384]{2,1,0:T(8,128)(2,1)S(1)}, u32[]{:S(2)}, u32[]{:S(2)}) async-start(bf16[32,32,384]{2,1,0:T(8,128)(2,1)} %get-tuple-element.34), calls=%async_computation | async-start | bytes 1572864 | tf_op jit(solution)/shard_map/all_to_all | solution.py:370
  17.7 10.0 %collective-permute-start = (bf16[64,1024]{1,0:T(8,128)(2,1)}, bf16[64,1024]{1,0:T(8,128)(2,1)S(1)}, u32[]{:S(2)}, u32[]{:S(2)}) collective-permute-start(bf16[64,1024]{1,0:T(8,128)(2,1)} %get-tuple-element.32.refs_2_.na_ref), channel_id=1, source_target_pairs={{0,1},{1,2},{2,3},{3,4},{4,5},{5,6},{6,7},{7,0},{8,9},{9,10},{10,1... | collective-permute-start | bytes 393224 | tf_op jit(solution)/shard_map/ppermute | solution.py:344
  19.7 8.0 %collective-permute-start.10 = (bf16[64,1024]{1,0:T(8,128)(2,1)}, bf16[64,1024]{1,0:T(8,128)(2,1)S(1)}, u32[]{:S(2)}, u32[]{:S(2)}) collective-permute-start(bf16[64,1024]{1,0:T(8,128)(2,1)} %get-tuple-element.33.refs_3_.nb_ref), channel_id=1, source_target_pairs={{0,7},{1,0},{2,1},{3,2},{4,3},{5,4},{6,5},{7,6},{8,15},{9,8},{10,9... | collective-permute-start | bytes 393224 | tf_op jit(solution)/shard_map/ppermute | solution.py:344
  23.8 7.2 %collective-permute-start.4 = (bf16[64,1024]{1,0:T(8,128)(2,1)}, bf16[64,1024]{1,0:T(8,128)(2,1)S(1)}, u32[]{:S(2)}, u32[]{:S(2)}) collective-permute-start(bf16[64,1024]{1,0:T(8,128)(2,1)} %get-tuple-element.33.refs_3_.nb_ref), channel_id=1, source_target_pairs={{0,1},{1,2},{2,3},{3,4},{4,5},{5,6},{6,7},{7,0},{8,9},{9,10},{10,1... | collective-permute-start | bytes 393224 | tf_op jit(solution)/shard_map/ppermute | solution.py:344
  23.8 7.2 %collective-permute-start.7 = (bf16[64,1024]{1,0:T(8,128)(2,1)}, bf16[64,1024]{1,0:T(8,128)(2,1)S(1)}, u32[]{:S(2)}, u32[]{:S(2)}) collective-permute-start(bf16[64,1024]{1,0:T(8,128)(2,1)} %get-tuple-element.32.refs_2_.na_ref), channel_id=1, source_target_pairs={{0,7},{1,0},{2,1},{3,2},{4,3},{5,4},{6,5},{7,6},{8,15},{9,8},{10,9... | collective-permute-start | bytes 393224 | tf_op jit(solution)/shard_map/ppermute | solution.py:344
  27.7 6.5 %collective-permute-start.1 = (bf16[64,1024]{1,0:T(8,128)(2,1)S(1)}, bf16[64,1024]{1,0:T(8,128)(2,1)S(1)}, u32[]{:S(2)}, u32[]{:S(2)}) collective-permute-start(bf16[64,1024]{1,0:T(8,128)(2,1)S(1)} %collective-permute-done.refs_4_), channel_id=1, source_target_pairs={{0,1},{1,2},{2,3},{3,4},{4,5},{5,6},{6,7},{7,0},{8,9},{9,10},{10,1... | collective-permute-start | bytes 393224 | tf_op jit(solution)/shard_map/ppermute | solution.py:344
  27.7 6.5 %collective-permute-start.11 = (bf16[64,1024]{1,0:T(8,128)(2,1)S(1)}, bf16[64,1024]{1,0:T(8,128)(2,1)S(1)}, u32[]{:S(2)}, u32[]{:S(2)}) collective-permute-start(bf16[64,1024]{1,0:T(8,128)(2,1)S(1)} %collective-permute-done.10.refs_14_), channel_id=1, source_target_pairs={{0,7},{1,0},{2,1},{3,2},{4,3},{5,4},{6,5},{7,6},{8,15},{9,8},{10,9... | collective-permute-start | bytes 393224 | tf_op jit(solution)/shard_map/ppermute | solution.py:344
  31.0 6.9 %collective-permute-start.5 = (bf16[64,1024]{1,0:T(8,128)(2,1)S(1)}, bf16[64,1024]{1,0:T(8,128)(2,1)S(1)}, u32[]{:S(2)}, u32[]{:S(2)}) collective-permute-start(bf16[64,1024]{1,0:T(8,128)(2,1)S(1)} %collective-permute-done.4.refs_8_), channel_id=1, source_target_pairs={{0,1},{1,2},{2,3},{3,4},{4,5},{5,6},{6,7},{7,0},{8,9},{9,10},{10,1... | collective-permute-start | bytes 393224 | tf_op jit(solution)/shard_map/ppermute | solution.py:344
  31.0 6.9 %collective-permute-start.8 = (bf16[64,1024]{1,0:T(8,128)(2,1)S(1)}, bf16[64,1024]{1,0:T(8,128)(2,1)S(1)}, u32[]{:S(2)}, u32[]{:S(2)}) collective-permute-start(bf16[64,1024]{1,0:T(8,128)(2,1)S(1)} %collective-permute-done.7.refs_11_), channel_id=1, source_target_pairs={{0,7},{1,0},{2,1},{3,2},{4,3},{5,4},{6,5},{7,6},{8,15},{9,8},{10,9... | collective-permute-start | bytes 393224 | tf_op jit(solution)/shard_map/ppermute | solution.py:344
  34.2 7.5 %collective-permute-start.2 = (bf16[64,1024]{1,0:T(8,128)(2,1)S(1)}, bf16[64,1024]{1,0:T(8,128)(2,1)S(1)}, u32[]{:S(2)}, u32[]{:S(2)}) collective-permute-start(bf16[64,1024]{1,0:T(8,128)(2,1)S(1)} %collective-permute-done.1.refs_5_), channel_id=1, source_target_pairs={{0,1},{1,2},{2,3},{3,4},{4,5},{5,6},{6,7},{7,0},{8,9},{9,10},{10,1... | collective-permute-start | bytes 393224 | tf_op jit(solution)/shard_map/ppermute | solution.py:344
  34.2 7.5 %collective-permute-start.12 = (bf16[64,1024]{1,0:T(8,128)(2,1)S(1)}, bf16[64,1024]{1,0:T(8,128)(2,1)S(1)}, u32[]{:S(2)}, u32[]{:S(2)}) collective-permute-start(bf16[64,1024]{1,0:T(8,128)(2,1)S(1)} %collective-permute-done.11.refs_15_), channel_id=1, source_target_pairs={{0,7},{1,0},{2,1},{3,2},{4,3},{5,4},{6,5},{7,6},{8,15},{9,8},{10,9... | collective-permute-start | bytes 393224 | tf_op jit(solution)/shard_map/ppermute | solution.py:344
  37.9 7.7 %collective-permute-start.6 = (bf16[64,1024]{1,0:T(8,128)(2,1)S(1)}, bf16[64,1024]{1,0:T(8,128)(2,1)S(1)}, u32[]{:S(2)}, u32[]{:S(2)}) collective-permute-start(bf16[64,1024]{1,0:T(8,128)(2,1)S(1)} %collective-permute-done.5.refs_9_), channel_id=1, source_target_pairs={{0,1},{1,2},{2,3},{3,4},{4,5},{5,6},{6,7},{7,0},{8,9},{9,10},{10,1... | collective-permute-start | bytes 393224 | tf_op jit(solution)/shard_map/ppermute | solution.py:344
  37.9 7.7 %collective-permute-start.9 = (bf16[64,1024]{1,0:T(8,128)(2,1)S(1)}, bf16[64,1024]{1,0:T(8,128)(2,1)S(1)}, u32[]{:S(2)}, u32[]{:S(2)}) collective-permute-start(bf16[64,1024]{1,0:T(8,128)(2,1)S(1)} %collective-permute-done.8.refs_12_), channel_id=1, source_target_pairs={{0,7},{1,0},{2,1},{3,2},{4,3},{5,4},{6,5},{7,6},{8,15},{9,8},{10,9... | collective-permute-start | bytes 393224 | tf_op jit(solution)/shard_map/ppermute | solution.py:344
  41.7 6.2 %collective-permute-start.3 = (bf16[64,1024]{1,0:T(8,128)(2,1)S(1)}, bf16[64,1024]{1,0:T(8,128)(2,1)S(1)}, u32[]{:S(2)}, u32[]{:S(2)}) collective-permute-start(bf16[64,1024]{1,0:T(8,128)(2,1)S(1)} %collective-permute-done.2.refs_6_), channel_id=1, source_target_pairs={{0,1},{1,2},{2,3},{3,4},{4,5},{5,6},{6,7},{7,0},{8,9},{9,10},{10,1... | collective-permute-start | bytes 393224 | tf_op jit(solution)/shard_map/ppermute | solution.py:344
  41.7 6.2 %collective-permute-start.13 = (bf16[64,1024]{1,0:T(8,128)(2,1)S(1)}, bf16[64,1024]{1,0:T(8,128)(2,1)S(1)}, u32[]{:S(2)}, u32[]{:S(2)}) collective-permute-start(bf16[64,1024]{1,0:T(8,128)(2,1)S(1)} %collective-permute-done.12.refs_16_), channel_id=1, source_target_pairs={{0,7},{1,0},{2,1},{3,2},{4,3},{5,4},{6,5},{7,6},{8,15},{9,8},{10,9... | collective-permute-start | bytes 393224 | tf_op jit(solution)/shard_map/ppermute | solution.py:344
  106.9 13.2 %collective-permute-start.29 = (bf16[32,1024]{1,0:T(8,128)(2,1)S(1)}, bf16[32,1024]{1,0:T(8,128)(2,1)S(1)}, u32[]{:S(2)}, u32[]{:S(2)}) collective-permute-start(bf16[32,1024]{1,0:T(8,128)(2,1)S(1)} %reduce_sum.12), channel_id=1, source_target_pairs={{0,1},{1,0},{2,3},{3,2},{4,5},{5,4},{6,7},{7,6},{8,9},{9,8},{10,11... | collective-permute-start | bytes 196616 | tf_op jit(solution)/shard_map/ppermute | solution.py:340
  107.5 7.6 %collective-permute-start.14 = (bf16[128,128]{1,0:T(8,128)(2,1)S(1)}, bf16[128,128]{1,0:T(8,128)(2,1)S(1)}, u32[]{:S(2)}, u32[]{:S(2)}) collective-permute-start(bf16[128,128]{1,0:T(8,128)(2,1)S(1)} %get-tuple-element.39), channel_id=1, source_target_pairs={{0,1},{1,2},{2,3},{3,4},{4,5},{5,6},{6,7},{7,0},{8,9},{9,10},{10,1... | collective-permute-start | bytes 98312 | tf_op jit(solution)/shard_map/ppermute | solution.py:344
  109.0 8.5 %collective-permute-start.15 = (bf16[128,128]{1,0:T(8,128)(2,1)S(1)}, bf16[128,128]{1,0:T(8,128)(2,1)S(1)}, u32[]{:S(2)}, u32[]{:S(2)}) collective-permute-start(bf16[128,128]{1,0:T(8,128)(2,1)S(1)} %get-tuple-element.40), channel_id=1, source_target_pairs={{0,2},{1,3},{2,4},{3,5},{4,6},{5,7},{6,0},{7,1},{8,10},{9,11},{10,... | collective-permute-start | bytes 98312 | tf_op jit(solution)/shard_map/ppermute | solution.py:344
  109.7 11.5 %collective-permute-start.16 = (bf16[128,128]{1,0:T(8,128)(2,1)S(1)}, bf16[128,128]{1,0:T(8,128)(2,1)S(1)}, u32[]{:S(2)}, u32[]{:S(2)}) collective-permute-start(bf16[128,128]{1,0:T(8,128)(2,1)S(1)} %get-tuple-element.41), channel_id=1, source_target_pairs={{0,3},{1,4},{2,5},{3,6},{4,7},{5,0},{6,1},{7,2},{8,11},{9,12},{10,... | collective-permute-start | bytes 98312 | tf_op jit(solution)/shard_map/ppermute | solution.py:344
  112.2 10.0 %collective-permute-start.17 = (bf16[128,128]{1,0:T(8,128)(2,1)S(1)}, bf16[128,128]{1,0:T(8,128)(2,1)S(1)}, u32[]{:S(2)}, u32[]{:S(2)}) collective-permute-start(bf16[128,128]{1,0:T(8,128)(2,1)S(1)} %get-tuple-element.42), channel_id=1, source_target_pairs={{0,4},{1,5},{2,6},{3,7},{4,0},{5,1},{6,2},{7,3},{8,12},{9,13},{10,... | collective-permute-start | bytes 98312 | tf_op jit(solution)/shard_map/ppermute | solution.py:344
  115.1 7.1 %collective-permute-start.18 = (bf16[128,128]{1,0:T(8,128)(2,1)S(1)}, bf16[128,128]{1,0:T(8,128)(2,1)S(1)}, u32[]{:S(2)}, u32[]{:S(2)}) collective-permute-start(bf16[128,128]{1,0:T(8,128)(2,1)S(1)} %get-tuple-element.43), channel_id=1, source_target_pairs={{0,5},{1,6},{2,7},{3,0},{4,1},{5,2},{6,3},{7,4},{8,13},{9,14},{10,... | collective-permute-start | bytes 98312 | tf_op jit(solution)/shard_map/ppermute | solution.py:344
  121.1 10.8 %collective-permute-start.30 = (bf16[32,1024]{1,0:T(8,128)(2,1)S(1)}, bf16[32,1024]{1,0:T(8,128)(2,1)S(1)}, u32[]{:S(2)}, u32[]{:S(2)}) collective-permute-start(bf16[32,1024]{1,0:T(8,128)(2,1)S(1)} %add_convert_fusion.2), channel_id=1, source_target_pairs={{0,3},{1,2},{2,1},{3,0},{4,7},{5,6},{6,5},{7,4},{8,11},{9,10},{10,... | collective-permute-start | bytes 196616 | tf_op jit(solution)/shard_map/ppermute | solution.py:340
  128.6 12.6 %collective-permute-start.21 = (bf16[128,384]{1,0:T(8,128)(2,1)S(1)}, bf16[128,384]{1,0:T(8,128)(2,1)S(1)}, u32[]{:S(2)}, u32[]{:S(2)}) collective-permute-start(bf16[128,384]{1,0:T(8,128)(2,1)S(1)} %get-tuple-element.50), channel_id=1, source_target_pairs={{0,1},{1,2},{2,3},{3,4},{4,5},{5,6},{6,7},{7,0},{8,9},{9,10},{10,1... | collective-permute-start | bytes 294920 | tf_op jit(solution)/shard_map/ppermute | solution.py:344
  129.5 14.5 %collective-permute-start.22 = (bf16[128,384]{1,0:T(8,128)(2,1)S(1)}, bf16[128,384]{1,0:T(8,128)(2,1)S(1)}, u32[]{:S(2)}, u32[]{:S(2)}) collective-permute-start(bf16[128,384]{1,0:T(8,128)(2,1)S(1)} %get-tuple-element.51), channel_id=1, source_target_pairs={{0,2},{1,3},{2,4},{3,5},{4,6},{5,7},{6,0},{7,1},{8,10},{9,11},{10,... | collective-permute-start | bytes 294920 | tf_op jit(solution)/shard_map/ppermute | solution.py:344
  131.9 15.2 %collective-permute-start.31 = (bf16[32,1024]{1,0:T(8,128)(2,1)S(1)}, bf16[32,1024]{1,0:T(8,128)(2,1)S(1)}, u32[]{:S(2)}, u32[]{:S(2)}) collective-permute-start(bf16[32,1024]{1,0:T(8,128)(2,1)S(1)} %add_convert_fusion.1), channel_id=1, source_target_pairs={{0,7},{1,6},{2,5},{3,4},{4,3},{5,2},{6,1},{7,0},{8,15},{9,14},{10,... | collective-permute-start | bytes 196616 | tf_op jit(solution)/shard_map/ppermute | solution.py:340
  136.8 11.9 %collective-permute-start.23 = (bf16[128,384]{1,0:T(8,128)(2,1)S(1)}, bf16[128,384]{1,0:T(8,128)(2,1)S(1)}, u32[]{:S(2)}, u32[]{:S(2)}) collective-permute-start(bf16[128,384]{1,0:T(8,128)(2,1)S(1)} %get-tuple-element.52), channel_id=1, source_target_pairs={{0,3},{1,4},{2,5},{3,6},{4,7},{5,0},{6,1},{7,2},{8,11},{9,12},{10,... | collective-permute-start | bytes 294920 | tf_op jit(solution)/shard_map/ppermute | solution.py:344
  137.6 11.1 %collective-permute-start.24 = (bf16[128,384]{1,0:T(8,128)(2,1)S(1)}, bf16[128,384]{1,0:T(8,128)(2,1)S(1)}, u32[]{:S(2)}, u32[]{:S(2)}) collective-permute-start(bf16[128,384]{1,0:T(8,128)(2,1)S(1)} %get-tuple-element.53), channel_id=1, source_target_pairs={{0,4},{1,5},{2,6},{3,7},{4,0},{5,1},{6,2},{7,3},{8,12},{9,13},{10,... | collective-permute-start | bytes 294920 | tf_op jit(solution)/shard_map/ppermute | solution.py:344
  141.2 11.5 %collective-permute-start.25 = (bf16[128,384]{1,0:T(8,128)(2,1)S(1)}, bf16[128,384]{1,0:T(8,128)(2,1)S(1)}, u32[]{:S(2)}, u32[]{:S(2)}) collective-permute-start(bf16[128,384]{1,0:T(8,128)(2,1)S(1)} %get-tuple-element.54), channel_id=1, source_target_pairs={{0,5},{1,6},{2,7},{3,0},{4,1},{5,2},{6,3},{7,4},{8,13},{9,14},{10,... | collective-permute-start | bytes 294920 | tf_op jit(solution)/shard_map/ppermute | solution.py:344
  144.0 12.5 %collective-permute-start.26 = (bf16[128,384]{1,0:T(8,128)(2,1)S(1)}, bf16[128,384]{1,0:T(8,128)(2,1)S(1)}, u32[]{:S(2)}, u32[]{:S(2)}) collective-permute-start(bf16[128,384]{1,0:T(8,128)(2,1)S(1)} %get-tuple-element.55), channel_id=1, source_target_pairs={{0,6},{1,7},{2,0},{3,1},{4,2},{5,3},{6,4},{7,5},{8,14},{9,15},{10,... | collective-permute-start | bytes 294920 | tf_op jit(solution)/shard_map/ppermute | solution.py:344
  147.1 10.4 %collective-permute-start.27 = (bf16[128,384]{1,0:T(8,128)(2,1)S(1)}, bf16[128,384]{1,0:T(8,128)(2,1)S(1)}, u32[]{:S(2)}, u32[]{:S(2)}) collective-permute-start(bf16[128,384]{1,0:T(8,128)(2,1)S(1)} %get-tuple-element.56), channel_id=1, source_target_pairs={{0,7},{1,0},{2,1},{3,2},{4,3},{5,4},{6,5},{7,6},{8,15},{9,8},{10,9... | collective-permute-start | bytes 294920 | tf_op jit(solution)/shard_map/ppermute | solution.py:344
  (14 other events, 289.0 us)
Sparse Core Ops, SparseCore 0:
  10.5 53.7 all-gather.2
  67.4 60.0 all-gather.4

commit v7 on v6

--- a/solution.py
+++ b/solution.py
@@ -47,13 +47,14 @@
 
 
 def prep_kernel(
-    x_ref, gain_ref, w_ref, wout_ref, a_ref, b_ref, early_ref, late_ref, copies_ref
+    x_ref, gain_ref, w_ref, wout_ref, a_ref, b_ref, own_ref, early_ref, late_ref, copies_ref
 ):
     me = lax.axis_index("seq")
     x = x_ref[...].astype(F32)
     c = x - jnp.mean(x, axis=-1, keepdims=True)
     var = jnp.mean(c * c, axis=-1, keepdims=True)
     n = (c * lax.rsqrt(var + EPS) * gain_ref[...]).astype(BF16)
+    own_ref[...] = n
     a_ref[...] = n[:64]
     b_ref[...] = n[64:]
     early_ref[:, :D] = w_ref[:, :D]
@@ -67,8 +68,7 @@
 
 
 ARRIVALS = (
-    [(0, 0), (0, 1)]
-    + [(-k, 0) for k in (1, 2, 3, 4)]
+    [(-k, 0) for k in (1, 2, 3, 4)]
     + [(-k, 1) for k in (1, 2, 3)]
     + [(k, 0) for k in (1, 2, 3)]
     + [(k, 1) for k in (1, 2, 3, 4)]
@@ -77,11 +77,12 @@
 
 def forward_kernel(*refs):
     length_ref, bias_ref = refs[0], refs[1]
-    blocks = refs[2:18]
-    ws_ref, row_ref = refs[18:20]
-    msg_ref, proj_ref, w_ref, g_ref = refs[20:24]
-    x_all, col_sc, q_sc, k_sc, vt_sc, s_sc = refs[24:]
+    own_ref, blocks = refs[2], refs[3:17]
+    ws_ref, row_ref = refs[17:19]
+    msg_ref, proj_ref, w_ref, g_ref = refs[19:23]
+    x_all, col_sc, q_sc, k_sc, vt_sc, s_sc = refs[23:]
     me, length = lax.axis_index("seq"), length_ref[0]
+    x_all[pl.ds(pl.multiple_of(me * T, T), T), :] = own_ref[...]
     for (far, half), blk in zip(ARRIVALS, blocks):
         at = lax.rem(me + far + H, H) * T + half * 64
         x_all[pl.ds(pl.multiple_of(at, 64), 64), :] = blk[...]
@@ -162,8 +163,7 @@
 def tail_kernel(
     length_ref,
     msg_ref,
-    na_ref,
-    nb_ref,
+    own_rows_ref,
     x_ref,
     cot_ref,
     wg_ref,
@@ -181,8 +181,7 @@
         blk = msg_ref[h].astype(F32)
         att_t = blk[:DH] + (blk[DH : DH + 1] + blk[DH + 1 : DH + 2] + blk[DH + 2 : DH + 3])
         att_sc[:, h * DH : (h + 1) * DH] = att_t.T
-    rows_sc[:64, :] = na_ref[...]
-    rows_sc[64:, :] = nb_ref[...]
+    rows_sc[...] = own_rows_ref[...]
     cot = cot_ref[...]
 
     def columns(n, carry):
@@ -350,17 +349,18 @@
     gain_in = gain_in.reshape(1, D)
     gain_out = gain_out.reshape(1, D)
 
-    na, nb, early, late, copies = pl.pallas_call(
+    na, nb, own_rows, early, late, copies = pl.pallas_call(
         prep_kernel,
         out_shape=[
             jax.ShapeDtypeStruct((64, D), BF16),
             jax.ShapeDtypeStruct((64, D), BF16),
+            jax.ShapeDtypeStruct((T, D), BF16),
             jax.ShapeDtypeStruct((32, 2 * D), BF16),
             jax.ShapeDtypeStruct((32, 3 * D), BF16),
             jax.ShapeDtypeStruct((32, 32, 3 * DH), BF16),
         ],
         in_specs=[VMEM] * 4,
-        out_specs=[VMEM] * 5,
+        out_specs=[VMEM] * 6,
         compiler_params=params(61500),
         cost_estimate=cost(2),
         name="prep",
@@ -386,7 +386,7 @@
             jax.ShapeDtypeStruct((S, S), BF16),
             jax.ShapeDtypeStruct((S, S), BF16),
         ],
-        in_specs=[SMEM, SMEM] + [VMEM] * 18,
+        in_specs=[SMEM, SMEM] + [VMEM] * 17,
         out_specs=[VMEM] * 4,
         scratch_shapes=[
             pltpu.VMEM((S, D), BF16),
@@ -399,7 +399,7 @@
         compiler_params=params(),
         cost_estimate=cost(10),
         name="attend",
-    )(lengths, bias_table, *[arrived[a] for a in ARRIVALS], ws, stamps)
+    )(lengths, bias_table, own_rows, *[arrived[a] for a in ARRIVALS], ws, stamps)
 
     att_msg = lax.all_to_all(msg, "seq", 0, 0, tiled=True)
 
@@ -414,7 +414,7 @@
         ]
         + [jax.ShapeDtypeStruct((T, DH), BF16)] * H,
         in_specs=[SMEM]
-        + [VMEM] * 5
+        + [VMEM] * 4
         + [
             pl.BlockSpec((D, D), lambda i: (0, 0)),
             pl.BlockSpec((D, D), lambda i: (0, 1)),
@@ -431,7 +431,7 @@
         compiler_params=params(),
         cost_estimate=cost(5),
         name="tail",
-    )(lengths, att_msg, na, nb, x, cot, w_early, w_early, gain_out)
+    )(lengths, att_msg, own_rows, x, cot, w_early, w_early, gain_out)
 
     d_all = {0: d_att[0]}
     for k in ORDER:

time: 174 us -> 173 us (level)
  transfers between devices with their start and end apart: 35 -> 35, of which waited for: 10 -> 8; matrix products, arithmetic and copies ran while one was open for 1% -> 1% of each run, Pallas kernels for 13% -> 13%
where the time goes in v7:
time: 173 us; the launch traced here: 170 us
  starting transfers between devices  65.9 us (38%)
  blocking collectives  37.9 us (22%)
  Pallas kernels  30.4 us (18%)
  waiting for transfers between devices  17.2 us (10%)
  between operations  14.9 us (9%)
  other arithmetic  2.52 us (1%)
    ppermute x28, starting transfers between devices, shifted(): return lax.ppermute(value, 'seq', [(i, (i + by) % H) for i in range(H)])  54.9 us
    all_to_all x1, blocking collectives, layer(): lax.all_to_all(pair.reshape(16, 32, D), ('dp_0', 'dp_1'), 0, 0, tiled=True)  20.3 us
    all_to_all x1, blocking collectives, layer(): att_msg = lax.all_to_all(msg, 'seq', 0, 0, tiled=True)  17.6 us
    ppermute x28, waiting for transfers between devices, shifted(): return lax.ppermute(value, 'seq', [(i, (i + by) % H) for i in range(H)])  13.6 us
    pallas_call x1, Pallas kernels, layer(): pl.pallas_call(forward_kernel, out_shape=[jax.ShapeDtypeStruct((H, MSG, T...  8.66 us
    all_to_all x1, starting transfers between devices, layer(): ws = lax.all_to_all(copies, DP, 0, 0, tiled=True)  7.38 us
    pallas_call x1, Pallas kernels, layer(): final(*[d_rows[k] for k in range(H)], gate_back, w_late, x, cot, gain_in)  6.52 us
    pallas_call x1, Pallas kernels, layer(): pl.pallas_call(tail_kernel, grid=(1,), out_shape=[jax.ShapeDtypeStruct((T...  6.11 us
  transfers between devices with their start and end apart: 35, of which 8 were waited for; matrix products, arithmetic and copies ran while one was open for 1% of the time, Pallas kernels for 13%

profile of v7, /device:TPU:22, one launch (start us, length us, event | category | flops | bytes accessed | tf_op | source)
XLA Modules:
  0.0 169.8 jit_solution(13894098197878476278)
XLA Ops:
  7.2 2.4 %prep.1 = (bf16[64,1024]{1,0:T(8,128)(2,1)}, bf16[64,1024]{1,0:T(8,128)(2,1)}, bf16[128,1024]{1,0:T(8,128)(2,1)}, bf16[32,2048]{1,0:T(8,128)(2,1)}, bf16[32,3072...) custom-call(bf16[128,1024]{1,0:T(8,128)(2,1)} %bitcast.8, f32[1,1024]{1,0:T(1,128)} %bitcast.15, bf16[32,4096]{1,0:T(8,128)(2,1)} %w_ref.1, ...), custom_call_target="tpu_custom_call" | custom-call | flops 600000000 | bytes 1048576 | tf_op jit(solution)/shard_map/prep/pallas_call | solution.py:352
  10.4 7.4 %all-to-all-start = ((bf16[32,32,384]{2,1,0:T(8,128)(2,1)}), bf16[32,32,384]{2,1,0:T(8,128)(2,1)S(1)}, u32[]{:S(2)}, u32[]{:S(2)}) async-start(bf16[32,32,384]{2,1,0:T(8,128)(2,1)} %get-tuple-element.36), calls=%async_computation | async-start | bytes 1572864 | tf_op jit(solution)/shard_map/all_to_all | solution.py:370
  17.8 2.0 %collective-permute-start = (bf16[64,1024]{1,0:T(8,128)(2,1)}, bf16[64,1024]{1,0:T(8,128)(2,1)S(1)}, u32[]{:S(2)}, u32[]{:S(2)}) collective-permute-start(bf16[64,1024]{1,0:T(8,128)(2,1)} %get-tuple-element.34), channel_id=1, source_target_pairs={{0,1},{1,2},{2,3},{3,4},{4,5},{5,6},{6,7},{7,0},{8,9},{9,10},{10,1... | collective-permute-start | bytes 393224 | tf_op jit(solution)/shard_map/ppermute | solution.py:343
  19.8 4.0 %collective-permute-start.10 = (bf16[64,1024]{1,0:T(8,128)(2,1)}, bf16[64,1024]{1,0:T(8,128)(2,1)S(1)}, u32[]{:S(2)}, u32[]{:S(2)}) collective-permute-start(bf16[64,1024]{1,0:T(8,128)(2,1)} %get-tuple-element.35), channel_id=1, source_target_pairs={{0,7},{1,0},{2,1},{3,2},{4,3},{5,4},{6,5},{7,6},{8,15},{9,8},{10,9... | collective-permute-start | bytes 393224 | tf_op jit(solution)/shard_map/ppermute | solution.py:343
  23.8 3.2 %collective-permute-start.7 = (bf16[64,1024]{1,0:T(8,128)(2,1)}, bf16[64,1024]{1,0:T(8,128)(2,1)S(1)}, u32[]{:S(2)}, u32[]{:S(2)}) collective-permute-start(bf16[64,1024]{1,0:T(8,128)(2,1)} %get-tuple-element.34), channel_id=1, source_target_pairs={{0,7},{1,0},{2,1},{3,2},{4,3},{5,4},{6,5},{7,6},{8,15},{9,8},{10,9... | collective-permute-start | bytes 393224 | tf_op jit(solution)/shard_map/ppermute | solution.py:343
  27.8 3.2 %collective-permute-start.11 = (bf16[64,1024]{1,0:T(8,128)(2,1)S(1)}, bf16[64,1024]{1,0:T(8,128)(2,1)S(1)}, u32[]{:S(2)}, u32[]{:S(2)}) collective-permute-start(bf16[64,1024]{1,0:T(8,128)(2,1)S(1)} %collective-permute-done.10.refs_13_), channel_id=1, source_target_pairs={{0,7},{1,0},{2,1},{3,2},{4,3},{5,4},{6,5},{7,6},{8,15},{9,8},{10,9... | collective-permute-start | bytes 393224 | tf_op jit(solution)/shard_map/ppermute | solution.py:343
  31.0 3.2 %collective-permute-start.8 = (bf16[64,1024]{1,0:T(8,128)(2,1)S(1)}, bf16[64,1024]{1,0:T(8,128)(2,1)S(1)}, u32[]{:S(2)}, u32[]{:S(2)}) collective-permute-start(bf16[64,1024]{1,0:T(8,128)(2,1)S(1)} %collective-permute-done.7.refs_10_), channel_id=1, source_target_pairs={{0,7},{1,0},{2,1},{3,2},{4,3},{5,4},{6,5},{7,6},{8,15},{9,8},{10,9... | collective-permute-start | bytes 393224 | tf_op jit(solution)/shard_map/ppermute | solution.py:343
  34.3 3.4 %collective-permute-start.12 = (bf16[64,1024]{1,0:T(8,128)(2,1)S(1)}, bf16[64,1024]{1,0:T(8,128)(2,1)S(1)}, u32[]{:S(2)}, u32[]{:S(2)}) collective-permute-start(bf16[64,1024]{1,0:T(8,128)(2,1)S(1)} %collective-permute-done.11.refs_14_), channel_id=1, source_target_pairs={{0,7},{1,0},{2,1},{3,2},{4,3},{5,4},{6,5},{7,6},{8,15},{9,8},{10,9... | collective-permute-start | bytes 393224 | tf_op jit(solution)/shard_map/ppermute | solution.py:343
  37.9 3.5 %collective-permute-start.9 = (bf16[64,1024]{1,0:T(8,128)(2,1)S(1)}, bf16[64,1024]{1,0:T(8,128)(2,1)S(1)}, u32[]{:S(2)}, u32[]{:S(2)}) collective-permute-start(bf16[64,1024]{1,0:T(8,128)(2,1)S(1)} %collective-permute-done.8.refs_11_), channel_id=1, source_target_pairs={{0,7},{1,0},{2,1},{3,2},{4,3},{5,4},{6,5},{7,6},{8,15},{9,8},{10,9... | collective-permute-start | bytes 393224 | tf_op jit(solution)/shard_map/ppermute | solution.py:343
  41.5 3.7 %collective-permute-start.13 = (bf16[64,1024]{1,0:T(8,128)(2,1)S(1)}, bf16[64,1024]{1,0:T(8,128)(2,1)S(1)}, u32[]{:S(2)}, u32[]{:S(2)}) collective-permute-start(bf16[64,1024]{1,0:T(8,128)(2,1)S(1)} %collective-permute-done.12.refs_15_), channel_id=1, source_target_pairs={{0,7},{1,0},{2,1},{3,2},{4,3},{5,4},{6,5},{7,6},{8,15},{9,8},{10,9... | collective-permute-start | bytes 393224 | tf_op jit(solution)/shard_map/ppermute | solution.py:343
  45.8 1.8 %collective-permute-done.3.refs_6_ = bf16[64,1024]{1,0:T(8,128)(2,1)S(1)} collective-permute-done((bf16[64,1024]{1,0:T(8,128)(2,1)S(1)}, bf16[64,1024]{1,0:T(8,128)(2,1)S(1)}, u32[]{:S(2)}, u32[]{:S(2)}) %collective-permute-start.3) | collective-permute-done | bytes 131104 | tf_op jit(solution)/shard_map/ppermute | solution.py:343
  48.7 8.7 %attend.1 = (bf16[8,144,128]{2,1,0:T(8,128)(2,1)S(1)}, f32[1024,384]{1,0:T(8,128)}, bf16[1024,1024]{1,0:T(8,128)(2,1)}, bf16[1024,1024]{1,0:T(8,128)(2,1)}) custom-call(s32[1]{0:T(128)S(6)} %copy.12.refs_0_.length_ref, f32[8,16]{1,0:T(8,128)S(1)} %copy-done.6, bf16[128,1024]{1,0:T(8,128)(2,1)S(1)} %copy-done.2, ...), custom_call_target="tpu_custom_call" | custom-call | flops 3000000000 | bytes 1048576 | tf_op jit(solution)/shard_map/attend/pallas_call | solution.py:381
  57.3 17.6 %all_to_all.15.msg_ref = bf16[8,144,128]{2,1,0:T(8,128)(2,1)S(1)} all-to-all(bf16[8,144,128]{2,1,0:T(8,128)(2,1)S(1)} %get-tuple-element.37), channel_id=1, replica_groups=mesh['dp_0'=4,'dp_1'=4,'dp_2'=2,'seq'=8] {'seq'}, dimensions={0} | all-to-all | bytes 589824 | tf_op jit(solution)/shard_map/all_to_all | solution.py:404
  74.9 6.1 %tail.1 = (bf16[128,1024]{1,0:T(8,128)(2,1)}, bf16[128,1024]{1,0:T(8,128)(2,1)S(1)}, bf16[512,1024]{1,0:T(8,128)(2,1)S(1)}, bf16[512,1024]{1,0:T(8,128)(2,1)}, b...) custom-call(s32[1]{0:T(128)S(6)} %copy.12.refs_0_.length_ref, ...), custom_call_target="tpu_custom_call" | custom-call | flops 1500000000 | bytes 1048576 | tf_op jit(solution)/shard_map/tail/pallas_call | solution.py:406
  81.0 2.9 %collective-permute-done.28 = bf16[512,1024]{1,0:T(8,128)(2,1)S(1)} collective-permute-done((bf16[512,1024]{1,0:T(8,128)(2,1)}, bf16[512,1024]{1,0:T(8,128)(2,1)S(1)}, u32[]{:S(2)}, u32[]{:S(2)}) %collective-permute-start.28) | collective-permute-done | bytes 1048608 | tf_op jit(solution)/shard_map/ppermute | solution.py:339
  84.3 20.3 %all_to_all.16 = bf16[16,32,1024]{2,1,0:T(8,128)(2,1)} all-to-all(bf16[16,32,1024]{2,1,0:T(8,128)(2,1)S(1)} %bitcast.17), channel_id=1, replica_groups=mesh['dp_0'=4,'dp_1'=4,'dp_2'=2,'seq'=8] {'dp_0','dp_1'}, dimensions={0} | all-to-all | bytes 2097152 | tf_op jit(solution)/shard_map/all_to_all | solution.py:442
  106.7 1.5 collective-permute-start.14
  109.0 2.4 %collective-permute-start.16 = (bf16[128,128]{1,0:T(8,128)(2,1)S(1)}, bf16[128,128]{1,0:T(8,128)(2,1)S(1)}, u32[]{:S(2)}, u32[]{:S(2)}) collective-permute-start(bf16[128,128]{1,0:T(8,128)(2,1)S(1)} %get-tuple-element.43), channel_id=1, source_target_pairs={{0,3},{1,4},{2,5},{3,6},{4,7},{5,0},{6,1},{7,2},{8,11},{9,12},{10,... | collective-permute-start | bytes 98312 | tf_op jit(solution)/shard_map/ppermute | solution.py:343
  111.4 2.9 %collective-permute-start.17 = (bf16[128,128]{1,0:T(8,128)(2,1)S(1)}, bf16[128,128]{1,0:T(8,128)(2,1)S(1)}, u32[]{:S(2)}, u32[]{:S(2)}) collective-permute-start(bf16[128,128]{1,0:T(8,128)(2,1)S(1)} %get-tuple-element.44), channel_id=1, source_target_pairs={{0,4},{1,5},{2,6},{3,7},{4,0},{5,1},{6,2},{7,3},{8,12},{9,13},{10,... | collective-permute-start | bytes 98312 | tf_op jit(solution)/shard_map/ppermute | solution.py:343
  114.3 2.5 %collective-permute-start.18 = (bf16[128,128]{1,0:T(8,128)(2,1)S(1)}, bf16[128,128]{1,0:T(8,128)(2,1)S(1)}, u32[]{:S(2)}, u32[]{:S(2)}) collective-permute-start(bf16[128,128]{1,0:T(8,128)(2,1)S(1)} %get-tuple-element.45), channel_id=1, source_target_pairs={{0,5},{1,6},{2,7},{3,0},{4,1},{5,2},{6,3},{7,4},{8,13},{9,14},{10,... | collective-permute-start | bytes 98312 | tf_op jit(solution)/shard_map/ppermute | solution.py:343
  116.9 2.4 %collective-permute-start.19 = (bf16[128,128]{1,0:T(8,128)(2,1)S(1)}, bf16[128,128]{1,0:T(8,128)(2,1)S(1)}, u32[]{:S(2)}, u32[]{:S(2)}) collective-permute-start(bf16[128,128]{1,0:T(8,128)(2,1)S(1)} %get-tuple-element.46), channel_id=1, source_target_pairs={{0,6},{1,7},{2,0},{3,1},{4,2},{5,3},{6,4},{7,5},{8,14},{9,15},{10,... | collective-permute-start | bytes 98312 | tf_op jit(solution)/shard_map/ppermute | solution.py:343
  121.4 2.2 %collective-permute-done.19.refs_6_ = bf16[128,128]{1,0:T(8,128)(2,1)S(1)} collective-permute-done((bf16[128,128]{1,0:T(8,128)(2,1)S(1)}, bf16[128,128]{1,0:T(8,128)(2,1)S(1)}, u32[]{:S(2)}, u32[]{:S(2)}) %collective-permute-start.19) | collective-permute-done | bytes 32800 | tf_op jit(solution)/shard_map/ppermute | solution.py:343
  123.6 4.2 %attend_back.1 = (bf16[128,384]{1,0:T(8,128)(2,1)S(1)}, bf16[128,384]{1,0:T(8,128)(2,1)S(1)}, bf16[128,384]{1,0:T(8,128)(2,1)S(1)}, bf16[128,384]{1,0:T(8,128)(2...) custom-call(bf16[128,128]{1,0:T(8,128)(2,1)S(1)} %get-tuple-element., ...), custom_call_target="tpu_custom_call" | custom-call | flops 1800000000 | bytes 1048576 | tf_op jit(solution)/shard_map/attend_back/pallas_call | solution.py:463
  128.8 2.4 %collective-permute-start.22 = (bf16[128,384]{1,0:T(8,128)(2,1)S(1)}, bf16[128,384]{1,0:T(8,128)(2,1)S(1)}, u32[]{:S(2)}, u32[]{:S(2)}) collective-permute-start(bf16[128,384]{1,0:T(8,128)(2,1)S(1)} %get-tuple-element.53), channel_id=1, source_target_pairs={{0,2},{1,3},{2,4},{3,5},{4,6},{5,7},{6,0},{7,1},{8,10},{9,11},{10,... | collective-permute-start | bytes 294920 | tf_op jit(solution)/shard_map/ppermute | solution.py:343
  131.2 2.2 %collective-permute-start.31 = (bf16[32,1024]{1,0:T(8,128)(2,1)S(1)}, bf16[32,1024]{1,0:T(8,128)(2,1)S(1)}, u32[]{:S(2)}, u32[]{:S(2)}) collective-permute-start(bf16[32,1024]{1,0:T(8,128)(2,1)S(1)} %add_convert_fusion.1), channel_id=1, source_target_pairs={{0,7},{1,6},{2,5},{3,4},{4,3},{5,2},{6,1},{7,0},{8,15},{9,14},{10,... | collective-permute-start | bytes 196616 | tf_op jit(solution)/shard_map/ppermute | solution.py:339
  133.4 2.6 %gate.1.refs_8_ = f32[128,1024]{1,0:T(8,128)S(1)} custom-call(bf16[128,1024]{1,0:T(8,128)(2,1)S(1)} %get-tuple-element.59.dpg_ref, bf16[1024,2048]{1,0:T(8,128)(2,1)} %all-gather.3.cloned.1.call-done.wg_ref.wo_ref), custom_call_target="tpu_custom_call" | custom-call | flops 600000000 | bytes 1048576 | tf_op jit(solution)/shard_map/gate/pallas_call | solution.py:486
  137.3 3.2 %collective-permute-start.24 = (bf16[128,384]{1,0:T(8,128)(2,1)S(1)}, bf16[128,384]{1,0:T(8,128)(2,1)S(1)}, u32[]{:S(2)}, u32[]{:S(2)}) collective-permute-start(bf16[128,384]{1,0:T(8,128)(2,1)S(1)} %get-tuple-element.55), channel_id=1, source_target_pairs={{0,4},{1,5},{2,6},{3,7},{4,0},{5,1},{6,2},{7,3},{8,12},{9,13},{10,... | collective-permute-start | bytes 294920 | tf_op jit(solution)/shard_map/ppermute | solution.py:343
  140.4 2.9 %collective-permute-start.25 = (bf16[128,384]{1,0:T(8,128)(2,1)S(1)}, bf16[128,384]{1,0:T(8,128)(2,1)S(1)}, u32[]{:S(2)}, u32[]{:S(2)}) collective-permute-start(bf16[128,384]{1,0:T(8,128)(2,1)S(1)} %get-tuple-element.56), channel_id=1, source_target_pairs={{0,5},{1,6},{2,7},{3,0},{4,1},{5,2},{6,3},{7,4},{8,13},{9,14},{10,... | collective-permute-start | bytes 294920 | tf_op jit(solution)/shard_map/ppermute | solution.py:343
  143.3 3.0 %collective-permute-start.26 = (bf16[128,384]{1,0:T(8,128)(2,1)S(1)}, bf16[128,384]{1,0:T(8,128)(2,1)S(1)}, u32[]{:S(2)}, u32[]{:S(2)}) collective-permute-start(bf16[128,384]{1,0:T(8,128)(2,1)S(1)} %get-tuple-element.57), channel_id=1, source_target_pairs={{0,6},{1,7},{2,0},{3,1},{4,2},{5,3},{6,4},{7,5},{8,14},{9,15},{10,... | collective-permute-start | bytes 294920 | tf_op jit(solution)/shard_map/ppermute | solution.py:343
  147.9 3.8 %collective-permute-done.25.refs_5_ = bf16[128,384]{1,0:T(8,128)(2,1)S(1)} collective-permute-done((bf16[128,384]{1,0:T(8,128)(2,1)S(1)}, bf16[128,384]{1,0:T(8,128)(2,1)S(1)}, u32[]{:S(2)}, u32[]{:S(2)}) %collective-permute-start.25) | collective-permute-done | bytes 98336 | tf_op jit(solution)/shard_map/ppermute | solution.py:343
  151.7 3.7 %collective-permute-done.26.refs_6_ = bf16[128,384]{1,0:T(8,128)(2,1)S(1)} collective-permute-done((bf16[128,384]{1,0:T(8,128)(2,1)S(1)}, bf16[128,384]{1,0:T(8,128)(2,1)S(1)}, u32[]{:S(2)}, u32[]{:S(2)}) %collective-permute-start.26) | collective-permute-done | bytes 98336 | tf_op jit(solution)/shard_map/ppermute | solution.py:343
  156.4 6.5 %final.1 = bf16[128,1024]{1,0:T(8,128)(2,1)} custom-call(bf16[128,384]{1,0:T(8,128)(2,1)S(1)} %get-tuple-element.51.refs_0_, bf16[128,384]{1,0:T(8,128)(2,1)S(1)} %collective-permute-done.21.refs_1_, bf16[128,384]{1,0:T(8,128)(2,1)S(1)} %collective-permute-done.22.refs_2_, bf16[128,384]{1,0:T(8,128)(2,1)S(1)} %collective-permute-done.23.refs_3_, ...), custom_call_target="tpu_custom_call" | custom-call | flops 1500000000 | bytes 1048576 | tf_op jit(solution)/shard_map/final/pallas_call | solution.py:500
  (71 shorter events, 13.2 us)
Async XLA Ops:
  7.2 67.7 %all-gather.3.cloned.1.call-start = ((), (), s32[]{:S(2)}) async-start(), calls=%async_computation.3 | async-start | bytes 4325376 | tf_op jit(solution)/shard_map/all_gather | solution.py:368
  9.7 146.7 %all-gather.5.cloned.1.call-start = ((), (), s32[]{:S(2)}) async-start(), calls=%async_computation.4 | async-start | bytes 6488064 | tf_op jit(solution)/shard_map/all_gather | solution.py:369
  10.4 37.3 %all-to-all-start = ((bf16[32,32,384]{2,1,0:T(8,128)(2,1)}), bf16[32,32,384]{2,1,0:T(8,128)(2,1)S(1)}, u32[]{:S(2)}, u32[]{:S(2)}) async-start(bf16[32,32,384]{2,1,0:T(8,128)(2,1)} %get-tuple-element.36), calls=%async_computation | async-start | bytes 1572864 | tf_op jit(solution)/shard_map/all_to_all | solution.py:370
  17.8 10.0 %collective-permute-start = (bf16[64,1024]{1,0:T(8,128)(2,1)}, bf16[64,1024]{1,0:T(8,128)(2,1)S(1)}, u32[]{:S(2)}, u32[]{:S(2)}) collective-permute-start(bf16[64,1024]{1,0:T(8,128)(2,1)} %get-tuple-element.34), channel_id=1, source_target_pairs={{0,1},{1,2},{2,3},{3,4},{4,5},{5,6},{6,7},{7,0},{8,9},{9,10},{10,1... | collective-permute-start | bytes 393224 | tf_op jit(solution)/shard_map/ppermute | solution.py:343
  19.8 8.0 %collective-permute-start.10 = (bf16[64,1024]{1,0:T(8,128)(2,1)}, bf16[64,1024]{1,0:T(8,128)(2,1)S(1)}, u32[]{:S(2)}, u32[]{:S(2)}) collective-permute-start(bf16[64,1024]{1,0:T(8,128)(2,1)} %get-tuple-element.35), channel_id=1, source_target_pairs={{0,7},{1,0},{2,1},{3,2},{4,3},{5,4},{6,5},{7,6},{8,15},{9,8},{10,9... | collective-permute-start | bytes 393224 | tf_op jit(solution)/shard_map/ppermute | solution.py:343
  23.8 7.2 %collective-permute-start.4 = (bf16[64,1024]{1,0:T(8,128)(2,1)}, bf16[64,1024]{1,0:T(8,128)(2,1)S(1)}, u32[]{:S(2)}, u32[]{:S(2)}) collective-permute-start(bf16[64,1024]{1,0:T(8,128)(2,1)} %get-tuple-element.35), channel_id=1, source_target_pairs={{0,1},{1,2},{2,3},{3,4},{4,5},{5,6},{6,7},{7,0},{8,9},{9,10},{10,1... | collective-permute-start | bytes 393224 | tf_op jit(solution)/shard_map/ppermute | solution.py:343
  23.8 7.2 %collective-permute-start.7 = (bf16[64,1024]{1,0:T(8,128)(2,1)}, bf16[64,1024]{1,0:T(8,128)(2,1)S(1)}, u32[]{:S(2)}, u32[]{:S(2)}) collective-permute-start(bf16[64,1024]{1,0:T(8,128)(2,1)} %get-tuple-element.34), channel_id=1, source_target_pairs={{0,7},{1,0},{2,1},{3,2},{4,3},{5,4},{6,5},{7,6},{8,15},{9,8},{10,9... | collective-permute-start | bytes 393224 | tf_op jit(solution)/shard_map/ppermute | solution.py:343
  27.8 6.5 %collective-permute-start.1 = (bf16[64,1024]{1,0:T(8,128)(2,1)S(1)}, bf16[64,1024]{1,0:T(8,128)(2,1)S(1)}, u32[]{:S(2)}, u32[]{:S(2)}) collective-permute-start(bf16[64,1024]{1,0:T(8,128)(2,1)S(1)} %collective-permute-done.refs_3_), channel_id=1, source_target_pairs={{0,1},{1,2},{2,3},{3,4},{4,5},{5,6},{6,7},{7,0},{8,9},{9,10},{10,1... | collective-permute-start | bytes 393224 | tf_op jit(solution)/shard_map/ppermute | solution.py:343
  27.8 6.5 %collective-permute-start.11 = (bf16[64,1024]{1,0:T(8,128)(2,1)S(1)}, bf16[64,1024]{1,0:T(8,128)(2,1)S(1)}, u32[]{:S(2)}, u32[]{:S(2)}) collective-permute-start(bf16[64,1024]{1,0:T(8,128)(2,1)S(1)} %collective-permute-done.10.refs_13_), channel_id=1, source_target_pairs={{0,7},{1,0},{2,1},{3,2},{4,3},{5,4},{6,5},{7,6},{8,15},{9,8},{10,9... | collective-permute-start | bytes 393224 | tf_op jit(solution)/shard_map/ppermute | solution.py:343
  31.0 6.9 %collective-permute-start.5 = (bf16[64,1024]{1,0:T(8,128)(2,1)S(1)}, bf16[64,1024]{1,0:T(8,128)(2,1)S(1)}, u32[]{:S(2)}, u32[]{:S(2)}) collective-permute-start(bf16[64,1024]{1,0:T(8,128)(2,1)S(1)} %collective-permute-done.4.refs_7_), channel_id=1, source_target_pairs={{0,1},{1,2},{2,3},{3,4},{4,5},{5,6},{6,7},{7,0},{8,9},{9,10},{10,1... | collective-permute-start | bytes 393224 | tf_op jit(solution)/shard_map/ppermute | solution.py:343
  31.0 6.9 %collective-permute-start.8 = (bf16[64,1024]{1,0:T(8,128)(2,1)S(1)}, bf16[64,1024]{1,0:T(8,128)(2,1)S(1)}, u32[]{:S(2)}, u32[]{:S(2)}) collective-permute-start(bf16[64,1024]{1,0:T(8,128)(2,1)S(1)} %collective-permute-done.7.refs_10_), channel_id=1, source_target_pairs={{0,7},{1,0},{2,1},{3,2},{4,3},{5,4},{6,5},{7,6},{8,15},{9,8},{10,9... | collective-permute-start | bytes 393224 | tf_op jit(solution)/shard_map/ppermute | solution.py:343
  34.3 7.2 %collective-permute-start.2 = (bf16[64,1024]{1,0:T(8,128)(2,1)S(1)}, bf16[64,1024]{1,0:T(8,128)(2,1)S(1)}, u32[]{:S(2)}, u32[]{:S(2)}) collective-permute-start(bf16[64,1024]{1,0:T(8,128)(2,1)S(1)} %collective-permute-done.1.refs_4_), channel_id=1, source_target_pairs={{0,1},{1,2},{2,3},{3,4},{4,5},{5,6},{6,7},{7,0},{8,9},{9,10},{10,1... | collective-permute-start | bytes 393224 | tf_op jit(solution)/shard_map/ppermute | solution.py:343
  34.3 7.2 %collective-permute-start.12 = (bf16[64,1024]{1,0:T(8,128)(2,1)S(1)}, bf16[64,1024]{1,0:T(8,128)(2,1)S(1)}, u32[]{:S(2)}, u32[]{:S(2)}) collective-permute-start(bf16[64,1024]{1,0:T(8,128)(2,1)S(1)} %collective-permute-done.11.refs_14_), channel_id=1, source_target_pairs={{0,7},{1,0},{2,1},{3,2},{4,3},{5,4},{6,5},{7,6},{8,15},{9,8},{10,9... | collective-permute-start | bytes 393224 | tf_op jit(solution)/shard_map/ppermute | solution.py:343
  37.9 7.9 %collective-permute-start.6 = (bf16[64,1024]{1,0:T(8,128)(2,1)S(1)}, bf16[64,1024]{1,0:T(8,128)(2,1)S(1)}, u32[]{:S(2)}, u32[]{:S(2)}) collective-permute-start(bf16[64,1024]{1,0:T(8,128)(2,1)S(1)} %collective-permute-done.5.refs_8_), channel_id=1, source_target_pairs={{0,1},{1,2},{2,3},{3,4},{4,5},{5,6},{6,7},{7,0},{8,9},{9,10},{10,1... | collective-permute-start | bytes 393224 | tf_op jit(solution)/shard_map/ppermute | solution.py:343
  37.9 7.9 %collective-permute-start.9 = (bf16[64,1024]{1,0:T(8,128)(2,1)S(1)}, bf16[64,1024]{1,0:T(8,128)(2,1)S(1)}, u32[]{:S(2)}, u32[]{:S(2)}) collective-permute-start(bf16[64,1024]{1,0:T(8,128)(2,1)S(1)} %collective-permute-done.8.refs_11_), channel_id=1, source_target_pairs={{0,7},{1,0},{2,1},{3,2},{4,3},{5,4},{6,5},{7,6},{8,15},{9,8},{10,9... | collective-permute-start | bytes 393224 | tf_op jit(solution)/shard_map/ppermute | solution.py:343
  41.5 6.2 %collective-permute-start.3 = (bf16[64,1024]{1,0:T(8,128)(2,1)S(1)}, bf16[64,1024]{1,0:T(8,128)(2,1)S(1)}, u32[]{:S(2)}, u32[]{:S(2)}) collective-permute-start(bf16[64,1024]{1,0:T(8,128)(2,1)S(1)} %collective-permute-done.2.refs_5_), channel_id=1, source_target_pairs={{0,1},{1,2},{2,3},{3,4},{4,5},{5,6},{6,7},{7,0},{8,9},{9,10},{10,1... | collective-permute-start | bytes 393224 | tf_op jit(solution)/shard_map/ppermute | solution.py:343
  106.1 13.2 %collective-permute-start.29 = (bf16[32,1024]{1,0:T(8,128)(2,1)S(1)}, bf16[32,1024]{1,0:T(8,128)(2,1)S(1)}, u32[]{:S(2)}, u32[]{:S(2)}) collective-permute-start(bf16[32,1024]{1,0:T(8,128)(2,1)S(1)} %reduce_sum.12), channel_id=1, source_target_pairs={{0,1},{1,0},{2,3},{3,2},{4,5},{5,4},{6,7},{7,6},{8,9},{9,8},{10,11... | collective-permute-start | bytes 196616 | tf_op jit(solution)/shard_map/ppermute | solution.py:339
  106.7 7.6 %collective-permute-start.14 = (bf16[128,128]{1,0:T(8,128)(2,1)S(1)}, bf16[128,128]{1,0:T(8,128)(2,1)S(1)}, u32[]{:S(2)}, u32[]{:S(2)}) collective-permute-start(bf16[128,128]{1,0:T(8,128)(2,1)S(1)} %get-tuple-element.41), channel_id=1, source_target_pairs={{0,1},{1,2},{2,3},{3,4},{4,5},{5,6},{6,7},{7,0},{8,9},{9,10},{10,1... | collective-permute-start | bytes 98312 | tf_op jit(solution)/shard_map/ppermute | solution.py:343
  108.2 8.7 %collective-permute-start.15 = (bf16[128,128]{1,0:T(8,128)(2,1)S(1)}, bf16[128,128]{1,0:T(8,128)(2,1)S(1)}, u32[]{:S(2)}, u32[]{:S(2)}) collective-permute-start(bf16[128,128]{1,0:T(8,128)(2,1)S(1)} %get-tuple-element.42), channel_id=1, source_target_pairs={{0,2},{1,3},{2,4},{3,5},{4,6},{5,7},{6,0},{7,1},{8,10},{9,11},{10,... | collective-permute-start | bytes 98312 | tf_op jit(solution)/shard_map/ppermute | solution.py:343
  109.0 11.7 %collective-permute-start.16 = (bf16[128,128]{1,0:T(8,128)(2,1)S(1)}, bf16[128,128]{1,0:T(8,128)(2,1)S(1)}, u32[]{:S(2)}, u32[]{:S(2)}) collective-permute-start(bf16[128,128]{1,0:T(8,128)(2,1)S(1)} %get-tuple-element.43), channel_id=1, source_target_pairs={{0,3},{1,4},{2,5},{3,6},{4,7},{5,0},{6,1},{7,2},{8,11},{9,12},{10,... | collective-permute-start | bytes 98312 | tf_op jit(solution)/shard_map/ppermute | solution.py:343
  111.4 10.0 %collective-permute-start.17 = (bf16[128,128]{1,0:T(8,128)(2,1)S(1)}, bf16[128,128]{1,0:T(8,128)(2,1)S(1)}, u32[]{:S(2)}, u32[]{:S(2)}) collective-permute-start(bf16[128,128]{1,0:T(8,128)(2,1)S(1)} %get-tuple-element.44), channel_id=1, source_target_pairs={{0,4},{1,5},{2,6},{3,7},{4,0},{5,1},{6,2},{7,3},{8,12},{9,13},{10,... | collective-permute-start | bytes 98312 | tf_op jit(solution)/shard_map/ppermute | solution.py:343
  114.3 7.1 %collective-permute-start.18 = (bf16[128,128]{1,0:T(8,128)(2,1)S(1)}, bf16[128,128]{1,0:T(8,128)(2,1)S(1)}, u32[]{:S(2)}, u32[]{:S(2)}) collective-permute-start(bf16[128,128]{1,0:T(8,128)(2,1)S(1)} %get-tuple-element.45), channel_id=1, source_target_pairs={{0,5},{1,6},{2,7},{3,0},{4,1},{5,2},{6,3},{7,4},{8,13},{9,14},{10,... | collective-permute-start | bytes 98312 | tf_op jit(solution)/shard_map/ppermute | solution.py:343
  116.9 6.7 %collective-permute-start.19 = (bf16[128,128]{1,0:T(8,128)(2,1)S(1)}, bf16[128,128]{1,0:T(8,128)(2,1)S(1)}, u32[]{:S(2)}, u32[]{:S(2)}) collective-permute-start(bf16[128,128]{1,0:T(8,128)(2,1)S(1)} %get-tuple-element.46), channel_id=1, source_target_pairs={{0,6},{1,7},{2,0},{3,1},{4,2},{5,3},{6,4},{7,5},{8,14},{9,15},{10,... | collective-permute-start | bytes 98312 | tf_op jit(solution)/shard_map/ppermute | solution.py:343
  120.7 10.5 %collective-permute-start.30 = (bf16[32,1024]{1,0:T(8,128)(2,1)S(1)}, bf16[32,1024]{1,0:T(8,128)(2,1)S(1)}, u32[]{:S(2)}, u32[]{:S(2)}) collective-permute-start(bf16[32,1024]{1,0:T(8,128)(2,1)S(1)} %add_convert_fusion.2), channel_id=1, source_target_pairs={{0,3},{1,2},{2,1},{3,0},{4,7},{5,6},{6,5},{7,4},{8,11},{9,10},{10,... | collective-permute-start | bytes 196616 | tf_op jit(solution)/shard_map/ppermute | solution.py:339
  127.8 12.7 %collective-permute-start.21 = (bf16[128,384]{1,0:T(8,128)(2,1)S(1)}, bf16[128,384]{1,0:T(8,128)(2,1)S(1)}, u32[]{:S(2)}, u32[]{:S(2)}) collective-permute-start(bf16[128,384]{1,0:T(8,128)(2,1)S(1)} %get-tuple-element.52), channel_id=1, source_target_pairs={{0,1},{1,2},{2,3},{3,4},{4,5},{5,6},{6,7},{7,0},{8,9},{9,10},{10,1... | collective-permute-start | bytes 294920 | tf_op jit(solution)/shard_map/ppermute | solution.py:343
  128.8 14.5 %collective-permute-start.22 = (bf16[128,384]{1,0:T(8,128)(2,1)S(1)}, bf16[128,384]{1,0:T(8,128)(2,1)S(1)}, u32[]{:S(2)}, u32[]{:S(2)}) collective-permute-start(bf16[128,384]{1,0:T(8,128)(2,1)S(1)} %get-tuple-element.53), channel_id=1, source_target_pairs={{0,2},{1,3},{2,4},{3,5},{4,6},{5,7},{6,0},{7,1},{8,10},{9,11},{10,... | collective-permute-start | bytes 294920 | tf_op jit(solution)/shard_map/ppermute | solution.py:343
  131.2 15.1 %collective-permute-start.31 = (bf16[32,1024]{1,0:T(8,128)(2,1)S(1)}, bf16[32,1024]{1,0:T(8,128)(2,1)S(1)}, u32[]{:S(2)}, u32[]{:S(2)}) collective-permute-start(bf16[32,1024]{1,0:T(8,128)(2,1)S(1)} %add_convert_fusion.1), channel_id=1, source_target_pairs={{0,7},{1,6},{2,5},{3,4},{4,3},{5,2},{6,1},{7,0},{8,15},{9,14},{10,... | collective-permute-start | bytes 196616 | tf_op jit(solution)/shard_map/ppermute | solution.py:339
  136.0 12.0 %collective-permute-start.23 = (bf16[128,384]{1,0:T(8,128)(2,1)S(1)}, bf16[128,384]{1,0:T(8,128)(2,1)S(1)}, u32[]{:S(2)}, u32[]{:S(2)}) collective-permute-start(bf16[128,384]{1,0:T(8,128)(2,1)S(1)} %get-tuple-element.54), channel_id=1, source_target_pairs={{0,3},{1,4},{2,5},{3,6},{4,7},{5,0},{6,1},{7,2},{8,11},{9,12},{10,... | collective-permute-start | bytes 294920 | tf_op jit(solution)/shard_map/ppermute | solution.py:343
  137.3 10.7 %collective-permute-start.24 = (bf16[128,384]{1,0:T(8,128)(2,1)S(1)}, bf16[128,384]{1,0:T(8,128)(2,1)S(1)}, u32[]{:S(2)}, u32[]{:S(2)}) collective-permute-start(bf16[128,384]{1,0:T(8,128)(2,1)S(1)} %get-tuple-element.55), channel_id=1, source_target_pairs={{0,4},{1,5},{2,6},{3,7},{4,0},{5,1},{6,2},{7,3},{8,12},{9,13},{10,... | collective-permute-start | bytes 294920 | tf_op jit(solution)/shard_map/ppermute | solution.py:343
  140.4 11.3 %collective-permute-start.25 = (bf16[128,384]{1,0:T(8,128)(2,1)S(1)}, bf16[128,384]{1,0:T(8,128)(2,1)S(1)}, u32[]{:S(2)}, u32[]{:S(2)}) collective-permute-start(bf16[128,384]{1,0:T(8,128)(2,1)S(1)} %get-tuple-element.56), channel_id=1, source_target_pairs={{0,5},{1,6},{2,7},{3,0},{4,1},{5,2},{6,3},{7,4},{8,13},{9,14},{10,... | collective-permute-start | bytes 294920 | tf_op jit(solution)/shard_map/ppermute | solution.py:343
  143.3 12.1 %collective-permute-start.26 = (bf16[128,384]{1,0:T(8,128)(2,1)S(1)}, bf16[128,384]{1,0:T(8,128)(2,1)S(1)}, u32[]{:S(2)}, u32[]{:S(2)}) collective-permute-start(bf16[128,384]{1,0:T(8,128)(2,1)S(1)} %get-tuple-element.57), channel_id=1, source_target_pairs={{0,6},{1,7},{2,0},{3,1},{4,2},{5,3},{6,4},{7,5},{8,14},{9,15},{10,... | collective-permute-start | bytes 294920 | tf_op jit(solution)/shard_map/ppermute | solution.py:343
  146.3 10.1 %collective-permute-start.27 = (bf16[128,384]{1,0:T(8,128)(2,1)S(1)}, bf16[128,384]{1,0:T(8,128)(2,1)S(1)}, u32[]{:S(2)}, u32[]{:S(2)}) collective-permute-start(bf16[128,384]{1,0:T(8,128)(2,1)S(1)} %get-tuple-element.58), channel_id=1, source_target_pairs={{0,7},{1,0},{2,1},{3,2},{4,3},{5,4},{6,5},{7,6},{8,15},{9,8},{10,9... | collective-permute-start | bytes 294920 | tf_op jit(solution)/shard_map/ppermute | solution.py:343
  (12 other events, 262.7 us)
Sparse Core Ops, SparseCore 0:
  10.5 53.7 all-gather.2
  66.9 62.0 all-gather.4

commit v8 on v7

--- a/solution.py
+++ b/solution.py
@@ -80,13 +80,17 @@
     own_ref, blocks = refs[2], refs[3:17]
     ws_ref, row_ref = refs[17:19]
     msg_ref, proj_ref, w_ref, g_ref = refs[19:23]
-    x_all, col_sc, q_sc, k_sc, vt_sc, s_sc = refs[23:]
+    x_all, col_sc, q_sc, k_sc, vt_sc, s_sc, own_sem = refs[23:]
     me, length = lax.axis_index("seq"), length_ref[0]
-    x_all[pl.ds(pl.multiple_of(me * T, T), T), :] = own_ref[...]
+    fetch = pltpu.make_async_copy(
+        own_ref, x_all.at[pl.ds(pl.multiple_of(me * T, T), T), :], own_sem
+    )
+    fetch.start()
     for (far, half), blk in zip(ARRIVALS, blocks):
         at = lax.rem(me + far + H, H) * T + half * 64
         x_all[pl.ds(pl.multiple_of(at, 64), 64), :] = blk[...]
 
+    fetch.wait()
     proj_ref[...] = mm(x_all[...], ws_ref[...])
     for c in range(8):
         cols = slice(c * T, (c + 1) * T)
@@ -386,7 +390,7 @@
             jax.ShapeDtypeStruct((S, S), BF16),
             jax.ShapeDtypeStruct((S, S), BF16),
         ],
-        in_specs=[SMEM, SMEM] + [VMEM] * 17,
+        in_specs=[SMEM, SMEM, pl.BlockSpec(memory_space=pl.ANY)] + [VMEM] * 16,
         out_specs=[VMEM] * 4,
         scratch_shapes=[
             pltpu.VMEM((S, D), BF16),
@@ -395,6 +399,7 @@
             pltpu.VMEM((S, DH), BF16),
             pltpu.VMEM((DH, S), BF16),
             pltpu.VMEM((TI, TI), F32),
+            pltpu.SemaphoreType.DMA,
         ],
         compiler_params=params(),
         cost_estimate=cost(10),

time: 173 us -> 173 us (level)
  transfers between devices with their start and end apart: 35 -> 35, of which waited for: 8 -> 9; matrix products, arithmetic and copies ran while one was open for 1% -> 1% of each run, Pallas kernels for 13% -> 13%
where the time goes in v8:
time: 173 us; the launch traced here: 170 us
  starting transfers between devices  65.9 us (38%)
  blocking collectives  38 us (22%)
  Pallas kernels  30.4 us (18%)
  waiting for transfers between devices  17.2 us (10%)
  between operations  14.9 us (9%)
  other arithmetic  2.52 us (1%)
    ppermute x28, starting transfers between devices, shifted(): return lax.ppermute(value, 'seq', [(i, (i + by) % H) for i in range(H)])  54.9 us
    all_to_all x1, blocking collectives, layer(): lax.all_to_all(pair.reshape(16, 32, D), ('dp_0', 'dp_1'), 0, 0, tiled=True)  20.3 us
    all_to_all x1, blocking collectives, layer(): att_msg = lax.all_to_all(msg, 'seq', 0, 0, tiled=True)  17.6 us
    ppermute x28, waiting for transfers between devices, shifted(): return lax.ppermute(value, 'seq', [(i, (i + by) % H) for i in range(H)])  13.6 us
    pallas_call x1, Pallas kernels, layer(): pl.pallas_call(forward_kernel, out_shape=[jax.ShapeDtypeStruct((H, MSG, T...  8.66 us
    all_to_all x1, starting transfers between devices, layer(): ws = lax.all_to_all(copies, DP, 0, 0, tiled=True)  7.38 us
    pallas_call x1, Pallas kernels, layer(): final(*[d_rows[k] for k in range(H)], gate_back, w_late, x, cot, gain_in)  6.52 us
    pallas_call x1, Pallas kernels, layer(): pl.pallas_call(tail_kernel, grid=(1,), out_shape=[jax.ShapeDtypeStruct((T...  6.11 us
  transfers between devices with their start and end apart: 35, of which 9 were waited for; matrix products, arithmetic and copies ran while one was open for 1% of the time, Pallas kernels for 13%

profile of v8, /device:TPU:22, one launch (start us, length us, event | category | flops | bytes accessed | tf_op | source)
XLA Modules:
  0.0 169.9 jit_solution(3778779559081314689)
XLA Ops:
  7.2 2.4 %prep.1 = (bf16[64,1024]{1,0:T(8,128)(2,1)}, bf16[64,1024]{1,0:T(8,128)(2,1)}, bf16[128,1024]{1,0:T(8,128)(2,1)}, bf16[32,2048]{1,0:T(8,128)(2,1)}, bf16[32,3072...) custom-call(bf16[128,1024]{1,0:T(8,128)(2,1)} %bitcast.8, f32[1,1024]{1,0:T(1,128)} %bitcast.15, bf16[32,4096]{1,0:T(8,128)(2,1)} %w_ref.1, ...), custom_call_target="tpu_custom_call" | custom-call | flops 600000000 | bytes 1048576 | tf_op jit(solution)/shard_map/prep/pallas_call | solution.py:356
  10.4 7.4 %all-to-all-start = ((bf16[32,32,384]{2,1,0:T(8,128)(2,1)}), bf16[32,32,384]{2,1,0:T(8,128)(2,1)S(1)}, u32[]{:S(2)}, u32[]{:S(2)}) async-start(bf16[32,32,384]{2,1,0:T(8,128)(2,1)} %get-tuple-element.36), calls=%async_computation | async-start | bytes 1572864 | tf_op jit(solution)/shard_map/all_to_all | solution.py:374
  17.8 2.0 %collective-permute-start = (bf16[64,1024]{1,0:T(8,128)(2,1)}, bf16[64,1024]{1,0:T(8,128)(2,1)S(1)}, u32[]{:S(2)}, u32[]{:S(2)}) collective-permute-start(bf16[64,1024]{1,0:T(8,128)(2,1)} %get-tuple-element.34), channel_id=1, source_target_pairs={{0,1},{1,2},{2,3},{3,4},{4,5},{5,6},{6,7},{7,0},{8,9},{9,10},{10,1... | collective-permute-start | bytes 393224 | tf_op jit(solution)/shard_map/ppermute | solution.py:347
  19.8 4.0 %collective-permute-start.10 = (bf16[64,1024]{1,0:T(8,128)(2,1)}, bf16[64,1024]{1,0:T(8,128)(2,1)S(1)}, u32[]{:S(2)}, u32[]{:S(2)}) collective-permute-start(bf16[64,1024]{1,0:T(8,128)(2,1)} %get-tuple-element.35), channel_id=1, source_target_pairs={{0,7},{1,0},{2,1},{3,2},{4,3},{5,4},{6,5},{7,6},{8,15},{9,8},{10,9... | collective-permute-start | bytes 393224 | tf_op jit(solution)/shard_map/ppermute | solution.py:347
  23.8 3.2 %collective-permute-start.7 = (bf16[64,1024]{1,0:T(8,128)(2,1)}, bf16[64,1024]{1,0:T(8,128)(2,1)S(1)}, u32[]{:S(2)}, u32[]{:S(2)}) collective-permute-start(bf16[64,1024]{1,0:T(8,128)(2,1)} %get-tuple-element.34), channel_id=1, source_target_pairs={{0,7},{1,0},{2,1},{3,2},{4,3},{5,4},{6,5},{7,6},{8,15},{9,8},{10,9... | collective-permute-start | bytes 393224 | tf_op jit(solution)/shard_map/ppermute | solution.py:347
  27.8 3.2 %collective-permute-start.11 = (bf16[64,1024]{1,0:T(8,128)(2,1)S(1)}, bf16[64,1024]{1,0:T(8,128)(2,1)S(1)}, u32[]{:S(2)}, u32[]{:S(2)}) collective-permute-start(bf16[64,1024]{1,0:T(8,128)(2,1)S(1)} %collective-permute-done.10.refs_13_), channel_id=1, source_target_pairs={{0,7},{1,0},{2,1},{3,2},{4,3},{5,4},{6,5},{7,6},{8,15},{9,8},{10,9... | collective-permute-start | bytes 393224 | tf_op jit(solution)/shard_map/ppermute | solution.py:347
  31.0 3.2 %collective-permute-start.8 = (bf16[64,1024]{1,0:T(8,128)(2,1)S(1)}, bf16[64,1024]{1,0:T(8,128)(2,1)S(1)}, u32[]{:S(2)}, u32[]{:S(2)}) collective-permute-start(bf16[64,1024]{1,0:T(8,128)(2,1)S(1)} %collective-permute-done.7.refs_10_), channel_id=1, source_target_pairs={{0,7},{1,0},{2,1},{3,2},{4,3},{5,4},{6,5},{7,6},{8,15},{9,8},{10,9... | collective-permute-start | bytes 393224 | tf_op jit(solution)/shard_map/ppermute | solution.py:347
  34.3 3.4 %collective-permute-start.12 = (bf16[64,1024]{1,0:T(8,128)(2,1)S(1)}, bf16[64,1024]{1,0:T(8,128)(2,1)S(1)}, u32[]{:S(2)}, u32[]{:S(2)}) collective-permute-start(bf16[64,1024]{1,0:T(8,128)(2,1)S(1)} %collective-permute-done.11.refs_14_), channel_id=1, source_target_pairs={{0,7},{1,0},{2,1},{3,2},{4,3},{5,4},{6,5},{7,6},{8,15},{9,8},{10,9... | collective-permute-start | bytes 393224 | tf_op jit(solution)/shard_map/ppermute | solution.py:347
  37.9 3.5 %collective-permute-start.9 = (bf16[64,1024]{1,0:T(8,128)(2,1)S(1)}, bf16[64,1024]{1,0:T(8,128)(2,1)S(1)}, u32[]{:S(2)}, u32[]{:S(2)}) collective-permute-start(bf16[64,1024]{1,0:T(8,128)(2,1)S(1)} %collective-permute-done.8.refs_11_), channel_id=1, source_target_pairs={{0,7},{1,0},{2,1},{3,2},{4,3},{5,4},{6,5},{7,6},{8,15},{9,8},{10,9... | collective-permute-start | bytes 393224 | tf_op jit(solution)/shard_map/ppermute | solution.py:347
  41.5 3.7 %collective-permute-start.13 = (bf16[64,1024]{1,0:T(8,128)(2,1)S(1)}, bf16[64,1024]{1,0:T(8,128)(2,1)S(1)}, u32[]{:S(2)}, u32[]{:S(2)}) collective-permute-start(bf16[64,1024]{1,0:T(8,128)(2,1)S(1)} %collective-permute-done.12.refs_15_), channel_id=1, source_target_pairs={{0,7},{1,0},{2,1},{3,2},{4,3},{5,4},{6,5},{7,6},{8,15},{9,8},{10,9... | collective-permute-start | bytes 393224 | tf_op jit(solution)/shard_map/ppermute | solution.py:347
  45.8 1.8 %collective-permute-done.3.refs_6_ = bf16[64,1024]{1,0:T(8,128)(2,1)S(1)} collective-permute-done((bf16[64,1024]{1,0:T(8,128)(2,1)S(1)}, bf16[64,1024]{1,0:T(8,128)(2,1)S(1)}, u32[]{:S(2)}, u32[]{:S(2)}) %collective-permute-start.3) | collective-permute-done | bytes 131104 | tf_op jit(solution)/shard_map/ppermute | solution.py:347
  48.7 8.7 %attend.1 = (bf16[8,144,128]{2,1,0:T(8,128)(2,1)S(1)}, f32[1024,384]{1,0:T(8,128)}, bf16[1024,1024]{1,0:T(8,128)(2,1)}, bf16[1024,1024]{1,0:T(8,128)(2,1)}) custom-call(s32[1]{0:T(128)S(6)} %copy.12.refs_0_.length_ref, f32[8,16]{1,0:T(8,128)S(1)} %copy-done.6, bf16[128,1024]{1,0:T(8,128)(2,1)S(1)} %copy-done.2, ...), custom_call_target="tpu_custom_call" | custom-call | flops 3000000000 | bytes 1048576 | tf_op jit(solution)/shard_map/attend/pallas_call | solution.py:385
  57.3 17.6 %all_to_all.15.msg_ref = bf16[8,144,128]{2,1,0:T(8,128)(2,1)S(1)} all-to-all(bf16[8,144,128]{2,1,0:T(8,128)(2,1)S(1)} %get-tuple-element.37), channel_id=1, replica_groups=mesh['dp_0'=4,'dp_1'=4,'dp_2'=2,'seq'=8] {'seq'}, dimensions={0} | all-to-all | bytes 589824 | tf_op jit(solution)/shard_map/all_to_all | solution.py:409
  75.0 6.1 %tail.1 = (bf16[128,1024]{1,0:T(8,128)(2,1)}, bf16[128,1024]{1,0:T(8,128)(2,1)S(1)}, bf16[512,1024]{1,0:T(8,128)(2,1)S(1)}, bf16[512,1024]{1,0:T(8,128)(2,1)}, b...) custom-call(s32[1]{0:T(128)S(6)} %copy.12.refs_0_.length_ref, ...), custom_call_target="tpu_custom_call" | custom-call | flops 1500000000 | bytes 1048576 | tf_op jit(solution)/shard_map/tail/pallas_call | solution.py:411
  81.1 2.9 %collective-permute-done.28 = bf16[512,1024]{1,0:T(8,128)(2,1)S(1)} collective-permute-done((bf16[512,1024]{1,0:T(8,128)(2,1)}, bf16[512,1024]{1,0:T(8,128)(2,1)S(1)}, u32[]{:S(2)}, u32[]{:S(2)}) %collective-permute-start.28) | collective-permute-done | bytes 1048608 | tf_op jit(solution)/shard_map/ppermute | solution.py:343
  84.4 20.3 %all_to_all.16 = bf16[16,32,1024]{2,1,0:T(8,128)(2,1)} all-to-all(bf16[16,32,1024]{2,1,0:T(8,128)(2,1)S(1)} %bitcast.17), channel_id=1, replica_groups=mesh['dp_0'=4,'dp_1'=4,'dp_2'=2,'seq'=8] {'dp_0','dp_1'}, dimensions={0} | all-to-all | bytes 2097152 | tf_op jit(solution)/shard_map/all_to_all | solution.py:447
  106.7 1.5 collective-permute-start.14
  109.0 2.4 %collective-permute-start.16 = (bf16[128,128]{1,0:T(8,128)(2,1)S(1)}, bf16[128,128]{1,0:T(8,128)(2,1)S(1)}, u32[]{:S(2)}, u32[]{:S(2)}) collective-permute-start(bf16[128,128]{1,0:T(8,128)(2,1)S(1)} %get-tuple-element.43), channel_id=1, source_target_pairs={{0,3},{1,4},{2,5},{3,6},{4,7},{5,0},{6,1},{7,2},{8,11},{9,12},{10,... | collective-permute-start | bytes 98312 | tf_op jit(solution)/shard_map/ppermute | solution.py:347
  111.5 2.9 %collective-permute-start.17 = (bf16[128,128]{1,0:T(8,128)(2,1)S(1)}, bf16[128,128]{1,0:T(8,128)(2,1)S(1)}, u32[]{:S(2)}, u32[]{:S(2)}) collective-permute-start(bf16[128,128]{1,0:T(8,128)(2,1)S(1)} %get-tuple-element.44), channel_id=1, source_target_pairs={{0,4},{1,5},{2,6},{3,7},{4,0},{5,1},{6,2},{7,3},{8,12},{9,13},{10,... | collective-permute-start | bytes 98312 | tf_op jit(solution)/shard_map/ppermute | solution.py:347
  114.4 2.5 %collective-permute-start.18 = (bf16[128,128]{1,0:T(8,128)(2,1)S(1)}, bf16[128,128]{1,0:T(8,128)(2,1)S(1)}, u32[]{:S(2)}, u32[]{:S(2)}) collective-permute-start(bf16[128,128]{1,0:T(8,128)(2,1)S(1)} %get-tuple-element.45), channel_id=1, source_target_pairs={{0,5},{1,6},{2,7},{3,0},{4,1},{5,2},{6,3},{7,4},{8,13},{9,14},{10,... | collective-permute-start | bytes 98312 | tf_op jit(solution)/shard_map/ppermute | solution.py:347
  116.9 2.4 %collective-permute-start.19 = (bf16[128,128]{1,0:T(8,128)(2,1)S(1)}, bf16[128,128]{1,0:T(8,128)(2,1)S(1)}, u32[]{:S(2)}, u32[]{:S(2)}) collective-permute-start(bf16[128,128]{1,0:T(8,128)(2,1)S(1)} %get-tuple-element.46), channel_id=1, source_target_pairs={{0,6},{1,7},{2,0},{3,1},{4,2},{5,3},{6,4},{7,5},{8,14},{9,15},{10,... | collective-permute-start | bytes 98312 | tf_op jit(solution)/shard_map/ppermute | solution.py:347
  121.4 2.2 %collective-permute-done.19.refs_6_ = bf16[128,128]{1,0:T(8,128)(2,1)S(1)} collective-permute-done((bf16[128,128]{1,0:T(8,128)(2,1)S(1)}, bf16[128,128]{1,0:T(8,128)(2,1)S(1)}, u32[]{:S(2)}, u32[]{:S(2)}) %collective-permute-start.19) | collective-permute-done | bytes 32800 | tf_op jit(solution)/shard_map/ppermute | solution.py:347
  123.6 4.1 %attend_back.1 = (bf16[128,384]{1,0:T(8,128)(2,1)S(1)}, bf16[128,384]{1,0:T(8,128)(2,1)S(1)}, bf16[128,384]{1,0:T(8,128)(2,1)S(1)}, bf16[128,384]{1,0:T(8,128)(2...) custom-call(bf16[128,128]{1,0:T(8,128)(2,1)S(1)} %get-tuple-element., ...), custom_call_target="tpu_custom_call" | custom-call | flops 1800000000 | bytes 1048576 | tf_op jit(solution)/shard_map/attend_back/pallas_call | solution.py:468
  128.8 2.4 %collective-permute-start.22 = (bf16[128,384]{1,0:T(8,128)(2,1)S(1)}, bf16[128,384]{1,0:T(8,128)(2,1)S(1)}, u32[]{:S(2)}, u32[]{:S(2)}) collective-permute-start(bf16[128,384]{1,0:T(8,128)(2,1)S(1)} %get-tuple-element.53), channel_id=1, source_target_pairs={{0,2},{1,3},{2,4},{3,5},{4,6},{5,7},{6,0},{7,1},{8,10},{9,11},{10,... | collective-permute-start | bytes 294920 | tf_op jit(solution)/shard_map/ppermute | solution.py:347
  131.2 2.2 %collective-permute-start.31 = (bf16[32,1024]{1,0:T(8,128)(2,1)S(1)}, bf16[32,1024]{1,0:T(8,128)(2,1)S(1)}, u32[]{:S(2)}, u32[]{:S(2)}) collective-permute-start(bf16[32,1024]{1,0:T(8,128)(2,1)S(1)} %add_convert_fusion.1), channel_id=1, source_target_pairs={{0,7},{1,6},{2,5},{3,4},{4,3},{5,2},{6,1},{7,0},{8,15},{9,14},{10,... | collective-permute-start | bytes 196616 | tf_op jit(solution)/shard_map/ppermute | solution.py:343
  133.4 2.6 %gate.1.refs_8_ = f32[128,1024]{1,0:T(8,128)S(1)} custom-call(bf16[128,1024]{1,0:T(8,128)(2,1)S(1)} %get-tuple-element.59.dpg_ref, bf16[1024,2048]{1,0:T(8,128)(2,1)} %all-gather.3.cloned.1.call-done.wg_ref.wo_ref), custom_call_target="tpu_custom_call" | custom-call | flops 600000000 | bytes 1048576 | tf_op jit(solution)/shard_map/gate/pallas_call | solution.py:491
  137.3 3.2 %collective-permute-start.24 = (bf16[128,384]{1,0:T(8,128)(2,1)S(1)}, bf16[128,384]{1,0:T(8,128)(2,1)S(1)}, u32[]{:S(2)}, u32[]{:S(2)}) collective-permute-start(bf16[128,384]{1,0:T(8,128)(2,1)S(1)} %get-tuple-element.55), channel_id=1, source_target_pairs={{0,4},{1,5},{2,6},{3,7},{4,0},{5,1},{6,2},{7,3},{8,12},{9,13},{10,... | collective-permute-start | bytes 294920 | tf_op jit(solution)/shard_map/ppermute | solution.py:347
  140.5 2.8 %collective-permute-start.25 = (bf16[128,384]{1,0:T(8,128)(2,1)S(1)}, bf16[128,384]{1,0:T(8,128)(2,1)S(1)}, u32[]{:S(2)}, u32[]{:S(2)}) collective-permute-start(bf16[128,384]{1,0:T(8,128)(2,1)S(1)} %get-tuple-element.56), channel_id=1, source_target_pairs={{0,5},{1,6},{2,7},{3,0},{4,1},{5,2},{6,3},{7,4},{8,13},{9,14},{10,... | collective-permute-start | bytes 294920 | tf_op jit(solution)/shard_map/ppermute | solution.py:347
  143.3 3.0 %collective-permute-start.26 = (bf16[128,384]{1,0:T(8,128)(2,1)S(1)}, bf16[128,384]{1,0:T(8,128)(2,1)S(1)}, u32[]{:S(2)}, u32[]{:S(2)}) collective-permute-start(bf16[128,384]{1,0:T(8,128)(2,1)S(1)} %get-tuple-element.57), channel_id=1, source_target_pairs={{0,6},{1,7},{2,0},{3,1},{4,2},{5,3},{6,4},{7,5},{8,14},{9,15},{10,... | collective-permute-start | bytes 294920 | tf_op jit(solution)/shard_map/ppermute | solution.py:347
  148.1 3.6 %collective-permute-done.25.refs_5_ = bf16[128,384]{1,0:T(8,128)(2,1)S(1)} collective-permute-done((bf16[128,384]{1,0:T(8,128)(2,1)S(1)}, bf16[128,384]{1,0:T(8,128)(2,1)S(1)}, u32[]{:S(2)}, u32[]{:S(2)}) %collective-permute-start.25) | collective-permute-done | bytes 98336 | tf_op jit(solution)/shard_map/ppermute | solution.py:347
  151.7 3.7 %collective-permute-done.26.refs_6_ = bf16[128,384]{1,0:T(8,128)(2,1)S(1)} collective-permute-done((bf16[128,384]{1,0:T(8,128)(2,1)S(1)}, bf16[128,384]{1,0:T(8,128)(2,1)S(1)}, u32[]{:S(2)}, u32[]{:S(2)}) %collective-permute-start.26) | collective-permute-done | bytes 98336 | tf_op jit(solution)/shard_map/ppermute | solution.py:347
  156.5 6.5 %final.1 = bf16[128,1024]{1,0:T(8,128)(2,1)} custom-call(bf16[128,384]{1,0:T(8,128)(2,1)S(1)} %get-tuple-element.51.refs_0_, bf16[128,384]{1,0:T(8,128)(2,1)S(1)} %collective-permute-done.21.refs_1_, bf16[128,384]{1,0:T(8,128)(2,1)S(1)} %collective-permute-done.22.refs_2_, bf16[128,384]{1,0:T(8,128)(2,1)S(1)} %collective-permute-done.23.refs_3_, ...), custom_call_target="tpu_custom_call" | custom-call | flops 1500000000 | bytes 1048576 | tf_op jit(solution)/shard_map/final/pallas_call | solution.py:505
  (71 shorter events, 13.5 us)
Async XLA Ops:
  7.2 67.8 %all-gather.3.cloned.1.call-start = ((), (), s32[]{:S(2)}) async-start(), calls=%async_computation.3 | async-start | bytes 4325376 | tf_op jit(solution)/shard_map/all_gather | solution.py:372
  9.7 146.9 %all-gather.5.cloned.1.call-start = ((), (), s32[]{:S(2)}) async-start(), calls=%async_computation.4 | async-start | bytes 6488064 | tf_op jit(solution)/shard_map/all_gather | solution.py:373
  10.4 37.3 %all-to-all-start = ((bf16[32,32,384]{2,1,0:T(8,128)(2,1)}), bf16[32,32,384]{2,1,0:T(8,128)(2,1)S(1)}, u32[]{:S(2)}, u32[]{:S(2)}) async-start(bf16[32,32,384]{2,1,0:T(8,128)(2,1)} %get-tuple-element.36), calls=%async_computation | async-start | bytes 1572864 | tf_op jit(solution)/shard_map/all_to_all | solution.py:374
  17.8 10.0 %collective-permute-start = (bf16[64,1024]{1,0:T(8,128)(2,1)}, bf16[64,1024]{1,0:T(8,128)(2,1)S(1)}, u32[]{:S(2)}, u32[]{:S(2)}) collective-permute-start(bf16[64,1024]{1,0:T(8,128)(2,1)} %get-tuple-element.34), channel_id=1, source_target_pairs={{0,1},{1,2},{2,3},{3,4},{4,5},{5,6},{6,7},{7,0},{8,9},{9,10},{10,1... | collective-permute-start | bytes 393224 | tf_op jit(solution)/shard_map/ppermute | solution.py:347
  19.8 8.0 %collective-permute-start.10 = (bf16[64,1024]{1,0:T(8,128)(2,1)}, bf16[64,1024]{1,0:T(8,128)(2,1)S(1)}, u32[]{:S(2)}, u32[]{:S(2)}) collective-permute-start(bf16[64,1024]{1,0:T(8,128)(2,1)} %get-tuple-element.35), channel_id=1, source_target_pairs={{0,7},{1,0},{2,1},{3,2},{4,3},{5,4},{6,5},{7,6},{8,15},{9,8},{10,9... | collective-permute-start | bytes 393224 | tf_op jit(solution)/shard_map/ppermute | solution.py:347
  23.8 7.2 %collective-permute-start.4 = (bf16[64,1024]{1,0:T(8,128)(2,1)}, bf16[64,1024]{1,0:T(8,128)(2,1)S(1)}, u32[]{:S(2)}, u32[]{:S(2)}) collective-permute-start(bf16[64,1024]{1,0:T(8,128)(2,1)} %get-tuple-element.35), channel_id=1, source_target_pairs={{0,1},{1,2},{2,3},{3,4},{4,5},{5,6},{6,7},{7,0},{8,9},{9,10},{10,1... | collective-permute-start | bytes 393224 | tf_op jit(solution)/shard_map/ppermute | solution.py:347
  23.8 7.2 %collective-permute-start.7 = (bf16[64,1024]{1,0:T(8,128)(2,1)}, bf16[64,1024]{1,0:T(8,128)(2,1)S(1)}, u32[]{:S(2)}, u32[]{:S(2)}) collective-permute-start(bf16[64,1024]{1,0:T(8,128)(2,1)} %get-tuple-element.34), channel_id=1, source_target_pairs={{0,7},{1,0},{2,1},{3,2},{4,3},{5,4},{6,5},{7,6},{8,15},{9,8},{10,9... | collective-permute-start | bytes 393224 | tf_op jit(solution)/shard_map/ppermute | solution.py:347
  27.8 6.5 %collective-permute-start.1 = (bf16[64,1024]{1,0:T(8,128)(2,1)S(1)}, bf16[64,1024]{1,0:T(8,128)(2,1)S(1)}, u32[]{:S(2)}, u32[]{:S(2)}) collective-permute-start(bf16[64,1024]{1,0:T(8,128)(2,1)S(1)} %collective-permute-done.refs_3_), channel_id=1, source_target_pairs={{0,1},{1,2},{2,3},{3,4},{4,5},{5,6},{6,7},{7,0},{8,9},{9,10},{10,1... | collective-permute-start | bytes 393224 | tf_op jit(solution)/shard_map/ppermute | solution.py:347
  27.8 6.5 %collective-permute-start.11 = (bf16[64,1024]{1,0:T(8,128)(2,1)S(1)}, bf16[64,1024]{1,0:T(8,128)(2,1)S(1)}, u32[]{:S(2)}, u32[]{:S(2)}) collective-permute-start(bf16[64,1024]{1,0:T(8,128)(2,1)S(1)} %collective-permute-done.10.refs_13_), channel_id=1, source_target_pairs={{0,7},{1,0},{2,1},{3,2},{4,3},{5,4},{6,5},{7,6},{8,15},{9,8},{10,9... | collective-permute-start | bytes 393224 | tf_op jit(solution)/shard_map/ppermute | solution.py:347
  31.0 6.9 %collective-permute-start.5 = (bf16[64,1024]{1,0:T(8,128)(2,1)S(1)}, bf16[64,1024]{1,0:T(8,128)(2,1)S(1)}, u32[]{:S(2)}, u32[]{:S(2)}) collective-permute-start(bf16[64,1024]{1,0:T(8,128)(2,1)S(1)} %collective-permute-done.4.refs_7_), channel_id=1, source_target_pairs={{0,1},{1,2},{2,3},{3,4},{4,5},{5,6},{6,7},{7,0},{8,9},{9,10},{10,1... | collective-permute-start | bytes 393224 | tf_op jit(solution)/shard_map/ppermute | solution.py:347
  31.0 6.9 %collective-permute-start.8 = (bf16[64,1024]{1,0:T(8,128)(2,1)S(1)}, bf16[64,1024]{1,0:T(8,128)(2,1)S(1)}, u32[]{:S(2)}, u32[]{:S(2)}) collective-permute-start(bf16[64,1024]{1,0:T(8,128)(2,1)S(1)} %collective-permute-done.7.refs_10_), channel_id=1, source_target_pairs={{0,7},{1,0},{2,1},{3,2},{4,3},{5,4},{6,5},{7,6},{8,15},{9,8},{10,9... | collective-permute-start | bytes 393224 | tf_op jit(solution)/shard_map/ppermute | solution.py:347
  34.3 7.2 %collective-permute-start.2 = (bf16[64,1024]{1,0:T(8,128)(2,1)S(1)}, bf16[64,1024]{1,0:T(8,128)(2,1)S(1)}, u32[]{:S(2)}, u32[]{:S(2)}) collective-permute-start(bf16[64,1024]{1,0:T(8,128)(2,1)S(1)} %collective-permute-done.1.refs_4_), channel_id=1, source_target_pairs={{0,1},{1,2},{2,3},{3,4},{4,5},{5,6},{6,7},{7,0},{8,9},{9,10},{10,1... | collective-permute-start | bytes 393224 | tf_op jit(solution)/shard_map/ppermute | solution.py:347
  34.3 7.2 %collective-permute-start.12 = (bf16[64,1024]{1,0:T(8,128)(2,1)S(1)}, bf16[64,1024]{1,0:T(8,128)(2,1)S(1)}, u32[]{:S(2)}, u32[]{:S(2)}) collective-permute-start(bf16[64,1024]{1,0:T(8,128)(2,1)S(1)} %collective-permute-done.11.refs_14_), channel_id=1, source_target_pairs={{0,7},{1,0},{2,1},{3,2},{4,3},{5,4},{6,5},{7,6},{8,15},{9,8},{10,9... | collective-permute-start | bytes 393224 | tf_op jit(solution)/shard_map/ppermute | solution.py:347
  37.9 7.9 %collective-permute-start.6 = (bf16[64,1024]{1,0:T(8,128)(2,1)S(1)}, bf16[64,1024]{1,0:T(8,128)(2,1)S(1)}, u32[]{:S(2)}, u32[]{:S(2)}) collective-permute-start(bf16[64,1024]{1,0:T(8,128)(2,1)S(1)} %collective-permute-done.5.refs_8_), channel_id=1, source_target_pairs={{0,1},{1,2},{2,3},{3,4},{4,5},{5,6},{6,7},{7,0},{8,9},{9,10},{10,1... | collective-permute-start | bytes 393224 | tf_op jit(solution)/shard_map/ppermute | solution.py:347
  37.9 7.9 %collective-permute-start.9 = (bf16[64,1024]{1,0:T(8,128)(2,1)S(1)}, bf16[64,1024]{1,0:T(8,128)(2,1)S(1)}, u32[]{:S(2)}, u32[]{:S(2)}) collective-permute-start(bf16[64,1024]{1,0:T(8,128)(2,1)S(1)} %collective-permute-done.8.refs_11_), channel_id=1, source_target_pairs={{0,7},{1,0},{2,1},{3,2},{4,3},{5,4},{6,5},{7,6},{8,15},{9,8},{10,9... | collective-permute-start | bytes 393224 | tf_op jit(solution)/shard_map/ppermute | solution.py:347
  41.5 6.2 %collective-permute-start.3 = (bf16[64,1024]{1,0:T(8,128)(2,1)S(1)}, bf16[64,1024]{1,0:T(8,128)(2,1)S(1)}, u32[]{:S(2)}, u32[]{:S(2)}) collective-permute-start(bf16[64,1024]{1,0:T(8,128)(2,1)S(1)} %collective-permute-done.2.refs_5_), channel_id=1, source_target_pairs={{0,1},{1,2},{2,3},{3,4},{4,5},{5,6},{6,7},{7,0},{8,9},{9,10},{10,1... | collective-permute-start | bytes 393224 | tf_op jit(solution)/shard_map/ppermute | solution.py:347
  106.1 13.1 %collective-permute-start.29 = (bf16[32,1024]{1,0:T(8,128)(2,1)S(1)}, bf16[32,1024]{1,0:T(8,128)(2,1)S(1)}, u32[]{:S(2)}, u32[]{:S(2)}) collective-permute-start(bf16[32,1024]{1,0:T(8,128)(2,1)S(1)} %reduce_sum.12), channel_id=1, source_target_pairs={{0,1},{1,0},{2,3},{3,2},{4,5},{5,4},{6,7},{7,6},{8,9},{9,8},{10,11... | collective-permute-start | bytes 196616 | tf_op jit(solution)/shard_map/ppermute | solution.py:343
  106.7 7.6 %collective-permute-start.14 = (bf16[128,128]{1,0:T(8,128)(2,1)S(1)}, bf16[128,128]{1,0:T(8,128)(2,1)S(1)}, u32[]{:S(2)}, u32[]{:S(2)}) collective-permute-start(bf16[128,128]{1,0:T(8,128)(2,1)S(1)} %get-tuple-element.41), channel_id=1, source_target_pairs={{0,1},{1,2},{2,3},{3,4},{4,5},{5,6},{6,7},{7,0},{8,9},{9,10},{10,1... | collective-permute-start | bytes 98312 | tf_op jit(solution)/shard_map/ppermute | solution.py:347
  108.2 8.7 %collective-permute-start.15 = (bf16[128,128]{1,0:T(8,128)(2,1)S(1)}, bf16[128,128]{1,0:T(8,128)(2,1)S(1)}, u32[]{:S(2)}, u32[]{:S(2)}) collective-permute-start(bf16[128,128]{1,0:T(8,128)(2,1)S(1)} %get-tuple-element.42), channel_id=1, source_target_pairs={{0,2},{1,3},{2,4},{3,5},{4,6},{5,7},{6,0},{7,1},{8,10},{9,11},{10,... | collective-permute-start | bytes 98312 | tf_op jit(solution)/shard_map/ppermute | solution.py:347
  109.0 11.7 %collective-permute-start.16 = (bf16[128,128]{1,0:T(8,128)(2,1)S(1)}, bf16[128,128]{1,0:T(8,128)(2,1)S(1)}, u32[]{:S(2)}, u32[]{:S(2)}) collective-permute-start(bf16[128,128]{1,0:T(8,128)(2,1)S(1)} %get-tuple-element.43), channel_id=1, source_target_pairs={{0,3},{1,4},{2,5},{3,6},{4,7},{5,0},{6,1},{7,2},{8,11},{9,12},{10,... | collective-permute-start | bytes 98312 | tf_op jit(solution)/shard_map/ppermute | solution.py:347
  111.5 10.0 %collective-permute-start.17 = (bf16[128,128]{1,0:T(8,128)(2,1)S(1)}, bf16[128,128]{1,0:T(8,128)(2,1)S(1)}, u32[]{:S(2)}, u32[]{:S(2)}) collective-permute-start(bf16[128,128]{1,0:T(8,128)(2,1)S(1)} %get-tuple-element.44), channel_id=1, source_target_pairs={{0,4},{1,5},{2,6},{3,7},{4,0},{5,1},{6,2},{7,3},{8,12},{9,13},{10,... | collective-permute-start | bytes 98312 | tf_op jit(solution)/shard_map/ppermute | solution.py:347
  114.4 7.1 %collective-permute-start.18 = (bf16[128,128]{1,0:T(8,128)(2,1)S(1)}, bf16[128,128]{1,0:T(8,128)(2,1)S(1)}, u32[]{:S(2)}, u32[]{:S(2)}) collective-permute-start(bf16[128,128]{1,0:T(8,128)(2,1)S(1)} %get-tuple-element.45), channel_id=1, source_target_pairs={{0,5},{1,6},{2,7},{3,0},{4,1},{5,2},{6,3},{7,4},{8,13},{9,14},{10,... | collective-permute-start | bytes 98312 | tf_op jit(solution)/shard_map/ppermute | solution.py:347
  116.9 6.7 %collective-permute-start.19 = (bf16[128,128]{1,0:T(8,128)(2,1)S(1)}, bf16[128,128]{1,0:T(8,128)(2,1)S(1)}, u32[]{:S(2)}, u32[]{:S(2)}) collective-permute-start(bf16[128,128]{1,0:T(8,128)(2,1)S(1)} %get-tuple-element.46), channel_id=1, source_target_pairs={{0,6},{1,7},{2,0},{3,1},{4,2},{5,3},{6,4},{7,5},{8,14},{9,15},{10,... | collective-permute-start | bytes 98312 | tf_op jit(solution)/shard_map/ppermute | solution.py:347
  120.7 10.5 %collective-permute-start.30 = (bf16[32,1024]{1,0:T(8,128)(2,1)S(1)}, bf16[32,1024]{1,0:T(8,128)(2,1)S(1)}, u32[]{:S(2)}, u32[]{:S(2)}) collective-permute-start(bf16[32,1024]{1,0:T(8,128)(2,1)S(1)} %add_convert_fusion.2), channel_id=1, source_target_pairs={{0,3},{1,2},{2,1},{3,0},{4,7},{5,6},{6,5},{7,4},{8,11},{9,10},{10,... | collective-permute-start | bytes 196616 | tf_op jit(solution)/shard_map/ppermute | solution.py:343
  127.8 12.7 %collective-permute-start.21 = (bf16[128,384]{1,0:T(8,128)(2,1)S(1)}, bf16[128,384]{1,0:T(8,128)(2,1)S(1)}, u32[]{:S(2)}, u32[]{:S(2)}) collective-permute-start(bf16[128,384]{1,0:T(8,128)(2,1)S(1)} %get-tuple-element.52), channel_id=1, source_target_pairs={{0,1},{1,2},{2,3},{3,4},{4,5},{5,6},{6,7},{7,0},{8,9},{9,10},{10,1... | collective-permute-start | bytes 294920 | tf_op jit(solution)/shard_map/ppermute | solution.py:347
  128.8 14.5 %collective-permute-start.22 = (bf16[128,384]{1,0:T(8,128)(2,1)S(1)}, bf16[128,384]{1,0:T(8,128)(2,1)S(1)}, u32[]{:S(2)}, u32[]{:S(2)}) collective-permute-start(bf16[128,384]{1,0:T(8,128)(2,1)S(1)} %get-tuple-element.53), channel_id=1, source_target_pairs={{0,2},{1,3},{2,4},{3,5},{4,6},{5,7},{6,0},{7,1},{8,10},{9,11},{10,... | collective-permute-start | bytes 294920 | tf_op jit(solution)/shard_map/ppermute | solution.py:347
  131.2 15.1 %collective-permute-start.31 = (bf16[32,1024]{1,0:T(8,128)(2,1)S(1)}, bf16[32,1024]{1,0:T(8,128)(2,1)S(1)}, u32[]{:S(2)}, u32[]{:S(2)}) collective-permute-start(bf16[32,1024]{1,0:T(8,128)(2,1)S(1)} %add_convert_fusion.1), channel_id=1, source_target_pairs={{0,7},{1,6},{2,5},{3,4},{4,3},{5,2},{6,1},{7,0},{8,15},{9,14},{10,... | collective-permute-start | bytes 196616 | tf_op jit(solution)/shard_map/ppermute | solution.py:343
  136.0 12.0 %collective-permute-start.23 = (bf16[128,384]{1,0:T(8,128)(2,1)S(1)}, bf16[128,384]{1,0:T(8,128)(2,1)S(1)}, u32[]{:S(2)}, u32[]{:S(2)}) collective-permute-start(bf16[128,384]{1,0:T(8,128)(2,1)S(1)} %get-tuple-element.54), channel_id=1, source_target_pairs={{0,3},{1,4},{2,5},{3,6},{4,7},{5,0},{6,1},{7,2},{8,11},{9,12},{10,... | collective-permute-start | bytes 294920 | tf_op jit(solution)/shard_map/ppermute | solution.py:347
  137.3 10.8 %collective-permute-start.24 = (bf16[128,384]{1,0:T(8,128)(2,1)S(1)}, bf16[128,384]{1,0:T(8,128)(2,1)S(1)}, u32[]{:S(2)}, u32[]{:S(2)}) collective-permute-start(bf16[128,384]{1,0:T(8,128)(2,1)S(1)} %get-tuple-element.55), channel_id=1, source_target_pairs={{0,4},{1,5},{2,6},{3,7},{4,0},{5,1},{6,2},{7,3},{8,12},{9,13},{10,... | collective-permute-start | bytes 294920 | tf_op jit(solution)/shard_map/ppermute | solution.py:347
  140.5 11.3 %collective-permute-start.25 = (bf16[128,384]{1,0:T(8,128)(2,1)S(1)}, bf16[128,384]{1,0:T(8,128)(2,1)S(1)}, u32[]{:S(2)}, u32[]{:S(2)}) collective-permute-start(bf16[128,384]{1,0:T(8,128)(2,1)S(1)} %get-tuple-element.56), channel_id=1, source_target_pairs={{0,5},{1,6},{2,7},{3,0},{4,1},{5,2},{6,3},{7,4},{8,13},{9,14},{10,... | collective-permute-start | bytes 294920 | tf_op jit(solution)/shard_map/ppermute | solution.py:347
  143.3 12.1 %collective-permute-start.26 = (bf16[128,384]{1,0:T(8,128)(2,1)S(1)}, bf16[128,384]{1,0:T(8,128)(2,1)S(1)}, u32[]{:S(2)}, u32[]{:S(2)}) collective-permute-start(bf16[128,384]{1,0:T(8,128)(2,1)S(1)} %get-tuple-element.57), channel_id=1, source_target_pairs={{0,6},{1,7},{2,0},{3,1},{4,2},{5,3},{6,4},{7,5},{8,14},{9,15},{10,... | collective-permute-start | bytes 294920 | tf_op jit(solution)/shard_map/ppermute | solution.py:347
  146.3 10.2 %collective-permute-start.27 = (bf16[128,384]{1,0:T(8,128)(2,1)S(1)}, bf16[128,384]{1,0:T(8,128)(2,1)S(1)}, u32[]{:S(2)}, u32[]{:S(2)}) collective-permute-start(bf16[128,384]{1,0:T(8,128)(2,1)S(1)} %get-tuple-element.58), channel_id=1, source_target_pairs={{0,7},{1,0},{2,1},{3,2},{4,3},{5,4},{6,5},{7,6},{8,15},{9,8},{10,9... | collective-permute-start | bytes 294920 | tf_op jit(solution)/shard_map/ppermute | solution.py:347
  (12 other events, 263.0 us)
Sparse Core Ops, SparseCore 0:
  10.5 53.7 all-gather.2
  66.9 62.0 all-gather.4
